TPU v7x, 512 devices: a whole 4x4x16 slice. The times are simulated.
512 devices in a mesh: gx: 8 (over x, core), gy: 8 (over z_lo), gz: 8 (over z_hi, y).
Axes of the slice: x: 4, y: 4, z: 16 (z_hi: 2, z_lo: 8; z = z_hi * 8 + z_lo), core: 2. Of those that a mesh axis runs over, the one named last changes fastest.
Arguments:
- attn_out: bfloat16 [1408, 8192], P('gx', ('gz', 'gy')), may hold values from -6 to 6
- residual: bfloat16 [1408, 8192], P('gx', ('gy', 'gz')), may hold values from -60 to 60
- proj_weight: bfloat16 [8192, 8192], P(('gz', 'gx'), 'gy'), may hold values from -0.0625 to 0.0625
- norm_gain: float32 [8192], P(('gy', 'gz')), may hold values from 0.1 to 1.9
- gate_proj: bfloat16 [8192, 14336], P(('gy', 'gx'), 'gz'), may hold values from -0.0625 to 0.0625
- up_proj: bfloat16 [8192, 14336], P(('gy', 'gx'), 'gz'), may hold values from -0.0625 to 0.0625
- down_proj: bfloat16 [14336, 8192], P(('gz', 'gx'), 'gy'), may hold values from -0.046875 to 0.046875
Outputs:
- layer_out: bfloat16 [1408, 8192], P('gx', ('gy', 'gz'))
All inputs are finite; a program needn't handle non-finite values.
Results may differ from a plain program's by a relative error of at most 0.0029.
Values may be sent and summed in bfloat16 or wider, within the bound.
No kernel may reach another device: no remote copies, remote signals or barrier semaphores. Data moves between devices by JAX's collectives and lax.ppermute only.
A program may use at most 64 MiB of HBM per device.

v0:
```python
import jax
import jax.numpy as jnp
from jax import lax
from jax.sharding import Mesh
from jax.sharding import PartitionSpec as P

D = 8192
GX = ("gx_0", "gx_1")
GZ_GX = ("gz", "gx_0", "gx_1")
GY_GX = ("gy", "gx_0", "gx_1")


def in_order(parts, dim):
    shape = list(parts.shape[1:])
    shape[dim] *= parts.shape[0]
    return jnp.moveaxis(parts, 0, dim).reshape(shape)


def from_everyone(value, axis):
    copies = jnp.broadcast_to(value, (lax.axis_size(axis), *value.shape))
    return lax.all_to_all(copies, axis, split_axis=0, concat_axis=0, tiled=True)


def gather_directly(value, axis, dim):
    return in_order(from_everyone(value, axis), dim)


def split_up(value, dim, size):
    shape = value.shape
    parts = value.reshape(*shape[:dim], size, shape[dim] // size, *shape[dim + 1 :])
    return jnp.moveaxis(parts, dim, 0)


def summed_on_arrival(value, axis, dim):
    parts = split_up(value, dim, lax.axis_size(axis))
    arrived = lax.all_to_all(parts, axis, split_axis=0, concat_axis=0, tiled=True)
    return arrived.sum(axis=0)


def over_copies(value, axis):
    return from_everyone(value, axis).sum(axis=0)


def sent_together(arrays, axis, dim, along):
    ends, at = ([], 0)
    for a in arrays[:-1]:
        at += a.shape[along]
        ends.append(at)
    both = jnp.concatenate(arrays, axis=along)
    return tuple(jnp.split(lax.all_gather(both, axis, axis=dim, tiled=True), ends, axis=along))


def side_by_side(arrays, axis, dim, along):
    widths = [a.shape[along] for a in arrays]
    both = jnp.concatenate(arrays, axis=along)
    whole = lax.psum_scatter(both, axis, scatter_dimension=dim, tiled=True)
    return tuple(jnp.split(whole, [sum(widths[:k]) for k in range(1, len(widths))], axis=along))


def edges_of(length, count):
    hop = length // count
    if hop >= 8:
        hop -= hop % 8
    return [hop * k for k in range(1, count)]


def all_blocks(value, axes, turns):
    parts = value
    for k in turns:
        parts = lax.all_gather(parts, axes[k])
    done = turns[::-1]
    back = [done.index(k) for k in range(len(axes))]
    parts = parts.transpose(*back, *range(len(axes), parts.ndim))
    return parts.reshape(-1, *value.shape)


def spread_gather(value, axes, dim):
    cut = max(range(max(1, value.ndim - 1)), key=lambda d: value.shape[d])
    count, outs = (len(axes), [])
    for initial, share in enumerate(jnp.split(value, edges_of(value.shape[cut], count), axis=cut)):
        if share.size:
            turns = [(initial - k) % count for k in range(count)]
            outs.append(all_blocks(share, axes, turns))
    return in_order(jnp.concatenate(outs, axis=cut + 1), dim)


def add_block(lefts, pieces):
    return jnp.dot(lefts, pieces, preferred_element_type=jnp.float32)


def on_device(attn_out, residual, proj_weight, norm_gain, gate_proj, up_proj, down_proj):
    attn_cols = gather_directly(attn_out, "gy", 1)
    proj_partial = add_block(attn_cols, gather_directly(proj_weight, GX, 0))
    projected = summed_on_arrival(proj_partial, "gz", 1)
    stream = residual.astype(jnp.float32) + projected
    squares = over_copies(jnp.sum(stream * stream, axis=1), ("gy", "gz"))
    scaled = (stream * norm_gain[None, :]).astype(jnp.bfloat16)
    model_cols = gather_directly(scaled, "gz", 1)
    inverse = lax.rsqrt(squares / D + 1e-05)[:, None]
    pieces = sent_together((gate_proj, up_proj), GX, 0, 1)
    gate_part = add_block(model_cols, pieces[0])
    up_part = add_block(model_cols, pieces[1])
    gate_sum, up_sum = side_by_side((gate_part, up_part), "gy", 1, 0)
    hidden = (jax.nn.silu(inverse * gate_sum) * (inverse * up_sum)).astype(jnp.bfloat16)
    hidden_cols = gather_directly(hidden, "gy", 1)
    down_partial = add_block(hidden_cols, spread_gather(down_proj, GX, 0))
    down_sum = summed_on_arrival(down_partial, "gz", 1)
    return (stream + down_sum).astype(jnp.bfloat16)


def solution(mesh):
    split = Mesh(
        mesh.devices.reshape(4, 2, mesh.shape["gy"], mesh.shape["gz"]), ("gx_0", "gx_1", "gy", "gz")
    )
    in_specs = (
        P(GX, ("gz", "gy")),
        P(GX, ("gy", "gz")),
        P(GZ_GX, "gy"),
        P(("gy", "gz")),
        P(GY_GX, "gz"),
        P(GY_GX, "gz"),
        P(GZ_GX, "gy"),
    )
    out_specs = P(GX, ("gy", "gz"))
    return jax.shard_map(
        on_device, mesh=split, in_specs=in_specs, out_specs=out_specs, check_vma=False
    )
```

profile of v0, /device:TPU:34, one launch (start us, length us, event | category | flops | bytes accessed | tf_op | source)
XLA Modules:
  0.0 361.7 jit_solution(11354125520535368602)
XLA Ops:
  7.4 2.2 pad_maximum_fusion.2
  9.6 0.8 broadcast_in_dim.17
  10.4 12.6 %all-to-all-start = ((bf16[8,176,128]{2,1,0:T(8,128)(2,1)}), bf16[8,176,128]{2,1,0:T(8,128)(2,1)S(1)}, u32[]{:S(2)}, u32[]{:S(2)}) async-start(bf16[8,176,128]{2,1,0:T(8,128)(2,1)} %broadcast_in_dim.17), calls=%async_computation | async-start | bytes 720896 | tf_op jit(solution)/shard_map/all_to_all | solution.py:21
  23.0 0.2 copy.41
  23.2 20.0 %all-to-all-done = bf16[8,176,128]{2,1,0:T(8,128)(2,1)S(1)} async-done(((bf16[8,176,128]{2,1,0:T(8,128)(2,1)}), bf16[8,176,128]{2,1,0:T(8,128)(2,1)S(1)}, u32[]{:S(2)}, u32[]{:S(2)}) %all-to-all-start) | async-done | bytes 360480 | tf_op jit(solution)/shard_map/all_to_all | solution.py:21
  43.2 1.7 broadcast_in_dim.18
  44.9 4.8 %all-to-all-start.1 = ((bf16[8,128,1024]{1,2,0:T(8,128)(2,1)}), bf16[8,128,1024]{1,2,0:T(8,128)(2,1)S(1)}, u32[]{:S(2)}, u32[]{:S(2)}) async-start(bf16[8,128,1024]{1,2,0:T(8,128)(2,1)} %broadcast_in_dim.18), calls=%async_computation.1 | async-start | bytes 4194304 | tf_op jit(solution)/shard_map/all_to_all | solution.py:21
  49.7 0.1 copy.40
  49.8 0.2 reshape.47
  50.0 38.0 %all-to-all-done.1 = bf16[8,128,1024]{1,2,0:T(8,128)(2,1)S(1)} async-done(((bf16[8,128,1024]{1,2,0:T(8,128)(2,1)}), bf16[8,128,1024]{1,2,0:T(8,128)(2,1)S(1)}, u32[]{:S(2)}, u32[]{:S(2)}) %all-to-all-start.1) | async-done | bytes 2097184 | tf_op jit(solution)/shard_map/all_to_all | solution.py:21
  88.0 2.6 copy.42
  90.6 2.9 copy.43
  93.5 0.8 convolution_bitcast_fusion.1
  94.3 57.8 %all_to_all.36 = f32[8,176,128]{2,1,0:T(8,128)S(1)} all-to-all(f32[8,176,128]{2,1,0:T(8,128)S(1)} %convolution_bitcast_fusion.1), channel_id=1, replica_groups=mesh['gx_0'=4,'gx_1'=2,'gy'=8,'gz'=8] {'gz'}, dimensions={0} | all-to-all | bytes 1441792 | tf_op jit(solution)/shard_map/all_to_all | solution.py:36
  152.2 0.1 multiply_reduce_fusion
  152.4 19.2 %all_to_all.37 = bf16[8,176,128]{2,1,0:T(8,128)(2,1)S(1)} all-to-all(bf16[8,176,128]{2,1,0:T(8,128)(2,1)S(1)} %broadcast_in_dim.20), channel_id=1, replica_groups=mesh['gx_0'=4,'gx_1'=2,'gy'=8,'gz'=8] {'gz'}, dimensions={0} | all-to-all | bytes 720896 | tf_op jit(solution)/shard_map/all_to_all | solution.py:21
  171.6 2.9 fusion
  174.5 2.9 fusion.2
  177.3 0.2 pad_maximum_fusion.1
  177.5 2.2 copy.49
  179.7 0.0 all-gather.10.cloned.1.call-start
  179.7 0.9 copy-done
  180.7 14.7 %all-gather = bf16[448,1024]{1,0:T(8,128)(2,1)} all-gather(bf16[112,1024]{1,0:T(8,128)(2,1)S(1)} %get-tuple-element.5), channel_id=2, replica_groups=mesh['gx_0'=4,'gx_1'=2,'gy'=8,'gz'=8] {'gx_0'}, dimensions={0}, use_global_device_ids=true | all-gather | bytes 1146880 | tf_op jit(solution)/shard_map/all_gather | solution.py:70
  195.5 0.0 all-gather.10.cloned.1.call-update
  195.5 0.7 broadcast_in_dim.19
  196.1 8.6 %all-to-all-start.3 = ((f32[64,1,176]{2,1,0:T(1,128)}), f32[64,1,176]{2,1,0:T(1,128)S(1)}, u32[]{:S(2)}, u32[]{:S(2)}) async-start(f32[64,1,176]{2,1,0:T(1,128)} %broadcast_in_dim.19), calls=%async_computation.3 | async-start | bytes 131072 | tf_op jit(solution)/shard_map/all_to_all | solution.py:21
  204.7 0.0 all-gather.12.cloned.1.call-start
  204.8 2.3 all-gather.2
  207.1 0.0 all-gather.12.cloned.1.call-update
  207.1 13.9 %all-to-all-done.3 = f32[64,1,176]{2,1,0:T(1,128)S(1)} async-done(((f32[64,1,176]{2,1,0:T(1,128)}), f32[64,1,176]{2,1,0:T(1,128)S(1)}, u32[]{:S(2)}, u32[]{:S(2)}) %all-to-all-start.3) | async-done | bytes 45088 | tf_op jit(solution)/shard_map/all_to_all | solution.py:21
  220.9 0.1 reduce_sum.38
  221.0 28.8 %reduce-scatter.4.cloned.1.call-done = f32[224,352]{1,0:T(8,128)} async-done(((f32[1792,352]{1,0:T(8,128)}), f32[224,352]{1,0:T(8,128)}) %reduce-scatter.4.cloned.1.call-update) | async-done | bytes 315408
  249.8 1.2 fusion.9
  251.0 0.1 copy.52
  251.1 0.1 copy.53
  251.3 0.1 multiply_convert_fusion
  251.4 0.9 broadcast_in_dim.21
  252.3 10.4 %all-to-all-start.5 = ((bf16[8,176,224]{2,1,0:T(8,128)(2,1)}), bf16[8,176,224]{2,1,0:T(8,128)(2,1)S(1)}, u32[]{:S(2)}, u32[]{:S(2)}) async-start(bf16[8,176,224]{2,1,0:T(8,128)(2,1)} %broadcast_in_dim.21), calls=%async_computation.5 | async-start | bytes 1441792 | tf_op jit(solution)/shard_map/all_to_all | solution.py:21
  262.7 1.7 copy.47
  264.4 0.0 all-gather.12.cloned.1.call-done
  264.4 3.9 %pad_maximum_fusion = bf16[8,224,1024]{2,1,0:T(8,128)(2,1)} fusion(bf16[8,112,1024]{2,1,0:T(8,128)(2,1)} %all-gather.12.cloned.1.call-done, bf16[8,112,1024]{2,1,0:T(8,128)(2,1)S(1)} %bitcast.44), kind=kLoop, calls=%fused_computation.4 | loop fusion | flops 7340032 | bytes 7340032 | tf_op jit(solution)/shard_map/concatenate | solution.py:84
  268.3 6.0 %copy.48 = bf16[1024,1792]{1,0:T(8,128)(2,1)} copy(bf16[1024,1792]{0,1:T(8,128)(2,1)} %bitcast.40) | data formatting | bytes 7340032 | tf_op jit(solution)/shard_map/dot_general | solution.py:88
  274.3 21.1 %all-to-all-done.5 = bf16[8,176,224]{2,1,0:T(8,128)(2,1)S(1)} async-done(((bf16[8,176,224]{2,1,0:T(8,128)(2,1)}), bf16[8,176,224]{2,1,0:T(8,128)(2,1)S(1)}, u32[]{:S(2)}, u32[]{:S(2)}) %all-to-all-start.5) | async-done | bytes 630816 | tf_op jit(solution)/shard_map/all_to_all | solution.py:21
  295.4 0.2 copy.46
  295.6 0.9 reshape.48
  296.5 3.4 convolution_bitcast_fusion
  299.9 53.7 %all_to_all.38 = f32[8,176,128]{2,1,0:T(8,128)S(1)} all-to-all(f32[8,176,128]{2,1,0:T(8,128)S(1)} %convolution_bitcast_fusion), channel_id=1, replica_groups=mesh['gx_0'=4,'gx_1'=2,'gy'=8,'gz'=8] {'gz'}, dimensions={0} | all-to-all | bytes 1441792 | tf_op jit(solution)/shard_map/all_to_all | solution.py:36
  353.6 0.6 add_convert_fusion
  (20 shorter events, 0.2 us)
Async XLA Ops:
  7.4 2.2 copy-start.3
  7.4 15.6 %copy-start.1 = (bf16[128,1024]{1,0:T(8,128)(2,1)S(1)}, bf16[128,1024]{1,0:T(8,128)(2,1)}, u32[]{:S(2)}) copy-start(bf16[128,1024]{1,0:T(8,128)(2,1)} %param.9) | copy-start | bytes 786436
  7.4 164.2 %all-gather.8.cloned.1.call-start = ((), (), s32[]{:S(2)}) async-start(), calls=%async_computation.8 | async-start | bytes 8257536 | tf_op jit(solution)/shard_map/all_gather | solution.py:50
  10.4 32.8 %all-to-all-start = ((bf16[8,176,128]{2,1,0:T(8,128)(2,1)}), bf16[8,176,128]{2,1,0:T(8,128)(2,1)S(1)}, u32[]{:S(2)}, u32[]{:S(2)}) async-start(bf16[8,176,128]{2,1,0:T(8,128)(2,1)} %broadcast_in_dim.17), calls=%async_computation | async-start | bytes 720896 | tf_op jit(solution)/shard_map/all_to_all | solution.py:21
  44.9 43.1 %all-to-all-start.1 = ((bf16[8,128,1024]{1,2,0:T(8,128)(2,1)}), bf16[8,128,1024]{1,2,0:T(8,128)(2,1)S(1)}, u32[]{:S(2)}, u32[]{:S(2)}) async-start(bf16[8,128,1024]{1,2,0:T(8,128)(2,1)} %broadcast_in_dim.18), calls=%async_computation.1 | async-start | bytes 4194304 | tf_op jit(solution)/shard_map/all_to_all | solution.py:21
  49.7 200.1 %reduce-scatter.4.cloned.1.call-start = ((), (), s32[]{:S(2)}) async-start(), calls=%async_computation.11 | async-start | bytes 3096576
  93.4 58.7 %copy-start.2 = (bf16[176,128]{1,0:T(8,128)(2,1)S(1)}, bf16[176,128]{1,0:T(8,128)(2,1)}, u32[]{:S(2)}) copy-start(bf16[176,128]{1,0:T(8,128)(2,1)} %param.8) | copy-start | bytes 135172
  93.5 58.7 %copy-start.4 = (f32[128]{0:T(128)S(1)}, f32[128]{0:T(128)}, u32[]{:S(2)}) copy-start(f32[128]{0:T(128)} %param.10) | copy-start | bytes 1540
  179.7 1.0 copy-start
  179.7 83.0 %all-gather.10.cloned.1.call-start = ((), (), s32[]{:S(2)}) async-start(), calls=%async_computation.9 | async-start | bytes 2752512 | tf_op jit(solution)/shard_map/all_gather | solution.py:70
  196.1 24.8 %all-to-all-start.3 = ((f32[64,1,176]{2,1,0:T(1,128)}), f32[64,1,176]{2,1,0:T(1,128)S(1)}, u32[]{:S(2)}, u32[]{:S(2)}) async-start(f32[64,1,176]{2,1,0:T(1,128)} %broadcast_in_dim.19), calls=%async_computation.3 | async-start | bytes 131072 | tf_op jit(solution)/shard_map/all_to_all | solution.py:21
  204.7 59.7 %all-gather.12.cloned.1.call-start = ((), (), s32[]{:S(2)}) async-start(), calls=%async_computation.10 | async-start | bytes 2293760 | tf_op jit(solution)/shard_map/all_gather | solution.py:70
  252.3 43.1 %all-to-all-start.5 = ((bf16[8,176,224]{2,1,0:T(8,128)(2,1)}), bf16[8,176,224]{2,1,0:T(8,128)(2,1)S(1)}, u32[]{:S(2)}, u32[]{:S(2)}) async-start(bf16[8,176,224]{2,1,0:T(8,128)(2,1)} %broadcast_in_dim.21), calls=%async_computation.5 | async-start | bytes 1441792 | tf_op jit(solution)/shard_map/all_to_all | solution.py:21
Sparse Core Ops, SparseCore 0:
  10.3 72.2 all-gather.7
  179.8 69.9 reduce-scatter.3
Sparse Core Ops, SparseCore 1:
  195.6 14.5 all-gather.9
  212.1 36.4 all-gather.11
where the time goes:
time: 363 us; the launch traced here: 362 us
  blocking collectives  148 us (41%)
  waiting for transfers between devices  122 us (34%)
  starting transfers between devices  36.5 us (10%)
  local copies, waits for them, and re-layouts  23.3 us (6%)
  between operations  15 us (4%)
  matrix products  9.94 us (3%)
  other arithmetic  7.31 us (2%)
    all_to_all x2, blocking collectives, summed_on_arrival(): lax.all_to_all(parts, axis, split_axis=0, concat_axis=0, tiled=True)  111 us
    all_to_all x4, waiting for transfers between devices, from_everyone(): return lax.all_to_all(copies, axis, split_axis=0, concat_axis=0, tiled=True)  93 us
    all_to_all x4, starting transfers between devices, from_everyone(): return lax.all_to_all(copies, axis, split_axis=0, concat_axis=0, tiled=True)  36.4 us
    unnamed x5, waiting for transfers between devices  28.9 us
    all_to_all x1, blocking collectives, from_everyone(): return lax.all_to_all(copies, axis, split_axis=0, concat_axis=0, tiled=True)  19.2 us
    all_gather x2, blocking collectives, all_blocks(): parts = lax.all_gather(parts, axes[k])  17 us
    dot_general x4, matrix products, add_block(): return jnp.dot(lefts, pieces, preferred_element_type=jnp.float32)  9.94 us
    dot_general x2, local copies, waits for them, and re-layouts, add_block(): return jnp.dot(lefts, pieces, preferred_element_type=jnp.float32)  8.82 us
  transfers between devices with their start and end apart: 8, of which 5 were waited for; matrix products, arithmetic and copies ran while one was open for 7% of the time, Pallas kernels for 0%

commit v1 on v0

v1 whole, which is shorter than its diff:
```python
import jax
import jax.numpy as jnp
from jax import lax
from jax.sharding import Mesh
from jax.sharding import PartitionSpec as P

D = 8192
BF = jnp.bfloat16
F32 = jnp.float32
AXES = ("x", "c", "zl", "zh", "y")


def shift(value, axis, step):
    n = lax.axis_size(axis)
    return lax.ppermute(value, axis, [(i, (i + step) % n) for i in range(n)])


def swap(value, axis, bit=1):
    n = lax.axis_size(axis)
    return lax.ppermute(value, axis, [(i, i ^ bit) for i in range(n)])


def pick(value, index, dim=0):
    return lax.dynamic_index_in_dim(value, index, dim, keepdims=False)


def from_everyone(value, axis):
    copies = jnp.broadcast_to(value, (lax.axis_size(axis), *value.shape))
    return lax.all_to_all(copies, axis, split_axis=0, concat_axis=0, tiled=True)


def in_bits(own, other, bit):
    first = jnp.where(bit == 0, own, other)
    second = jnp.where(bit == 0, other, own)
    return first, second


def ring_shards(w):
    return [w, shift(w, "x", 1), shift(w, "x", 2), shift(w, "x", -1)]


def dot(a, b):
    return jnp.dot(a, b, preferred_element_type=F32)


def relative(blocks, xi, core):
    parts = [pick(pick(blocks, (xi - k) % 4), core) for k in range(4)]
    return jnp.concatenate(parts, axis=1)


def sums_over_y(part):
    blocks = part.astype(BF).reshape(-1, 2, 4, 128).transpose(2, 1, 0, 3)
    arrived = lax.all_to_all(blocks, "y", split_axis=0, concat_axis=0, tiled=True)
    return arrived.astype(F32).sum(axis=0)


def exact(value):
    return lax.reduce_precision(value, 8, 7)


def on_device(attn_out, residual, proj_weight, norm_gain, gate_proj, up_proj, down_proj):
    xi, ci = lax.axis_index("x"), lax.axis_index("c")
    zl, zh = lax.axis_index("zl"), lax.axis_index("zh")
    bit0, bit1, bit2 = zl & 1, (zl >> 1) & 1, (zl >> 2) & 1
    rows = attn_out.shape[0]
    half = rows // 2
    top = 48
    step = half - top
    ffw = gate_proj.shape[1] // 2

    proj_own = jnp.concatenate(ring_shards(proj_weight))
    proj_other = swap(proj_own, "c")
    cols = from_everyone(attn_out, "zl").reshape(4, 2, rows, 128)

    high = exact(norm_gain)
    mid = exact(norm_gain - high)
    low = norm_gain - high - mid
    gains = jnp.stack([high, mid, low]).astype(BF)
    facing = swap(jnp.concatenate([residual, jnp.pad(gains, ((0, 5), (0, 0)))]), "zh")
    other_gain = facing[rows : rows + 3].astype(F32).sum(axis=0)
    residual2 = jnp.stack(in_bits(residual, facing[:rows], zh)).astype(F32)
    gain2 = jnp.stack(in_bits(norm_gain, other_gain, zh))

    pieces = [gate_proj[:, :ffw], up_proj[:, :ffw], gate_proj[:, ffw:], up_proj[:, ffw:]]
    both_own = jnp.concatenate(ring_shards(jnp.concatenate(pieces, axis=1)))
    both_other = swap(both_own, "c")
    down_own = jnp.concatenate(ring_shards(down_proj))
    down_other = swap(down_own, "c")
    height = down_proj.shape[0]
    down_all = jnp.zeros((4, 2, height, down_proj.shape[1]), BF)
    for k in range(4):
        at = (xi - k) % 4
        mine = down_own[k * height : (k + 1) * height][None, None]
        theirs = down_other[k * height : (k + 1) * height][None, None]
        down_all = lax.dynamic_update_slice(down_all, mine, (at, ci, 0, 0))
        down_all = lax.dynamic_update_slice(down_all, theirs, (at, 1 - ci, 0, 0))
    down_all = down_all.reshape(8 * height, -1)

    part = dot(relative(cols, xi, ci), proj_own) + dot(relative(cols, xi, 1 - ci), proj_other)
    near = sums_over_y(part)
    stream2 = residual2 + near + swap(near.astype(BF), "zh").astype(F32)
    squares = jnp.sum(stream2 * stream2, axis=(0, 2))
    scaled2 = (stream2 * gain2[:, None, :]).astype(BF)
    squares = jnp.pad(squares, (0, 256 - rows)).reshape(2, 128)
    high = exact(squares)
    tail = jnp.concatenate([high, squares - high, jnp.zeros((4, 128), F32)]).astype(BF)
    sent = jnp.concatenate([scaled2.reshape(2 * rows, 128), tail])
    arrived = from_everyone(sent, "y")
    squares = arrived[:, 2 * rows : 2 * rows + 4].astype(F32).sum(axis=0)
    squares = squares[:2] + squares[2:]
    model = arrived[:, : 2 * rows].reshape(2, 2, 2, rows, 128)
    model = model.transpose(2, 0, 1, 3, 4).reshape(4, 2, rows, 128)

    both = dot(relative(model, xi, ci), both_own) + dot(relative(model, xi, 1 - ci), both_other)
    both = both.reshape(2, half, 4 * ffw)
    got = swap(pick(both, 1 - bit0).astype(BF), "zl", 1)
    squares = squares + swap(squares, "zl", 1)
    both = (pick(both, bit0) + got.astype(F32)).reshape(half, 2, 2 * ffw)
    got = swap(pick(both, 1 - bit1, 1).astype(BF), "zl", 2)
    squares = squares + swap(squares, "zl", 2)
    both = pick(both, bit1, 1) + got.astype(F32)
    sent = lax.dynamic_slice_in_dim(both, step * (1 - bit2), top, 0)
    got = swap(sent.astype(BF), "zl", 4)
    squares = squares + swap(squares, "zl", 4)
    both = lax.dynamic_slice_in_dim(both, step * bit2, top, 0) + got.astype(F32)
    squares = lax.dynamic_slice_in_dim(squares.reshape(256), half * bit0 + step * bit2, top, 0)
    inverse = lax.rsqrt(squares / D + 1e-05)[:, None]
    gate_sum, up_sum = inverse * both[:, :ffw], inverse * both[:, ffw:]
    hidden = (jax.nn.silu(gate_sum) * up_sum).astype(BF)

    upper, lower = in_bits(hidden, swap(hidden, "zl", 4), bit2)
    hidden = jnp.concatenate([upper, lower[2 * top - half :]])
    hidden = jnp.stack(in_bits(hidden, swap(hidden, "zl", 2), bit1))
    hidden = jnp.stack(in_bits(hidden, swap(hidden, "zl", 1), bit0))
    hidden = hidden.transpose(0, 2, 1, 3).reshape(rows, 2 * ffw)

    near = sums_over_y(dot(hidden, down_all))
    far = swap(pick(near, 1 - zh).astype(BF), "zh")
    return (pick(stream2, zh) + pick(near, zh) + far.astype(F32)).astype(BF)


def solution(mesh):
    z = mesh.shape["gz"] // 4
    split = Mesh(mesh.devices.reshape(4, 2, mesh.shape["gy"], z, 4), AXES)
    gx, gz = ("x", "c"), ("zh", "y")
    in_specs = (
        P(gx, (*gz, "zl")),
        P(gx, ("zl", *gz)),
        P((*gz, *gx), "zl"),
        P(("zl", *gz)),
        P(("zl", *gx), gz),
        P(("zl", *gx), gz),
        P((*gz, *gx), "zl"),
    )
    return jax.shard_map(
        on_device, mesh=split, in_specs=in_specs, out_specs=P(gx, ("zl", *gz)), check_vma=False
    )
```

time: 363 us -> 289 us (0.80)
  the two profiles are of different devices: /device:TPU:34 before, /device:TPU:2 now
where the time goes in v1:
time: 289 us; the launch traced here: 288 us
  starting transfers between devices  124 us (43%)
  waiting for transfers between devices  112 us (39%)
  local copies, waits for them, and re-layouts  23.9 us (8%)
  other arithmetic  15.8 us (5%)
  matrix products  10.7 us (4%)
    ppermute x15, waiting for transfers between devices, swap(): return lax.ppermute(value, axis, [(i, i ^ bit) for i in range(n)])  62.6 us
    ppermute x15, starting transfers between devices, swap(): return lax.ppermute(value, axis, [(i, i ^ bit) for i in range(n)])  61.9 us
    ppermute x9, starting transfers between devices, shift(): return lax.ppermute(value, axis, [(i, (i + step) % n) for i in range(n)])  35.3 us
    ppermute x9, waiting for transfers between devices, shift(): return lax.ppermute(value, axis, [(i, (i + step) % n) for i in range(n)])  31.7 us
    all_to_all x2, waiting for transfers between devices, sums_over_y(): lax.all_to_all(blocks, 'y', split_axis=0, concat_axis=0, tiled=True)  14.2 us
    all_to_all x2, starting transfers between devices, sums_over_y(): lax.all_to_all(blocks, 'y', split_axis=0, concat_axis=0, tiled=True)  13.9 us
    all_to_all x2, starting transfers between devices, from_everyone(): return lax.all_to_all(copies, axis, split_axis=0, concat_axis=0, tiled=True)  13 us
    dot_general x5, matrix products, dot(): return jnp.dot(a, b, preferred_element_type=F32)  10.7 us
  transfers between devices with their start and end apart: 28, of which 14 were waited for; matrix products, arithmetic and copies ran while one was open for 13% of the time, Pallas kernels for 0%

profile of v1, /device:TPU:2, one launch (start us, length us, event | category | flops | bytes accessed | tf_op | source)
XLA Modules:
  0.0 287.6 jit_solution(425879261301079774)
XLA Ops:
  2.4 7.8 %collective-permute-start.11 = (bf16[128,3584]{1,0:T(8,128)(2,1)}, bf16[128,3584]{1,0:T(8,128)(2,1)}, u32[]{:S(2)}, u32[]{:S(2)}) collective-permute-start(bf16[128,3584]{1,0:T(8,128)(2,1)} %pad_maximum_fusion.2), channel_id=1, source_target_pairs={{0,384},{128,0},{256,128},{384,256},{1,385},{129,1},{257,129},{385... | collective-permute-start | bytes 2752520 | tf_op jit(solution)/shard_map/ppermute | solution.py:15
  10.2 1.9 collective-permute-start.10
  12.1 3.4 %collective-permute-start.9 = (bf16[128,3584]{1,0:T(8,128)(2,1)}, bf16[128,3584]{1,0:T(8,128)(2,1)}, u32[]{:S(2)}, u32[]{:S(2)}) collective-permute-start(bf16[128,3584]{1,0:T(8,128)(2,1)} %pad_maximum_fusion.2), channel_id=1, source_target_pairs={{0,128},{128,256},{256,384},{384,0},{1,129},{129,257},{257,385},{3... | collective-permute-start | bytes 2752520 | tf_op jit(solution)/shard_map/ppermute | solution.py:15
  15.5 4.5 %collective-permute-start.1 = (bf16[128,1024]{1,0:T(8,128)(2,1)S(1)}, bf16[128,1024]{1,0:T(8,128)(2,1)S(1)}, u32[]{:S(2)}, u32[]{:S(2)}) collective-permute-start(bf16[128,1024]{1,0:T(8,128)(2,1)S(1)} %copy-done.7), channel_id=1, source_target_pairs={{0,128},{128,256},{256,384},{384,0},{1,129},{129,257},{257,385},{3... | collective-permute-start | bytes 786440 | tf_op jit(solution)/shard_map/ppermute | solution.py:15
  20.0 1.9 collective-permute-start.2
  22.8 9.6 %all-to-all-start = ((bf16[8,176,128]{2,1,0:T(8,128)(2,1)}), bf16[8,176,128]{2,1,0:T(8,128)(2,1)S(1)}, u32[]{:S(2)}, u32[]{:S(2)}) async-start(bf16[8,176,128]{2,1,0:T(8,128)(2,1)} %broadcast_in_dim.38), calls=%async_computation | async-start | bytes 720896 | tf_op jit(solution)/shard_map/all_to_all | solution.py:29
  32.4 26.0 %collective-permute-done.1 = bf16[128,1024]{1,0:T(8,128)(2,1)S(1)} collective-permute-done((bf16[128,1024]{1,0:T(8,128)(2,1)S(1)}, bf16[128,1024]{1,0:T(8,128)(2,1)S(1)}, u32[]{:S(2)}, u32[]{:S(2)}) %collective-permute-start.1) | collective-permute-done | bytes 262176 | tf_op jit(solution)/shard_map/ppermute | solution.py:15
  58.4 4.6 %collective-permute-start.3 = (bf16[128,1024]{1,0:T(8,128)(2,1)S(1)}, bf16[128,1024]{1,0:T(8,128)(2,1)S(1)}, u32[]{:S(2)}, u32[]{:S(2)}) collective-permute-start(bf16[128,1024]{1,0:T(8,128)(2,1)S(1)} %copy-done.7), channel_id=1, source_target_pairs={{0,384},{128,0},{256,128},{384,256},{1,385},{129,1},{257,129},{385... | collective-permute-start | bytes 786440 | tf_op jit(solution)/shard_map/ppermute | solution.py:15
  63.1 5.6 %collective-permute-done.3 = bf16[128,1024]{1,0:T(8,128)(2,1)S(1)} collective-permute-done((bf16[128,1024]{1,0:T(8,128)(2,1)S(1)}, bf16[128,1024]{1,0:T(8,128)(2,1)S(1)}, u32[]{:S(2)}, u32[]{:S(2)}) %collective-permute-start.3) | collective-permute-done | bytes 262176 | tf_op jit(solution)/shard_map/ppermute | solution.py:15
  68.8 2.1 collective-permute-start.4
  70.9 7.8 %pad_maximum_fusion = bf16[512,3584]{1,0:T(8,128)(2,1)} fusion(bf16[128,3584]{1,0:T(8,128)(2,1)} %collective-permute-done.11, bf16[128,3584]{1,0:T(8,128)(2,1)} %collective-permute-done.10, bf16[128,3584]{1,0:T(8,128)(2,1)} %collective-permute-done.9, bf16[128,896]{1,0:T(8,128)(2,1)S(1)} %get-tuple-element.40, bf16[128,896]{1,0:T(8,128)(2,1)S(1)} %get-tuple-element.10, ...), kind=kLoop, calls=%fused_computation.1 | loop fusion | flops 25690112 | bytes 7340032 | tf_op jit(solution)/shard_map/concatenate | solution.py:85
  78.7 2.4 collective-permute-start.12
  81.2 14.2 %collective-permute-start = (bf16[184,128]{1,0:T(8,128)(2,1)S(1)}, bf16[184,128]{1,0:T(8,128)(2,1)S(1)}, u32[]{:S(2)}, u32[]{:S(2)}) collective-permute-start(bf16[184,128]{1,0:T(8,128)(2,1)S(1)} %pad_maximum_fusion.5), channel_id=1, source_target_pairs={{0,4},{4,0},{1,5},{5,1},{2,6},{6,2},{3,7},{7,3},{8,12},{12,8},{9,1... | collective-permute-start | bytes 141320 | tf_op jit(solution)/shard_map/ppermute | solution.py:20
  95.4 4.4 %collective-permute-start.21 = (bf16[224,1024]{1,0:T(8,128)(2,1)S(1)}, bf16[224,1024]{1,0:T(8,128)(2,1)S(1)}, u32[]{:S(2)}, u32[]{:S(2)}) collective-permute-start(bf16[224,1024]{1,0:T(8,128)(2,1)S(1)} %copy-done), channel_id=1, source_target_pairs={{0,384},{128,0},{256,128},{384,256},{1,385},{129,1},{257,129},{385... | collective-permute-start | bytes 1376264 | tf_op jit(solution)/shard_map/ppermute | solution.py:15
  99.8 2.3 collective-permute-start.20
  102.2 4.5 %collective-permute-start.19 = (bf16[224,1024]{1,0:T(8,128)(2,1)S(1)}, bf16[224,1024]{1,0:T(8,128)(2,1)S(1)}, u32[]{:S(2)}, u32[]{:S(2)}) collective-permute-start(bf16[224,1024]{1,0:T(8,128)(2,1)S(1)} %copy-done), channel_id=1, source_target_pairs={{0,128},{128,256},{256,384},{384,0},{1,129},{129,257},{257,385},{3... | collective-permute-start | bytes 1376264 | tf_op jit(solution)/shard_map/ppermute | solution.py:15
  110.1 4.5 %all-to-all-start.1 = ((bf16[4,2,176,128]{3,1,2,0:T(2,128)(2,1)}), bf16[4,2,176,128]{3,1,2,0:T(2,128)(2,1)S(1)}, u32[]{:S(2)}, u32[]{:S(2)}) async-start(bf16[4,2,176,128]{3,1,2,0:T(2,128)(2,1)} %bitcast.122), calls=%async_computation.1 | async-start | bytes 720896 | tf_op jit(solution)/shard_map/all_to_all | solution.py:53
  114.7 7.0 %all-to-all-done.1 = bf16[4,2,176,128]{3,1,2,0:T(2,128)(2,1)S(1)} async-done(((bf16[4,2,176,128]{3,1,2,0:T(2,128)(2,1)}), bf16[4,2,176,128]{3,1,2,0:T(2,128)(2,1)S(1)}, u32[]{:S(2)}, u32[]{:S(2)}) %all-to-all-start.1) | async-done | bytes 360480 | tf_op jit(solution)/shard_map/all_to_all | solution.py:53
  121.9 7.8 %collective-permute-start.5 = (bf16[2,176,128]{2,0,1:T(2,128)(2,1)S(1)}, bf16[2,176,128]{2,0,1:T(2,128)(2,1)S(1)}, u32[]{:S(2)}, u32[]{:S(2)}) collective-permute-start(bf16[2,176,128]{2,0,1:T(2,128)(2,1)S(1)} %copy.66), channel_id=1, source_target_pairs={{0,4},{4,0},{1,5},{5,1},{2,6},{6,2},{3,7},{7,3},{8,12},{12,8},{9,1... | collective-permute-start | bytes 270344 | tf_op jit(solution)/shard_map/ppermute | solution.py:20
  129.7 7.7 %collective-permute-done.5 = bf16[2,176,128]{2,0,1:T(2,128)(2,1)S(1)} collective-permute-done((bf16[2,176,128]{2,0,1:T(2,128)(2,1)S(1)}, bf16[2,176,128]{2,0,1:T(2,128)(2,1)S(1)}, u32[]{:S(2)}, u32[]{:S(2)}) %collective-permute-start.5) | collective-permute-done | bytes 90144 | tf_op jit(solution)/shard_map/ppermute | solution.py:20
  139.7 3.5 %all-to-all-start.2 = ((bf16[4,360,128]{2,1,0:T(8,128)(2,1)}), bf16[4,360,128]{2,1,0:T(8,128)(2,1)S(1)}, u32[]{:S(2)}, u32[]{:S(2)}) async-start(bf16[4,360,128]{2,1,0:T(8,128)(2,1)} %broadcast_in_dim.40), calls=%async_computation.2 | async-start | bytes 737280 | tf_op jit(solution)/shard_map/all_to_all | solution.py:29
  144.8 1.9 collective-permute-start.22
  146.7 3.7 %all-to-all-done.2 = bf16[4,360,128]{2,1,0:T(8,128)(2,1)S(1)} async-done(((bf16[4,360,128]{2,1,0:T(8,128)(2,1)}), bf16[4,360,128]{2,1,0:T(8,128)(2,1)S(1)}, u32[]{:S(2)}, u32[]{:S(2)}) %all-to-all-start.2) | async-done | bytes 368672 | tf_op jit(solution)/shard_map/all_to_all | solution.py:29
  150.5 4.5 %collective-permute-start.6 = (f32[2,128]{1,0:T(2,128)S(1)}, f32[2,128]{1,0:T(2,128)S(1)}, u32[]{:S(2)}, u32[]{:S(2)}) collective-permute-start(f32[2,128]{1,0:T(2,128)S(1)} %slice_add_fusion), channel_id=1, source_target_pairs={{0,8},{8,0},{16,24},{24,16},{32,40},{40,32},{48,56},{56,48},{1,9},... | collective-permute-start | bytes 3080 | tf_op jit(solution)/shard_map/ppermute | solution.py:20
  156.5 4.8 %collective-permute-start.7 = (f32[2,128]{1,0:T(2,128)S(1)}, f32[2,128]{1,0:T(2,128)S(1)}, u32[]{:S(2)}, u32[]{:S(2)}) collective-permute-start(f32[2,128]{1,0:T(2,128)S(1)} %fusion.63), channel_id=1, source_target_pairs={{0,16},{8,24},{16,0},{24,8},{32,48},{40,56},{48,32},{56,40},{1,17}... | collective-permute-start | bytes 3080 | tf_op jit(solution)/shard_map/ppermute | solution.py:20
  161.4 2.9 %fusion.28 = f32[176,3584]{1,0:T(8,128)S(1)} fusion(bf16[512,3584]{1,0:T(8,128)(2,1)} %collective-permute-done.12, bf16[176,128]{1,0:T(8,128)(2,1)S(1)} %get-tuple-element.14, bf16[176,128]{1,0:T(8,128)(2,1)S(1)} %get-tuple-element.15, bf16[176,128]{1,0:T(8,128)(2,1)S(1)} %get-tuple-element.16, bf16[176,128]{1,0:T(8,128)(2,1)S(1)} %get-tuple-element.17), kind=kOutput, calls=%fused_computation.57 | convolution fusion | flops 646643712 | bytes 6373376 | tf_op jit(solution)/shard_map/dot_general | solution.py:43
  164.3 2.9 %convolution_add_fusion = f32[176,3584]{1,0:T(8,128)S(1)} fusion(f32[176,3584]{1,0:T(8,128)S(1)} %fusion.28, bf16[512,3584]{1,0:T(8,128)(2,1)} %pad_maximum_fusion, bf16[176,128]{1,0:T(8,128)(2,1)S(1)} %get-tuple-element.18, bf16[176,128]{1,0:T(8,128)(2,1)S(1)} %get-tuple-element.19, bf16[176,128]{1,0:T(8,128)(2,1)S(1)} %get-tuple-element.20, ...), kind=kOutput, calls=%fused_computation | convolution fusion | flops 647274496 | bytes 8896512 | tf_op jit(solution)/shard_map/dot_general | solution.py:43
  168.1 2.5 collective-permute-start.13
  170.6 2.3 broadcast_in_dim.41
  173.8 2.8 collective-permute-start.8
  176.6 6.5 %collective-permute-done.8 = f32[2,128]{1,0:T(2,128)S(1)} collective-permute-done((f32[2,128]{1,0:T(2,128)S(1)}, f32[2,128]{1,0:T(2,128)S(1)}, u32[]{:S(2)}, u32[]{:S(2)}) %collective-permute-start.8) | collective-permute-done | bytes 1056 | tf_op jit(solution)/shard_map/ppermute | solution.py:20
  185.1 2.4 bitcast_add_fusion
  187.4 2.1 reshape.82
  190.2 3.6 %collective-permute-start.14 = (bf16[88,1792]{1,0:T(8,128)(2,1)S(1)}, bf16[88,1792]{1,0:T(8,128)(2,1)S(1)}, u32[]{:S(2)}, u32[]{:S(2)}) collective-permute-start(bf16[88,1792]{1,0:T(8,128)(2,1)S(1)} %bitcast.134), channel_id=1, source_target_pairs={{0,16},{8,24},{16,0},{24,8},{32,48},{40,56},{48,32},{56,40},{1,17}... | collective-permute-start | bytes 946184 | tf_op jit(solution)/shard_map/ppermute | solution.py:20
  195.2 8.3 %collective-permute-done.14 = bf16[88,1792]{1,0:T(8,128)(2,1)S(1)} collective-permute-done((bf16[88,1792]{1,0:T(8,128)(2,1)S(1)}, bf16[88,1792]{1,0:T(8,128)(2,1)S(1)}, u32[]{:S(2)}, u32[]{:S(2)}) %collective-permute-start.14) | collective-permute-done | bytes 315424 | tf_op jit(solution)/shard_map/ppermute | solution.py:20
  203.7 3.3 %collective-permute-start.15 = (bf16[48,1792]{1,0:T(8,128)(2,1)S(1)}, bf16[48,1792]{1,0:T(8,128)(2,1)S(1)}, u32[]{:S(2)}, u32[]{:S(2)}) collective-permute-start(bf16[48,1792]{1,0:T(8,128)(2,1)S(1)} %dynamic-slice_convert_fusion.2), channel_id=1, source_target_pairs={{0,32},{8,40},{16,48},{24,56},{32,0},{40,8},{48,16},{56,24},{1,33}... | collective-permute-start | bytes 516104 | tf_op jit(solution)/shard_map/ppermute | solution.py:20
  208.8 14.3 %collective-permute-done.15 = bf16[48,1792]{1,0:T(8,128)(2,1)S(1)} collective-permute-done((bf16[48,1792]{1,0:T(8,128)(2,1)S(1)}, bf16[48,1792]{1,0:T(8,128)(2,1)S(1)}, u32[]{:S(2)}, u32[]{:S(2)}) %collective-permute-start.15) | collective-permute-done | bytes 172064 | tf_op jit(solution)/shard_map/ppermute | solution.py:20
  223.2 1.9 collective-permute-start.16
  226.0 7.5 %collective-permute-done.16 = bf16[48,896]{1,0:T(8,128)(2,1)S(1)} collective-permute-done((bf16[48,896]{1,0:T(8,128)(2,1)S(1)}, bf16[48,896]{1,0:T(8,128)(2,1)S(1)}, u32[]{:S(2)}, u32[]{:S(2)}) %collective-permute-start.16) | collective-permute-done | bytes 86048 | tf_op jit(solution)/shard_map/ppermute | solution.py:20
  233.7 1.9 collective-permute-start.17
  237.5 4.3 %collective-permute-done.17 = bf16[88,896]{1,0:T(8,128)(2,1)S(1)} collective-permute-done((bf16[88,896]{1,0:T(8,128)(2,1)S(1)}, bf16[88,896]{1,0:T(8,128)(2,1)S(1)}, u32[]{:S(2)}, u32[]{:S(2)}) %collective-permute-start.17) | collective-permute-done | bytes 157728 | tf_op jit(solution)/shard_map/ppermute | solution.py:20
  241.9 1.9 collective-permute-start.18
  246.4 4.3 %collective-permute-done.18 = bf16[2,88,896]{2,1,0:T(8,128)(2,1)S(1)} collective-permute-done((bf16[2,88,896]{2,1,0:T(8,128)(2,1)S(1)}, bf16[2,88,896]{2,1,0:T(8,128)(2,1)S(1)}, u32[]{:S(2)}, u32[]{:S(2)}) %collective-permute-start.18) | collective-permute-done | bytes 315424 | tf_op jit(solution)/shard_map/ppermute | solution.py:20
  251.4 2.9 %convolution_convert_fusion = bf16[176,1024]{1,0:T(8,128)(2,1)S(1)} fusion(bf16[176,1792]{1,0:T(8,128)(2,1)S(1)} %bitcast.126, bf16[1792,1024]{1,0:T(8,128)(2,1)} %bitcast.47), kind=kOutput, calls=%fused_computation.7 | convolution fusion | flops 646103040 | bytes 4661248 | tf_op jit(solution)/shard_map/dot_general | solution.py:43
  255.6 9.4 %all-to-all-start.3 = ((bf16[4,2,176,128]{3,1,2,0:T(2,128)(2,1)}), bf16[4,2,176,128]{3,1,2,0:T(2,128)(2,1)S(1)}, u32[]{:S(2)}, u32[]{:S(2)}) async-start(bf16[4,2,176,128]{3,1,2,0:T(2,128)(2,1)} %bitcast.121), calls=%async_computation.3 | async-start | bytes 720896 | tf_op jit(solution)/shard_map/all_to_all | solution.py:53
  265.0 7.2 %all-to-all-done.3 = bf16[4,2,176,128]{3,1,2,0:T(2,128)(2,1)S(1)} async-done(((bf16[4,2,176,128]{3,1,2,0:T(2,128)(2,1)}), bf16[4,2,176,128]{3,1,2,0:T(2,128)(2,1)S(1)}, u32[]{:S(2)}, u32[]{:S(2)}) %all-to-all-start.3) | async-done | bytes 360480 | tf_op jit(solution)/shard_map/all_to_all | solution.py:53
  272.3 6.3 %collective-permute-start.23 = (bf16[176,128]{1,0:T(8,128)(2,1)S(1)}, bf16[176,128]{1,0:T(8,128)(2,1)S(1)}, u32[]{:S(2)}, u32[]{:S(2)}) collective-permute-start(bf16[176,128]{1,0:T(8,128)(2,1)S(1)} %fusion.38), channel_id=1, source_target_pairs={{0,4},{4,0},{1,5},{5,1},{2,6},{6,2},{3,7},{7,3},{8,12},{12,8},{9,1... | collective-permute-start | bytes 135176 | tf_op jit(solution)/shard_map/ppermute | solution.py:20
  278.8 8.2 %collective-permute-done.23 = bf16[176,128]{1,0:T(8,128)(2,1)S(1)} collective-permute-done((bf16[176,128]{1,0:T(8,128)(2,1)S(1)}, bf16[176,128]{1,0:T(8,128)(2,1)S(1)}, u32[]{:S(2)}, u32[]{:S(2)}) %collective-permute-start.23) | collective-permute-done | bytes 45088 | tf_op jit(solution)/shard_map/ppermute | solution.py:20
  (110 shorter events, 28.5 us)
Async XLA Ops:
  0.0 15.5 %copy-start.7 = (bf16[128,1024]{1,0:T(8,128)(2,1)S(1)}, bf16[128,1024]{1,0:T(8,128)(2,1)}, u32[]{:S(2)}) copy-start(bf16[128,1024]{1,0:T(8,128)(2,1)} %param.9) | copy-start | bytes 786436
  0.0 22.0 %copy-start.9 = (bf16[176,128]{1,0:T(8,128)(2,1)S(1)}, bf16[176,128]{1,0:T(8,128)(2,1)}, u32[]{:S(2)}) copy-start(bf16[176,128]{1,0:T(8,128)(2,1)} %param.7) | copy-start | bytes 135172
  2.4 68.5 %collective-permute-start.11 = (bf16[128,3584]{1,0:T(8,128)(2,1)}, bf16[128,3584]{1,0:T(8,128)(2,1)}, u32[]{:S(2)}, u32[]{:S(2)}) collective-permute-start(bf16[128,3584]{1,0:T(8,128)(2,1)} %pad_maximum_fusion.2), channel_id=1, source_target_pairs={{0,384},{128,0},{256,128},{384,256},{1,385},{129,1},{257,129},{385... | collective-permute-start | bytes 2752520 | tf_op jit(solution)/shard_map/ppermute | solution.py:15
  10.2 60.7 %collective-permute-start.10 = (bf16[128,3584]{1,0:T(8,128)(2,1)}, bf16[128,3584]{1,0:T(8,128)(2,1)}, u32[]{:S(2)}, u32[]{:S(2)}) collective-permute-start(bf16[128,3584]{1,0:T(8,128)(2,1)} %pad_maximum_fusion.2), channel_id=1, source_target_pairs={{0,256},{128,384},{256,0},{384,128},{1,257},{129,385},{257,1},{385... | collective-permute-start | bytes 2752520 | tf_op jit(solution)/shard_map/ppermute | solution.py:15
  12.1 58.8 %collective-permute-start.9 = (bf16[128,3584]{1,0:T(8,128)(2,1)}, bf16[128,3584]{1,0:T(8,128)(2,1)}, u32[]{:S(2)}, u32[]{:S(2)}) collective-permute-start(bf16[128,3584]{1,0:T(8,128)(2,1)} %pad_maximum_fusion.2), channel_id=1, source_target_pairs={{0,128},{128,256},{256,384},{384,0},{1,129},{129,257},{257,385},{3... | collective-permute-start | bytes 2752520 | tf_op jit(solution)/shard_map/ppermute | solution.py:15
  15.5 42.9 %collective-permute-start.1 = (bf16[128,1024]{1,0:T(8,128)(2,1)S(1)}, bf16[128,1024]{1,0:T(8,128)(2,1)S(1)}, u32[]{:S(2)}, u32[]{:S(2)}) collective-permute-start(bf16[128,1024]{1,0:T(8,128)(2,1)S(1)} %copy-done.7), channel_id=1, source_target_pairs={{0,128},{128,256},{256,384},{384,0},{1,129},{129,257},{257,385},{3... | collective-permute-start | bytes 786440 | tf_op jit(solution)/shard_map/ppermute | solution.py:15
  20.0 43.0 %collective-permute-start.2 = (bf16[128,1024]{1,0:T(8,128)(2,1)S(1)}, bf16[128,1024]{1,0:T(8,128)(2,1)S(1)}, u32[]{:S(2)}, u32[]{:S(2)}) collective-permute-start(bf16[128,1024]{1,0:T(8,128)(2,1)S(1)} %copy-done.7), channel_id=1, source_target_pairs={{0,256},{128,384},{256,0},{384,128},{1,257},{129,385},{257,1},{385... | collective-permute-start | bytes 786440 | tf_op jit(solution)/shard_map/ppermute | solution.py:15
  22.8 84.0 %all-to-all-start = ((bf16[8,176,128]{2,1,0:T(8,128)(2,1)}), bf16[8,176,128]{2,1,0:T(8,128)(2,1)S(1)}, u32[]{:S(2)}, u32[]{:S(2)}) async-start(bf16[8,176,128]{2,1,0:T(8,128)(2,1)} %broadcast_in_dim.38), calls=%async_computation | async-start | bytes 720896 | tf_op jit(solution)/shard_map/all_to_all | solution.py:29
  58.4 10.3 %collective-permute-start.3 = (bf16[128,1024]{1,0:T(8,128)(2,1)S(1)}, bf16[128,1024]{1,0:T(8,128)(2,1)S(1)}, u32[]{:S(2)}, u32[]{:S(2)}) collective-permute-start(bf16[128,1024]{1,0:T(8,128)(2,1)S(1)} %copy-done.7), channel_id=1, source_target_pairs={{0,384},{128,0},{256,128},{384,256},{1,385},{129,1},{257,129},{385... | collective-permute-start | bytes 786440 | tf_op jit(solution)/shard_map/ppermute | solution.py:15
  68.8 12.3 %copy-start.10 = (f32[128]{0:T(128)S(1)}, f32[128]{0:T(128)}, u32[]{:S(2)}) copy-start(f32[128]{0:T(128)} %param.10) | copy-start | bytes 1540
  68.8 12.4 %copy-start.8 = (bf16[176,128]{1,0:T(8,128)(2,1)S(1)}, bf16[176,128]{1,0:T(8,128)(2,1)}, u32[]{:S(2)}) copy-start(bf16[176,128]{1,0:T(8,128)(2,1)} %param.8) | copy-start | bytes 135172
  68.8 26.6 %copy-start = (bf16[224,1024]{1,0:T(8,128)(2,1)S(1)}, bf16[224,1024]{1,0:T(8,128)(2,1)}, u32[]{:S(2)}) copy-start(bf16[224,1024]{1,0:T(8,128)(2,1)} %param.13) | copy-start | bytes 1376260
  68.8 38.0 %collective-permute-start.4 = (bf16[512,1024]{1,0:T(8,128)(2,1)S(1)}, bf16[512,1024]{1,0:T(8,128)(2,1)}, u32[]{:S(2)}, u32[]{:S(2)}) collective-permute-start(bf16[512,1024]{1,0:T(8,128)(2,1)S(1)} %constant_dynamic-update-slice_fusion), channel_id=1, source_target_pairs={{0,64},{64,0},{1,65},{65,1},{2,66},{66,2},{3,67},{67,3},{4,68},{68... | collective-permute-start | bytes 3145736 | tf_op jit(solution)/shard_map/ppermute | solution.py:20
  78.7 82.6 %collective-permute-start.12 = (bf16[512,3584]{1,0:T(8,128)(2,1)}, bf16[512,3584]{1,0:T(8,128)(2,1)}, u32[]{:S(2)}, u32[]{:S(2)}) collective-permute-start(bf16[512,3584]{1,0:T(8,128)(2,1)} %pad_maximum_fusion), channel_id=1, source_target_pairs={{0,64},{64,0},{1,65},{65,1},{2,66},{66,2},{3,67},{67,3},{4,68},{68... | collective-permute-start | bytes 11010056 | tf_op jit(solution)/shard_map/ppermute | solution.py:20
  81.2 21.1 %collective-permute-start = (bf16[184,128]{1,0:T(8,128)(2,1)S(1)}, bf16[184,128]{1,0:T(8,128)(2,1)S(1)}, u32[]{:S(2)}, u32[]{:S(2)}) collective-permute-start(bf16[184,128]{1,0:T(8,128)(2,1)S(1)} %pad_maximum_fusion.5), channel_id=1, source_target_pairs={{0,4},{4,0},{1,5},{5,1},{2,6},{6,2},{3,7},{7,3},{8,12},{12,8},{9,1... | collective-permute-start | bytes 141320 | tf_op jit(solution)/shard_map/ppermute | solution.py:20
  95.4 47.8 %collective-permute-start.21 = (bf16[224,1024]{1,0:T(8,128)(2,1)S(1)}, bf16[224,1024]{1,0:T(8,128)(2,1)S(1)}, u32[]{:S(2)}, u32[]{:S(2)}) collective-permute-start(bf16[224,1024]{1,0:T(8,128)(2,1)S(1)} %copy-done), channel_id=1, source_target_pairs={{0,384},{128,0},{256,128},{384,256},{1,385},{129,1},{257,129},{385... | collective-permute-start | bytes 1376264 | tf_op jit(solution)/shard_map/ppermute | solution.py:15
  99.8 43.4 %collective-permute-start.20 = (bf16[224,1024]{1,0:T(8,128)(2,1)S(1)}, bf16[224,1024]{1,0:T(8,128)(2,1)S(1)}, u32[]{:S(2)}, u32[]{:S(2)}) collective-permute-start(bf16[224,1024]{1,0:T(8,128)(2,1)S(1)} %copy-done), channel_id=1, source_target_pairs={{0,256},{128,384},{256,0},{384,128},{1,257},{129,385},{257,1},{385... | collective-permute-start | bytes 1376264 | tf_op jit(solution)/shard_map/ppermute | solution.py:15
  102.2 41.0 %collective-permute-start.19 = (bf16[224,1024]{1,0:T(8,128)(2,1)S(1)}, bf16[224,1024]{1,0:T(8,128)(2,1)S(1)}, u32[]{:S(2)}, u32[]{:S(2)}) collective-permute-start(bf16[224,1024]{1,0:T(8,128)(2,1)S(1)} %copy-done), channel_id=1, source_target_pairs={{0,128},{128,256},{256,384},{384,0},{1,129},{129,257},{257,385},{3... | collective-permute-start | bytes 1376264 | tf_op jit(solution)/shard_map/ppermute | solution.py:15
  110.1 11.7 %all-to-all-start.1 = ((bf16[4,2,176,128]{3,1,2,0:T(2,128)(2,1)}), bf16[4,2,176,128]{3,1,2,0:T(2,128)(2,1)S(1)}, u32[]{:S(2)}, u32[]{:S(2)}) async-start(bf16[4,2,176,128]{3,1,2,0:T(2,128)(2,1)} %bitcast.122), calls=%async_computation.1 | async-start | bytes 720896 | tf_op jit(solution)/shard_map/all_to_all | solution.py:53
  121.9 15.5 %collective-permute-start.5 = (bf16[2,176,128]{2,0,1:T(2,128)(2,1)S(1)}, bf16[2,176,128]{2,0,1:T(2,128)(2,1)S(1)}, u32[]{:S(2)}, u32[]{:S(2)}) collective-permute-start(bf16[2,176,128]{2,0,1:T(2,128)(2,1)S(1)} %copy.66), channel_id=1, source_target_pairs={{0,4},{4,0},{1,5},{5,1},{2,6},{6,2},{3,7},{7,3},{8,12},{12,8},{9,1... | collective-permute-start | bytes 270344 | tf_op jit(solution)/shard_map/ppermute | solution.py:20
  137.7 2.0 copy-start.5
  139.7 10.7 %all-to-all-start.2 = ((bf16[4,360,128]{2,1,0:T(8,128)(2,1)}), bf16[4,360,128]{2,1,0:T(8,128)(2,1)S(1)}, u32[]{:S(2)}, u32[]{:S(2)}) async-start(bf16[4,360,128]{2,1,0:T(8,128)(2,1)} %broadcast_in_dim.40), calls=%async_computation.2 | async-start | bytes 737280 | tf_op jit(solution)/shard_map/all_to_all | solution.py:29
  143.2 21.0 %copy-start.1 = (bf16[224,1024]{1,0:T(8,128)(2,1)}, bf16[224,1024]{1,0:T(8,128)(2,1)S(1)}, u32[]{:S(2)}) copy-start(bf16[224,1024]{1,0:T(8,128)(2,1)S(1)} %collective-permute-done.20) | copy-start | bytes 1376260
  143.2 21.0 %copy-start.3 = (bf16[224,1024]{1,0:T(8,128)(2,1)}, bf16[224,1024]{1,0:T(8,128)(2,1)S(1)}, u32[]{:S(2)}) copy-start(bf16[224,1024]{1,0:T(8,128)(2,1)S(1)} %collective-permute-done.19) | copy-start | bytes 1376260
  144.8 38.5 %collective-permute-start.22 = (bf16[896,1024]{1,0:T(8,128)(2,1)}, bf16[896,1024]{1,0:T(8,128)(2,1)}, u32[]{:S(2)}, u32[]{:S(2)}) collective-permute-start(bf16[896,1024]{1,0:T(8,128)(2,1)} %pad_maximum_fusion.1), channel_id=1, source_target_pairs={{0,64},{64,0},{1,65},{65,1},{2,66},{66,2},{3,67},{67,3},{4,68},{68... | collective-permute-start | bytes 5505032 | tf_op jit(solution)/shard_map/ppermute | solution.py:20
  150.5 6.0 %collective-permute-start.6 = (f32[2,128]{1,0:T(2,128)S(1)}, f32[2,128]{1,0:T(2,128)S(1)}, u32[]{:S(2)}, u32[]{:S(2)}) collective-permute-start(f32[2,128]{1,0:T(2,128)S(1)} %slice_add_fusion), channel_id=1, source_target_pairs={{0,8},{8,0},{16,24},{24,16},{32,40},{40,32},{48,56},{56,48},{1,9},... | collective-permute-start | bytes 3080 | tf_op jit(solution)/shard_map/ppermute | solution.py:20
  156.5 17.2 %collective-permute-start.7 = (f32[2,128]{1,0:T(2,128)S(1)}, f32[2,128]{1,0:T(2,128)S(1)}, u32[]{:S(2)}, u32[]{:S(2)}) collective-permute-start(f32[2,128]{1,0:T(2,128)S(1)} %fusion.63), channel_id=1, source_target_pairs={{0,16},{8,24},{16,0},{24,8},{32,48},{40,56},{48,32},{56,40},{1,17}... | collective-permute-start | bytes 3080 | tf_op jit(solution)/shard_map/ppermute | solution.py:20
  168.1 16.9 %collective-permute-start.13 = (bf16[88,3584]{1,0:T(8,128)(2,1)}, bf16[88,3584]{1,0:T(8,128)(2,1)}, u32[]{:S(2)}, u32[]{:S(2)}) collective-permute-start(bf16[88,3584]{1,0:T(8,128)(2,1)} %fusion.1), channel_id=1, source_target_pairs={{0,8},{8,0},{16,24},{24,16},{32,40},{40,32},{48,56},{56,48},{1,9},... | collective-permute-start | bytes 1892360 | tf_op jit(solution)/shard_map/ppermute | solution.py:20
  173.8 9.4 %collective-permute-start.8 = (f32[2,128]{1,0:T(2,128)S(1)}, f32[2,128]{1,0:T(2,128)S(1)}, u32[]{:S(2)}, u32[]{:S(2)}) collective-permute-start(f32[2,128]{1,0:T(2,128)S(1)} %add.268), channel_id=1, source_target_pairs={{0,32},{8,40},{16,48},{24,56},{32,0},{40,8},{48,16},{56,24},{1,33}... | collective-permute-start | bytes 3080 | tf_op jit(solution)/shard_map/ppermute | solution.py:20
  185.0 8.8 %copy-start.4 = (bf16[224,1024]{1,0:T(8,128)(2,1)S(1)}, bf16[224,1024]{1,0:T(8,128)(2,1)}, u32[]{:S(2)}) copy-start(bf16[224,1024]{1,0:T(8,128)(2,1)} %copy-done.3) | copy-start | bytes 1376260
  190.2 35.0 %copy-start.2 = (bf16[224,1024]{1,0:T(8,128)(2,1)S(1)}, bf16[224,1024]{1,0:T(8,128)(2,1)}, u32[]{:S(2)}) copy-start(bf16[224,1024]{1,0:T(8,128)(2,1)} %copy-done.1) | copy-start | bytes 1376260
  190.2 13.3 %collective-permute-start.14 = (bf16[88,1792]{1,0:T(8,128)(2,1)S(1)}, bf16[88,1792]{1,0:T(8,128)(2,1)S(1)}, u32[]{:S(2)}, u32[]{:S(2)}) collective-permute-start(bf16[88,1792]{1,0:T(8,128)(2,1)S(1)} %bitcast.134), channel_id=1, source_target_pairs={{0,16},{8,24},{16,0},{24,8},{32,48},{40,56},{48,32},{56,40},{1,17}... | collective-permute-start | bytes 946184 | tf_op jit(solution)/shard_map/ppermute | solution.py:20
  203.7 19.4 %collective-permute-start.15 = (bf16[48,1792]{1,0:T(8,128)(2,1)S(1)}, bf16[48,1792]{1,0:T(8,128)(2,1)S(1)}, u32[]{:S(2)}, u32[]{:S(2)}) collective-permute-start(bf16[48,1792]{1,0:T(8,128)(2,1)S(1)} %dynamic-slice_convert_fusion.2), channel_id=1, source_target_pairs={{0,32},{8,40},{16,48},{24,56},{32,0},{40,8},{48,16},{56,24},{1,33}... | collective-permute-start | bytes 516104 | tf_op jit(solution)/shard_map/ppermute | solution.py:20
  223.2 10.3 %collective-permute-start.16 = (bf16[48,896]{1,0:T(8,128)(2,1)S(1)}, bf16[48,896]{1,0:T(8,128)(2,1)S(1)}, u32[]{:S(2)}, u32[]{:S(2)}) collective-permute-start(bf16[48,896]{1,0:T(8,128)(2,1)S(1)} %fusion.37), channel_id=1, source_target_pairs={{0,32},{8,40},{16,48},{24,56},{32,0},{40,8},{48,16},{56,24},{1,33}... | collective-permute-start | bytes 258056 | tf_op jit(solution)/shard_map/ppermute | solution.py:20
  233.7 8.0 %collective-permute-start.17 = (bf16[88,896]{1,0:T(8,128)(2,1)S(1)}, bf16[88,896]{1,0:T(8,128)(2,1)S(1)}, u32[]{:S(2)}, u32[]{:S(2)}) collective-permute-start(bf16[88,896]{1,0:T(8,128)(2,1)S(1)} %pad_maximum_fusion.4), channel_id=1, source_target_pairs={{0,16},{8,24},{16,0},{24,8},{32,48},{40,56},{48,32},{56,40},{1,17}... | collective-permute-start | bytes 473096 | tf_op jit(solution)/shard_map/ppermute | solution.py:20
  241.9 8.8 %collective-permute-start.18 = (bf16[2,88,896]{2,1,0:T(8,128)(2,1)S(1)}, bf16[2,88,896]{2,1,0:T(8,128)(2,1)S(1)}, u32[]{:S(2)}, u32[]{:S(2)}) collective-permute-start(bf16[2,88,896]{2,1,0:T(8,128)(2,1)S(1)} %pad_maximum_fusion.3), channel_id=1, source_target_pairs={{0,8},{8,0},{16,24},{24,16},{32,40},{40,32},{48,56},{56,48},{1,9},... | collective-permute-start | bytes 946184 | tf_op jit(solution)/shard_map/ppermute | solution.py:20
  251.4 27.2 %copy-start.6 = (f32[2,176,128]{2,0,1:T(2,128)S(1)}, f32[2,176,128]{2,0,1:T(2,128)}, u32[]{:S(2)}) copy-start(f32[2,176,128]{2,0,1:T(2,128)} %copy-done.5) | copy-start | bytes 540676
  255.6 16.6 %all-to-all-start.3 = ((bf16[4,2,176,128]{3,1,2,0:T(2,128)(2,1)}), bf16[4,2,176,128]{3,1,2,0:T(2,128)(2,1)S(1)}, u32[]{:S(2)}, u32[]{:S(2)}) async-start(bf16[4,2,176,128]{3,1,2,0:T(2,128)(2,1)} %bitcast.121), calls=%async_computation.3 | async-start | bytes 720896 | tf_op jit(solution)/shard_map/all_to_all | solution.py:53
  272.3 14.7 %collective-permute-start.23 = (bf16[176,128]{1,0:T(8,128)(2,1)S(1)}, bf16[176,128]{1,0:T(8,128)(2,1)S(1)}, u32[]{:S(2)}, u32[]{:S(2)}) collective-permute-start(bf16[176,128]{1,0:T(8,128)(2,1)S(1)} %fusion.38), channel_id=1, source_target_pairs={{0,4},{4,0},{1,5},{5,1},{2,6},{6,2},{3,7},{7,3},{8,12},{12,8},{9,1... | collective-permute-start | bytes 135176 | tf_op jit(solution)/shard_map/ppermute | solution.py:20

commit v2 on v1

v2 whole, which is shorter than its diff:
```python
import jax
import jax.numpy as jnp
from jax import lax
from jax.experimental import pallas as pl
from jax.experimental.pallas import tpu as pltpu
from jax.sharding import Mesh
from jax.sharding import PartitionSpec as P


D = 8192
BF = jnp.bfloat16
F32 = jnp.float32
AXES = ("x", "c", "zl", "zh", "y")


def shift(value, axis, step):
    n = lax.axis_size(axis)
    return lax.ppermute(value, axis, [(i, (i + step) % n) for i in range(n)])


def swap(value, axis, bit):
    n = lax.axis_size(axis)
    return lax.ppermute(value, axis, [(i, i ^ bit) for i in range(n)])


def pick(value, index, dim=0):
    return lax.dynamic_index_in_dim(value, index, dim, keepdims=False)


def exchange(parts, axis):
    return lax.all_to_all(parts, axis, split_axis=0, concat_axis=0, tiled=True)


def from_everyone(value, axis):
    copies = jnp.broadcast_to(value, (lax.axis_size(axis), *value.shape))
    return exchange(copies, axis)


def in_bits(own, other, bit):
    first = jnp.where(bit == 0, own, other)
    second = jnp.where(bit == 0, other, own)
    return first, second


def stack_kernel(*refs):
    *ins, out, sems = refs
    height = ins[0].shape[0]
    copies = [
        pltpu.make_async_copy(ref, out.at[pl.ds(k * height, height)], sems.at[k])
        for k, ref in enumerate(ins)
    ]
    for copy in copies:
        copy.start()
    for copy in copies:
        copy.wait()


def stacked(parts):
    height, width = parts[0].shape
    hbm, anywhere = pl.BlockSpec(memory_space=pltpu.HBM), pl.BlockSpec(memory_space=pl.ANY)
    return pl.pallas_call(
        stack_kernel,
        out_shape=jax.ShapeDtypeStruct((len(parts) * height, width), BF),
        in_specs=[anywhere] * len(parts),
        out_specs=hbm,
        scratch_shapes=[pltpu.SemaphoreType.DMA((len(parts),))],
        name="stack",
    )(*parts)


def gathered(w):
    parts = [w, shift(w, "x", 1), shift(w, "x", 2), shift(w, "x", -1)]
    own = stacked(parts)
    return own, swap(own, "c", 1)


def dot(a, b):
    return jnp.dot(a, b, preferred_element_type=F32)


def proj_kernel(at, x, own, other, out):
    xi, ci = at[0], at[1]
    rows = x.shape[1]
    blocks = [((xi + 4 - k) & 3) * 2 for k in range(4)]
    mine = jnp.concatenate([x[b + ci] for b in blocks], axis=1)
    theirs = jnp.concatenate([x[b + 1 - ci] for b in blocks], axis=1)
    part = (dot(mine, own[...]) + dot(theirs, other[...])).astype(BF)
    for zh in range(2):
        for y in range(4):
            n = (zh * 4 + y) * 128
            out[y, zh * rows : (zh + 1) * rows] = part[:, n : n + 128]


def proj_parts(at, x, own, other):
    rows = x.shape[1]
    vmem = pl.BlockSpec(memory_space=pltpu.VMEM)
    return pl.pallas_call(
        proj_kernel,
        out_shape=jax.ShapeDtypeStruct((4, 2 * rows, 128), BF),
        in_specs=[pl.BlockSpec(memory_space=pltpu.SMEM), vmem, vmem, vmem],
        out_specs=vmem,
        cost_estimate=pl.CostEstimate(
            flops=2 * rows * 1024 * 1024, bytes_accessed=3 << 20, transcendentals=0
        ),
        name="proj_mm",
    )(at, x, own, other)


def both_kernel(at, x, own, other, send, keep):
    xi, ci, bit = at[0], at[1], at[2]
    rows = 2 * send.shape[1]
    blocks = [(xi + 4 - k) & 3 for k in range(4)]

    def block(b, core):
        start = pl.multiple_of((b // 2) * rows, 16)
        return x[(b % 2) * 2 + core, pl.ds(start, rows)]

    mine = jnp.concatenate([block(b, ci) for b in blocks], axis=1)
    theirs = jnp.concatenate([block(b, 1 - ci) for b in blocks], axis=1)
    part = dot(mine, own[...]) + dot(theirs, other[...])
    upper, lower = part[: rows // 2], part[rows // 2 :]
    send[0] = jnp.where(bit == 0, lower, upper).astype(BF)
    keep[0] = jnp.where(bit == 0, upper, lower)


def both_parts(at, x, own, other, rows):
    depth, wide = own.shape
    tile = wide // 4
    halves = (2, rows // 2, wide // 2)
    weights = pl.BlockSpec((depth, tile), lambda n: (0, n))
    result = pl.BlockSpec((1, rows // 2, tile), lambda n: (n // 2, 0, n % 2))
    return pl.pallas_call(
        both_kernel,
        grid=(4,),
        out_shape=(jax.ShapeDtypeStruct(halves, BF), jax.ShapeDtypeStruct(halves, F32)),
        in_specs=[
            pl.BlockSpec(memory_space=pltpu.SMEM),
            pl.BlockSpec(x.shape, lambda n: (0, 0, 0)),
            weights,
            weights,
        ],
        out_specs=(result, result),
        cost_estimate=pl.CostEstimate(
            flops=4 * rows * depth * wide, bytes_accessed=9 << 20, transcendentals=0
        ),
        name="both_mm",
    )(at, x, own, other)


def down_kernel(at, x, own, other, out, whole, sems):
    xi, ci = at[0], at[1]
    rows = x.shape[0]
    height = own.shape[0] // 4
    copies = []
    for j, (ref, core) in enumerate(((own, ci), (other, 1 - ci))):
        for k in range(4):
            b = ((xi + 4 - k) & 3) * 2 + core
            to = whole.at[pl.ds(pl.multiple_of(b * height, 16), height)]
            source = ref.at[pl.ds(k * height, height)]
            copies.append(pltpu.make_async_copy(source, to, sems.at[j * 4 + k]))
    for copy in copies:
        copy.start()
    for copy in copies:
        copy.wait()
    part = dot(x[...], whole[...]).astype(BF)
    for zh in range(2):
        for y in range(4):
            n = (zh * 4 + y) * 128
            out[y, zh * rows : (zh + 1) * rows] = part[:, n : n + 128]


def down_parts(at, x, own, other):
    rows, depth = x.shape
    vmem, hbm = pl.BlockSpec(memory_space=pltpu.VMEM), pl.BlockSpec(memory_space=pltpu.HBM)
    return pl.pallas_call(
        down_kernel,
        out_shape=jax.ShapeDtypeStruct((4, 2 * rows, 128), BF),
        in_specs=[pl.BlockSpec(memory_space=pltpu.SMEM), vmem, hbm, hbm],
        out_specs=vmem,
        scratch_shapes=[pltpu.VMEM((depth, 1024), BF), pltpu.SemaphoreType.DMA((8,))],
        cost_estimate=pl.CostEstimate(
            flops=2 * rows * depth * 1024, bytes_accessed=5 << 20, transcendentals=0
        ),
        name="down_mm",
    )(at, x, own, other)


def exact(value):
    return lax.reduce_precision(value, 8, 7)


def on_device(attn_out, residual, proj_weight, norm_gain, gate_proj, up_proj, down_proj):
    xi, ci = lax.axis_index("x"), lax.axis_index("c")
    zl, zh = lax.axis_index("zl"), lax.axis_index("zh")
    bit0, bit1, bit2 = zl & 1, (zl >> 1) & 1, (zl >> 2) & 1
    at = jnp.stack([xi, ci, bit0]).astype(jnp.int32)
    rows = attn_out.shape[0]
    half = rows // 2
    top = 48
    step = half - top
    ffw = gate_proj.shape[1] // 2

    cols = from_everyone(attn_out, "zl")
    proj_own, proj_other = gathered(proj_weight)
    pieces = [gate_proj[:, :ffw], up_proj[:, :ffw], gate_proj[:, ffw:], up_proj[:, ffw:]]
    both_own, both_other = gathered(jnp.concatenate(pieces, axis=1))
    down_own, down_other = gathered(down_proj)

    high = exact(norm_gain)
    mid = exact(norm_gain - high)
    low = norm_gain - high - mid
    gains = jnp.stack([high, mid, low]).astype(BF)
    sent = jnp.concatenate([residual, jnp.pad(gains, ((0, 5), (0, 0)))])
    facing = swap(sent, "zh", 1)
    other_gain = facing[rows : rows + 3].astype(F32).sum(axis=0)
    residual2 = jnp.concatenate(in_bits(residual, facing[:rows], zh)).astype(F32)
    gain2 = jnp.repeat(jnp.stack(in_bits(norm_gain, other_gain, zh)), rows, axis=0)

    part = proj_parts(at, cols, proj_own, proj_other)
    near = exchange(part, "y").astype(F32).sum(axis=0)
    stream2 = residual2 + near + swap(near.astype(BF), "zh", 1).astype(F32)
    squares = jnp.sum((stream2 * stream2).reshape(2, rows, 128), axis=(0, 2))
    scaled2 = (stream2 * gain2).astype(BF)
    squares = jnp.pad(squares, (0, 256 - rows)).reshape(2, 128)
    high = exact(squares)
    tail = jnp.concatenate([high, squares - high, jnp.zeros((4, 128), F32)]).astype(BF)
    model = from_everyone(jnp.concatenate([scaled2, tail]), "y")
    squares = model[:, 2 * rows : 2 * rows + 4].astype(F32).sum(axis=0)
    squares = squares[:2] + squares[2:]

    send, keep = both_parts(at, model, both_own, both_other, rows)
    got = swap(send, "zl", 1).astype(F32)
    squares = squares + swap(squares, "zl", 1)
    sent = (pick(keep, 1 - bit1) + pick(got, 1 - bit1)).astype(BF)
    keep = pick(keep, bit1) + pick(got, bit1)
    got = swap(sent, "zl", 2).astype(F32)
    squares = squares + swap(squares, "zl", 2)
    both = keep + got
    sent = lax.dynamic_slice_in_dim(both, step * (1 - bit2), top, 0).astype(BF)
    got = swap(sent, "zl", 4).astype(F32)
    squares = squares + swap(squares, "zl", 4)
    both = lax.dynamic_slice_in_dim(both, step * bit2, top, 0) + got
    squares = lax.dynamic_slice_in_dim(squares.reshape(256), half * bit0 + step * bit2, top, 0)
    inverse = lax.rsqrt(squares / D + 1e-05)[:, None]
    gate_sum, up_sum = inverse * both[:, :ffw], inverse * both[:, ffw:]
    hidden = (jax.nn.silu(gate_sum) * up_sum).astype(BF)

    upper, lower = in_bits(hidden, swap(hidden, "zl", 4), bit2)
    hidden = jnp.concatenate([upper, lower[2 * top - half :]])
    hidden = jnp.concatenate(in_bits(hidden, swap(hidden, "zl", 2), bit1), axis=1)
    hidden = jnp.concatenate(in_bits(hidden, swap(hidden, "zl", 1), bit0))

    part = down_parts(at, hidden, down_own, down_other)
    near = exchange(part, "y").astype(F32).sum(axis=0).reshape(2, rows, 128)
    far = swap(pick(near, 1 - zh).astype(BF), "zh", 1)
    stream = pick(stream2.reshape(2, rows, 128), zh)
    return (stream + pick(near, zh) + far.astype(F32)).astype(BF)


def solution(mesh):
    z = mesh.shape["gz"] // 4
    split = Mesh(mesh.devices.reshape(4, 2, mesh.shape["gy"], z, 4), AXES)
    gx, gz = ("x", "c"), ("zh", "y")
    in_specs = (
        P(gx, (*gz, "zl")),
        P(gx, ("zl", *gz)),
        P((*gz, *gx), "zl"),
        P(("zl", *gz)),
        P(("zl", *gx), gz),
        P(("zl", *gx), gz),
        P((*gz, *gx), "zl"),
    )
    return jax.shard_map(
        on_device, mesh=split, in_specs=in_specs, out_specs=P(gx, ("zl", *gz)), check_vma=False
    )
```

time: 289 us -> 481 us (1.66)
  the two profiles are of different devices: /device:TPU:2 before, /device:TPU:4 now
where the time goes in v2:
time: 481 us; the launch traced here: 479 us
  Pallas kernels  216 us (45%)
  starting transfers between devices  125 us (26%)
  waiting for transfers between devices  115 us (24%)
  blocking collectives  10.3 us (2%)
  local copies, waits for them, and re-layouts  7.63 us (2%)
  other arithmetic  5.05 us (1%)
    pallas_call x3, Pallas kernels, stacked(): pl.pallas_call(stack_kernel, out_shape=jax.ShapeDtypeStruct((len(parts) *...  202 us
    ppermute x15, starting transfers between devices, swap(): return lax.ppermute(value, axis, [(i, i ^ bit) for i in range(n)])  72.9 us
    ppermute x15, waiting for transfers between devices, swap(): return lax.ppermute(value, axis, [(i, i ^ bit) for i in range(n)])  66.9 us
    ppermute x9, waiting for transfers between devices, shift(): return lax.ppermute(value, axis, [(i, (i + step) % n) for i in range(n)])  33.3 us
    ppermute x9, starting transfers between devices, shift(): return lax.ppermute(value, axis, [(i, (i + step) % n) for i in range(n)])  31.9 us
    all_to_all x3, starting transfers between devices, exchange(): return lax.all_to_all(parts, axis, split_axis=0, concat_axis=0, tiled=True)  20.6 us
    all_to_all x3, waiting for transfers between devices, exchange(): return lax.all_to_all(parts, axis, split_axis=0, concat_axis=0, tiled=True)  14.5 us
    all_to_all x1, blocking collectives, exchange(): return lax.all_to_all(parts, axis, split_axis=0, concat_axis=0, tiled=True)  10.3 us
  transfers between devices with their start and end apart: 27, of which 13 were waited for; matrix products, arithmetic and copies ran while one was open for 1% of the time, Pallas kernels for 19%

profile of v2, /device:TPU:4, one launch (start us, length us, event | category | flops | bytes accessed | tf_op | source)
XLA Modules:
  0.0 479.5 jit_solution(15354030049765180054)
XLA Ops:
  0.0 1.4 fusion.18
  1.5 3.2 collective-permute-start.9
  4.7 6.6 %collective-permute-start.10 = (bf16[128,3584]{1,0:T(8,128)(2,1)S(1)}, bf16[128,3584]{1,0:T(8,128)(2,1)S(1)}, u32[]{:S(2)}, u32[]{:S(2)}) collective-permute-start(bf16[128,3584]{1,0:T(8,128)(2,1)S(1)} %pad_maximum_fusion.refs_0_), channel_id=1, source_target_pairs={{0,256},{128,384},{256,0},{384,128},{1,257},{129,385},{257,1},{385... | collective-permute-start | bytes 2752520 | tf_op jit(solution)/shard_map/ppermute | solution.py:18
  11.3 4.5 collective-permute-start.11
  15.8 14.8 %collective-permute-done.9.refs_1_ = bf16[128,3584]{1,0:T(8,128)(2,1)S(1)} collective-permute-done((bf16[128,3584]{1,0:T(8,128)(2,1)S(1)}, bf16[128,3584]{1,0:T(8,128)(2,1)S(1)}, u32[]{:S(2)}, u32[]{:S(2)}) %collective-permute-start.9) | collective-permute-done | bytes 917536 | tf_op jit(solution)/shard_map/ppermute | solution.py:18
  30.6 14.7 %collective-permute-done.10.refs_2_ = bf16[128,3584]{1,0:T(8,128)(2,1)S(1)} collective-permute-done((bf16[128,3584]{1,0:T(8,128)(2,1)S(1)}, bf16[128,3584]{1,0:T(8,128)(2,1)S(1)}, u32[]{:S(2)}, u32[]{:S(2)}) %collective-permute-start.10) | collective-permute-done | bytes 917536 | tf_op jit(solution)/shard_map/ppermute | solution.py:18
  45.2 3.9 collective-permute-done.11.refs_3_
  49.1 112.3 %stack.52.own = bf16[512,3584]{1,0:T(8,128)(2,1)} custom-call(bf16[128,3584]{1,0:T(8,128)(2,1)} %copy-done, bf16[128,3584]{1,0:T(8,128)(2,1)} %copy-done.5, bf16[128,3584]{1,0:T(8,128)(2,1)} %copy-done.6, bf16[128,3584]{1,0:T(8,128)(2,1)} %collective-permute-done.11.refs_3_), custom_call_target="tpu_custom_call" | custom-call | tf_op jit(solution)/shard_map/stack/pallas_call | solution.py:61
  161.5 2.1 collective-permute-start.12
  163.5 2.8 collective-permute-start.1
  166.3 3.9 collective-permute-start.2
  170.2 2.0 collective-permute-start.3
  173.0 12.7 %all-to-all-start = ((bf16[8,176,128]{2,1,0:T(8,128)(2,1)}), bf16[8,176,128]{2,1,0:T(8,128)(2,1)S(1)}, u32[]{:S(2)}, u32[]{:S(2)}) async-start(bf16[8,176,128]{2,1,0:T(8,128)(2,1)} %broadcast_in_dim.13), calls=%async_computation | async-start | bytes 720896 | tf_op jit(solution)/shard_map/all_to_all | solution.py:31
  187.3 32.9 %stack.51.own = bf16[512,1024]{1,0:T(8,128)(2,1)} custom-call(bf16[128,1024]{1,0:T(8,128)(2,1)} %refs_0_.2, bf16[128,1024]{1,0:T(8,128)(2,1)} %copy-done.9, bf16[128,1024]{1,0:T(8,128)(2,1)} %copy-done.10, bf16[128,1024]{1,0:T(8,128)(2,1)} %copy-done.11), custom_call_target="tpu_custom_call" | custom-call | tf_op jit(solution)/shard_map/stack/pallas_call | solution.py:61
  220.2 1.9 collective-permute-start.4
  222.2 12.7 %collective-permute-start = (bf16[184,128]{1,0:T(8,128)(2,1)S(1)}, bf16[184,128]{1,0:T(8,128)(2,1)S(1)}, u32[]{:S(2)}, u32[]{:S(2)}) collective-permute-start(bf16[184,128]{1,0:T(8,128)(2,1)S(1)} %pad_maximum_fusion.4), channel_id=1, source_target_pairs={{0,4},{4,0},{1,5},{5,1},{2,6},{6,2},{3,7},{7,3},{8,12},{12,8},{9,1... | collective-permute-start | bytes 141320 | tf_op jit(solution)/shard_map/ppermute | solution.py:23
  235.6 3.9 collective-permute-done
  241.3 3.0 proj_mm.1
  244.3 4.5 all-to-all-start.1
  248.7 7.2 %all-to-all-done.1 = bf16[4,352,128]{2,1,0:T(8,128)(2,1)S(1)} async-done(((bf16[4,352,128]{2,1,0:T(8,128)(2,1)}), bf16[4,352,128]{2,1,0:T(8,128)(2,1)S(1)}, u32[]{:S(2)}, u32[]{:S(2)}) %all-to-all-start.1) | async-done | bytes 360480 | tf_op jit(solution)/shard_map/all_to_all | solution.py:31
  256.0 13.1 %collective-permute-start.5 = (bf16[352,128]{1,0:T(8,128)(2,1)S(1)}, bf16[352,128]{1,0:T(8,128)(2,1)S(1)}, u32[]{:S(2)}, u32[]{:S(2)}) collective-permute-start(bf16[352,128]{1,0:T(8,128)(2,1)S(1)} %convert_element_type.65), channel_id=1, source_target_pairs={{0,4},{4,0},{1,5},{5,1},{2,6},{6,2},{3,7},{7,3},{8,12},{12,8},{9,1... | collective-permute-start | bytes 270344 | tf_op jit(solution)/shard_map/ppermute | solution.py:23
  269.1 4.5 collective-permute-done.5
  274.1 10.3 %all_to_all.20.x = bf16[4,360,128]{2,1,0:T(8,128)(2,1)} all-to-all(bf16[4,360,128]{2,1,0:T(8,128)(2,1)S(1)} %broadcast_in_dim.16), channel_id=1, replica_groups=mesh['x'=4,'c'=2,'zl'=8,'zh'=2,'y'=4] {'y'}, dimensions={0} | all-to-all | bytes 737280 | tf_op jit(solution)/shard_map/all_to_all | solution.py:31
  284.5 6.0 %both_mm.1 = (bf16[2,88,1792]{2,1,0:T(8,128)(2,1)}, f32[2,88,1792]{2,1,0:T(8,128)}) custom-call(s32[3]{0:T(128)} %pad_add_fusion.at, bf16[4,360,128]{2,1,0:T(8,128)(2,1)} %all_to_all.20.x, bf16[512,3584]{1,0:T(8,128)(2,1)} %stack.52.own, bf16[512,3584]{1,0:T(8,128)(2,1)} %collective-permute-done.12.other), custom_call_target="tpu_custom_call" | custom-call | flops 1291845632 | bytes 9437184 | tf_op jit(solution)/shard_map/both_mm/pallas_call | solution.py:132
  290.5 2.0 collective-permute-start.13
  293.2 10.3 %collective-permute-done.13 = bf16[2,88,1792]{2,1,0:T(8,128)(2,1)S(1)} collective-permute-done((bf16[2,88,1792]{2,1,0:T(8,128)(2,1)}, bf16[2,88,1792]{2,1,0:T(8,128)(2,1)S(1)}, u32[]{:S(2)}, u32[]{:S(2)}) %collective-permute-start.13) | collective-permute-done | bytes 630816 | tf_op jit(solution)/shard_map/ppermute | solution.py:23
  304.4 4.7 collective-permute-start.14
  309.2 2.7 collective-permute-start.6
  311.8 1.9 collective-permute-start.19
  313.8 3.3 collective-permute-start.20
  317.1 3.7 collective-permute-start.21
  320.7 2.2 collective-permute-start.7
  323.0 4.1 collective-permute-done.7
  327.1 14.3 %collective-permute-start.8 = (f32[2,128]{1,0:T(2,128)S(1)}, f32[2,128]{1,0:T(2,128)S(1)}, u32[]{:S(2)}, u32[]{:S(2)}) collective-permute-start(f32[2,128]{1,0:T(2,128)S(1)} %add.93), channel_id=1, source_target_pairs={{0,32},{8,40},{16,48},{24,56},{32,0},{40,8},{48,16},{56,24},{1,33}... | collective-permute-start | bytes 3080 | tf_op jit(solution)/shard_map/ppermute | solution.py:23
  341.6 1.9 collective-permute-start.15
  343.6 17.7 %collective-permute-done.15 = bf16[48,1792]{1,0:T(8,128)(2,1)S(1)} collective-permute-done((bf16[48,1792]{1,0:T(8,128)(2,1)S(1)}, bf16[48,1792]{1,0:T(8,128)(2,1)S(1)}, u32[]{:S(2)}, u32[]{:S(2)}) %collective-permute-start.15) | collective-permute-done | bytes 172064 | tf_op jit(solution)/shard_map/ppermute | solution.py:23
  361.5 1.9 collective-permute-start.16
  364.3 56.7 %stack.53.own = bf16[896,1024]{1,0:T(8,128)(2,1)} custom-call(bf16[224,1024]{1,0:T(8,128)(2,1)} %refs_0_.3, bf16[224,1024]{1,0:T(8,128)(2,1)} %copy-done.7, bf16[224,1024]{1,0:T(8,128)(2,1)} %collective-permute-done.20.refs_2_, bf16[224,1024]{1,0:T(8,128)(2,1)} %collective-permute-done.21.refs_3_), custom_call_target="tpu_custom_call" | custom-call | tf_op jit(solution)/shard_map/stack/pallas_call | solution.py:61
  421.0 1.9 collective-permute-start.22
  423.1 1.9 collective-permute-start.17
  425.0 9.9 %collective-permute-done.17 = bf16[88,896]{1,0:T(8,128)(2,1)S(1)} collective-permute-done((bf16[88,896]{1,0:T(8,128)(2,1)S(1)}, bf16[88,896]{1,0:T(8,128)(2,1)S(1)}, u32[]{:S(2)}, u32[]{:S(2)}) %collective-permute-start.17) | collective-permute-done | bytes 157728 | tf_op jit(solution)/shard_map/ppermute | solution.py:23
  435.0 1.9 collective-permute-start.18
  436.9 9.4 %collective-permute-done.18 = bf16[88,1792]{1,0:T(8,128)(2,1)S(1)} collective-permute-done((bf16[88,1792]{1,0:T(8,128)(2,1)S(1)}, bf16[88,1792]{1,0:T(8,128)(2,1)S(1)}, u32[]{:S(2)}, u32[]{:S(2)}) %collective-permute-start.18) | collective-permute-done | bytes 315424 | tf_op jit(solution)/shard_map/ppermute | solution.py:23
  448.6 4.7 down_mm.1
  453.3 3.5 all-to-all-start.3
  456.8 7.3 %all-to-all-done.3 = bf16[4,352,128]{2,1,0:T(8,128)(2,1)S(1)} async-done(((bf16[4,352,128]{2,1,0:T(8,128)(2,1)}), bf16[4,352,128]{2,1,0:T(8,128)(2,1)S(1)}, u32[]{:S(2)}, u32[]{:S(2)}) %all-to-all-start.3) | async-done | bytes 360480 | tf_op jit(solution)/shard_map/all_to_all | solution.py:31
  464.2 7.6 %collective-permute-start.23 = (bf16[176,128]{1,0:T(8,128)(2,1)S(1)}, bf16[176,128]{1,0:T(8,128)(2,1)S(1)}, u32[]{:S(2)}, u32[]{:S(2)}) collective-permute-start(bf16[176,128]{1,0:T(8,128)(2,1)S(1)} %fusion.5), channel_id=1, source_target_pairs={{0,4},{4,0},{1,5},{5,1},{2,6},{6,2},{3,7},{7,3},{8,12},{12,8},{9,1... | collective-permute-start | bytes 135176 | tf_op jit(solution)/shard_map/ppermute | solution.py:23
  471.8 7.0 %collective-permute-done.23 = bf16[176,128]{1,0:T(8,128)(2,1)S(1)} collective-permute-done((bf16[176,128]{1,0:T(8,128)(2,1)S(1)}, bf16[176,128]{1,0:T(8,128)(2,1)S(1)}, u32[]{:S(2)}, u32[]{:S(2)}) %collective-permute-start.23) | collective-permute-done | bytes 45088 | tf_op jit(solution)/shard_map/ppermute | solution.py:23
  (87 shorter events, 11.4 us)
Async XLA Ops:
  1.4 47.7 %copy-start = (bf16[128,3584]{1,0:T(8,128)(2,1)}, bf16[128,3584]{1,0:T(8,128)(2,1)S(1)}, u32[]{:S(2)}) copy-start(bf16[128,3584]{1,0:T(8,128)(2,1)S(1)} %pad_maximum_fusion.refs_0_) | copy-start | bytes 2752516
  1.4 162.1 %copy-start.8 = (bf16[128,1024]{1,0:T(8,128)(2,1)S(1)}, bf16[128,1024]{1,0:T(8,128)(2,1)}, u32[]{:S(2)}) copy-start(bf16[128,1024]{1,0:T(8,128)(2,1)} %refs_0_.2) | copy-start | bytes 786436
  1.5 170.8 %copy-start.13 = (bf16[176,128]{1,0:T(8,128)(2,1)S(1)}, bf16[176,128]{1,0:T(8,128)(2,1)}, u32[]{:S(2)}) copy-start(bf16[176,128]{1,0:T(8,128)(2,1)} %param.7) | copy-start | bytes 135172
  1.5 29.1 %collective-permute-start.9 = (bf16[128,3584]{1,0:T(8,128)(2,1)S(1)}, bf16[128,3584]{1,0:T(8,128)(2,1)S(1)}, u32[]{:S(2)}, u32[]{:S(2)}) collective-permute-start(bf16[128,3584]{1,0:T(8,128)(2,1)S(1)} %pad_maximum_fusion.refs_0_), channel_id=1, source_target_pairs={{0,128},{128,256},{256,384},{384,0},{1,129},{129,257},{257,385},{3... | collective-permute-start | bytes 2752520 | tf_op jit(solution)/shard_map/ppermute | solution.py:18
  4.7 40.5 %collective-permute-start.10 = (bf16[128,3584]{1,0:T(8,128)(2,1)S(1)}, bf16[128,3584]{1,0:T(8,128)(2,1)S(1)}, u32[]{:S(2)}, u32[]{:S(2)}) collective-permute-start(bf16[128,3584]{1,0:T(8,128)(2,1)S(1)} %pad_maximum_fusion.refs_0_), channel_id=1, source_target_pairs={{0,256},{128,384},{256,0},{384,128},{1,257},{129,385},{257,1},{385... | collective-permute-start | bytes 2752520 | tf_op jit(solution)/shard_map/ppermute | solution.py:18
  11.3 37.8 %collective-permute-start.11 = (bf16[128,3584]{1,0:T(8,128)(2,1)S(1)}, bf16[128,3584]{1,0:T(8,128)(2,1)}, u32[]{:S(2)}, u32[]{:S(2)}) collective-permute-start(bf16[128,3584]{1,0:T(8,128)(2,1)S(1)} %pad_maximum_fusion.refs_0_), channel_id=1, source_target_pairs={{0,384},{128,0},{256,128},{384,256},{1,385},{129,1},{257,129},{385... | collective-permute-start | bytes 2752520 | tf_op jit(solution)/shard_map/ppermute | solution.py:18
  30.6 18.5 %copy-start.5 = (bf16[128,3584]{1,0:T(8,128)(2,1)}, bf16[128,3584]{1,0:T(8,128)(2,1)S(1)}, u32[]{:S(2)}) copy-start(bf16[128,3584]{1,0:T(8,128)(2,1)S(1)} %collective-permute-done.9.refs_1_) | copy-start | bytes 2752516
  45.2 3.9 copy-start.6
  161.4 60.7 %copy-start.14 = (f32[128]{0:T(128)S(1)}, f32[128]{0:T(128)}, u32[]{:S(2)}) copy-start(f32[128]{0:T(128)} %param.10) | copy-start | bytes 1540
  161.4 60.7 %copy-start.12 = (bf16[176,128]{1,0:T(8,128)(2,1)S(1)}, bf16[176,128]{1,0:T(8,128)(2,1)}, u32[]{:S(2)}) copy-start(bf16[176,128]{1,0:T(8,128)(2,1)} %param.8) | copy-start | bytes 135172
  161.5 123.0 %collective-permute-start.12 = (bf16[512,3584]{1,0:T(8,128)(2,1)}, bf16[512,3584]{1,0:T(8,128)(2,1)}, u32[]{:S(2)}, u32[]{:S(2)}) collective-permute-start(bf16[512,3584]{1,0:T(8,128)(2,1)} %stack.52.own), channel_id=1, source_target_pairs={{0,64},{64,0},{1,65},{65,1},{2,66},{66,2},{3,67},{67,3},{4,68},{68... | collective-permute-start | bytes 11010056 | tf_op jit(solution)/shard_map/ppermute | solution.py:23
  163.5 22.2 %collective-permute-start.1 = (bf16[128,1024]{1,0:T(8,128)(2,1)S(1)}, bf16[128,1024]{1,0:T(8,128)(2,1)S(1)}, u32[]{:S(2)}, u32[]{:S(2)}) collective-permute-start(bf16[128,1024]{1,0:T(8,128)(2,1)S(1)} %copy-done.8), channel_id=1, source_target_pairs={{0,128},{128,256},{256,384},{384,0},{1,129},{129,257},{257,385},{3... | collective-permute-start | bytes 786440 | tf_op jit(solution)/shard_map/ppermute | solution.py:18
  166.3 19.4 %collective-permute-start.2 = (bf16[128,1024]{1,0:T(8,128)(2,1)S(1)}, bf16[128,1024]{1,0:T(8,128)(2,1)S(1)}, u32[]{:S(2)}, u32[]{:S(2)}) collective-permute-start(bf16[128,1024]{1,0:T(8,128)(2,1)S(1)} %copy-done.8), channel_id=1, source_target_pairs={{0,256},{128,384},{256,0},{384,128},{1,257},{129,385},{257,1},{385... | collective-permute-start | bytes 786440 | tf_op jit(solution)/shard_map/ppermute | solution.py:18
  170.2 15.6 %collective-permute-start.3 = (bf16[128,1024]{1,0:T(8,128)(2,1)S(1)}, bf16[128,1024]{1,0:T(8,128)(2,1)S(1)}, u32[]{:S(2)}, u32[]{:S(2)}) collective-permute-start(bf16[128,1024]{1,0:T(8,128)(2,1)S(1)} %copy-done.8), channel_id=1, source_target_pairs={{0,384},{128,0},{256,128},{384,256},{1,385},{129,1},{257,129},{385... | collective-permute-start | bytes 786440 | tf_op jit(solution)/shard_map/ppermute | solution.py:18
  173.0 66.5 %all-to-all-start = ((bf16[8,176,128]{2,1,0:T(8,128)(2,1)}), bf16[8,176,128]{2,1,0:T(8,128)(2,1)S(1)}, u32[]{:S(2)}, u32[]{:S(2)}) async-start(bf16[8,176,128]{2,1,0:T(8,128)(2,1)} %broadcast_in_dim.13), calls=%async_computation | async-start | bytes 720896 | tf_op jit(solution)/shard_map/all_to_all | solution.py:31
  185.8 0.7 copy-start.9
  185.8 0.8 copy-start.10
  186.6 0.7 copy-start.11
  220.2 19.4 %collective-permute-start.4 = (bf16[512,1024]{1,0:T(8,128)(2,1)}, bf16[512,1024]{1,0:T(8,128)(2,1)S(1)}, u32[]{:S(2)}, u32[]{:S(2)}) collective-permute-start(bf16[512,1024]{1,0:T(8,128)(2,1)} %stack.51.own), channel_id=1, source_target_pairs={{0,64},{64,0},{1,65},{65,1},{2,66},{66,2},{3,67},{67,3},{4,68},{68... | collective-permute-start | bytes 3145736 | tf_op jit(solution)/shard_map/ppermute | solution.py:23
  222.2 17.3 %collective-permute-start = (bf16[184,128]{1,0:T(8,128)(2,1)S(1)}, bf16[184,128]{1,0:T(8,128)(2,1)S(1)}, u32[]{:S(2)}, u32[]{:S(2)}) collective-permute-start(bf16[184,128]{1,0:T(8,128)(2,1)S(1)} %pad_maximum_fusion.4), channel_id=1, source_target_pairs={{0,4},{4,0},{1,5},{5,1},{2,6},{6,2},{3,7},{7,3},{8,12},{12,8},{9,1... | collective-permute-start | bytes 141320 | tf_op jit(solution)/shard_map/ppermute | solution.py:23
  239.5 0.7 copy-start.2
  240.2 1.0 copy-start.4
  244.3 11.7 %all-to-all-start.1 = ((bf16[4,352,128]{2,1,0:T(8,128)(2,1)}), bf16[4,352,128]{2,1,0:T(8,128)(2,1)S(1)}, u32[]{:S(2)}, u32[]{:S(2)}) async-start(bf16[4,352,128]{2,1,0:T(8,128)(2,1)} %proj_mm.1), calls=%async_computation.1 | async-start | bytes 720896 | tf_op jit(solution)/shard_map/all_to_all | solution.py:31
  256.0 17.6 %collective-permute-start.5 = (bf16[352,128]{1,0:T(8,128)(2,1)S(1)}, bf16[352,128]{1,0:T(8,128)(2,1)S(1)}, u32[]{:S(2)}, u32[]{:S(2)}) collective-permute-start(bf16[352,128]{1,0:T(8,128)(2,1)S(1)} %convert_element_type.65), channel_id=1, source_target_pairs={{0,4},{4,0},{1,5},{5,1},{2,6},{6,2},{3,7},{7,3},{8,12},{12,8},{9,1... | collective-permute-start | bytes 270344 | tf_op jit(solution)/shard_map/ppermute | solution.py:23
  290.4 13.2 %copy-start.3 = (f32[2,88,1792]{2,1,0:T(8,128)S(1)}, f32[2,88,1792]{2,1,0:T(8,128)}, u32[]{:S(2)}) copy-start(f32[2,88,1792]{2,1,0:T(8,128)} %get-tuple-element.7) | copy-start | bytes 3784708
  290.5 13.1 %collective-permute-start.13 = (bf16[2,88,1792]{2,1,0:T(8,128)(2,1)}, bf16[2,88,1792]{2,1,0:T(8,128)(2,1)S(1)}, u32[]{:S(2)}, u32[]{:S(2)}) collective-permute-start(bf16[2,88,1792]{2,1,0:T(8,128)(2,1)} %get-tuple-element.8), channel_id=1, source_target_pairs={{0,8},{8,0},{16,24},{24,16},{32,40},{40,32},{48,56},{56,48},{1,9},... | collective-permute-start | bytes 1892360 | tf_op jit(solution)/shard_map/ppermute | solution.py:23
  304.4 37.0 %collective-permute-start.14 = (bf16[88,1792]{1,0:T(8,128)(2,1)}, bf16[88,1792]{1,0:T(8,128)(2,1)S(1)}, u32[]{:S(2)}, u32[]{:S(2)}) collective-permute-start(bf16[88,1792]{1,0:T(8,128)(2,1)} %fusion), channel_id=1, source_target_pairs={{0,16},{8,24},{16,0},{24,8},{32,48},{40,56},{48,32},{56,40},{1,17}... | collective-permute-start | bytes 946184 | tf_op jit(solution)/shard_map/ppermute | solution.py:23
  309.2 11.6 %collective-permute-start.6 = (f32[2,128]{1,0:T(2,128)S(1)}, f32[2,128]{1,0:T(2,128)S(1)}, u32[]{:S(2)}, u32[]{:S(2)}) collective-permute-start(f32[2,128]{1,0:T(2,128)S(1)} %slice_add_fusion), channel_id=1, source_target_pairs={{0,8},{8,0},{16,24},{24,16},{32,40},{40,32},{48,56},{56,48},{1,9},... | collective-permute-start | bytes 3080 | tf_op jit(solution)/shard_map/ppermute | solution.py:23
  311.8 51.6 %collective-permute-start.19 = (bf16[224,1024]{1,0:T(8,128)(2,1)}, bf16[224,1024]{1,0:T(8,128)(2,1)S(1)}, u32[]{:S(2)}, u32[]{:S(2)}) collective-permute-start(bf16[224,1024]{1,0:T(8,128)(2,1)} %refs_0_.3), channel_id=1, source_target_pairs={{0,128},{128,256},{256,384},{384,0},{1,129},{129,257},{257,385},{3... | collective-permute-start | bytes 1376264 | tf_op jit(solution)/shard_map/ppermute | solution.py:18
  313.8 49.7 %collective-permute-start.20 = (bf16[224,1024]{1,0:T(8,128)(2,1)}, bf16[224,1024]{1,0:T(8,128)(2,1)}, u32[]{:S(2)}, u32[]{:S(2)}) collective-permute-start(bf16[224,1024]{1,0:T(8,128)(2,1)} %refs_0_.3), channel_id=1, source_target_pairs={{0,256},{128,384},{256,0},{384,128},{1,257},{129,385},{257,1},{385... | collective-permute-start | bytes 1376264 | tf_op jit(solution)/shard_map/ppermute | solution.py:18
  317.1 46.4 %collective-permute-start.21 = (bf16[224,1024]{1,0:T(8,128)(2,1)}, bf16[224,1024]{1,0:T(8,128)(2,1)}, u32[]{:S(2)}, u32[]{:S(2)}) collective-permute-start(bf16[224,1024]{1,0:T(8,128)(2,1)} %refs_0_.3), channel_id=1, source_target_pairs={{0,384},{128,0},{256,128},{384,256},{1,385},{129,1},{257,129},{385... | collective-permute-start | bytes 1376264 | tf_op jit(solution)/shard_map/ppermute | solution.py:18
  320.7 6.4 %collective-permute-start.7 = (f32[2,128]{1,0:T(2,128)S(1)}, f32[2,128]{1,0:T(2,128)S(1)}, u32[]{:S(2)}, u32[]{:S(2)}) collective-permute-start(f32[2,128]{1,0:T(2,128)S(1)} %fusion.20), channel_id=1, source_target_pairs={{0,16},{8,24},{16,0},{24,8},{32,48},{40,56},{48,32},{56,40},{1,17}... | collective-permute-start | bytes 3080 | tf_op jit(solution)/shard_map/ppermute | solution.py:23
  327.1 16.4 %collective-permute-start.8 = (f32[2,128]{1,0:T(2,128)S(1)}, f32[2,128]{1,0:T(2,128)S(1)}, u32[]{:S(2)}, u32[]{:S(2)}) collective-permute-start(f32[2,128]{1,0:T(2,128)S(1)} %add.93), channel_id=1, source_target_pairs={{0,32},{8,40},{16,48},{24,56},{32,0},{40,8},{48,16},{56,24},{1,33}... | collective-permute-start | bytes 3080 | tf_op jit(solution)/shard_map/ppermute | solution.py:23
  341.6 19.8 %collective-permute-start.15 = (bf16[48,1792]{1,0:T(8,128)(2,1)S(1)}, bf16[48,1792]{1,0:T(8,128)(2,1)S(1)}, u32[]{:S(2)}, u32[]{:S(2)}) collective-permute-start(bf16[48,1792]{1,0:T(8,128)(2,1)S(1)} %dynamic-slice_convert_fusion), channel_id=1, source_target_pairs={{0,32},{8,40},{16,48},{24,56},{32,0},{40,8},{48,16},{56,24},{1,33}... | collective-permute-start | bytes 516104 | tf_op jit(solution)/shard_map/ppermute | solution.py:23
  361.5 61.4 %collective-permute-start.16 = (bf16[48,896]{1,0:T(8,128)(2,1)S(1)}, bf16[48,896]{1,0:T(8,128)(2,1)S(1)}, u32[]{:S(2)}, u32[]{:S(2)}) collective-permute-start(bf16[48,896]{1,0:T(8,128)(2,1)S(1)} %fusion.3), channel_id=1, source_target_pairs={{0,32},{8,40},{16,48},{24,56},{32,0},{40,8},{48,16},{56,24},{1,33}... | collective-permute-start | bytes 258056 | tf_op jit(solution)/shard_map/ppermute | solution.py:23
  363.5 0.8 copy-start.7
  421.0 26.4 %collective-permute-start.22 = (bf16[896,1024]{1,0:T(8,128)(2,1)}, bf16[896,1024]{1,0:T(8,128)(2,1)S(1)}, u32[]{:S(2)}, u32[]{:S(2)}) collective-permute-start(bf16[896,1024]{1,0:T(8,128)(2,1)} %stack.53.own), channel_id=1, source_target_pairs={{0,64},{64,0},{1,65},{65,1},{2,66},{66,2},{3,67},{67,3},{4,68},{68... | collective-permute-start | bytes 5505032 | tf_op jit(solution)/shard_map/ppermute | solution.py:23
  423.1 11.8 %collective-permute-start.17 = (bf16[88,896]{1,0:T(8,128)(2,1)S(1)}, bf16[88,896]{1,0:T(8,128)(2,1)S(1)}, u32[]{:S(2)}, u32[]{:S(2)}) collective-permute-start(bf16[88,896]{1,0:T(8,128)(2,1)S(1)} %pad_maximum_fusion.3), channel_id=1, source_target_pairs={{0,16},{8,24},{16,0},{24,8},{32,48},{40,56},{48,32},{56,40},{1,17}... | collective-permute-start | bytes 473096 | tf_op jit(solution)/shard_map/ppermute | solution.py:23
  435.0 11.3 %collective-permute-start.18 = (bf16[88,1792]{1,0:T(8,128)(2,1)S(1)}, bf16[88,1792]{1,0:T(8,128)(2,1)S(1)}, u32[]{:S(2)}, u32[]{:S(2)}) collective-permute-start(bf16[88,1792]{1,0:T(8,128)(2,1)S(1)} %pad_maximum_fusion.2), channel_id=1, source_target_pairs={{0,8},{8,0},{16,24},{24,16},{32,40},{40,32},{48,56},{56,48},{1,9},... | collective-permute-start | bytes 946184 | tf_op jit(solution)/shard_map/ppermute | solution.py:23
  447.3 1.2 copy-start.1
  453.3 10.8 %all-to-all-start.3 = ((bf16[4,352,128]{2,1,0:T(8,128)(2,1)}), bf16[4,352,128]{2,1,0:T(8,128)(2,1)S(1)}, u32[]{:S(2)}, u32[]{:S(2)}) async-start(bf16[4,352,128]{2,1,0:T(8,128)(2,1)} %down_mm.1), calls=%async_computation.3 | async-start | bytes 720896 | tf_op jit(solution)/shard_map/all_to_all | solution.py:31
  464.2 14.7 %collective-permute-start.23 = (bf16[176,128]{1,0:T(8,128)(2,1)S(1)}, bf16[176,128]{1,0:T(8,128)(2,1)S(1)}, u32[]{:S(2)}, u32[]{:S(2)}) collective-permute-start(bf16[176,128]{1,0:T(8,128)(2,1)S(1)} %fusion.5), channel_id=1, source_target_pairs={{0,4},{4,0},{1,5},{5,1},{2,6},{6,2},{3,7},{7,3},{8,12},{12,8},{9,1... | collective-permute-start | bytes 135176 | tf_op jit(solution)/shard_map/ppermute | solution.py:23

commit v3 on v2

--- a/solution.py
+++ b/solution.py
@@ -43,27 +43,20 @@
 
 
 def stack_kernel(*refs):
-    *ins, out, sems = refs
+    *ins, out = refs
     height = ins[0].shape[0]
-    copies = [
-        pltpu.make_async_copy(ref, out.at[pl.ds(k * height, height)], sems.at[k])
-        for k, ref in enumerate(ins)
-    ]
-    for copy in copies:
-        copy.start()
-    for copy in copies:
-        copy.wait()
+    for k, ref in enumerate(ins):
+        out[k * height : (k + 1) * height] = ref[...]
 
 
 def stacked(parts):
     height, width = parts[0].shape
-    hbm, anywhere = pl.BlockSpec(memory_space=pltpu.HBM), pl.BlockSpec(memory_space=pl.ANY)
+    vmem = pl.BlockSpec(memory_space=pltpu.VMEM)
     return pl.pallas_call(
         stack_kernel,
         out_shape=jax.ShapeDtypeStruct((len(parts) * height, width), BF),
-        in_specs=[anywhere] * len(parts),
-        out_specs=hbm,
-        scratch_shapes=[pltpu.SemaphoreType.DMA((len(parts),))],
+        in_specs=[vmem] * len(parts),
+        out_specs=vmem,
         name="stack",
     )(*parts)
 

time: 481 us -> 286 us (0.59)
  the two profiles are of different devices: /device:TPU:4 before, /device:TPU:8 now
where the time goes in v3:
time: 286 us; the launch traced here: 285 us
  starting transfers between devices  121 us (42%)
  waiting for transfers between devices  118 us (41%)
  Pallas kernels  22.9 us (8%)
  blocking collectives  10.3 us (4%)
  local copies, waits for them, and re-layouts  7.64 us (3%)
  other arithmetic  5.05 us (2%)
    ppermute x15, waiting for transfers between devices, swap(): return lax.ppermute(value, axis, [(i, i ^ bit) for i in range(n)])  67.3 us
    ppermute x15, starting transfers between devices, swap(): return lax.ppermute(value, axis, [(i, i ^ bit) for i in range(n)])  64.3 us
    ppermute x9, waiting for transfers between devices, shift(): return lax.ppermute(value, axis, [(i, (i + step) % n) for i in range(n)])  36.1 us
    ppermute x9, starting transfers between devices, shift(): return lax.ppermute(value, axis, [(i, (i + step) % n) for i in range(n)])  34 us
    all_to_all x3, starting transfers between devices, exchange(): return lax.all_to_all(parts, axis, split_axis=0, concat_axis=0, tiled=True)  22.3 us
    all_to_all x3, waiting for transfers between devices, exchange(): return lax.all_to_all(parts, axis, split_axis=0, concat_axis=0, tiled=True)  14.5 us
    all_to_all x1, blocking collectives, exchange(): return lax.all_to_all(parts, axis, split_axis=0, concat_axis=0, tiled=True)  10.3 us
    pallas_call x3, Pallas kernels, stacked(): pl.pallas_call(stack_kernel, out_shape=jax.ShapeDtypeStruct((len(parts) *...  9.17 us
  transfers between devices with their start and end apart: 27, of which 15 were waited for; matrix products, arithmetic and copies ran while one was open for 2% of the time, Pallas kernels for 3%

profile of v3, /device:TPU:8, one launch (start us, length us, event | category | flops | bytes accessed | tf_op | source)
XLA Modules:
  0.0 285.1 jit_solution(8407538242414927002)
XLA Ops:
  1.5 3.5 %collective-permute-start.9 = (bf16[128,3584]{1,0:T(8,128)(2,1)S(1)}, bf16[128,3584]{1,0:T(8,128)(2,1)S(1)}, u32[]{:S(2)}, u32[]{:S(2)}) collective-permute-start(bf16[128,3584]{1,0:T(8,128)(2,1)S(1)} %pad_maximum_fusion.refs_0_), channel_id=1, source_target_pairs={{0,128},{128,256},{256,384},{384,0},{1,129},{129,257},{257,385},{3... | collective-permute-start | bytes 2752520 | tf_op jit(solution)/shard_map/ppermute | solution.py:18
  5.0 4.6 %collective-permute-start.10 = (bf16[128,3584]{1,0:T(8,128)(2,1)S(1)}, bf16[128,3584]{1,0:T(8,128)(2,1)S(1)}, u32[]{:S(2)}, u32[]{:S(2)}) collective-permute-start(bf16[128,3584]{1,0:T(8,128)(2,1)S(1)} %pad_maximum_fusion.refs_0_), channel_id=1, source_target_pairs={{0,256},{128,384},{256,0},{384,128},{1,257},{129,385},{257,1},{385... | collective-permute-start | bytes 2752520 | tf_op jit(solution)/shard_map/ppermute | solution.py:18
  9.7 3.3 %collective-permute-start.11 = (bf16[128,3584]{1,0:T(8,128)(2,1)S(1)}, bf16[128,3584]{1,0:T(8,128)(2,1)}, u32[]{:S(2)}, u32[]{:S(2)}) collective-permute-start(bf16[128,3584]{1,0:T(8,128)(2,1)S(1)} %pad_maximum_fusion.refs_0_), channel_id=1, source_target_pairs={{0,384},{128,0},{256,128},{384,256},{1,385},{129,1},{257,129},{385... | collective-permute-start | bytes 2752520 | tf_op jit(solution)/shard_map/ppermute | solution.py:18
  13.0 13.9 %collective-permute-done.9.refs_1_ = bf16[128,3584]{1,0:T(8,128)(2,1)S(1)} collective-permute-done((bf16[128,3584]{1,0:T(8,128)(2,1)S(1)}, bf16[128,3584]{1,0:T(8,128)(2,1)S(1)}, u32[]{:S(2)}, u32[]{:S(2)}) %collective-permute-start.9) | collective-permute-done | bytes 917536 | tf_op jit(solution)/shard_map/ppermute | solution.py:18
  26.9 20.5 %collective-permute-done.10.refs_2_ = bf16[128,3584]{1,0:T(8,128)(2,1)S(1)} collective-permute-done((bf16[128,3584]{1,0:T(8,128)(2,1)S(1)}, bf16[128,3584]{1,0:T(8,128)(2,1)S(1)}, u32[]{:S(2)}, u32[]{:S(2)}) %collective-permute-start.10) | collective-permute-done | bytes 917536 | tf_op jit(solution)/shard_map/ppermute | solution.py:18
  49.1 4.0 %stack.52.own = bf16[512,3584]{1,0:T(8,128)(2,1)} custom-call(bf16[128,3584]{1,0:T(8,128)(2,1)} %copy-done, bf16[128,3584]{1,0:T(8,128)(2,1)} %copy-done.5, bf16[128,3584]{1,0:T(8,128)(2,1)} %copy-done.6, bf16[128,3584]{1,0:T(8,128)(2,1)} %collective-permute-done.11.refs_3_), custom_call_target="tpu_custom_call" | custom-call | tf_op jit(solution)/shard_map/stack/pallas_call | solution.py:55
  53.1 2.0 collective-permute-start.12
  55.2 4.3 %collective-permute-start.1 = (bf16[128,1024]{1,0:T(8,128)(2,1)S(1)}, bf16[128,1024]{1,0:T(8,128)(2,1)S(1)}, u32[]{:S(2)}, u32[]{:S(2)}) collective-permute-start(bf16[128,1024]{1,0:T(8,128)(2,1)S(1)} %copy-done.8), channel_id=1, source_target_pairs={{0,128},{128,256},{256,384},{384,0},{1,129},{129,257},{257,385},{3... | collective-permute-start | bytes 786440 | tf_op jit(solution)/shard_map/ppermute | solution.py:18
  59.5 3.6 %collective-permute-start.2 = (bf16[128,1024]{1,0:T(8,128)(2,1)S(1)}, bf16[128,1024]{1,0:T(8,128)(2,1)S(1)}, u32[]{:S(2)}, u32[]{:S(2)}) collective-permute-start(bf16[128,1024]{1,0:T(8,128)(2,1)S(1)} %copy-done.8), channel_id=1, source_target_pairs={{0,256},{128,384},{256,0},{384,128},{1,257},{129,385},{257,1},{385... | collective-permute-start | bytes 786440 | tf_op jit(solution)/shard_map/ppermute | solution.py:18
  63.1 3.5 %collective-permute-start.3 = (bf16[128,1024]{1,0:T(8,128)(2,1)S(1)}, bf16[128,1024]{1,0:T(8,128)(2,1)S(1)}, u32[]{:S(2)}, u32[]{:S(2)}) collective-permute-start(bf16[128,1024]{1,0:T(8,128)(2,1)S(1)} %copy-done.8), channel_id=1, source_target_pairs={{0,384},{128,0},{256,128},{384,256},{1,385},{129,1},{257,129},{385... | collective-permute-start | bytes 786440 | tf_op jit(solution)/shard_map/ppermute | solution.py:18
  67.4 12.5 %all-to-all-start = ((bf16[8,176,128]{2,1,0:T(8,128)(2,1)}), bf16[8,176,128]{2,1,0:T(8,128)(2,1)S(1)}, u32[]{:S(2)}, u32[]{:S(2)}) async-start(bf16[8,176,128]{2,1,0:T(8,128)(2,1)} %broadcast_in_dim.13), calls=%async_computation | async-start | bytes 720896 | tf_op jit(solution)/shard_map/all_to_all | solution.py:31
  81.5 2.3 stack.51.own
  83.8 1.9 collective-permute-start.4
  85.8 10.1 %collective-permute-start = (bf16[184,128]{1,0:T(8,128)(2,1)S(1)}, bf16[184,128]{1,0:T(8,128)(2,1)S(1)}, u32[]{:S(2)}, u32[]{:S(2)}) collective-permute-start(bf16[184,128]{1,0:T(8,128)(2,1)S(1)} %pad_maximum_fusion.4), channel_id=1, source_target_pairs={{0,4},{4,0},{1,5},{5,1},{2,6},{6,2},{3,7},{7,3},{8,12},{12,8},{9,1... | collective-permute-start | bytes 141320 | tf_op jit(solution)/shard_map/ppermute | solution.py:23
  96.6 4.1 %collective-permute-done = bf16[184,128]{1,0:T(8,128)(2,1)S(1)} collective-permute-done((bf16[184,128]{1,0:T(8,128)(2,1)S(1)}, bf16[184,128]{1,0:T(8,128)(2,1)S(1)}, u32[]{:S(2)}, u32[]{:S(2)}) %collective-permute-start) | collective-permute-done | bytes 47136 | tf_op jit(solution)/shard_map/ppermute | solution.py:23
  100.7 2.9 %all-to-all-done.x = bf16[8,176,128]{2,1,0:T(8,128)(2,1)S(1)} async-done(((bf16[8,176,128]{2,1,0:T(8,128)(2,1)}), bf16[8,176,128]{2,1,0:T(8,128)(2,1)S(1)}, u32[]{:S(2)}, u32[]{:S(2)}) %all-to-all-start) | async-done | bytes 360480 | tf_op jit(solution)/shard_map/all_to_all | solution.py:31
  105.4 3.0 %proj_mm.1 = bf16[4,352,128]{2,1,0:T(8,128)(2,1)} custom-call(s32[3]{0:T(128)} %pad_add_fusion.at, bf16[8,176,128]{2,1,0:T(8,128)(2,1)} %copy-done.2, bf16[512,1024]{1,0:T(8,128)(2,1)} %stack.51.own, bf16[512,1024]{1,0:T(8,128)(2,1)} %copy-done.4), custom_call_target="tpu_custom_call" | custom-call | flops 369098752 | bytes 3145728 | tf_op jit(solution)/shard_map/proj_mm/pallas_call | solution.py:90
  108.4 4.9 %all-to-all-start.1 = ((bf16[4,352,128]{2,1,0:T(8,128)(2,1)}), bf16[4,352,128]{2,1,0:T(8,128)(2,1)S(1)}, u32[]{:S(2)}, u32[]{:S(2)}) async-start(bf16[4,352,128]{2,1,0:T(8,128)(2,1)} %proj_mm.1), calls=%async_computation.1 | async-start | bytes 720896 | tf_op jit(solution)/shard_map/all_to_all | solution.py:31
  113.3 5.7 %all-to-all-done.1 = bf16[4,352,128]{2,1,0:T(8,128)(2,1)S(1)} async-done(((bf16[4,352,128]{2,1,0:T(8,128)(2,1)}), bf16[4,352,128]{2,1,0:T(8,128)(2,1)S(1)}, u32[]{:S(2)}, u32[]{:S(2)}) %all-to-all-start.1) | async-done | bytes 360480 | tf_op jit(solution)/shard_map/all_to_all | solution.py:31
  119.1 9.7 %collective-permute-start.5 = (bf16[352,128]{1,0:T(8,128)(2,1)S(1)}, bf16[352,128]{1,0:T(8,128)(2,1)S(1)}, u32[]{:S(2)}, u32[]{:S(2)}) collective-permute-start(bf16[352,128]{1,0:T(8,128)(2,1)S(1)} %convert_element_type.65), channel_id=1, source_target_pairs={{0,4},{4,0},{1,5},{5,1},{2,6},{6,2},{3,7},{7,3},{8,12},{12,8},{9,1... | collective-permute-start | bytes 270344 | tf_op jit(solution)/shard_map/ppermute | solution.py:23
  128.9 6.6 %collective-permute-done.5 = bf16[352,128]{1,0:T(8,128)(2,1)S(1)} collective-permute-done((bf16[352,128]{1,0:T(8,128)(2,1)S(1)}, bf16[352,128]{1,0:T(8,128)(2,1)S(1)}, u32[]{:S(2)}, u32[]{:S(2)}) %collective-permute-start.5) | collective-permute-done | bytes 90144 | tf_op jit(solution)/shard_map/ppermute | solution.py:23
  135.9 10.3 %all_to_all.20.x = bf16[4,360,128]{2,1,0:T(8,128)(2,1)} all-to-all(bf16[4,360,128]{2,1,0:T(8,128)(2,1)S(1)} %broadcast_in_dim.16), channel_id=1, replica_groups=mesh['x'=4,'c'=2,'zl'=8,'zh'=2,'y'=4] {'y'}, dimensions={0} | all-to-all | bytes 737280 | tf_op jit(solution)/shard_map/all_to_all | solution.py:31
  146.3 6.0 %both_mm.1 = (bf16[2,88,1792]{2,1,0:T(8,128)(2,1)}, f32[2,88,1792]{2,1,0:T(8,128)}) custom-call(s32[3]{0:T(128)} %pad_add_fusion.at, bf16[4,360,128]{2,1,0:T(8,128)(2,1)} %all_to_all.20.x, bf16[512,3584]{1,0:T(8,128)(2,1)} %stack.52.own, bf16[512,3584]{1,0:T(8,128)(2,1)} %collective-permute-done.12.other), custom_call_target="tpu_custom_call" | custom-call | flops 1291845632 | bytes 9437184 | tf_op jit(solution)/shard_map/both_mm/pallas_call | solution.py:125
  152.3 2.0 collective-permute-start.13
  155.0 9.8 %collective-permute-done.13 = bf16[2,88,1792]{2,1,0:T(8,128)(2,1)S(1)} collective-permute-done((bf16[2,88,1792]{2,1,0:T(8,128)(2,1)}, bf16[2,88,1792]{2,1,0:T(8,128)(2,1)S(1)}, u32[]{:S(2)}, u32[]{:S(2)}) %collective-permute-start.13) | collective-permute-done | bytes 630816 | tf_op jit(solution)/shard_map/ppermute | solution.py:23
  165.7 6.5 %collective-permute-start.14 = (bf16[88,1792]{1,0:T(8,128)(2,1)}, bf16[88,1792]{1,0:T(8,128)(2,1)S(1)}, u32[]{:S(2)}, u32[]{:S(2)}) collective-permute-start(bf16[88,1792]{1,0:T(8,128)(2,1)} %fusion), channel_id=1, source_target_pairs={{0,16},{8,24},{16,0},{24,8},{32,48},{40,56},{48,32},{56,40},{1,17}... | collective-permute-start | bytes 946184 | tf_op jit(solution)/shard_map/ppermute | solution.py:23
  172.2 3.4 %collective-permute-start.6 = (f32[2,128]{1,0:T(2,128)S(1)}, f32[2,128]{1,0:T(2,128)S(1)}, u32[]{:S(2)}, u32[]{:S(2)}) collective-permute-start(f32[2,128]{1,0:T(2,128)S(1)} %slice_add_fusion), channel_id=1, source_target_pairs={{0,8},{8,0},{16,24},{24,16},{32,40},{40,32},{48,56},{56,48},{1,9},... | collective-permute-start | bytes 3080 | tf_op jit(solution)/shard_map/ppermute | solution.py:23
  175.6 4.6 %collective-permute-start.19 = (bf16[224,1024]{1,0:T(8,128)(2,1)}, bf16[224,1024]{1,0:T(8,128)(2,1)S(1)}, u32[]{:S(2)}, u32[]{:S(2)}) collective-permute-start(bf16[224,1024]{1,0:T(8,128)(2,1)} %refs_0_.3), channel_id=1, source_target_pairs={{0,128},{128,256},{256,384},{384,0},{1,129},{129,257},{257,385},{3... | collective-permute-start | bytes 1376264 | tf_op jit(solution)/shard_map/ppermute | solution.py:18
  180.2 3.8 %collective-permute-start.20 = (bf16[224,1024]{1,0:T(8,128)(2,1)}, bf16[224,1024]{1,0:T(8,128)(2,1)}, u32[]{:S(2)}, u32[]{:S(2)}) collective-permute-start(bf16[224,1024]{1,0:T(8,128)(2,1)} %refs_0_.3), channel_id=1, source_target_pairs={{0,256},{128,384},{256,0},{384,128},{1,257},{129,385},{257,1},{385... | collective-permute-start | bytes 1376264 | tf_op jit(solution)/shard_map/ppermute | solution.py:18
  184.0 2.7 collective-permute-start.21
  186.7 1.9 collective-permute-start.7
  188.7 4.4 %collective-permute-done.7 = f32[2,128]{1,0:T(2,128)S(1)} collective-permute-done((f32[2,128]{1,0:T(2,128)S(1)}, f32[2,128]{1,0:T(2,128)S(1)}, u32[]{:S(2)}, u32[]{:S(2)}) %collective-permute-start.7) | collective-permute-done | bytes 1056 | tf_op jit(solution)/shard_map/ppermute | solution.py:23
  193.1 5.0 %collective-permute-start.8 = (f32[2,128]{1,0:T(2,128)S(1)}, f32[2,128]{1,0:T(2,128)S(1)}, u32[]{:S(2)}, u32[]{:S(2)}) collective-permute-start(f32[2,128]{1,0:T(2,128)S(1)} %add.93), channel_id=1, source_target_pairs={{0,32},{8,40},{16,48},{24,56},{32,0},{40,8},{48,16},{56,24},{1,33}... | collective-permute-start | bytes 3080 | tf_op jit(solution)/shard_map/ppermute | solution.py:23
  198.2 4.8 %collective-permute-start.15 = (bf16[48,1792]{1,0:T(8,128)(2,1)S(1)}, bf16[48,1792]{1,0:T(8,128)(2,1)S(1)}, u32[]{:S(2)}, u32[]{:S(2)}) collective-permute-start(bf16[48,1792]{1,0:T(8,128)(2,1)S(1)} %dynamic-slice_convert_fusion), channel_id=1, source_target_pairs={{0,32},{8,40},{16,48},{24,56},{32,0},{40,8},{48,16},{56,24},{1,33}... | collective-permute-start | bytes 516104 | tf_op jit(solution)/shard_map/ppermute | solution.py:23
  203.1 15.0 %collective-permute-done.15 = bf16[48,1792]{1,0:T(8,128)(2,1)S(1)} collective-permute-done((bf16[48,1792]{1,0:T(8,128)(2,1)S(1)}, bf16[48,1792]{1,0:T(8,128)(2,1)S(1)}, u32[]{:S(2)}, u32[]{:S(2)}) %collective-permute-start.15) | collective-permute-done | bytes 172064 | tf_op jit(solution)/shard_map/ppermute | solution.py:23
  218.3 1.9 collective-permute-start.16
  221.0 2.8 stack.53.own
  223.8 1.9 collective-permute-start.22
  225.7 3.1 %collective-permute-done.16 = bf16[48,896]{1,0:T(8,128)(2,1)S(1)} collective-permute-done((bf16[48,896]{1,0:T(8,128)(2,1)S(1)}, bf16[48,896]{1,0:T(8,128)(2,1)S(1)}, u32[]{:S(2)}, u32[]{:S(2)}) %collective-permute-start.16) | collective-permute-done | bytes 86048 | tf_op jit(solution)/shard_map/ppermute | solution.py:23
  229.0 1.9 collective-permute-start.17
  230.9 8.8 %collective-permute-done.17 = bf16[88,896]{1,0:T(8,128)(2,1)S(1)} collective-permute-done((bf16[88,896]{1,0:T(8,128)(2,1)S(1)}, bf16[88,896]{1,0:T(8,128)(2,1)S(1)}, u32[]{:S(2)}, u32[]{:S(2)}) %collective-permute-start.17) | collective-permute-done | bytes 157728 | tf_op jit(solution)/shard_map/ppermute | solution.py:23
  239.8 1.9 collective-permute-start.18
  241.8 9.3 %collective-permute-done.18 = bf16[88,1792]{1,0:T(8,128)(2,1)S(1)} collective-permute-done((bf16[88,1792]{1,0:T(8,128)(2,1)S(1)}, bf16[88,1792]{1,0:T(8,128)(2,1)S(1)}, u32[]{:S(2)}, u32[]{:S(2)}) %collective-permute-start.18) | collective-permute-done | bytes 315424 | tf_op jit(solution)/shard_map/ppermute | solution.py:23
  253.3 4.7 %down_mm.1 = bf16[4,352,128]{2,1,0:T(8,128)(2,1)} custom-call(s32[3]{0:T(128)} %pad_add_fusion.at, bf16[176,1792]{1,0:T(8,128)(2,1)} %pad_maximum_fusion.1.x, bf16[896,1024]{1,0:T(8,128)(2,1)} %stack.53.own, bf16[896,1024]{1,0:T(8,128)(2,1)} %copy-done.1), custom_call_target="tpu_custom_call" | custom-call | flops 645922816 | bytes 5242880 | tf_op jit(solution)/shard_map/down_mm/pallas_call | solution.py:168
  258.0 4.9 %all-to-all-start.3 = ((bf16[4,352,128]{2,1,0:T(8,128)(2,1)}), bf16[4,352,128]{2,1,0:T(8,128)(2,1)S(1)}, u32[]{:S(2)}, u32[]{:S(2)}) async-start(bf16[4,352,128]{2,1,0:T(8,128)(2,1)} %down_mm.1), calls=%async_computation.3 | async-start | bytes 720896 | tf_op jit(solution)/shard_map/all_to_all | solution.py:31
  262.9 5.9 %all-to-all-done.3 = bf16[4,352,128]{2,1,0:T(8,128)(2,1)S(1)} async-done(((bf16[4,352,128]{2,1,0:T(8,128)(2,1)}), bf16[4,352,128]{2,1,0:T(8,128)(2,1)S(1)}, u32[]{:S(2)}, u32[]{:S(2)}) %all-to-all-start.3) | async-done | bytes 360480 | tf_op jit(solution)/shard_map/all_to_all | solution.py:31
  268.9 9.3 %collective-permute-start.23 = (bf16[176,128]{1,0:T(8,128)(2,1)S(1)}, bf16[176,128]{1,0:T(8,128)(2,1)S(1)}, u32[]{:S(2)}, u32[]{:S(2)}) collective-permute-start(bf16[176,128]{1,0:T(8,128)(2,1)S(1)} %fusion.5), channel_id=1, source_target_pairs={{0,4},{4,0},{1,5},{5,1},{2,6},{6,2},{3,7},{7,3},{8,12},{12,8},{9,1... | collective-permute-start | bytes 135176 | tf_op jit(solution)/shard_map/ppermute | solution.py:23
  278.2 6.3 %collective-permute-done.23 = bf16[176,128]{1,0:T(8,128)(2,1)S(1)} collective-permute-done((bf16[176,128]{1,0:T(8,128)(2,1)S(1)}, bf16[176,128]{1,0:T(8,128)(2,1)S(1)}, u32[]{:S(2)}, u32[]{:S(2)}) %collective-permute-start.23) | collective-permute-done | bytes 45088 | tf_op jit(solution)/shard_map/ppermute | solution.py:23
  (87 shorter events, 14.4 us)
Async XLA Ops:
  1.4 47.7 %copy-start = (bf16[128,3584]{1,0:T(8,128)(2,1)}, bf16[128,3584]{1,0:T(8,128)(2,1)S(1)}, u32[]{:S(2)}) copy-start(bf16[128,3584]{1,0:T(8,128)(2,1)S(1)} %pad_maximum_fusion.refs_0_) | copy-start | bytes 2752516
  1.4 53.7 %copy-start.8 = (bf16[128,1024]{1,0:T(8,128)(2,1)S(1)}, bf16[128,1024]{1,0:T(8,128)(2,1)}, u32[]{:S(2)}) copy-start(bf16[128,1024]{1,0:T(8,128)(2,1)} %refs_0_.2) | copy-start | bytes 786436
  1.5 65.2 %copy-start.13 = (bf16[176,128]{1,0:T(8,128)(2,1)S(1)}, bf16[176,128]{1,0:T(8,128)(2,1)}, u32[]{:S(2)}) copy-start(bf16[176,128]{1,0:T(8,128)(2,1)} %param.7) | copy-start | bytes 135172
  1.5 25.5 %collective-permute-start.9 = (bf16[128,3584]{1,0:T(8,128)(2,1)S(1)}, bf16[128,3584]{1,0:T(8,128)(2,1)S(1)}, u32[]{:S(2)}, u32[]{:S(2)}) collective-permute-start(bf16[128,3584]{1,0:T(8,128)(2,1)S(1)} %pad_maximum_fusion.refs_0_), channel_id=1, source_target_pairs={{0,128},{128,256},{256,384},{384,0},{1,129},{129,257},{257,385},{3... | collective-permute-start | bytes 2752520 | tf_op jit(solution)/shard_map/ppermute | solution.py:18
  5.0 42.4 %collective-permute-start.10 = (bf16[128,3584]{1,0:T(8,128)(2,1)S(1)}, bf16[128,3584]{1,0:T(8,128)(2,1)S(1)}, u32[]{:S(2)}, u32[]{:S(2)}) collective-permute-start(bf16[128,3584]{1,0:T(8,128)(2,1)S(1)} %pad_maximum_fusion.refs_0_), channel_id=1, source_target_pairs={{0,256},{128,384},{256,0},{384,128},{1,257},{129,385},{257,1},{385... | collective-permute-start | bytes 2752520 | tf_op jit(solution)/shard_map/ppermute | solution.py:18
  9.7 39.4 %collective-permute-start.11 = (bf16[128,3584]{1,0:T(8,128)(2,1)S(1)}, bf16[128,3584]{1,0:T(8,128)(2,1)}, u32[]{:S(2)}, u32[]{:S(2)}) collective-permute-start(bf16[128,3584]{1,0:T(8,128)(2,1)S(1)} %pad_maximum_fusion.refs_0_), channel_id=1, source_target_pairs={{0,384},{128,0},{256,128},{384,256},{1,385},{129,1},{257,129},{385... | collective-permute-start | bytes 2752520 | tf_op jit(solution)/shard_map/ppermute | solution.py:18
  26.9 22.2 %copy-start.5 = (bf16[128,3584]{1,0:T(8,128)(2,1)}, bf16[128,3584]{1,0:T(8,128)(2,1)S(1)}, u32[]{:S(2)}) copy-start(bf16[128,3584]{1,0:T(8,128)(2,1)S(1)} %collective-permute-done.9.refs_1_) | copy-start | bytes 2752516
  47.4 1.7 copy-start.6
  53.1 32.6 %copy-start.14 = (f32[128]{0:T(128)S(1)}, f32[128]{0:T(128)}, u32[]{:S(2)}) copy-start(f32[128]{0:T(128)} %param.10) | copy-start | bytes 1540
  53.1 32.6 %copy-start.12 = (bf16[176,128]{1,0:T(8,128)(2,1)S(1)}, bf16[176,128]{1,0:T(8,128)(2,1)}, u32[]{:S(2)}) copy-start(bf16[176,128]{1,0:T(8,128)(2,1)} %param.8) | copy-start | bytes 135172
  53.1 93.1 %collective-permute-start.12 = (bf16[512,3584]{1,0:T(8,128)(2,1)}, bf16[512,3584]{1,0:T(8,128)(2,1)}, u32[]{:S(2)}, u32[]{:S(2)}) collective-permute-start(bf16[512,3584]{1,0:T(8,128)(2,1)} %stack.52.own), channel_id=1, source_target_pairs={{0,64},{64,0},{1,65},{65,1},{2,66},{66,2},{3,67},{67,3},{4,68},{68... | collective-permute-start | bytes 11010056 | tf_op jit(solution)/shard_map/ppermute | solution.py:23
  55.2 24.8 %collective-permute-start.1 = (bf16[128,1024]{1,0:T(8,128)(2,1)S(1)}, bf16[128,1024]{1,0:T(8,128)(2,1)S(1)}, u32[]{:S(2)}, u32[]{:S(2)}) collective-permute-start(bf16[128,1024]{1,0:T(8,128)(2,1)S(1)} %copy-done.8), channel_id=1, source_target_pairs={{0,128},{128,256},{256,384},{384,0},{1,129},{129,257},{257,385},{3... | collective-permute-start | bytes 786440 | tf_op jit(solution)/shard_map/ppermute | solution.py:18
  59.5 20.5 %collective-permute-start.2 = (bf16[128,1024]{1,0:T(8,128)(2,1)S(1)}, bf16[128,1024]{1,0:T(8,128)(2,1)S(1)}, u32[]{:S(2)}, u32[]{:S(2)}) collective-permute-start(bf16[128,1024]{1,0:T(8,128)(2,1)S(1)} %copy-done.8), channel_id=1, source_target_pairs={{0,256},{128,384},{256,0},{384,128},{1,257},{129,385},{257,1},{385... | collective-permute-start | bytes 786440 | tf_op jit(solution)/shard_map/ppermute | solution.py:18
  63.1 16.9 %collective-permute-start.3 = (bf16[128,1024]{1,0:T(8,128)(2,1)S(1)}, bf16[128,1024]{1,0:T(8,128)(2,1)S(1)}, u32[]{:S(2)}, u32[]{:S(2)}) collective-permute-start(bf16[128,1024]{1,0:T(8,128)(2,1)S(1)} %copy-done.8), channel_id=1, source_target_pairs={{0,384},{128,0},{256,128},{384,256},{1,385},{129,1},{257,129},{385... | collective-permute-start | bytes 786440 | tf_op jit(solution)/shard_map/ppermute | solution.py:18
  67.4 36.2 %all-to-all-start = ((bf16[8,176,128]{2,1,0:T(8,128)(2,1)}), bf16[8,176,128]{2,1,0:T(8,128)(2,1)S(1)}, u32[]{:S(2)}, u32[]{:S(2)}) async-start(bf16[8,176,128]{2,1,0:T(8,128)(2,1)} %broadcast_in_dim.13), calls=%async_computation | async-start | bytes 720896 | tf_op jit(solution)/shard_map/all_to_all | solution.py:31
  80.0 0.7 copy-start.9
  80.0 0.8 copy-start.10
  80.8 0.7 copy-start.11
  83.8 19.8 %collective-permute-start.4 = (bf16[512,1024]{1,0:T(8,128)(2,1)}, bf16[512,1024]{1,0:T(8,128)(2,1)S(1)}, u32[]{:S(2)}, u32[]{:S(2)}) collective-permute-start(bf16[512,1024]{1,0:T(8,128)(2,1)} %stack.51.own), channel_id=1, source_target_pairs={{0,64},{64,0},{1,65},{65,1},{2,66},{66,2},{3,67},{67,3},{4,68},{68... | collective-permute-start | bytes 3145736 | tf_op jit(solution)/shard_map/ppermute | solution.py:23
  85.8 14.9 %collective-permute-start = (bf16[184,128]{1,0:T(8,128)(2,1)S(1)}, bf16[184,128]{1,0:T(8,128)(2,1)S(1)}, u32[]{:S(2)}, u32[]{:S(2)}) collective-permute-start(bf16[184,128]{1,0:T(8,128)(2,1)S(1)} %pad_maximum_fusion.4), channel_id=1, source_target_pairs={{0,4},{4,0},{1,5},{5,1},{2,6},{6,2},{3,7},{7,3},{8,12},{12,8},{9,1... | collective-permute-start | bytes 141320 | tf_op jit(solution)/shard_map/ppermute | solution.py:23
  103.6 0.7 copy-start.2
  104.4 1.0 copy-start.4
  108.4 10.7 %all-to-all-start.1 = ((bf16[4,352,128]{2,1,0:T(8,128)(2,1)}), bf16[4,352,128]{2,1,0:T(8,128)(2,1)S(1)}, u32[]{:S(2)}, u32[]{:S(2)}) async-start(bf16[4,352,128]{2,1,0:T(8,128)(2,1)} %proj_mm.1), calls=%async_computation.1 | async-start | bytes 720896 | tf_op jit(solution)/shard_map/all_to_all | solution.py:31
  119.1 16.3 %collective-permute-start.5 = (bf16[352,128]{1,0:T(8,128)(2,1)S(1)}, bf16[352,128]{1,0:T(8,128)(2,1)S(1)}, u32[]{:S(2)}, u32[]{:S(2)}) collective-permute-start(bf16[352,128]{1,0:T(8,128)(2,1)S(1)} %convert_element_type.65), channel_id=1, source_target_pairs={{0,4},{4,0},{1,5},{5,1},{2,6},{6,2},{3,7},{7,3},{8,12},{12,8},{9,1... | collective-permute-start | bytes 270344 | tf_op jit(solution)/shard_map/ppermute | solution.py:23
  152.2 12.6 %copy-start.3 = (f32[2,88,1792]{2,1,0:T(8,128)S(1)}, f32[2,88,1792]{2,1,0:T(8,128)}, u32[]{:S(2)}) copy-start(f32[2,88,1792]{2,1,0:T(8,128)} %get-tuple-element.7) | copy-start | bytes 3784708
  152.3 12.6 %collective-permute-start.13 = (bf16[2,88,1792]{2,1,0:T(8,128)(2,1)}, bf16[2,88,1792]{2,1,0:T(8,128)(2,1)S(1)}, u32[]{:S(2)}, u32[]{:S(2)}) collective-permute-start(bf16[2,88,1792]{2,1,0:T(8,128)(2,1)} %get-tuple-element.8), channel_id=1, source_target_pairs={{0,8},{8,0},{16,24},{24,16},{32,40},{40,32},{48,56},{56,48},{1,9},... | collective-permute-start | bytes 1892360 | tf_op jit(solution)/shard_map/ppermute | solution.py:23
  165.7 32.4 %collective-permute-start.14 = (bf16[88,1792]{1,0:T(8,128)(2,1)}, bf16[88,1792]{1,0:T(8,128)(2,1)S(1)}, u32[]{:S(2)}, u32[]{:S(2)}) collective-permute-start(bf16[88,1792]{1,0:T(8,128)(2,1)} %fusion), channel_id=1, source_target_pairs={{0,16},{8,24},{16,0},{24,8},{32,48},{40,56},{48,32},{56,40},{1,17}... | collective-permute-start | bytes 946184 | tf_op jit(solution)/shard_map/ppermute | solution.py:23
  172.2 14.5 %collective-permute-start.6 = (f32[2,128]{1,0:T(2,128)S(1)}, f32[2,128]{1,0:T(2,128)S(1)}, u32[]{:S(2)}, u32[]{:S(2)}) collective-permute-start(f32[2,128]{1,0:T(2,128)S(1)} %slice_add_fusion), channel_id=1, source_target_pairs={{0,8},{8,0},{16,24},{24,16},{32,40},{40,32},{48,56},{56,48},{1,9},... | collective-permute-start | bytes 3080 | tf_op jit(solution)/shard_map/ppermute | solution.py:23
  175.6 44.7 %collective-permute-start.19 = (bf16[224,1024]{1,0:T(8,128)(2,1)}, bf16[224,1024]{1,0:T(8,128)(2,1)S(1)}, u32[]{:S(2)}, u32[]{:S(2)}) collective-permute-start(bf16[224,1024]{1,0:T(8,128)(2,1)} %refs_0_.3), channel_id=1, source_target_pairs={{0,128},{128,256},{256,384},{384,0},{1,129},{129,257},{257,385},{3... | collective-permute-start | bytes 1376264 | tf_op jit(solution)/shard_map/ppermute | solution.py:18
  180.2 40.1 %collective-permute-start.20 = (bf16[224,1024]{1,0:T(8,128)(2,1)}, bf16[224,1024]{1,0:T(8,128)(2,1)}, u32[]{:S(2)}, u32[]{:S(2)}) collective-permute-start(bf16[224,1024]{1,0:T(8,128)(2,1)} %refs_0_.3), channel_id=1, source_target_pairs={{0,256},{128,384},{256,0},{384,128},{1,257},{129,385},{257,1},{385... | collective-permute-start | bytes 1376264 | tf_op jit(solution)/shard_map/ppermute | solution.py:18
  184.0 36.3 %collective-permute-start.21 = (bf16[224,1024]{1,0:T(8,128)(2,1)}, bf16[224,1024]{1,0:T(8,128)(2,1)}, u32[]{:S(2)}, u32[]{:S(2)}) collective-permute-start(bf16[224,1024]{1,0:T(8,128)(2,1)} %refs_0_.3), channel_id=1, source_target_pairs={{0,384},{128,0},{256,128},{384,256},{1,385},{129,1},{257,129},{385... | collective-permute-start | bytes 1376264 | tf_op jit(solution)/shard_map/ppermute | solution.py:18
  186.7 6.4 %collective-permute-start.7 = (f32[2,128]{1,0:T(2,128)S(1)}, f32[2,128]{1,0:T(2,128)S(1)}, u32[]{:S(2)}, u32[]{:S(2)}) collective-permute-start(f32[2,128]{1,0:T(2,128)S(1)} %fusion.20), channel_id=1, source_target_pairs={{0,16},{8,24},{16,0},{24,8},{32,48},{40,56},{48,32},{56,40},{1,17}... | collective-permute-start | bytes 3080 | tf_op jit(solution)/shard_map/ppermute | solution.py:23
  193.1 9.9 %collective-permute-start.8 = (f32[2,128]{1,0:T(2,128)S(1)}, f32[2,128]{1,0:T(2,128)S(1)}, u32[]{:S(2)}, u32[]{:S(2)}) collective-permute-start(f32[2,128]{1,0:T(2,128)S(1)} %add.93), channel_id=1, source_target_pairs={{0,32},{8,40},{16,48},{24,56},{32,0},{40,8},{48,16},{56,24},{1,33}... | collective-permute-start | bytes 3080 | tf_op jit(solution)/shard_map/ppermute | solution.py:23
  198.2 19.9 %collective-permute-start.15 = (bf16[48,1792]{1,0:T(8,128)(2,1)S(1)}, bf16[48,1792]{1,0:T(8,128)(2,1)S(1)}, u32[]{:S(2)}, u32[]{:S(2)}) collective-permute-start(bf16[48,1792]{1,0:T(8,128)(2,1)S(1)} %dynamic-slice_convert_fusion), channel_id=1, source_target_pairs={{0,32},{8,40},{16,48},{24,56},{32,0},{40,8},{48,16},{56,24},{1,33}... | collective-permute-start | bytes 516104 | tf_op jit(solution)/shard_map/ppermute | solution.py:23
  218.3 10.5 %collective-permute-start.16 = (bf16[48,896]{1,0:T(8,128)(2,1)S(1)}, bf16[48,896]{1,0:T(8,128)(2,1)S(1)}, u32[]{:S(2)}, u32[]{:S(2)}) collective-permute-start(bf16[48,896]{1,0:T(8,128)(2,1)S(1)} %fusion.3), channel_id=1, source_target_pairs={{0,32},{8,40},{16,48},{24,56},{32,0},{40,8},{48,16},{56,24},{1,33}... | collective-permute-start | bytes 258056 | tf_op jit(solution)/shard_map/ppermute | solution.py:23
  220.2 0.8 copy-start.7
  223.8 28.3 %collective-permute-start.22 = (bf16[896,1024]{1,0:T(8,128)(2,1)}, bf16[896,1024]{1,0:T(8,128)(2,1)S(1)}, u32[]{:S(2)}, u32[]{:S(2)}) collective-permute-start(bf16[896,1024]{1,0:T(8,128)(2,1)} %stack.53.own), channel_id=1, source_target_pairs={{0,64},{64,0},{1,65},{65,1},{2,66},{66,2},{3,67},{67,3},{4,68},{68... | collective-permute-start | bytes 5505032 | tf_op jit(solution)/shard_map/ppermute | solution.py:23
  229.0 10.8 %collective-permute-start.17 = (bf16[88,896]{1,0:T(8,128)(2,1)S(1)}, bf16[88,896]{1,0:T(8,128)(2,1)S(1)}, u32[]{:S(2)}, u32[]{:S(2)}) collective-permute-start(bf16[88,896]{1,0:T(8,128)(2,1)S(1)} %pad_maximum_fusion.3), channel_id=1, source_target_pairs={{0,16},{8,24},{16,0},{24,8},{32,48},{40,56},{48,32},{56,40},{1,17}... | collective-permute-start | bytes 473096 | tf_op jit(solution)/shard_map/ppermute | solution.py:23
  239.8 11.3 %collective-permute-start.18 = (bf16[88,1792]{1,0:T(8,128)(2,1)S(1)}, bf16[88,1792]{1,0:T(8,128)(2,1)S(1)}, u32[]{:S(2)}, u32[]{:S(2)}) collective-permute-start(bf16[88,1792]{1,0:T(8,128)(2,1)S(1)} %pad_maximum_fusion.2), channel_id=1, source_target_pairs={{0,8},{8,0},{16,24},{24,16},{32,40},{40,32},{48,56},{56,48},{1,9},... | collective-permute-start | bytes 946184 | tf_op jit(solution)/shard_map/ppermute | solution.py:23
  252.1 1.2 copy-start.1
  258.0 10.8 %all-to-all-start.3 = ((bf16[4,352,128]{2,1,0:T(8,128)(2,1)}), bf16[4,352,128]{2,1,0:T(8,128)(2,1)S(1)}, u32[]{:S(2)}, u32[]{:S(2)}) async-start(bf16[4,352,128]{2,1,0:T(8,128)(2,1)} %down_mm.1), calls=%async_computation.3 | async-start | bytes 720896 | tf_op jit(solution)/shard_map/all_to_all | solution.py:31
  268.9 15.6 %collective-permute-start.23 = (bf16[176,128]{1,0:T(8,128)(2,1)S(1)}, bf16[176,128]{1,0:T(8,128)(2,1)S(1)}, u32[]{:S(2)}, u32[]{:S(2)}) collective-permute-start(bf16[176,128]{1,0:T(8,128)(2,1)S(1)} %fusion.5), channel_id=1, source_target_pairs={{0,4},{4,0},{1,5},{5,1},{2,6},{6,2},{3,7},{7,3},{8,12},{12,8},{9,1... | collective-permute-start | bytes 135176 | tf_op jit(solution)/shard_map/ppermute | solution.py:23

commit v4 on v3

--- a/solution.py
+++ b/solution.py
@@ -72,11 +72,16 @@
 
 
 def proj_kernel(at, x, own, other, out):
-    xi, ci = at[0], at[1]
+    xi, ci, zl = at[0], at[1], at[2]
     rows = x.shape[1]
+
+    def block(b):
+        off = b ^ zl
+        return x[((off >> 2) & 1) | (off & 2) | ((off & 1) << 2)]
+
     blocks = [((xi + 4 - k) & 3) * 2 for k in range(4)]
-    mine = jnp.concatenate([x[b + ci] for b in blocks], axis=1)
-    theirs = jnp.concatenate([x[b + 1 - ci] for b in blocks], axis=1)
+    mine = jnp.concatenate([block(b + ci) for b in blocks], axis=1)
+    theirs = jnp.concatenate([block(b + 1 - ci) for b in blocks], axis=1)
     part = (dot(mine, own[...]) + dot(theirs, other[...])).astype(BF)
     for zh in range(2):
         for y in range(4):
@@ -100,7 +105,7 @@
 
 
 def both_kernel(at, x, own, other, send, keep):
-    xi, ci, bit = at[0], at[1], at[2]
+    xi, ci, bit = at[0], at[1], at[2] & 1
     rows = 2 * send.shape[1]
     blocks = [(xi + 4 - k) & 3 for k in range(4)]
 
@@ -140,21 +145,15 @@
     )(at, x, own, other)
 
 
-def down_kernel(at, x, own, other, out, whole, sems):
+def down_kernel(at, x, own, other, out, whole):
     xi, ci = at[0], at[1]
     rows = x.shape[0]
     height = own.shape[0] // 4
-    copies = []
-    for j, (ref, core) in enumerate(((own, ci), (other, 1 - ci))):
+    for ref, core in ((own, ci), (other, 1 - ci)):
         for k in range(4):
             b = ((xi + 4 - k) & 3) * 2 + core
-            to = whole.at[pl.ds(pl.multiple_of(b * height, 16), height)]
-            source = ref.at[pl.ds(k * height, height)]
-            copies.append(pltpu.make_async_copy(source, to, sems.at[j * 4 + k]))
-    for copy in copies:
-        copy.start()
-    for copy in copies:
-        copy.wait()
+            to = pl.ds(pl.multiple_of(b * height, 16), height)
+            whole[to] = ref[k * height : (k + 1) * height]
     part = dot(x[...], whole[...]).astype(BF)
     for zh in range(2):
         for y in range(4):
@@ -164,13 +163,13 @@
 
 def down_parts(at, x, own, other):
     rows, depth = x.shape
-    vmem, hbm = pl.BlockSpec(memory_space=pltpu.VMEM), pl.BlockSpec(memory_space=pltpu.HBM)
+    vmem = pl.BlockSpec(memory_space=pltpu.VMEM)
     return pl.pallas_call(
         down_kernel,
         out_shape=jax.ShapeDtypeStruct((4, 2 * rows, 128), BF),
-        in_specs=[pl.BlockSpec(memory_space=pltpu.SMEM), vmem, hbm, hbm],
+        in_specs=[pl.BlockSpec(memory_space=pltpu.SMEM), vmem, vmem, vmem],
         out_specs=vmem,
-        scratch_shapes=[pltpu.VMEM((depth, 1024), BF), pltpu.SemaphoreType.DMA((8,))],
+        scratch_shapes=[pltpu.VMEM((depth, 1024), BF)],
         cost_estimate=pl.CostEstimate(
             flops=2 * rows * depth * 1024, bytes_accessed=5 << 20, transcendentals=0
         ),
@@ -186,14 +185,16 @@
     xi, ci = lax.axis_index("x"), lax.axis_index("c")
     zl, zh = lax.axis_index("zl"), lax.axis_index("zh")
     bit0, bit1, bit2 = zl & 1, (zl >> 1) & 1, (zl >> 2) & 1
-    at = jnp.stack([xi, ci, bit0]).astype(jnp.int32)
+    at = jnp.stack([xi, ci, zl]).astype(jnp.int32)
     rows = attn_out.shape[0]
     half = rows // 2
     top = 48
     step = half - top
     ffw = gate_proj.shape[1] // 2
 
-    cols = from_everyone(attn_out, "zl")
+    cols = attn_out[None]
+    for step_bit in (4, 2, 1):
+        cols = jnp.concatenate([cols, swap(cols, "zl", step_bit)])
     proj_own, proj_other = gathered(proj_weight)
     pieces = [gate_proj[:, :ffw], up_proj[:, :ffw], gate_proj[:, ffw:], up_proj[:, ffw:]]
     both_own, both_other = gathered(jnp.concatenate(pieces, axis=1))
@@ -202,16 +203,16 @@
     high = exact(norm_gain)
     mid = exact(norm_gain - high)
     low = norm_gain - high - mid
-    gains = jnp.stack([high, mid, low]).astype(BF)
-    sent = jnp.concatenate([residual, jnp.pad(gains, ((0, 5), (0, 0)))])
-    facing = swap(sent, "zh", 1)
-    other_gain = facing[rows : rows + 3].astype(F32).sum(axis=0)
-    residual2 = jnp.concatenate(in_bits(residual, facing[:rows], zh)).astype(F32)
+    gains = jnp.pad(jnp.stack([high, mid, low]), ((0, 5), (0, 0)))
+
+    part = proj_parts(at, cols, proj_own, proj_other)
+    near = exchange(part, "y").astype(F32).sum(axis=0).reshape(2, rows, 128)
+    mine = jnp.arange(2)[:, None, None] == zh
+    near = jnp.where(mine, near + residual.astype(F32), near).reshape(2 * rows, 128)
+    far = swap(jnp.concatenate([near, gains]).astype(BF), "zh", 1).astype(F32)
+    stream2 = near + far[: 2 * rows]
+    other_gain = far[2 * rows : 2 * rows + 3].sum(axis=0)
     gain2 = jnp.repeat(jnp.stack(in_bits(norm_gain, other_gain, zh)), rows, axis=0)
-
-    part = proj_parts(at, cols, proj_own, proj_other)
-    near = exchange(part, "y").astype(F32).sum(axis=0)
-    stream2 = residual2 + near + swap(near.astype(BF), "zh", 1).astype(F32)
     squares = jnp.sum((stream2 * stream2).reshape(2, rows, 128), axis=(0, 2))
     scaled2 = (stream2 * gain2).astype(BF)
     squares = jnp.pad(squares, (0, 256 - rows)).reshape(2, 128)

time: 286 us -> 293 us (1.024)
  waiting for transfers between devices: 118 us -> 130 us
  starting transfers between devices: 121 us -> 117 us
    all_to_all x3 -> x2, starting transfers between devices: 22.3 us -> 9.82 us  [exchange(): return lax.all_to_all(parts, axis, split_axis=0, concat_axis=0, tiled=True)]
    ppermute x15 -> x17, starting transfers between devices: 64.3 us -> 73.2 us  [swap(): return lax.ppermute(value, axis, [(i, i ^ bit) for i in range(n)])]
    ppermute x9, waiting for transfers between devices: 36.1 us -> 44.6 us  [shift(): return lax.ppermute(value, axis, [(i, (i + step) % n) for i in range(n)])]
    ppermute x15 -> x17, waiting for transfers between devices: 67.3 us -> 74 us  [swap(): return lax.ppermute(value, axis, [(i, i ^ bit) for i in range(n)])]
    all_to_all x3 -> x2, waiting for transfers between devices: 14.5 us -> 11.5 us  [exchange(): return lax.all_to_all(parts, axis, split_axis=0, concat_axis=0, tiled=True)]
  transfers between devices with their start and end apart: 27 -> 28, of which waited for: 15 -> 20; matrix products, arithmetic and copies ran while one was open for 2% -> 2% of each run, Pallas kernels for 3% -> 3%
where the time goes in v4:
time: 293 us; the launch traced here: 292 us
  waiting for transfers between devices  130 us (44%)
  starting transfers between devices  117 us (40%)
  Pallas kernels  22.2 us (8%)
  blocking collectives  10.3 us (4%)
  other arithmetic  6 us (2%)
  local copies, waits for them, and re-layouts  5.51 us (2%)
    ppermute x17, waiting for transfers between devices, swap(): return lax.ppermute(value, axis, [(i, i ^ bit) for i in range(n)])  74 us
    ppermute x17, starting transfers between devices, swap(): return lax.ppermute(value, axis, [(i, i ^ bit) for i in range(n)])  73.2 us
    ppermute x9, waiting for transfers between devices, shift(): return lax.ppermute(value, axis, [(i, (i + step) % n) for i in range(n)])  44.6 us
    ppermute x9, starting transfers between devices, shift(): return lax.ppermute(value, axis, [(i, (i + step) % n) for i in range(n)])  34.3 us
    all_to_all x2, waiting for transfers between devices, exchange(): return lax.all_to_all(parts, axis, split_axis=0, concat_axis=0, tiled=True)  11.5 us
    all_to_all x1, blocking collectives, exchange(): return lax.all_to_all(parts, axis, split_axis=0, concat_axis=0, tiled=True)  10.3 us
    all_to_all x2, starting transfers between devices, exchange(): return lax.all_to_all(parts, axis, split_axis=0, concat_axis=0, tiled=True)  9.82 us
    pallas_call x3, Pallas kernels, stacked(): pl.pallas_call(stack_kernel, out_shape=jax.ShapeDtypeStruct((len(parts) *...  9.17 us
  transfers between devices with their start and end apart: 28, of which 20 were waited for; matrix products, arithmetic and copies ran while one was open for 2% of the time, Pallas kernels for 3%

profile of v4, /device:TPU:8, one launch (start us, length us, event | category | flops | bytes accessed | tf_op | source)
XLA Modules:
  0.0 292.1 jit_solution(3018582763869193950)
XLA Ops:
  1.5 3.5 %collective-permute-start.11 = (bf16[128,3584]{1,0:T(8,128)(2,1)S(1)}, bf16[128,3584]{1,0:T(8,128)(2,1)S(1)}, u32[]{:S(2)}, u32[]{:S(2)}) collective-permute-start(bf16[128,3584]{1,0:T(8,128)(2,1)S(1)} %pad_maximum_fusion.refs_0_), channel_id=1, source_target_pairs={{0,128},{128,256},{256,384},{384,0},{1,129},{129,257},{257,385},{3... | collective-permute-start | bytes 2752520 | tf_op jit(solution)/shard_map/ppermute | solution.py:18
  5.0 4.6 %collective-permute-start.12 = (bf16[128,3584]{1,0:T(8,128)(2,1)S(1)}, bf16[128,3584]{1,0:T(8,128)(2,1)S(1)}, u32[]{:S(2)}, u32[]{:S(2)}) collective-permute-start(bf16[128,3584]{1,0:T(8,128)(2,1)S(1)} %pad_maximum_fusion.refs_0_), channel_id=1, source_target_pairs={{0,256},{128,384},{256,0},{384,128},{1,257},{129,385},{257,1},{385... | collective-permute-start | bytes 2752520 | tf_op jit(solution)/shard_map/ppermute | solution.py:18
  9.6 3.3 %collective-permute-start.13 = (bf16[128,3584]{1,0:T(8,128)(2,1)S(1)}, bf16[128,3584]{1,0:T(8,128)(2,1)}, u32[]{:S(2)}, u32[]{:S(2)}) collective-permute-start(bf16[128,3584]{1,0:T(8,128)(2,1)S(1)} %pad_maximum_fusion.refs_0_), channel_id=1, source_target_pairs={{0,384},{128,0},{256,128},{384,256},{1,385},{129,1},{257,129},{385... | collective-permute-start | bytes 2752520 | tf_op jit(solution)/shard_map/ppermute | solution.py:18
  13.0 13.9 %collective-permute-done.11.refs_1_ = bf16[128,3584]{1,0:T(8,128)(2,1)S(1)} collective-permute-done((bf16[128,3584]{1,0:T(8,128)(2,1)S(1)}, bf16[128,3584]{1,0:T(8,128)(2,1)S(1)}, u32[]{:S(2)}, u32[]{:S(2)}) %collective-permute-start.11) | collective-permute-done | bytes 917536 | tf_op jit(solution)/shard_map/ppermute | solution.py:18
  26.9 20.5 %collective-permute-done.12.refs_2_ = bf16[128,3584]{1,0:T(8,128)(2,1)S(1)} collective-permute-done((bf16[128,3584]{1,0:T(8,128)(2,1)S(1)}, bf16[128,3584]{1,0:T(8,128)(2,1)S(1)}, u32[]{:S(2)}, u32[]{:S(2)}) %collective-permute-start.12) | collective-permute-done | bytes 917536 | tf_op jit(solution)/shard_map/ppermute | solution.py:18
  49.1 4.0 %stack.52.own = bf16[512,3584]{1,0:T(8,128)(2,1)} custom-call(bf16[128,3584]{1,0:T(8,128)(2,1)} %copy-done, bf16[128,3584]{1,0:T(8,128)(2,1)} %copy-done.4, bf16[128,3584]{1,0:T(8,128)(2,1)} %copy-done.5, bf16[128,3584]{1,0:T(8,128)(2,1)} %collective-permute-done.13.refs_3_), custom_call_target="tpu_custom_call" | custom-call | tf_op jit(solution)/shard_map/stack/pallas_call | solution.py:55
  53.1 2.0 collective-permute-start.14
  55.2 4.3 %collective-permute-start.3 = (bf16[128,1024]{1,0:T(8,128)(2,1)S(1)}, bf16[128,1024]{1,0:T(8,128)(2,1)S(1)}, u32[]{:S(2)}, u32[]{:S(2)}) collective-permute-start(bf16[128,1024]{1,0:T(8,128)(2,1)S(1)} %copy-done.8), channel_id=1, source_target_pairs={{0,128},{128,256},{256,384},{384,0},{1,129},{129,257},{257,385},{3... | collective-permute-start | bytes 786440 | tf_op jit(solution)/shard_map/ppermute | solution.py:18
  59.5 3.6 %collective-permute-start.4 = (bf16[128,1024]{1,0:T(8,128)(2,1)S(1)}, bf16[128,1024]{1,0:T(8,128)(2,1)S(1)}, u32[]{:S(2)}, u32[]{:S(2)}) collective-permute-start(bf16[128,1024]{1,0:T(8,128)(2,1)S(1)} %copy-done.8), channel_id=1, source_target_pairs={{0,256},{128,384},{256,0},{384,128},{1,257},{129,385},{257,1},{385... | collective-permute-start | bytes 786440 | tf_op jit(solution)/shard_map/ppermute | solution.py:18
  63.1 3.5 %collective-permute-start.5 = (bf16[128,1024]{1,0:T(8,128)(2,1)S(1)}, bf16[128,1024]{1,0:T(8,128)(2,1)S(1)}, u32[]{:S(2)}, u32[]{:S(2)}) collective-permute-start(bf16[128,1024]{1,0:T(8,128)(2,1)S(1)} %copy-done.8), channel_id=1, source_target_pairs={{0,384},{128,0},{256,128},{384,256},{1,385},{129,1},{257,129},{385... | collective-permute-start | bytes 786440 | tf_op jit(solution)/shard_map/ppermute | solution.py:18
  67.0 6.5 %collective-permute-done.4.refs_2_ = bf16[128,1024]{1,0:T(8,128)(2,1)S(1)} collective-permute-done((bf16[128,1024]{1,0:T(8,128)(2,1)S(1)}, bf16[128,1024]{1,0:T(8,128)(2,1)S(1)}, u32[]{:S(2)}, u32[]{:S(2)}) %collective-permute-start.4) | collective-permute-done | bytes 262176 | tf_op jit(solution)/shard_map/ppermute | solution.py:18
  75.8 2.3 stack.51.own
  80.1 9.1 %collective-permute-start = (bf16[1,176,128]{2,1,0:T(8,128)(2,1)S(1)}, bf16[1,176,128]{2,1,0:T(8,128)(2,1)S(1)}, u32[]{:S(2)}, u32[]{:S(2)}) collective-permute-start(bf16[1,176,128]{2,1,0:T(8,128)(2,1)S(1)} %bitcast.45), channel_id=1, source_target_pairs={{0,32},{8,40},{16,48},{24,56},{32,0},{40,8},{48,16},{56,24},{1,33}... | collective-permute-start | bytes 135176 | tf_op jit(solution)/shard_map/ppermute | solution.py:23
  89.2 2.3 collective-permute-done
  91.5 5.5 %collective-permute-start.1 = (bf16[2,176,128]{2,1,0:T(8,128)(2,1)S(1)}, bf16[2,176,128]{2,1,0:T(8,128)(2,1)S(1)}, u32[]{:S(2)}, u32[]{:S(2)}) collective-permute-start(bf16[2,176,128]{2,1,0:T(8,128)(2,1)S(1)} %pad_maximum_fusion.7), channel_id=1, source_target_pairs={{0,16},{8,24},{16,0},{24,8},{32,48},{40,56},{48,32},{56,40},{1,17}... | collective-permute-start | bytes 270344 | tf_op jit(solution)/shard_map/ppermute | solution.py:23
  97.0 4.7 %collective-permute-done.1 = bf16[2,176,128]{2,1,0:T(8,128)(2,1)S(1)} collective-permute-done((bf16[2,176,128]{2,1,0:T(8,128)(2,1)S(1)}, bf16[2,176,128]{2,1,0:T(8,128)(2,1)S(1)}, u32[]{:S(2)}, u32[]{:S(2)}) %collective-permute-start.1) | collective-permute-done | bytes 90144 | tf_op jit(solution)/shard_map/ppermute | solution.py:23
  101.7 2.6 collective-permute-start.2
  105.2 4.0 %collective-permute-done.2 = bf16[4,176,128]{2,1,0:T(8,128)(2,1)S(1)} collective-permute-done((bf16[4,176,128]{2,1,0:T(8,128)(2,1)S(1)}, bf16[4,176,128]{2,1,0:T(8,128)(2,1)S(1)}, u32[]{:S(2)}, u32[]{:S(2)}) %collective-permute-start.2) | collective-permute-done | bytes 180256 | tf_op jit(solution)/shard_map/ppermute | solution.py:23
  110.9 3.0 %proj_mm.1 = bf16[4,352,128]{2,1,0:T(8,128)(2,1)} custom-call(s32[3]{0:T(128)} %pad_add_fusion.at, bf16[8,176,128]{2,1,0:T(8,128)(2,1)} %pad_maximum_fusion.2.x, bf16[512,1024]{1,0:T(8,128)(2,1)} %stack.51.own, bf16[512,1024]{1,0:T(8,128)(2,1)} %copy-done.3), custom_call_target="tpu_custom_call" | custom-call | flops 369098752 | bytes 3145728 | tf_op jit(solution)/shard_map/proj_mm/pallas_call | solution.py:95
  113.9 4.9 %all-to-all-start = ((bf16[4,352,128]{2,1,0:T(8,128)(2,1)}), bf16[4,352,128]{2,1,0:T(8,128)(2,1)S(1)}, u32[]{:S(2)}, u32[]{:S(2)}) async-start(bf16[4,352,128]{2,1,0:T(8,128)(2,1)} %proj_mm.1), calls=%async_computation | async-start | bytes 720896 | tf_op jit(solution)/shard_map/all_to_all | solution.py:31
  118.9 5.7 %all-to-all-done = bf16[4,352,128]{2,1,0:T(8,128)(2,1)S(1)} async-done(((bf16[4,352,128]{2,1,0:T(8,128)(2,1)}), bf16[4,352,128]{2,1,0:T(8,128)(2,1)S(1)}, u32[]{:S(2)}, u32[]{:S(2)}) %all-to-all-start) | async-done | bytes 360480 | tf_op jit(solution)/shard_map/all_to_all | solution.py:31
  124.8 14.7 %collective-permute-start.7 = (bf16[360,128]{1,0:T(8,128)(2,1)S(1)}, bf16[360,128]{1,0:T(8,128)(2,1)S(1)}, u32[]{:S(2)}, u32[]{:S(2)}) collective-permute-start(bf16[360,128]{1,0:T(8,128)(2,1)S(1)} %pad_maximum_fusion.6), channel_id=1, source_target_pairs={{0,4},{4,0},{1,5},{5,1},{2,6},{6,2},{3,7},{7,3},{8,12},{12,8},{9,1... | collective-permute-start | bytes 276488 | tf_op jit(solution)/shard_map/ppermute | solution.py:23
  139.6 4.4 %collective-permute-done.7 = bf16[360,128]{1,0:T(8,128)(2,1)S(1)} collective-permute-done((bf16[360,128]{1,0:T(8,128)(2,1)S(1)}, bf16[360,128]{1,0:T(8,128)(2,1)S(1)}, u32[]{:S(2)}, u32[]{:S(2)}) %collective-permute-start.7) | collective-permute-done | bytes 92192 | tf_op jit(solution)/shard_map/ppermute | solution.py:23
  144.6 10.3 %all_to_all.15.x = bf16[4,360,128]{2,1,0:T(8,128)(2,1)} all-to-all(bf16[4,360,128]{2,1,0:T(8,128)(2,1)S(1)} %broadcast_in_dim.33), channel_id=1, replica_groups=mesh['x'=4,'c'=2,'zl'=8,'zh'=2,'y'=4] {'y'}, dimensions={0} | all-to-all | bytes 737280 | tf_op jit(solution)/shard_map/all_to_all | solution.py:31
  155.0 6.0 %both_mm.1 = (bf16[2,88,1792]{2,1,0:T(8,128)(2,1)}, f32[2,88,1792]{2,1,0:T(8,128)}) custom-call(s32[3]{0:T(128)} %pad_add_fusion.at, bf16[4,360,128]{2,1,0:T(8,128)(2,1)} %all_to_all.15.x, bf16[512,3584]{1,0:T(8,128)(2,1)} %stack.52.own, bf16[512,3584]{1,0:T(8,128)(2,1)} %collective-permute-done.14.other), custom_call_target="tpu_custom_call" | custom-call | flops 1291845632 | bytes 9437184 | tf_op jit(solution)/shard_map/both_mm/pallas_call | solution.py:130
  161.0 2.0 collective-permute-start.15
  163.8 11.8 %collective-permute-done.15 = bf16[2,88,1792]{2,1,0:T(8,128)(2,1)S(1)} collective-permute-done((bf16[2,88,1792]{2,1,0:T(8,128)(2,1)}, bf16[2,88,1792]{2,1,0:T(8,128)(2,1)S(1)}, u32[]{:S(2)}, u32[]{:S(2)}) %collective-permute-start.15) | collective-permute-done | bytes 630816 | tf_op jit(solution)/shard_map/ppermute | solution.py:23
  176.4 2.7 collective-permute-start.16
  179.1 2.7 collective-permute-start.8
  181.8 4.4 %collective-permute-start.21 = (bf16[224,1024]{1,0:T(8,128)(2,1)}, bf16[224,1024]{1,0:T(8,128)(2,1)S(1)}, u32[]{:S(2)}, u32[]{:S(2)}) collective-permute-start(bf16[224,1024]{1,0:T(8,128)(2,1)} %refs_0_.3), channel_id=1, source_target_pairs={{0,128},{128,256},{256,384},{384,0},{1,129},{129,257},{257,385},{3... | collective-permute-start | bytes 1376264 | tf_op jit(solution)/shard_map/ppermute | solution.py:18
  186.3 3.6 %collective-permute-start.22 = (bf16[224,1024]{1,0:T(8,128)(2,1)}, bf16[224,1024]{1,0:T(8,128)(2,1)}, u32[]{:S(2)}, u32[]{:S(2)}) collective-permute-start(bf16[224,1024]{1,0:T(8,128)(2,1)} %refs_0_.3), channel_id=1, source_target_pairs={{0,256},{128,384},{256,0},{384,128},{1,257},{129,385},{257,1},{385... | collective-permute-start | bytes 1376264 | tf_op jit(solution)/shard_map/ppermute | solution.py:18
  189.9 3.4 %collective-permute-start.23 = (bf16[224,1024]{1,0:T(8,128)(2,1)}, bf16[224,1024]{1,0:T(8,128)(2,1)}, u32[]{:S(2)}, u32[]{:S(2)}) collective-permute-start(bf16[224,1024]{1,0:T(8,128)(2,1)} %refs_0_.3), channel_id=1, source_target_pairs={{0,384},{128,0},{256,128},{384,256},{1,385},{129,1},{257,129},{385... | collective-permute-start | bytes 1376264 | tf_op jit(solution)/shard_map/ppermute | solution.py:18
  193.3 3.1 %collective-permute-start.9 = (f32[2,128]{1,0:T(2,128)S(1)}, f32[2,128]{1,0:T(2,128)S(1)}, u32[]{:S(2)}, u32[]{:S(2)}) collective-permute-start(f32[2,128]{1,0:T(2,128)S(1)} %fusion.21), channel_id=1, source_target_pairs={{0,16},{8,24},{16,0},{24,8},{32,48},{40,56},{48,32},{56,40},{1,17}... | collective-permute-start | bytes 3080 | tf_op jit(solution)/shard_map/ppermute | solution.py:23
  196.5 3.2 %collective-permute-done.9 = f32[2,128]{1,0:T(2,128)S(1)} collective-permute-done((f32[2,128]{1,0:T(2,128)S(1)}, f32[2,128]{1,0:T(2,128)S(1)}, u32[]{:S(2)}, u32[]{:S(2)}) %collective-permute-start.9) | collective-permute-done | bytes 1056 | tf_op jit(solution)/shard_map/ppermute | solution.py:23
  199.7 9.5 %collective-permute-start.10 = (f32[2,128]{1,0:T(2,128)S(1)}, f32[2,128]{1,0:T(2,128)S(1)}, u32[]{:S(2)}, u32[]{:S(2)}) collective-permute-start(f32[2,128]{1,0:T(2,128)S(1)} %add.103), channel_id=1, source_target_pairs={{0,32},{8,40},{16,48},{24,56},{32,0},{40,8},{48,16},{56,24},{1,33}... | collective-permute-start | bytes 3080 | tf_op jit(solution)/shard_map/ppermute | solution.py:23
  209.3 1.9 collective-permute-start.17
  212.2 16.4 %collective-permute-done.17 = bf16[48,1792]{1,0:T(8,128)(2,1)S(1)} collective-permute-done((bf16[48,1792]{1,0:T(8,128)(2,1)S(1)}, bf16[48,1792]{1,0:T(8,128)(2,1)S(1)}, u32[]{:S(2)}, u32[]{:S(2)}) %collective-permute-start.17) | collective-permute-done | bytes 172064 | tf_op jit(solution)/shard_map/ppermute | solution.py:23
  228.8 1.9 collective-permute-start.18
  231.5 2.8 stack.53.own
  236.2 2.8 collective-permute-done.18
  241.2 7.5 %collective-permute-done.19 = bf16[88,896]{1,0:T(8,128)(2,1)S(1)} collective-permute-done((bf16[88,896]{1,0:T(8,128)(2,1)S(1)}, bf16[88,896]{1,0:T(8,128)(2,1)S(1)}, u32[]{:S(2)}, u32[]{:S(2)}) %collective-permute-start.19) | collective-permute-done | bytes 157728 | tf_op jit(solution)/shard_map/ppermute | solution.py:23
  248.7 1.9 collective-permute-start.20
  250.7 9.1 %collective-permute-done.20 = bf16[88,1792]{1,0:T(8,128)(2,1)S(1)} collective-permute-done((bf16[88,1792]{1,0:T(8,128)(2,1)S(1)}, bf16[88,1792]{1,0:T(8,128)(2,1)S(1)}, u32[]{:S(2)}, u32[]{:S(2)}) %collective-permute-start.20) | collective-permute-done | bytes 315424 | tf_op jit(solution)/shard_map/ppermute | solution.py:23
  262.0 4.1 %down_mm.1 = bf16[4,352,128]{2,1,0:T(8,128)(2,1)} custom-call(s32[3]{0:T(128)} %pad_add_fusion.at, bf16[176,1792]{1,0:T(8,128)(2,1)} %pad_maximum_fusion.1.x, bf16[896,1024]{1,0:T(8,128)(2,1)} %stack.53.own, bf16[896,1024]{1,0:T(8,128)(2,1)} %copy-done.1), custom_call_target="tpu_custom_call" | custom-call | flops 645922816 | bytes 5242880 | tf_op jit(solution)/shard_map/down_mm/pallas_call | solution.py:167
  266.1 4.9 %all-to-all-start.2 = ((bf16[4,352,128]{2,1,0:T(8,128)(2,1)}), bf16[4,352,128]{2,1,0:T(8,128)(2,1)S(1)}, u32[]{:S(2)}, u32[]{:S(2)}) async-start(bf16[4,352,128]{2,1,0:T(8,128)(2,1)} %down_mm.1), calls=%async_computation.2 | async-start | bytes 720896 | tf_op jit(solution)/shard_map/all_to_all | solution.py:31
  270.9 5.8 %all-to-all-done.2 = bf16[4,352,128]{2,1,0:T(8,128)(2,1)S(1)} async-done(((bf16[4,352,128]{2,1,0:T(8,128)(2,1)}), bf16[4,352,128]{2,1,0:T(8,128)(2,1)S(1)}, u32[]{:S(2)}, u32[]{:S(2)}) %all-to-all-start.2) | async-done | bytes 360480 | tf_op jit(solution)/shard_map/all_to_all | solution.py:31
  276.8 7.7 %collective-permute-start.25 = (bf16[176,128]{1,0:T(8,128)(2,1)S(1)}, bf16[176,128]{1,0:T(8,128)(2,1)S(1)}, u32[]{:S(2)}, u32[]{:S(2)}) collective-permute-start(bf16[176,128]{1,0:T(8,128)(2,1)S(1)} %fusion.6), channel_id=1, source_target_pairs={{0,4},{4,0},{1,5},{5,1},{2,6},{6,2},{3,7},{7,3},{8,12},{12,8},{9,1... | collective-permute-start | bytes 135176 | tf_op jit(solution)/shard_map/ppermute | solution.py:23
  284.5 7.0 %collective-permute-done.25 = bf16[176,128]{1,0:T(8,128)(2,1)S(1)} collective-permute-done((bf16[176,128]{1,0:T(8,128)(2,1)S(1)}, bf16[176,128]{1,0:T(8,128)(2,1)S(1)}, u32[]{:S(2)}, u32[]{:S(2)}) %collective-permute-start.25) | collective-permute-done | bytes 45088 | tf_op jit(solution)/shard_map/ppermute | solution.py:23
  (93 shorter events, 21.9 us)
Async XLA Ops:
  1.4 47.7 %copy-start = (bf16[128,3584]{1,0:T(8,128)(2,1)}, bf16[128,3584]{1,0:T(8,128)(2,1)S(1)}, u32[]{:S(2)}) copy-start(bf16[128,3584]{1,0:T(8,128)(2,1)S(1)} %pad_maximum_fusion.refs_0_) | copy-start | bytes 2752516
  1.4 53.7 %copy-start.8 = (bf16[128,1024]{1,0:T(8,128)(2,1)S(1)}, bf16[128,1024]{1,0:T(8,128)(2,1)}, u32[]{:S(2)}) copy-start(bf16[128,1024]{1,0:T(8,128)(2,1)} %refs_0_.2) | copy-start | bytes 786436
  1.5 25.5 %collective-permute-start.11 = (bf16[128,3584]{1,0:T(8,128)(2,1)S(1)}, bf16[128,3584]{1,0:T(8,128)(2,1)S(1)}, u32[]{:S(2)}, u32[]{:S(2)}) collective-permute-start(bf16[128,3584]{1,0:T(8,128)(2,1)S(1)} %pad_maximum_fusion.refs_0_), channel_id=1, source_target_pairs={{0,128},{128,256},{256,384},{384,0},{1,129},{129,257},{257,385},{3... | collective-permute-start | bytes 2752520 | tf_op jit(solution)/shard_map/ppermute | solution.py:18
  5.0 42.4 %collective-permute-start.12 = (bf16[128,3584]{1,0:T(8,128)(2,1)S(1)}, bf16[128,3584]{1,0:T(8,128)(2,1)S(1)}, u32[]{:S(2)}, u32[]{:S(2)}) collective-permute-start(bf16[128,3584]{1,0:T(8,128)(2,1)S(1)} %pad_maximum_fusion.refs_0_), channel_id=1, source_target_pairs={{0,256},{128,384},{256,0},{384,128},{1,257},{129,385},{257,1},{385... | collective-permute-start | bytes 2752520 | tf_op jit(solution)/shard_map/ppermute | solution.py:18
  9.6 39.4 %collective-permute-start.13 = (bf16[128,3584]{1,0:T(8,128)(2,1)S(1)}, bf16[128,3584]{1,0:T(8,128)(2,1)}, u32[]{:S(2)}, u32[]{:S(2)}) collective-permute-start(bf16[128,3584]{1,0:T(8,128)(2,1)S(1)} %pad_maximum_fusion.refs_0_), channel_id=1, source_target_pairs={{0,384},{128,0},{256,128},{384,256},{1,385},{129,1},{257,129},{385... | collective-permute-start | bytes 2752520 | tf_op jit(solution)/shard_map/ppermute | solution.py:18
  26.9 22.2 %copy-start.4 = (bf16[128,3584]{1,0:T(8,128)(2,1)}, bf16[128,3584]{1,0:T(8,128)(2,1)S(1)}, u32[]{:S(2)}) copy-start(bf16[128,3584]{1,0:T(8,128)(2,1)S(1)} %collective-permute-done.11.refs_1_) | copy-start | bytes 2752516
  47.4 1.7 copy-start.5
  53.1 26.9 %copy-start.7 = (bf16[176,128]{1,0:T(8,128)(2,1)S(1)}, bf16[176,128]{1,0:T(8,128)(2,1)}, u32[]{:S(2)}) copy-start(bf16[176,128]{1,0:T(8,128)(2,1)} %param.7) | copy-start | bytes 135172
  53.1 43.9 %copy-start.12 = (bf16[176,128]{1,0:T(8,128)(2,1)S(1)}, bf16[176,128]{1,0:T(8,128)(2,1)}, u32[]{:S(2)}) copy-start(bf16[176,128]{1,0:T(8,128)(2,1)} %param.8) | copy-start | bytes 135172
  53.1 101.8 %collective-permute-start.14 = (bf16[512,3584]{1,0:T(8,128)(2,1)}, bf16[512,3584]{1,0:T(8,128)(2,1)}, u32[]{:S(2)}, u32[]{:S(2)}) collective-permute-start(bf16[512,3584]{1,0:T(8,128)(2,1)} %stack.52.own), channel_id=1, source_target_pairs={{0,64},{64,0},{1,65},{65,1},{2,66},{66,2},{3,67},{67,3},{4,68},{68... | collective-permute-start | bytes 11010056 | tf_op jit(solution)/shard_map/ppermute | solution.py:23
  55.2 11.8 %collective-permute-start.3 = (bf16[128,1024]{1,0:T(8,128)(2,1)S(1)}, bf16[128,1024]{1,0:T(8,128)(2,1)S(1)}, u32[]{:S(2)}, u32[]{:S(2)}) collective-permute-start(bf16[128,1024]{1,0:T(8,128)(2,1)S(1)} %copy-done.8), channel_id=1, source_target_pairs={{0,128},{128,256},{256,384},{384,0},{1,129},{129,257},{257,385},{3... | collective-permute-start | bytes 786440 | tf_op jit(solution)/shard_map/ppermute | solution.py:18
  59.5 14.0 %collective-permute-start.4 = (bf16[128,1024]{1,0:T(8,128)(2,1)S(1)}, bf16[128,1024]{1,0:T(8,128)(2,1)S(1)}, u32[]{:S(2)}, u32[]{:S(2)}) collective-permute-start(bf16[128,1024]{1,0:T(8,128)(2,1)S(1)} %copy-done.8), channel_id=1, source_target_pairs={{0,256},{128,384},{256,0},{384,128},{1,257},{129,385},{257,1},{385... | collective-permute-start | bytes 786440 | tf_op jit(solution)/shard_map/ppermute | solution.py:18
  63.1 12.0 %collective-permute-start.5 = (bf16[128,1024]{1,0:T(8,128)(2,1)S(1)}, bf16[128,1024]{1,0:T(8,128)(2,1)S(1)}, u32[]{:S(2)}, u32[]{:S(2)}) collective-permute-start(bf16[128,1024]{1,0:T(8,128)(2,1)S(1)} %copy-done.8), channel_id=1, source_target_pairs={{0,384},{128,0},{256,128},{384,256},{1,385},{129,1},{257,129},{385... | collective-permute-start | bytes 786440 | tf_op jit(solution)/shard_map/ppermute | solution.py:18
  67.0 8.1 %copy-start.9 = (bf16[128,1024]{1,0:T(8,128)(2,1)}, bf16[128,1024]{1,0:T(8,128)(2,1)S(1)}, u32[]{:S(2)}) copy-start(bf16[128,1024]{1,0:T(8,128)(2,1)S(1)} %collective-permute-done.3.refs_1_) | copy-start | bytes 786436
  73.5 1.6 copy-start.10
  75.1 0.7 copy-start.11
  78.1 31.8 %collective-permute-start.6 = (bf16[512,1024]{1,0:T(8,128)(2,1)}, bf16[512,1024]{1,0:T(8,128)(2,1)S(1)}, u32[]{:S(2)}, u32[]{:S(2)}) collective-permute-start(bf16[512,1024]{1,0:T(8,128)(2,1)} %stack.51.own), channel_id=1, source_target_pairs={{0,64},{64,0},{1,65},{65,1},{2,66},{66,2},{3,67},{67,3},{4,68},{68... | collective-permute-start | bytes 3145736 | tf_op jit(solution)/shard_map/ppermute | solution.py:23
  80.1 11.4 %collective-permute-start = (bf16[1,176,128]{2,1,0:T(8,128)(2,1)S(1)}, bf16[1,176,128]{2,1,0:T(8,128)(2,1)S(1)}, u32[]{:S(2)}, u32[]{:S(2)}) collective-permute-start(bf16[1,176,128]{2,1,0:T(8,128)(2,1)S(1)} %bitcast.45), channel_id=1, source_target_pairs={{0,32},{8,40},{16,48},{24,56},{32,0},{40,8},{48,16},{56,24},{1,33}... | collective-permute-start | bytes 135176 | tf_op jit(solution)/shard_map/ppermute | solution.py:23
  91.5 10.2 %collective-permute-start.1 = (bf16[2,176,128]{2,1,0:T(8,128)(2,1)S(1)}, bf16[2,176,128]{2,1,0:T(8,128)(2,1)S(1)}, u32[]{:S(2)}, u32[]{:S(2)}) collective-permute-start(bf16[2,176,128]{2,1,0:T(8,128)(2,1)S(1)} %pad_maximum_fusion.7), channel_id=1, source_target_pairs={{0,16},{8,24},{16,0},{24,8},{32,48},{40,56},{48,32},{56,40},{1,17}... | collective-permute-start | bytes 270344 | tf_op jit(solution)/shard_map/ppermute | solution.py:23
  101.7 7.4 %collective-permute-start.2 = (bf16[4,176,128]{2,1,0:T(8,128)(2,1)S(1)}, bf16[4,176,128]{2,1,0:T(8,128)(2,1)S(1)}, u32[]{:S(2)}, u32[]{:S(2)}) collective-permute-start(bf16[4,176,128]{2,1,0:T(8,128)(2,1)S(1)} %pad_maximum_fusion.4), channel_id=1, source_target_pairs={{0,8},{8,0},{16,24},{24,16},{32,40},{40,32},{48,56},{56,48},{1,9},... | collective-permute-start | bytes 540680 | tf_op jit(solution)/shard_map/ppermute | solution.py:23
  109.9 9.0 %copy-start.13 = (f32[128]{0:T(128)S(1)}, f32[128]{0:T(128)}, u32[]{:S(2)}) copy-start(f32[128]{0:T(128)} %param.10) | copy-start | bytes 1540
  109.9 1.0 copy-start.3
  113.9 10.7 %all-to-all-start = ((bf16[4,352,128]{2,1,0:T(8,128)(2,1)}), bf16[4,352,128]{2,1,0:T(8,128)(2,1)S(1)}, u32[]{:S(2)}, u32[]{:S(2)}) async-start(bf16[4,352,128]{2,1,0:T(8,128)(2,1)} %proj_mm.1), calls=%async_computation | async-start | bytes 720896 | tf_op jit(solution)/shard_map/all_to_all | solution.py:31
  124.8 19.2 %collective-permute-start.7 = (bf16[360,128]{1,0:T(8,128)(2,1)S(1)}, bf16[360,128]{1,0:T(8,128)(2,1)S(1)}, u32[]{:S(2)}, u32[]{:S(2)}) collective-permute-start(bf16[360,128]{1,0:T(8,128)(2,1)S(1)} %pad_maximum_fusion.6), channel_id=1, source_target_pairs={{0,4},{4,0},{1,5},{5,1},{2,6},{6,2},{3,7},{7,3},{8,12},{12,8},{9,1... | collective-permute-start | bytes 276488 | tf_op jit(solution)/shard_map/ppermute | solution.py:23
  161.0 14.6 %copy-start.2 = (f32[2,88,1792]{2,1,0:T(8,128)S(1)}, f32[2,88,1792]{2,1,0:T(8,128)}, u32[]{:S(2)}) copy-start(f32[2,88,1792]{2,1,0:T(8,128)} %get-tuple-element.7) | copy-start | bytes 3784708
  161.0 14.5 %collective-permute-start.15 = (bf16[2,88,1792]{2,1,0:T(8,128)(2,1)}, bf16[2,88,1792]{2,1,0:T(8,128)(2,1)S(1)}, u32[]{:S(2)}, u32[]{:S(2)}) collective-permute-start(bf16[2,88,1792]{2,1,0:T(8,128)(2,1)} %get-tuple-element.8), channel_id=1, source_target_pairs={{0,8},{8,0},{16,24},{24,16},{32,40},{40,32},{48,56},{56,48},{1,9},... | collective-permute-start | bytes 1892360 | tf_op jit(solution)/shard_map/ppermute | solution.py:23
  176.4 32.8 %collective-permute-start.16 = (bf16[88,1792]{1,0:T(8,128)(2,1)}, bf16[88,1792]{1,0:T(8,128)(2,1)S(1)}, u32[]{:S(2)}, u32[]{:S(2)}) collective-permute-start(bf16[88,1792]{1,0:T(8,128)(2,1)} %fusion), channel_id=1, source_target_pairs={{0,16},{8,24},{16,0},{24,8},{32,48},{40,56},{48,32},{56,40},{1,17}... | collective-permute-start | bytes 946184 | tf_op jit(solution)/shard_map/ppermute | solution.py:23
  179.1 14.2 %collective-permute-start.8 = (f32[2,128]{1,0:T(2,128)S(1)}, f32[2,128]{1,0:T(2,128)S(1)}, u32[]{:S(2)}, u32[]{:S(2)}) collective-permute-start(f32[2,128]{1,0:T(2,128)S(1)} %slice_add_fusion.1), channel_id=1, source_target_pairs={{0,8},{8,0},{16,24},{24,16},{32,40},{40,32},{48,56},{56,48},{1,9},... | collective-permute-start | bytes 3080 | tf_op jit(solution)/shard_map/ppermute | solution.py:23
  181.8 48.8 %collective-permute-start.21 = (bf16[224,1024]{1,0:T(8,128)(2,1)}, bf16[224,1024]{1,0:T(8,128)(2,1)S(1)}, u32[]{:S(2)}, u32[]{:S(2)}) collective-permute-start(bf16[224,1024]{1,0:T(8,128)(2,1)} %refs_0_.3), channel_id=1, source_target_pairs={{0,128},{128,256},{256,384},{384,0},{1,129},{129,257},{257,385},{3... | collective-permute-start | bytes 1376264 | tf_op jit(solution)/shard_map/ppermute | solution.py:18
  186.3 44.4 %collective-permute-start.22 = (bf16[224,1024]{1,0:T(8,128)(2,1)}, bf16[224,1024]{1,0:T(8,128)(2,1)}, u32[]{:S(2)}, u32[]{:S(2)}) collective-permute-start(bf16[224,1024]{1,0:T(8,128)(2,1)} %refs_0_.3), channel_id=1, source_target_pairs={{0,256},{128,384},{256,0},{384,128},{1,257},{129,385},{257,1},{385... | collective-permute-start | bytes 1376264 | tf_op jit(solution)/shard_map/ppermute | solution.py:18
  189.9 40.8 %collective-permute-start.23 = (bf16[224,1024]{1,0:T(8,128)(2,1)}, bf16[224,1024]{1,0:T(8,128)(2,1)}, u32[]{:S(2)}, u32[]{:S(2)}) collective-permute-start(bf16[224,1024]{1,0:T(8,128)(2,1)} %refs_0_.3), channel_id=1, source_target_pairs={{0,384},{128,0},{256,128},{384,256},{1,385},{129,1},{257,129},{385... | collective-permute-start | bytes 1376264 | tf_op jit(solution)/shard_map/ppermute | solution.py:18
  193.3 6.4 %collective-permute-start.9 = (f32[2,128]{1,0:T(2,128)S(1)}, f32[2,128]{1,0:T(2,128)S(1)}, u32[]{:S(2)}, u32[]{:S(2)}) collective-permute-start(f32[2,128]{1,0:T(2,128)S(1)} %fusion.21), channel_id=1, source_target_pairs={{0,16},{8,24},{16,0},{24,8},{32,48},{40,56},{48,32},{56,40},{1,17}... | collective-permute-start | bytes 3080 | tf_op jit(solution)/shard_map/ppermute | solution.py:23
  199.7 12.4 %collective-permute-start.10 = (f32[2,128]{1,0:T(2,128)S(1)}, f32[2,128]{1,0:T(2,128)S(1)}, u32[]{:S(2)}, u32[]{:S(2)}) collective-permute-start(f32[2,128]{1,0:T(2,128)S(1)} %add.103), channel_id=1, source_target_pairs={{0,32},{8,40},{16,48},{24,56},{32,0},{40,8},{48,16},{56,24},{1,33}... | collective-permute-start | bytes 3080 | tf_op jit(solution)/shard_map/ppermute | solution.py:23
  209.3 19.3 %collective-permute-start.17 = (bf16[48,1792]{1,0:T(8,128)(2,1)S(1)}, bf16[48,1792]{1,0:T(8,128)(2,1)S(1)}, u32[]{:S(2)}, u32[]{:S(2)}) collective-permute-start(bf16[48,1792]{1,0:T(8,128)(2,1)S(1)} %dynamic-slice_convert_fusion), channel_id=1, source_target_pairs={{0,32},{8,40},{16,48},{24,56},{32,0},{40,8},{48,16},{56,24},{1,33}... | collective-permute-start | bytes 516104 | tf_op jit(solution)/shard_map/ppermute | solution.py:23
  228.8 10.3 %collective-permute-start.18 = (bf16[48,896]{1,0:T(8,128)(2,1)S(1)}, bf16[48,896]{1,0:T(8,128)(2,1)S(1)}, u32[]{:S(2)}, u32[]{:S(2)}) collective-permute-start(bf16[48,896]{1,0:T(8,128)(2,1)S(1)} %fusion.3), channel_id=1, source_target_pairs={{0,32},{8,40},{16,48},{24,56},{32,0},{40,8},{48,16},{56,24},{1,33}... | collective-permute-start | bytes 258056 | tf_op jit(solution)/shard_map/ppermute | solution.py:23
  230.7 0.8 copy-start.6
  234.3 26.5 %collective-permute-start.24 = (bf16[896,1024]{1,0:T(8,128)(2,1)}, bf16[896,1024]{1,0:T(8,128)(2,1)S(1)}, u32[]{:S(2)}, u32[]{:S(2)}) collective-permute-start(bf16[896,1024]{1,0:T(8,128)(2,1)} %stack.53.own), channel_id=1, source_target_pairs={{0,64},{64,0},{1,65},{65,1},{2,66},{66,2},{3,67},{67,3},{4,68},{68... | collective-permute-start | bytes 5505032 | tf_op jit(solution)/shard_map/ppermute | solution.py:23
  239.2 9.4 %collective-permute-start.19 = (bf16[88,896]{1,0:T(8,128)(2,1)S(1)}, bf16[88,896]{1,0:T(8,128)(2,1)S(1)}, u32[]{:S(2)}, u32[]{:S(2)}) collective-permute-start(bf16[88,896]{1,0:T(8,128)(2,1)S(1)} %pad_maximum_fusion.5), channel_id=1, source_target_pairs={{0,16},{8,24},{16,0},{24,8},{32,48},{40,56},{48,32},{56,40},{1,17}... | collective-permute-start | bytes 473096 | tf_op jit(solution)/shard_map/ppermute | solution.py:23
  248.7 11.0 %collective-permute-start.20 = (bf16[88,1792]{1,0:T(8,128)(2,1)S(1)}, bf16[88,1792]{1,0:T(8,128)(2,1)S(1)}, u32[]{:S(2)}, u32[]{:S(2)}) collective-permute-start(bf16[88,1792]{1,0:T(8,128)(2,1)S(1)} %pad_maximum_fusion.3), channel_id=1, source_target_pairs={{0,8},{8,0},{16,24},{24,16},{32,40},{40,32},{48,56},{56,48},{1,9},... | collective-permute-start | bytes 946184 | tf_op jit(solution)/shard_map/ppermute | solution.py:23
  260.7 1.2 copy-start.1
  266.1 10.6 %all-to-all-start.2 = ((bf16[4,352,128]{2,1,0:T(8,128)(2,1)}), bf16[4,352,128]{2,1,0:T(8,128)(2,1)S(1)}, u32[]{:S(2)}, u32[]{:S(2)}) async-start(bf16[4,352,128]{2,1,0:T(8,128)(2,1)} %down_mm.1), calls=%async_computation.2 | async-start | bytes 720896 | tf_op jit(solution)/shard_map/all_to_all | solution.py:31
  276.8 14.7 %collective-permute-start.25 = (bf16[176,128]{1,0:T(8,128)(2,1)S(1)}, bf16[176,128]{1,0:T(8,128)(2,1)S(1)}, u32[]{:S(2)}, u32[]{:S(2)}) collective-permute-start(bf16[176,128]{1,0:T(8,128)(2,1)S(1)} %fusion.6), channel_id=1, source_target_pairs={{0,4},{4,0},{1,5},{5,1},{2,6},{6,2},{3,7},{7,3},{8,12},{12,8},{9,1... | collective-permute-start | bytes 135176 | tf_op jit(solution)/shard_map/ppermute | solution.py:23

commit v5 on v4

--- a/solution.py
+++ b/solution.py
@@ -13,11 +13,6 @@
 AXES = ("x", "c", "zl", "zh", "y")
 
 
-def shift(value, axis, step):
-    n = lax.axis_size(axis)
-    return lax.ppermute(value, axis, [(i, (i + step) % n) for i in range(n)])
-
-
 def swap(value, axis, bit):
     n = lax.axis_size(axis)
     return lax.ppermute(value, axis, [(i, i ^ bit) for i in range(n)])
@@ -42,28 +37,8 @@
     return first, second
 
 
-def stack_kernel(*refs):
-    *ins, out = refs
-    height = ins[0].shape[0]
-    for k, ref in enumerate(ins):
-        out[k * height : (k + 1) * height] = ref[...]
-
-
-def stacked(parts):
-    height, width = parts[0].shape
-    vmem = pl.BlockSpec(memory_space=pltpu.VMEM)
-    return pl.pallas_call(
-        stack_kernel,
-        out_shape=jax.ShapeDtypeStruct((len(parts) * height, width), BF),
-        in_specs=[vmem] * len(parts),
-        out_specs=vmem,
-        name="stack",
-    )(*parts)
-
-
 def gathered(w):
-    parts = [w, shift(w, "x", 1), shift(w, "x", 2), shift(w, "x", -1)]
-    own = stacked(parts)
+    own = from_everyone(w, "x").reshape(-1, w.shape[1])
     return own, swap(own, "c", 1)
 
 
@@ -71,22 +46,24 @@
     return jnp.dot(a, b, preferred_element_type=F32)
 
 
-def proj_kernel(at, x, own, other, out):
-    xi, ci, zl = at[0], at[1], at[2]
+def proj_kernel(at, x, own, other, *outs):
+    ci, zl, yi = at[0], at[2], at[3]
     rows = x.shape[1]
 
-    def block(b):
-        off = b ^ zl
-        return x[((off >> 2) & 1) | (off & 2) | ((off & 1) << 2)]
-
-    blocks = [((xi + 4 - k) & 3) * 2 for k in range(4)]
-    mine = jnp.concatenate([block(b + ci) for b in blocks], axis=1)
-    theirs = jnp.concatenate([block(b + 1 - ci) for b in blocks], axis=1)
+    def blocks(core):
+        offs = [(2 * k + core) ^ zl for k in range(4)]
+        return [x[((off >> 2) & 1) | (off & 2) | ((off & 1) << 2)] for off in offs]
+
+    mine = jnp.concatenate(blocks(ci), axis=1)
+    theirs = jnp.concatenate(blocks(1 - ci), axis=1)
     part = (dot(mine, own[...]) + dot(theirs, other[...])).astype(BF)
+    *outs, parts = outs
     for zh in range(2):
         for y in range(4):
             n = (zh * 4 + y) * 128
-            out[y, zh * rows : (zh + 1) * rows] = part[:, n : n + 128]
+            parts[y, zh * rows : (zh + 1) * rows] = part[:, n : n + 128]
+    for k, out in enumerate(outs):
+        out[...] = parts[yi ^ k]
 
 
 def proj_parts(at, x, own, other):
@@ -94,9 +71,10 @@
     vmem = pl.BlockSpec(memory_space=pltpu.VMEM)
     return pl.pallas_call(
         proj_kernel,
-        out_shape=jax.ShapeDtypeStruct((4, 2 * rows, 128), BF),
+        out_shape=[jax.ShapeDtypeStruct((2 * rows, 128), BF)] * 4,
         in_specs=[pl.BlockSpec(memory_space=pltpu.SMEM), vmem, vmem, vmem],
-        out_specs=vmem,
+        out_specs=[vmem] * 4,
+        scratch_shapes=[pltpu.VMEM((4, 2 * rows, 128), BF)],
         cost_estimate=pl.CostEstimate(
             flops=2 * rows * 1024 * 1024, bytes_accessed=3 << 20, transcendentals=0
         ),
@@ -104,54 +82,54 @@
     )(at, x, own, other)
 
 
-def both_kernel(at, x, own, other, send, keep):
-    xi, ci, bit = at[0], at[1], at[2] & 1
+def both_kernel(at, x0, x1, x2, x3, own, other, send, keep, x):
+    ci, bit, yi = at[0], at[1], at[3]
     rows = 2 * send.shape[1]
-    blocks = [(xi + 4 - k) & 3 for k in range(4)]
-
-    def block(b, core):
-        start = pl.multiple_of((b // 2) * rows, 16)
-        return x[(b % 2) * 2 + core, pl.ds(start, rows)]
-
-    mine = jnp.concatenate([block(b, ci) for b in blocks], axis=1)
-    theirs = jnp.concatenate([block(b, 1 - ci) for b in blocks], axis=1)
+
+    @pl.when(pl.program_id(0) == 0)
+    def _():
+        for k, ref in enumerate((x0, x1, x2, x3)):
+            x[yi ^ k] = ref[...]
+
+    def blocks(core):
+        parts = [x[(k % 2) * 2 + core, pl.ds((k // 2) * rows, rows)] for k in range(4)]
+        return jnp.concatenate(parts, axis=1)
+
+    mine, theirs = blocks(ci), blocks(1 - ci)
     part = dot(mine, own[...]) + dot(theirs, other[...])
     upper, lower = part[: rows // 2], part[rows // 2 :]
     send[0] = jnp.where(bit == 0, lower, upper).astype(BF)
     keep[0] = jnp.where(bit == 0, upper, lower)
 
 
-def both_parts(at, x, own, other, rows):
+def both_parts(at, xs, own, other, rows):
     depth, wide = own.shape
     tile = wide // 4
     halves = (2, rows // 2, wide // 2)
+    model = pl.BlockSpec(memory_space=pltpu.VMEM)
     weights = pl.BlockSpec((depth, tile), lambda n: (0, n))
     result = pl.BlockSpec((1, rows // 2, tile), lambda n: (n // 2, 0, n % 2))
     return pl.pallas_call(
         both_kernel,
         grid=(4,),
         out_shape=(jax.ShapeDtypeStruct(halves, BF), jax.ShapeDtypeStruct(halves, F32)),
-        in_specs=[
-            pl.BlockSpec(memory_space=pltpu.SMEM),
-            pl.BlockSpec(x.shape, lambda n: (0, 0, 0)),
-            weights,
-            weights,
-        ],
+        in_specs=[pl.BlockSpec(memory_space=pltpu.SMEM)] + [model] * 4 + [weights] * 2,
         out_specs=(result, result),
+        scratch_shapes=[pltpu.VMEM((4, *xs[0].shape), BF)],
         cost_estimate=pl.CostEstimate(
             flops=4 * rows * depth * wide, bytes_accessed=9 << 20, transcendentals=0
         ),
         name="both_mm",
-    )(at, x, own, other)
+    )(at, *xs, own, other)
 
 
 def down_kernel(at, x, own, other, out, whole):
-    xi, ci = at[0], at[1]
+    ci = at[0]
     rows = x.shape[0]
     height = own.shape[0] // 4
     for ref, core in ((own, ci), (other, 1 - ci)):
         for k in range(4):
-            b = ((xi + 4 - k) & 3) * 2 + core
+            b = 2 * k + core
             to = pl.ds(pl.multiple_of(b * height, 16), height)
             whole[to] = ref[k * height : (k + 1) * height]
     part = dot(x[...], whole[...]).astype(BF)
@@ -182,10 +160,10 @@
 
 
 def on_device(attn_out, residual, proj_weight, norm_gain, gate_proj, up_proj, down_proj):
-    xi, ci = lax.axis_index("x"), lax.axis_index("c")
-    zl, zh = lax.axis_index("zl"), lax.axis_index("zh")
+    ci, zl, zh = lax.axis_index("c"), lax.axis_index("zl"), lax.axis_index("zh")
+    yi = lax.axis_index("y")
     bit0, bit1, bit2 = zl & 1, (zl >> 1) & 1, (zl >> 2) & 1
-    at = jnp.stack([xi, ci, zl]).astype(jnp.int32)
+    at = jnp.stack([ci, bit0, zl, yi]).astype(jnp.int32)
     rows = attn_out.shape[0]
     half = rows // 2
     top = 48
@@ -206,7 +184,8 @@
     gains = jnp.pad(jnp.stack([high, mid, low]), ((0, 5), (0, 0)))
 
     part = proj_parts(at, cols, proj_own, proj_other)
-    near = exchange(part, "y").astype(F32).sum(axis=0).reshape(2, rows, 128)
+    near = [part[0]] + [swap(part[k], "y", k) for k in (1, 2, 3)]
+    near = sum(p.astype(F32) for p in near).reshape(2, rows, 128)
     mine = jnp.arange(2)[:, None, None] == zh
     near = jnp.where(mine, near + residual.astype(F32), near).reshape(2 * rows, 128)
     far = swap(jnp.concatenate([near, gains]).astype(BF), "zh", 1).astype(F32)
@@ -218,8 +197,9 @@
     squares = jnp.pad(squares, (0, 256 - rows)).reshape(2, 128)
     high = exact(squares)
     tail = jnp.concatenate([high, squares - high, jnp.zeros((4, 128), F32)]).astype(BF)
-    model = from_everyone(jnp.concatenate([scaled2, tail]), "y")
-    squares = model[:, 2 * rows : 2 * rows + 4].astype(F32).sum(axis=0)
+    model = jnp.concatenate([scaled2, tail])
+    model = [model] + [swap(model, "y", k) for k in (1, 2, 3)]
+    squares = sum(m[2 * rows : 2 * rows + 4].astype(F32) for m in model)
     squares = squares[:2] + squares[2:]
 
     send, keep = both_parts(at, model, both_own, both_other, rows)

time: 293 us -> 288 us (0.983)
  the two profiles are of different devices: /device:TPU:8 before, /device:TPU:2 now
where the time goes in v5:
time: 288 us; the launch traced here: 287 us
  starting transfers between devices  103 us (36%)
  waiting for transfers between devices  89.3 us (31%)
  blocking collectives  65 us (23%)
  Pallas kernels  13.1 us (5%)
  other arithmetic  9.96 us (3%)
  local copies, waits for them, and re-layouts  5.27 us (2%)
    ppermute x23, starting transfers between devices, swap(): return lax.ppermute(value, axis, [(i, i ^ bit) for i in range(n)])  95 us
    ppermute x23, waiting for transfers between devices, swap(): return lax.ppermute(value, axis, [(i, i ^ bit) for i in range(n)])  82.2 us
    all_to_all x2, blocking collectives, exchange(): return lax.all_to_all(parts, axis, split_axis=0, concat_axis=0, tiled=True)  65 us
    all_to_all x2, starting transfers between devices, exchange(): return lax.all_to_all(parts, axis, split_axis=0, concat_axis=0, tiled=True)  8.46 us
    all_to_all x2, waiting for transfers between devices, exchange(): return lax.all_to_all(parts, axis, split_axis=0, concat_axis=0, tiled=True)  7.17 us
    pallas_call x1, Pallas kernels, both_parts(): pl.pallas_call(both_kernel, grid=(4,), out_shape=(jax.ShapeDtypeStruct(ha...  6.02 us
  transfers between devices with their start and end apart: 25, of which 16 were waited for; matrix products, arithmetic and copies ran while one was open for 3% of the time, Pallas kernels for 1%

profile of v5, /device:TPU:2, one launch (start us, length us, event | category | flops | bytes accessed | tf_op | source)
XLA Modules:
  0.0 286.7 jit_solution(9022984967267885378)
XLA Ops:
  0.0 1.4 fusion.19
  1.7 46.6 %all_to_all.20 = bf16[4,128,3584]{2,1,0:T(8,128)(2,1)} all-to-all(bf16[4,128,3584]{2,1,0:T(8,128)(2,1)S(1)} %broadcast_in_dim.40), channel_id=1, replica_groups=mesh['x'=4,'c'=2,'zl'=8,'zh'=2,'y'=4] {'x'}, dimensions={0} | all-to-all | bytes 7340032 | tf_op jit(solution)/shard_map/all_to_all | solution.py:26
  48.3 2.0 collective-permute-start.14
  50.5 18.5 %all_to_all.21 = bf16[4,128,1024]{2,1,0:T(8,128)(2,1)S(1)} all-to-all(bf16[4,128,1024]{2,1,0:T(8,128)(2,1)S(1)} %broadcast_in_dim.37), channel_id=1, replica_groups=mesh['x'=4,'c'=2,'zl'=8,'zh'=2,'y'=4] {'x'}, dimensions={0} | all-to-all | bytes 2097152 | tf_op jit(solution)/shard_map/all_to_all | solution.py:26
  69.0 1.9 collective-permute-start.3
  70.9 9.1 %collective-permute-start = (bf16[1,176,128]{2,1,0:T(8,128)(2,1)S(1)}, bf16[1,176,128]{2,1,0:T(8,128)(2,1)S(1)}, u32[]{:S(2)}, u32[]{:S(2)}) collective-permute-start(bf16[1,176,128]{2,1,0:T(8,128)(2,1)S(1)} %bitcast.53), channel_id=1, source_target_pairs={{0,32},{8,40},{16,48},{24,56},{32,0},{40,8},{48,16},{56,24},{1,33}... | collective-permute-start | bytes 135176 | tf_op jit(solution)/shard_map/ppermute | solution.py:18
  80.2 2.1 collective-permute-done
  82.3 5.5 %collective-permute-start.1 = (bf16[2,176,128]{2,1,0:T(8,128)(2,1)S(1)}, bf16[2,176,128]{2,1,0:T(8,128)(2,1)S(1)}, u32[]{:S(2)}, u32[]{:S(2)}) collective-permute-start(bf16[2,176,128]{2,1,0:T(8,128)(2,1)S(1)} %pad_maximum_fusion.7), channel_id=1, source_target_pairs={{0,16},{8,24},{16,0},{24,8},{32,48},{40,56},{48,32},{56,40},{1,17}... | collective-permute-start | bytes 270344 | tf_op jit(solution)/shard_map/ppermute | solution.py:18
  88.4 4.2 %collective-permute-done.1 = bf16[2,176,128]{2,1,0:T(8,128)(2,1)S(1)} collective-permute-done((bf16[2,176,128]{2,1,0:T(8,128)(2,1)S(1)}, bf16[2,176,128]{2,1,0:T(8,128)(2,1)S(1)}, u32[]{:S(2)}, u32[]{:S(2)}) %collective-permute-start.1) | collective-permute-done | bytes 90144 | tf_op jit(solution)/shard_map/ppermute | solution.py:18
  92.6 2.6 collective-permute-start.2
  95.2 4.7 %collective-permute-done.2 = bf16[4,176,128]{2,1,0:T(8,128)(2,1)S(1)} collective-permute-done((bf16[4,176,128]{2,1,0:T(8,128)(2,1)S(1)}, bf16[4,176,128]{2,1,0:T(8,128)(2,1)S(1)}, u32[]{:S(2)}, u32[]{:S(2)}) %collective-permute-start.2) | collective-permute-done | bytes 180256 | tf_op jit(solution)/shard_map/ppermute | solution.py:18
  101.8 3.0 %proj_mm.1 = (bf16[352,128]{1,0:T(8,128)(2,1)}, bf16[352,128]{1,0:T(8,128)(2,1)}, bf16[352,128]{1,0:T(8,128)(2,1)}, bf16[352,128]{1,0:T(8,128)(2,1)}) custom-call(s32[4]{0:T(128)} %pad_add_fusion.at, bf16[8,176,128]{2,1,0:T(8,128)(2,1)} %pad_maximum_fusion.2.x, bf16[512,1024]{1,0:T(8,128)(2,1)} %bitcast.49, bf16[512,1024]{1,0:T(8,128)(2,1)} %copy-done.3), custom_call_target="tpu_custom_call" | custom-call | flops 369098752 | bytes 3145728 | tf_op jit(solution)/shard_map/proj_mm/pallas_call | solution.py:72
  104.8 4.9 %collective-permute-start.6 = (bf16[352,128]{1,0:T(8,128)(2,1)}, bf16[352,128]{1,0:T(8,128)(2,1)S(1)}, u32[]{:S(2)}, u32[]{:S(2)}) collective-permute-start(bf16[352,128]{1,0:T(8,128)(2,1)} %get-tuple-element.14), channel_id=1, source_target_pairs={{0,3},{1,2},{2,1},{3,0},{4,7},{5,6},{6,5},{7,4},{8,11},{9,10},{10,... | collective-permute-start | bytes 270344 | tf_op jit(solution)/shard_map/ppermute | solution.py:18
  109.7 2.5 collective-permute-start.5
  112.2 2.4 collective-permute-start.4
  114.6 3.7 %collective-permute-done.5 = bf16[352,128]{1,0:T(8,128)(2,1)S(1)} collective-permute-done((bf16[352,128]{1,0:T(8,128)(2,1)}, bf16[352,128]{1,0:T(8,128)(2,1)S(1)}, u32[]{:S(2)}, u32[]{:S(2)}) %collective-permute-start.5) | collective-permute-done | bytes 90144 | tf_op jit(solution)/shard_map/ppermute | solution.py:18
  119.9 14.7 %collective-permute-start.7 = (bf16[360,128]{1,0:T(8,128)(2,1)S(1)}, bf16[360,128]{1,0:T(8,128)(2,1)S(1)}, u32[]{:S(2)}, u32[]{:S(2)}) collective-permute-start(bf16[360,128]{1,0:T(8,128)(2,1)S(1)} %pad_maximum_fusion.6), channel_id=1, source_target_pairs={{0,4},{4,0},{1,5},{5,1},{2,6},{6,2},{3,7},{7,3},{8,12},{12,8},{9,1... | collective-permute-start | bytes 276488 | tf_op jit(solution)/shard_map/ppermute | solution.py:18
  134.7 4.4 %collective-permute-done.7 = bf16[360,128]{1,0:T(8,128)(2,1)S(1)} collective-permute-done((bf16[360,128]{1,0:T(8,128)(2,1)S(1)}, bf16[360,128]{1,0:T(8,128)(2,1)S(1)}, u32[]{:S(2)}, u32[]{:S(2)}) %collective-permute-start.7) | collective-permute-done | bytes 92192 | tf_op jit(solution)/shard_map/ppermute | solution.py:18
  140.6 2.3 collective-permute-start.8
  142.9 4.8 %collective-permute-start.9 = (bf16[360,128]{1,0:T(8,128)(2,1)S(1)}, bf16[360,128]{1,0:T(8,128)(2,1)S(1)}, u32[]{:S(2)}, u32[]{:S(2)}) collective-permute-start(bf16[360,128]{1,0:T(8,128)(2,1)S(1)} %maximum_maximum_fusion.x0), channel_id=1, source_target_pairs={{0,2},{1,3},{2,0},{3,1},{4,6},{5,7},{6,4},{7,5},{8,10},{9,11},{10,... | collective-permute-start | bytes 276488 | tf_op jit(solution)/shard_map/ppermute | solution.py:18
  147.8 3.2 %collective-permute-start.10 = (bf16[360,128]{1,0:T(8,128)(2,1)S(1)}, bf16[360,128]{1,0:T(8,128)(2,1)S(1)}, u32[]{:S(2)}, u32[]{:S(2)}) collective-permute-start(bf16[360,128]{1,0:T(8,128)(2,1)S(1)} %maximum_maximum_fusion.x0), channel_id=1, source_target_pairs={{0,3},{1,2},{2,1},{3,0},{4,7},{5,6},{6,5},{7,4},{8,11},{9,10},{10,... | collective-permute-start | bytes 276488 | tf_op jit(solution)/shard_map/ppermute | solution.py:18
  151.1 4.4 %collective-permute-done.10.x3 = bf16[360,128]{1,0:T(8,128)(2,1)S(1)} collective-permute-done((bf16[360,128]{1,0:T(8,128)(2,1)S(1)}, bf16[360,128]{1,0:T(8,128)(2,1)S(1)}, u32[]{:S(2)}, u32[]{:S(2)}) %collective-permute-start.10) | collective-permute-done | bytes 92192 | tf_op jit(solution)/shard_map/ppermute | solution.py:18
  156.1 6.0 %both_mm.1 = (bf16[2,88,1792]{2,1,0:T(8,128)(2,1)}, f32[2,88,1792]{2,1,0:T(8,128)}) custom-call(s32[4]{0:T(128)} %pad_add_fusion.at, bf16[360,128]{1,0:T(8,128)(2,1)} %copy-done.6, bf16[360,128]{1,0:T(8,128)(2,1)} %copy-done.8, bf16[360,128]{1,0:T(8,128)(2,1)} %copy-done.9, bf16[360,128]{1,0:T(8,128)(2,1)} %copy-done.10, bf16[512,3584]{1,0:T(8,128)(2,1)} %bitcast.16.own, ...), custom_call_target="tpu_custom_call" | custom-call | flops 1291845632 | bytes 9437184 | tf_op jit(solution)/shard_map/both_mm/pallas_call | solution.py:112
  162.1 2.1 collective-permute-start.15
  164.9 9.9 %collective-permute-done.15 = bf16[2,88,1792]{2,1,0:T(8,128)(2,1)} collective-permute-done((bf16[2,88,1792]{2,1,0:T(8,128)(2,1)}, bf16[2,88,1792]{2,1,0:T(8,128)(2,1)}, u32[]{:S(2)}, u32[]{:S(2)}) %collective-permute-start.15) | collective-permute-done | bytes 630816 | tf_op jit(solution)/shard_map/ppermute | solution.py:18
  176.8 4.5 %collective-permute-start.16 = (bf16[88,1792]{1,0:T(8,128)(2,1)}, bf16[88,1792]{1,0:T(8,128)(2,1)}, u32[]{:S(2)}, u32[]{:S(2)}) collective-permute-start(bf16[88,1792]{1,0:T(8,128)(2,1)} %fusion), channel_id=1, source_target_pairs={{0,16},{8,24},{16,0},{24,8},{32,48},{40,56},{48,32},{56,40},{1,17}... | collective-permute-start | bytes 946184 | tf_op jit(solution)/shard_map/ppermute | solution.py:18
  181.3 3.8 %collective-permute-start.11 = (f32[2,128]{1,0:T(2,128)S(1)}, f32[2,128]{1,0:T(2,128)S(1)}, u32[]{:S(2)}, u32[]{:S(2)}) collective-permute-start(f32[2,128]{1,0:T(2,128)S(1)} %slice_add_fusion.1), channel_id=1, source_target_pairs={{0,8},{8,0},{16,24},{24,16},{32,40},{40,32},{48,56},{56,48},{1,9},... | collective-permute-start | bytes 3080 | tf_op jit(solution)/shard_map/ppermute | solution.py:18
  185.2 1.5 broadcast_in_dim.41
  186.6 5.0 %all-to-all-start.2 = ((bf16[4,224,1024]{2,1,0:T(8,128)(2,1)}), bf16[4,224,1024]{2,1,0:T(8,128)(2,1)S(1)}, u32[]{:S(2)}, u32[]{:S(2)}) async-start(bf16[4,224,1024]{2,1,0:T(8,128)(2,1)} %broadcast_in_dim.41), calls=%async_computation.2 | async-start | bytes 3670016 | tf_op jit(solution)/shard_map/all_to_all | solution.py:26
  191.7 1.9 collective-permute-start.12
  193.6 4.4 %collective-permute-done.12 = f32[2,128]{1,0:T(2,128)S(1)} collective-permute-done((f32[2,128]{1,0:T(2,128)S(1)}, f32[2,128]{1,0:T(2,128)S(1)}, u32[]{:S(2)}, u32[]{:S(2)}) %collective-permute-start.12) | collective-permute-done | bytes 1056 | tf_op jit(solution)/shard_map/ppermute | solution.py:18
  198.0 8.8 %collective-permute-start.13 = (f32[2,128]{1,0:T(2,128)S(1)}, f32[2,128]{1,0:T(2,128)S(1)}, u32[]{:S(2)}, u32[]{:S(2)}) collective-permute-start(f32[2,128]{1,0:T(2,128)S(1)} %add.127), channel_id=1, source_target_pairs={{0,32},{8,40},{16,48},{24,56},{32,0},{40,8},{48,16},{56,24},{1,33}... | collective-permute-start | bytes 3080 | tf_op jit(solution)/shard_map/ppermute | solution.py:18
  206.9 1.3 bitcast_add_fusion
  208.2 1.9 collective-permute-start.17
  210.1 1.9 collective-permute-done.13
  212.1 15.4 %collective-permute-done.17 = bf16[48,1792]{1,0:T(8,128)(2,1)S(1)} collective-permute-done((bf16[48,1792]{1,0:T(8,128)(2,1)S(1)}, bf16[48,1792]{1,0:T(8,128)(2,1)S(1)}, u32[]{:S(2)}, u32[]{:S(2)}) %collective-permute-start.17) | collective-permute-done | bytes 172064 | tf_op jit(solution)/shard_map/ppermute | solution.py:18
  227.7 1.9 collective-permute-start.18
  229.7 1.9 collective-permute-start.21
  231.6 6.4 %collective-permute-done.18 = bf16[48,896]{1,0:T(8,128)(2,1)S(1)} collective-permute-done((bf16[48,896]{1,0:T(8,128)(2,1)S(1)}, bf16[48,896]{1,0:T(8,128)(2,1)S(1)}, u32[]{:S(2)}, u32[]{:S(2)}) %collective-permute-start.18) | collective-permute-done | bytes 86048 | tf_op jit(solution)/shard_map/ppermute | solution.py:18
  238.2 1.9 collective-permute-start.19
  240.1 6.2 %collective-permute-done.19 = bf16[88,896]{1,0:T(8,128)(2,1)S(1)} collective-permute-done((bf16[88,896]{1,0:T(8,128)(2,1)S(1)}, bf16[88,896]{1,0:T(8,128)(2,1)S(1)}, u32[]{:S(2)}, u32[]{:S(2)}) %collective-permute-start.19) | collective-permute-done | bytes 157728 | tf_op jit(solution)/shard_map/ppermute | solution.py:18
  246.4 1.9 collective-permute-start.20
  248.4 6.9 %collective-permute-done.20 = bf16[88,1792]{1,0:T(8,128)(2,1)S(1)} collective-permute-done((bf16[88,1792]{1,0:T(8,128)(2,1)S(1)}, bf16[88,1792]{1,0:T(8,128)(2,1)S(1)}, u32[]{:S(2)}, u32[]{:S(2)}) %collective-permute-start.20) | collective-permute-done | bytes 315424 | tf_op jit(solution)/shard_map/ppermute | solution.py:18
  256.3 4.1 %down_mm.1 = bf16[4,352,128]{2,1,0:T(8,128)(2,1)} custom-call(s32[4]{0:T(128)} %pad_add_fusion.at, bf16[176,1792]{1,0:T(8,128)(2,1)} %pad_maximum_fusion.1.x, bf16[896,1024]{1,0:T(8,128)(2,1)} %bitcast.47, bf16[896,1024]{1,0:T(8,128)(2,1)} %collective-permute-done.21.other), custom_call_target="tpu_custom_call" | custom-call | flops 645922816 | bytes 5242880 | tf_op jit(solution)/shard_map/down_mm/pallas_call | solution.py:145
  260.3 3.5 %all-to-all-start.3 = ((bf16[4,352,128]{2,1,0:T(8,128)(2,1)}), bf16[4,352,128]{2,1,0:T(8,128)(2,1)S(1)}, u32[]{:S(2)}, u32[]{:S(2)}) async-start(bf16[4,352,128]{2,1,0:T(8,128)(2,1)} %down_mm.1), calls=%async_computation.3 | async-start | bytes 720896 | tf_op jit(solution)/shard_map/all_to_all | solution.py:26
  263.8 7.2 %all-to-all-done.3 = bf16[4,352,128]{2,1,0:T(8,128)(2,1)S(1)} async-done(((bf16[4,352,128]{2,1,0:T(8,128)(2,1)}), bf16[4,352,128]{2,1,0:T(8,128)(2,1)S(1)}, u32[]{:S(2)}, u32[]{:S(2)}) %all-to-all-start.3) | async-done | bytes 360480 | tf_op jit(solution)/shard_map/all_to_all | solution.py:26
  271.1 8.1 %collective-permute-start.22 = (bf16[176,128]{1,0:T(8,128)(2,1)S(1)}, bf16[176,128]{1,0:T(8,128)(2,1)S(1)}, u32[]{:S(2)}, u32[]{:S(2)}) collective-permute-start(bf16[176,128]{1,0:T(8,128)(2,1)S(1)} %fusion.5), channel_id=1, source_target_pairs={{0,4},{4,0},{1,5},{5,1},{2,6},{6,2},{3,7},{7,3},{8,12},{12,8},{9,1... | collective-permute-start | bytes 135176 | tf_op jit(solution)/shard_map/ppermute | solution.py:18
  279.2 6.9 %collective-permute-done.22 = bf16[176,128]{1,0:T(8,128)(2,1)S(1)} collective-permute-done((bf16[176,128]{1,0:T(8,128)(2,1)S(1)}, bf16[176,128]{1,0:T(8,128)(2,1)S(1)}, u32[]{:S(2)}, u32[]{:S(2)}) %collective-permute-start.22) | collective-permute-done | bytes 45088 | tf_op jit(solution)/shard_map/ppermute | solution.py:18
  (84 shorter events, 11.7 us)
Async XLA Ops:
  1.7 48.7 %copy-start.7 = (bf16[128,1024]{1,0:T(8,128)(2,1)S(1)}, bf16[128,1024]{1,0:T(8,128)(2,1)}, u32[]{:S(2)}) copy-start(bf16[128,1024]{1,0:T(8,128)(2,1)} %param.9) | copy-start | bytes 786436
  48.3 22.6 %copy-start.5 = (bf16[176,128]{1,0:T(8,128)(2,1)S(1)}, bf16[176,128]{1,0:T(8,128)(2,1)}, u32[]{:S(2)}) copy-start(bf16[176,128]{1,0:T(8,128)(2,1)} %param.7) | copy-start | bytes 135172
  48.3 31.7 %copy-start.11 = (bf16[176,128]{1,0:T(8,128)(2,1)S(1)}, bf16[176,128]{1,0:T(8,128)(2,1)}, u32[]{:S(2)}) copy-start(bf16[176,128]{1,0:T(8,128)(2,1)} %param.8) | copy-start | bytes 135172
  48.3 46.9 %copy-start.12 = (f32[128]{0:T(128)S(1)}, f32[128]{0:T(128)}, u32[]{:S(2)}) copy-start(f32[128]{0:T(128)} %param.10) | copy-start | bytes 1540
  48.3 107.1 %collective-permute-start.14 = (bf16[512,3584]{1,0:T(8,128)(2,1)}, bf16[512,3584]{1,0:T(8,128)(2,1)}, u32[]{:S(2)}, u32[]{:S(2)}) collective-permute-start(bf16[512,3584]{1,0:T(8,128)(2,1)} %bitcast.16.own), channel_id=1, source_target_pairs={{0,64},{64,0},{1,65},{65,1},{2,66},{66,2},{3,67},{67,3},{4,68},{68... | collective-permute-start | bytes 11010056 | tf_op jit(solution)/shard_map/ppermute | solution.py:18
  69.0 31.8 %copy-start.1 = (bf16[4,128,1024]{2,1,0:T(8,128)(2,1)}, bf16[4,128,1024]{2,1,0:T(8,128)(2,1)S(1)}, u32[]{:S(2)}) copy-start(bf16[4,128,1024]{2,1,0:T(8,128)(2,1)S(1)} %all_to_all.21) | copy-start | bytes 3145732
  69.0 31.8 %collective-permute-start.3 = (bf16[512,1024]{1,0:T(8,128)(2,1)S(1)}, bf16[512,1024]{1,0:T(8,128)(2,1)S(1)}, u32[]{:S(2)}, u32[]{:S(2)}) collective-permute-start(bf16[512,1024]{1,0:T(8,128)(2,1)S(1)} %bitcast.48), channel_id=1, source_target_pairs={{0,64},{64,0},{1,65},{65,1},{2,66},{66,2},{3,67},{67,3},{4,68},{68... | collective-permute-start | bytes 3145736 | tf_op jit(solution)/shard_map/ppermute | solution.py:18
  70.9 11.4 %collective-permute-start = (bf16[1,176,128]{2,1,0:T(8,128)(2,1)S(1)}, bf16[1,176,128]{2,1,0:T(8,128)(2,1)S(1)}, u32[]{:S(2)}, u32[]{:S(2)}) collective-permute-start(bf16[1,176,128]{2,1,0:T(8,128)(2,1)S(1)} %bitcast.53), channel_id=1, source_target_pairs={{0,32},{8,40},{16,48},{24,56},{32,0},{40,8},{48,16},{56,24},{1,33}... | collective-permute-start | bytes 135176 | tf_op jit(solution)/shard_map/ppermute | solution.py:18
  82.3 10.2 %collective-permute-start.1 = (bf16[2,176,128]{2,1,0:T(8,128)(2,1)S(1)}, bf16[2,176,128]{2,1,0:T(8,128)(2,1)S(1)}, u32[]{:S(2)}, u32[]{:S(2)}) collective-permute-start(bf16[2,176,128]{2,1,0:T(8,128)(2,1)S(1)} %pad_maximum_fusion.7), channel_id=1, source_target_pairs={{0,16},{8,24},{16,0},{24,8},{32,48},{40,56},{48,32},{56,40},{1,17}... | collective-permute-start | bytes 270344 | tf_op jit(solution)/shard_map/ppermute | solution.py:18
  92.6 7.4 %collective-permute-start.2 = (bf16[4,176,128]{2,1,0:T(8,128)(2,1)S(1)}, bf16[4,176,128]{2,1,0:T(8,128)(2,1)S(1)}, u32[]{:S(2)}, u32[]{:S(2)}) collective-permute-start(bf16[4,176,128]{2,1,0:T(8,128)(2,1)S(1)} %pad_maximum_fusion.4), channel_id=1, source_target_pairs={{0,8},{8,0},{16,24},{24,16},{32,40},{40,32},{48,56},{56,48},{1,9},... | collective-permute-start | bytes 540680 | tf_op jit(solution)/shard_map/ppermute | solution.py:18
  100.8 1.0 copy-start.3
  104.8 9.8 %collective-permute-start.6 = (bf16[352,128]{1,0:T(8,128)(2,1)}, bf16[352,128]{1,0:T(8,128)(2,1)S(1)}, u32[]{:S(2)}, u32[]{:S(2)}) collective-permute-start(bf16[352,128]{1,0:T(8,128)(2,1)} %get-tuple-element.14), channel_id=1, source_target_pairs={{0,3},{1,2},{2,1},{3,0},{4,7},{5,6},{6,5},{7,4},{8,11},{9,10},{10,... | collective-permute-start | bytes 270344 | tf_op jit(solution)/shard_map/ppermute | solution.py:18
  109.7 8.6 %collective-permute-start.5 = (bf16[352,128]{1,0:T(8,128)(2,1)}, bf16[352,128]{1,0:T(8,128)(2,1)S(1)}, u32[]{:S(2)}, u32[]{:S(2)}) collective-permute-start(bf16[352,128]{1,0:T(8,128)(2,1)} %get-tuple-element.13), channel_id=1, source_target_pairs={{0,2},{1,3},{2,0},{3,1},{4,6},{5,7},{6,4},{7,5},{8,10},{9,11},{10,... | collective-permute-start | bytes 270344 | tf_op jit(solution)/shard_map/ppermute | solution.py:18
  112.2 6.6 %collective-permute-start.4 = (bf16[352,128]{1,0:T(8,128)(2,1)}, bf16[352,128]{1,0:T(8,128)(2,1)S(1)}, u32[]{:S(2)}, u32[]{:S(2)}) collective-permute-start(bf16[352,128]{1,0:T(8,128)(2,1)} %get-tuple-element.12), channel_id=1, source_target_pairs={{0,1},{1,0},{2,3},{3,2},{4,5},{5,4},{6,7},{7,6},{8,9},{9,8},{10,11... | collective-permute-start | bytes 270344 | tf_op jit(solution)/shard_map/ppermute | solution.py:18
  119.9 19.2 %collective-permute-start.7 = (bf16[360,128]{1,0:T(8,128)(2,1)S(1)}, bf16[360,128]{1,0:T(8,128)(2,1)S(1)}, u32[]{:S(2)}, u32[]{:S(2)}) collective-permute-start(bf16[360,128]{1,0:T(8,128)(2,1)S(1)} %pad_maximum_fusion.6), channel_id=1, source_target_pairs={{0,4},{4,0},{1,5},{5,1},{2,6},{6,2},{3,7},{7,3},{8,12},{12,8},{9,1... | collective-permute-start | bytes 276488 | tf_op jit(solution)/shard_map/ppermute | solution.py:18
  140.6 14.9 %copy-start.6 = (bf16[360,128]{1,0:T(8,128)(2,1)}, bf16[360,128]{1,0:T(8,128)(2,1)S(1)}, u32[]{:S(2)}) copy-start(bf16[360,128]{1,0:T(8,128)(2,1)S(1)} %maximum_maximum_fusion.x0) | copy-start | bytes 276484
  140.6 10.4 %collective-permute-start.8 = (bf16[360,128]{1,0:T(8,128)(2,1)S(1)}, bf16[360,128]{1,0:T(8,128)(2,1)S(1)}, u32[]{:S(2)}, u32[]{:S(2)}) collective-permute-start(bf16[360,128]{1,0:T(8,128)(2,1)S(1)} %maximum_maximum_fusion.x0), channel_id=1, source_target_pairs={{0,1},{1,0},{2,3},{3,2},{4,5},{5,4},{6,7},{7,6},{8,9},{9,8},{10,11... | collective-permute-start | bytes 276488 | tf_op jit(solution)/shard_map/ppermute | solution.py:18
  142.9 8.1 %collective-permute-start.9 = (bf16[360,128]{1,0:T(8,128)(2,1)S(1)}, bf16[360,128]{1,0:T(8,128)(2,1)S(1)}, u32[]{:S(2)}, u32[]{:S(2)}) collective-permute-start(bf16[360,128]{1,0:T(8,128)(2,1)S(1)} %maximum_maximum_fusion.x0), channel_id=1, source_target_pairs={{0,2},{1,3},{2,0},{3,1},{4,6},{5,7},{6,4},{7,5},{8,10},{9,11},{10,... | collective-permute-start | bytes 276488 | tf_op jit(solution)/shard_map/ppermute | solution.py:18
  147.8 7.7 %collective-permute-start.10 = (bf16[360,128]{1,0:T(8,128)(2,1)S(1)}, bf16[360,128]{1,0:T(8,128)(2,1)S(1)}, u32[]{:S(2)}, u32[]{:S(2)}) collective-permute-start(bf16[360,128]{1,0:T(8,128)(2,1)S(1)} %maximum_maximum_fusion.x0), channel_id=1, source_target_pairs={{0,3},{1,2},{2,1},{3,0},{4,7},{5,6},{6,5},{7,4},{8,11},{9,10},{10,... | collective-permute-start | bytes 276488 | tf_op jit(solution)/shard_map/ppermute | solution.py:18
  151.1 4.4 %copy-start.8 = (bf16[360,128]{1,0:T(8,128)(2,1)}, bf16[360,128]{1,0:T(8,128)(2,1)S(1)}, u32[]{:S(2)}) copy-start(bf16[360,128]{1,0:T(8,128)(2,1)S(1)} %collective-permute-done.8.x1) | copy-start | bytes 276484
  151.1 4.4 %copy-start.9 = (bf16[360,128]{1,0:T(8,128)(2,1)}, bf16[360,128]{1,0:T(8,128)(2,1)S(1)}, u32[]{:S(2)}) copy-start(bf16[360,128]{1,0:T(8,128)(2,1)S(1)} %collective-permute-done.9.x2) | copy-start | bytes 276484
  155.5 0.6 copy-start.10
  162.1 13.8 %copy-start.2 = (f32[2,88,1792]{2,1,0:T(8,128)S(1)}, f32[2,88,1792]{2,1,0:T(8,128)}, u32[]{:S(2)}) copy-start(f32[2,88,1792]{2,1,0:T(8,128)} %get-tuple-element.15) | copy-start | bytes 3784708
  162.1 23.0 %copy-start.4 = (bf16[224,1024]{1,0:T(8,128)(2,1)S(1)}, bf16[224,1024]{1,0:T(8,128)(2,1)}, u32[]{:S(2)}) copy-start(bf16[224,1024]{1,0:T(8,128)(2,1)} %param.13) | copy-start | bytes 1376260
  162.1 12.7 %collective-permute-start.15 = (bf16[2,88,1792]{2,1,0:T(8,128)(2,1)}, bf16[2,88,1792]{2,1,0:T(8,128)(2,1)}, u32[]{:S(2)}, u32[]{:S(2)}) collective-permute-start(bf16[2,88,1792]{2,1,0:T(8,128)(2,1)} %get-tuple-element.16), channel_id=1, source_target_pairs={{0,8},{8,0},{16,24},{24,16},{32,40},{40,32},{48,56},{56,48},{1,9},... | collective-permute-start | bytes 1892360 | tf_op jit(solution)/shard_map/ppermute | solution.py:18
  176.8 30.1 %collective-permute-start.16 = (bf16[88,1792]{1,0:T(8,128)(2,1)}, bf16[88,1792]{1,0:T(8,128)(2,1)}, u32[]{:S(2)}, u32[]{:S(2)}) collective-permute-start(bf16[88,1792]{1,0:T(8,128)(2,1)} %fusion), channel_id=1, source_target_pairs={{0,16},{8,24},{16,0},{24,8},{32,48},{40,56},{48,32},{56,40},{1,17}... | collective-permute-start | bytes 946184 | tf_op jit(solution)/shard_map/ppermute | solution.py:18
  181.3 10.4 %collective-permute-start.11 = (f32[2,128]{1,0:T(2,128)S(1)}, f32[2,128]{1,0:T(2,128)S(1)}, u32[]{:S(2)}, u32[]{:S(2)}) collective-permute-start(f32[2,128]{1,0:T(2,128)S(1)} %slice_add_fusion.1), channel_id=1, source_target_pairs={{0,8},{8,0},{16,24},{24,16},{32,40},{40,32},{48,56},{56,48},{1,9},... | collective-permute-start | bytes 3080 | tf_op jit(solution)/shard_map/ppermute | solution.py:18
  186.6 43.0 %all-to-all-start.2 = ((bf16[4,224,1024]{2,1,0:T(8,128)(2,1)}), bf16[4,224,1024]{2,1,0:T(8,128)(2,1)S(1)}, u32[]{:S(2)}, u32[]{:S(2)}) async-start(bf16[4,224,1024]{2,1,0:T(8,128)(2,1)} %broadcast_in_dim.41), calls=%async_computation.2 | async-start | bytes 3670016 | tf_op jit(solution)/shard_map/all_to_all | solution.py:26
  191.7 6.4 %collective-permute-start.12 = (f32[2,128]{1,0:T(2,128)S(1)}, f32[2,128]{1,0:T(2,128)S(1)}, u32[]{:S(2)}, u32[]{:S(2)}) collective-permute-start(f32[2,128]{1,0:T(2,128)S(1)} %fusion.21), channel_id=1, source_target_pairs={{0,16},{8,24},{16,0},{24,8},{32,48},{40,56},{48,32},{56,40},{1,17}... | collective-permute-start | bytes 3080 | tf_op jit(solution)/shard_map/ppermute | solution.py:18
  198.0 14.0 %collective-permute-start.13 = (f32[2,128]{1,0:T(2,128)S(1)}, f32[2,128]{1,0:T(2,128)S(1)}, u32[]{:S(2)}, u32[]{:S(2)}) collective-permute-start(f32[2,128]{1,0:T(2,128)S(1)} %add.127), channel_id=1, source_target_pairs={{0,32},{8,40},{16,48},{24,56},{32,0},{40,8},{48,16},{56,24},{1,33}... | collective-permute-start | bytes 3080 | tf_op jit(solution)/shard_map/ppermute | solution.py:18
  208.2 19.3 %collective-permute-start.17 = (bf16[48,1792]{1,0:T(8,128)(2,1)S(1)}, bf16[48,1792]{1,0:T(8,128)(2,1)S(1)}, u32[]{:S(2)}, u32[]{:S(2)}) collective-permute-start(bf16[48,1792]{1,0:T(8,128)(2,1)S(1)} %dynamic-slice_convert_fusion), channel_id=1, source_target_pairs={{0,32},{8,40},{16,48},{24,56},{32,0},{40,8},{48,16},{56,24},{1,33}... | collective-permute-start | bytes 516104 | tf_op jit(solution)/shard_map/ppermute | solution.py:18
  227.7 10.3 %collective-permute-start.18 = (bf16[48,896]{1,0:T(8,128)(2,1)S(1)}, bf16[48,896]{1,0:T(8,128)(2,1)S(1)}, u32[]{:S(2)}, u32[]{:S(2)}) collective-permute-start(bf16[48,896]{1,0:T(8,128)(2,1)S(1)} %fusion.3), channel_id=1, source_target_pairs={{0,32},{8,40},{16,48},{24,56},{32,0},{40,8},{48,16},{56,24},{1,33}... | collective-permute-start | bytes 258056 | tf_op jit(solution)/shard_map/ppermute | solution.py:18
  229.6 26.6 %copy-start = (bf16[4,224,1024]{2,1,0:T(8,128)(2,1)}, bf16[4,224,1024]{2,1,0:T(8,128)(2,1)S(1)}, u32[]{:S(2)}) copy-start(bf16[4,224,1024]{2,1,0:T(8,128)(2,1)S(1)} %all-to-all-done.2) | copy-start | bytes 5505028
  229.7 26.6 %collective-permute-start.21 = (bf16[896,1024]{1,0:T(8,128)(2,1)S(1)}, bf16[896,1024]{1,0:T(8,128)(2,1)}, u32[]{:S(2)}, u32[]{:S(2)}) collective-permute-start(bf16[896,1024]{1,0:T(8,128)(2,1)S(1)} %bitcast.46), channel_id=1, source_target_pairs={{0,64},{64,0},{1,65},{65,1},{2,66},{66,2},{3,67},{67,3},{4,68},{68... | collective-permute-start | bytes 5505032 | tf_op jit(solution)/shard_map/ppermute | solution.py:18
  238.2 8.1 %collective-permute-start.19 = (bf16[88,896]{1,0:T(8,128)(2,1)S(1)}, bf16[88,896]{1,0:T(8,128)(2,1)S(1)}, u32[]{:S(2)}, u32[]{:S(2)}) collective-permute-start(bf16[88,896]{1,0:T(8,128)(2,1)S(1)} %pad_maximum_fusion.5), channel_id=1, source_target_pairs={{0,16},{8,24},{16,0},{24,8},{32,48},{40,56},{48,32},{56,40},{1,17}... | collective-permute-start | bytes 473096 | tf_op jit(solution)/shard_map/ppermute | solution.py:18
  246.4 8.8 %collective-permute-start.20 = (bf16[88,1792]{1,0:T(8,128)(2,1)S(1)}, bf16[88,1792]{1,0:T(8,128)(2,1)S(1)}, u32[]{:S(2)}, u32[]{:S(2)}) collective-permute-start(bf16[88,1792]{1,0:T(8,128)(2,1)S(1)} %pad_maximum_fusion.3), channel_id=1, source_target_pairs={{0,8},{8,0},{16,24},{24,16},{32,40},{40,32},{48,56},{56,48},{1,9},... | collective-permute-start | bytes 946184 | tf_op jit(solution)/shard_map/ppermute | solution.py:18
  260.3 10.6 %all-to-all-start.3 = ((bf16[4,352,128]{2,1,0:T(8,128)(2,1)}), bf16[4,352,128]{2,1,0:T(8,128)(2,1)S(1)}, u32[]{:S(2)}, u32[]{:S(2)}) async-start(bf16[4,352,128]{2,1,0:T(8,128)(2,1)} %down_mm.1), calls=%async_computation.3 | async-start | bytes 720896 | tf_op jit(solution)/shard_map/all_to_all | solution.py:26
  271.1 15.1 %collective-permute-start.22 = (bf16[176,128]{1,0:T(8,128)(2,1)S(1)}, bf16[176,128]{1,0:T(8,128)(2,1)S(1)}, u32[]{:S(2)}, u32[]{:S(2)}) collective-permute-start(bf16[176,128]{1,0:T(8,128)(2,1)S(1)} %fusion.5), channel_id=1, source_target_pairs={{0,4},{4,0},{1,5},{5,1},{2,6},{6,2},{3,7},{7,3},{8,12},{12,8},{9,1... | collective-permute-start | bytes 135176 | tf_op jit(solution)/shard_map/ppermute | solution.py:18

commit v6 on v5

v6 whole, which is shorter than its diff:
```python
import jax
import jax.numpy as jnp
from jax import lax
from jax.experimental import pallas as pl
from jax.experimental.pallas import tpu as pltpu
from jax.sharding import Mesh
from jax.sharding import PartitionSpec as P


D = 8192
BF = jnp.bfloat16
F32 = jnp.float32
AXES = ("x", "c", "zq", "zp", "zh", "y")
ZL = ("zq", "zp")
TOP = 48
STARTS_OF = (0, 48, 88, 128)
SPANS = ((0, 0, 48), (1, 48, 96), (2, 96, 136), (3, 136, 176))


def size_of(axis):
    return lax.axis_size(axis)


def shift(value, axis, step):
    n = size_of(axis)
    return lax.ppermute(value, axis, [(i, (i + step) % n) for i in range(n)])


def swap(value, axis, bit):
    n = size_of(axis)
    return lax.ppermute(value, axis, [(i, i ^ bit) for i in range(n)])


def pick(value, index, dim=0):
    return lax.dynamic_index_in_dim(value, index, dim, keepdims=False)


def exchange(parts, axis):
    return lax.all_to_all(parts, axis, split_axis=0, concat_axis=0, tiled=True)


def from_everyone(value, axis):
    copies = jnp.broadcast_to(value, (size_of(axis), *value.shape))
    return exchange(copies, axis)


def in_bits(own, other, bit):
    first = jnp.where(bit == 0, own, other)
    second = jnp.where(bit == 0, other, own)
    return first, second


def stack_kernel(*refs):
    *ins, out = refs
    height = ins[0].shape[0]
    for k, ref in enumerate(ins):
        out[k * height : (k + 1) * height] = ref[...]


def stacked(parts):
    height, width = parts[0].shape
    vmem = pl.BlockSpec(memory_space=pltpu.VMEM)
    return pl.pallas_call(
        stack_kernel,
        out_shape=jax.ShapeDtypeStruct((len(parts) * height, width), BF),
        in_specs=[vmem] * len(parts),
        out_specs=vmem,
        name="stack",
    )(*parts)


def dot(a, b):
    return jnp.dot(a, b, preferred_element_type=F32)


def proj_kernel(at, x, own, other, *outs):
    ci, zl, yi = at[0], at[2], at[3]
    rows = x.shape[1]

    def blocks(core):
        offs = [(2 * k + core) ^ zl for k in range(4)]
        return [x[((off >> 2) & 1) | (off & 2) | ((off & 1) << 2)] for off in offs]

    mine = jnp.concatenate(blocks(ci), axis=1)
    theirs = jnp.concatenate(blocks(1 - ci), axis=1)
    part = (dot(mine, own[...]) + dot(theirs, other[...])).astype(BF)
    *outs, parts = outs
    for zh in range(2):
        for y in range(4):
            n = (zh * 4 + y) * 128
            parts[y, zh * rows : (zh + 1) * rows] = part[:, n : n + 128]
    for k, out in enumerate(outs):
        out[...] = parts[yi ^ k]


def proj_parts(at, x, own, other):
    rows = x.shape[1]
    vmem = pl.BlockSpec(memory_space=pltpu.VMEM)
    return pl.pallas_call(
        proj_kernel,
        out_shape=[jax.ShapeDtypeStruct((2 * rows, 128), BF)] * 4,
        in_specs=[pl.BlockSpec(memory_space=pltpu.SMEM), vmem, vmem, vmem],
        out_specs=[vmem] * 4,
        scratch_shapes=[pltpu.VMEM((4, 2 * rows, 128), BF)],
        cost_estimate=pl.CostEstimate(
            flops=2 * rows * 1024 * 1024, bytes_accessed=3 << 20, transcendentals=0
        ),
        name="proj_mm",
    )(at, x, own, other)


def both_kernel(at, x, own, other, out):
    ci, zp = at[0], at[1]
    rows = (x.shape[1] - 8) // 2

    def blocks(core):
        parts = []
        for k in range(4):
            for turn in range(2):
                at_block = (zp ^ turn) * 4 + (k % 2) * 2 + core
                parts.append(x[at_block, pl.ds((k // 2) * rows, rows)])
        return jnp.concatenate(parts, axis=1)

    part = (dot(blocks(ci), own[...]) + dot(blocks(1 - ci), other[...])).astype(BF)
    for q in range(4):
        out[q] = part[STARTS_OF[q] : STARTS_OF[q] + TOP]


def both_parts(at, x, own, other):
    depth, wide = own.shape
    tile = 256
    vmem = pl.BlockSpec(memory_space=pltpu.VMEM)
    weights = pl.BlockSpec((depth, tile), lambda n: (0, n))
    return pl.pallas_call(
        both_kernel,
        grid=(wide // tile,),
        out_shape=jax.ShapeDtypeStruct((4, TOP, wide), BF),
        in_specs=[pl.BlockSpec(memory_space=pltpu.SMEM), vmem, weights, weights],
        out_specs=pl.BlockSpec((4, TOP, tile), lambda n: (0, 0, n)),
        cost_estimate=pl.CostEstimate(
            flops=4 * 176 * depth * wide, bytes_accessed=9 << 20, transcendentals=0
        ),
        name="both_mm",
    )(at, x, own, other)


def down_kernel(at, x, own, other, out, whole):
    ci, xi = at[0], at[4]
    height = own.shape[0] // 4
    rows = x.shape[0]
    for ref, core in ((own, ci), (other, 1 - ci)):
        for k in range(4):
            b = ((xi + 4 - k) & 3) * 2 + core
            to = pl.ds(pl.multiple_of(b * height, 16), height)
            whole[to] = ref[k * height : (k + 1) * height]
    part = dot(x[...], whole[...]).astype(BF)
    for zh in range(2):
        for y in range(4):
            n = (zh * 4 + y) * 128
            out[y, zh * rows : (zh + 1) * rows] = part[:, n : n + 128]


def down_parts(at, x, own, other):
    rows, depth = x.shape
    vmem = pl.BlockSpec(memory_space=pltpu.VMEM)
    return pl.pallas_call(
        down_kernel,
        out_shape=jax.ShapeDtypeStruct((4, 2 * rows, 128), BF),
        in_specs=[pl.BlockSpec(memory_space=pltpu.SMEM), vmem, vmem, vmem],
        out_specs=vmem,
        scratch_shapes=[pltpu.VMEM((depth, 1024), BF)],
        cost_estimate=pl.CostEstimate(
            flops=2 * rows * depth * 1024, bytes_accessed=5 << 20, transcendentals=0
        ),
        name="down_mm",
    )(at, x, own, other)


def exact(value):
    return lax.reduce_precision(value, 8, 7)


def on_device(attn_out, residual, proj_weight, norm_gain, gate_proj, up_proj, down_proj):
    xi, ci, zh, yi = (lax.axis_index(name) for name in ("x", "c", "zh", "y"))
    zq, zp = lax.axis_index("zq"), lax.axis_index("zp")
    at = jnp.stack([ci, zp, 2 * zq + zp, yi, xi]).astype(jnp.int32)
    rows = attn_out.shape[0]
    ffw = gate_proj.shape[1] // 2

    cols = attn_out[None]
    for bit in (4, 2, 1):
        cols = jnp.concatenate([cols, swap(cols, ZL, bit)])

    def columns(which):
        halves = [lax.dynamic_slice_in_dim(w, which * ffw, ffw, 1) for w in (gate_proj, up_proj)]
        return jnp.concatenate(halves, axis=1)

    facing = swap(columns(1 - zp), "zp", 1)
    both = jnp.concatenate([columns(zp), facing])
    both_own = from_everyone(both, "x").reshape(-1, 2 * ffw)
    both_other = swap(both_own, "c", 1)
    proj_own = from_everyone(proj_weight, "x").reshape(-1, proj_weight.shape[1])
    proj_other = swap(proj_own, "c", 1)
    ring = [1, 2, -1]
    shards = [down_proj] + [shift(down_proj, "x", k) for k in ring]
    down_own = stacked(shards)
    down_other = swap(down_own, "c", 1)

    high = exact(norm_gain)
    mid = exact(norm_gain - high)
    low = norm_gain - high - mid
    gains = jnp.pad(jnp.stack([high, mid, low]), ((0, 5), (0, 0)))

    part = proj_parts(at, cols, proj_own, proj_other)
    near = [part[0]] + [swap(part[k], "y", k) for k in (1, 2, 3)]
    near = sum(p.astype(F32) for p in near).reshape(2, rows, 128)
    mine = jnp.arange(2)[:, None, None] == zh
    near = jnp.where(mine, near + residual.astype(F32), near).reshape(2 * rows, 128)
    far = swap(jnp.concatenate([near, gains]).astype(BF), "zh", 1).astype(F32)
    stream2 = near + far[: 2 * rows]
    other_gain = far[2 * rows : 2 * rows + 3].sum(axis=0)
    gain2 = jnp.repeat(jnp.stack(in_bits(norm_gain, other_gain, zh)), rows, axis=0)
    squares = jnp.sum((stream2 * stream2).reshape(2, rows, 128), axis=(0, 2))
    scaled2 = (stream2 * gain2).astype(BF)
    squares = jnp.pad(squares, (0, 256 - rows)).reshape(2, 128)
    high = exact(squares)
    tail = jnp.concatenate([high, squares - high, jnp.zeros((4, 128), F32)]).astype(BF)
    model = from_everyone(jnp.concatenate([scaled2, tail]), ("zp", "y"))
    squares = model[:, 2 * rows : 2 * rows + 4].astype(F32).sum(axis=0)
    squares = squares[:2] + squares[2:]

    parts = exchange(both_parts(at, model, both_own, both_other), "zq")
    squares = squares + swap(squares, "zq", 1)
    squares = squares + swap(squares, "zq", 2)
    start = 40 * zq + 8 * jnp.minimum(zq, 1)
    squares = lax.dynamic_slice_in_dim(squares.reshape(256), start, TOP, 0)
    inverse = lax.rsqrt(squares / D + 1e-05)[:, None]
    sums = parts.astype(F32).sum(axis=0)
    gate_sum, up_sum = inverse * sums[:, :ffw], inverse * sums[:, ffw:]
    hidden = (jax.nn.silu(gate_sum) * up_sum).astype(BF)
    hidden = from_everyone(hidden, "zq")
    hidden = [hidden[q, TOP - (end - begin) :] for q, begin, end in SPANS]
    hidden = jnp.concatenate(hidden)
    hidden = jnp.concatenate(in_bits(hidden, swap(hidden, "zp", 1), zp), axis=1)

    part = down_parts(at, hidden, down_own, down_other)
    near = exchange(part, "y").astype(F32).sum(axis=0).reshape(2, rows, 128)
    far = swap(pick(near, 1 - zh).astype(BF), "zh", 1)
    stream = pick(stream2.reshape(2, rows, 128), zh)
    return (stream + pick(near, zh) + far.astype(F32)).astype(BF)


def solution(mesh):
    z = mesh.shape["gz"] // 4
    split = Mesh(mesh.devices.reshape(4, 2, mesh.shape["gy"] // 2, 2, z, 4), AXES)
    gx, gz = ("x", "c"), ("zh", "y")
    in_specs = (
        P(gx, (*gz, *ZL)),
        P(gx, (*ZL, *gz)),
        P((*gz, *gx), ZL),
        P((*ZL, *gz)),
        P((*ZL, *gx), gz),
        P((*ZL, *gx), gz),
        P((*gz, *gx), ZL),
    )
    return jax.shard_map(
        on_device, mesh=split, in_specs=in_specs, out_specs=P(gx, (*ZL, *gz)), check_vma=False
    )
```

time: 288 us -> 260 us (0.903)
  blocking collectives: 65 us -> 15.6 us
  starting transfers between devices: 103 us -> 129 us
  waiting for transfers between devices: 89.3 us -> 80.4 us
  Pallas kernels: 13.1 us -> 17.4 us
  local copies, waits for them, and re-layouts: 5.27 us -> 9.23 us
  other arithmetic: 9.96 us -> 6.09 us
    all_to_all x2 -> x1, blocking collectives: 65 us -> 15.6 us  [exchange(): return lax.all_to_all(parts, axis, split_axis=0, concat_axis=0, tiled=True)]
    all_to_all x2 -> x5, starting transfers between devices: 8.46 us -> 36.7 us  [exchange(): return lax.all_to_all(parts, axis, split_axis=0, concat_axis=0, tiled=True)]
    ppermute x23 -> x15, waiting for transfers between devices: 82.2 us -> 56.3 us  [swap(): return lax.ppermute(value, axis, [(i, i ^ bit) for i in range(n)])]
    ppermute x0 -> x3, waiting for transfers between devices: none -> 16.3 us  [shift(): return lax.ppermute(value, axis, [(i, (i + step) % n) for i in range(n)])]
    ppermute x23 -> x15, starting transfers between devices: 95 us -> 82 us  [swap(): return lax.ppermute(value, axis, [(i, i ^ bit) for i in range(n)])]
    ppermute x0 -> x3, starting transfers between devices: none -> 10.4 us  [shift(): return lax.ppermute(value, axis, [(i, (i + step) % n) for i in range(n)])]
    pallas_call x1 -> x2, Pallas kernels: 6.02 us -> 10.4 us  [the longest x1 7.55 us: both_parts(): pl.pallas_call(both_kernel, grid=(wide // tile,), out_shape=jax.ShapeDtyp...]
    broadcast_in_dim x3 -> x4, local copies, waits for them, and re-layouts: 1.88 us -> 5.11 us  [from_everyone(): copies = jnp.broadcast_to(value, (size_of(axis), *value.shape))]
  transfers between devices with their start and end apart: 25 -> 23, of which waited for: 16 -> 15; matrix products, arithmetic and copies ran while one was open for 3% -> 2% of each run, Pallas kernels for 1% -> 2%
where the time goes in v6:
time: 260 us; the launch traced here: 258 us
  starting transfers between devices  129 us (50%)
  waiting for transfers between devices  80.4 us (31%)
  Pallas kernels  17.4 us (7%)
  blocking collectives  15.6 us (6%)
  local copies, waits for them, and re-layouts  9.23 us (4%)
  other arithmetic  6.09 us (2%)
    ppermute x15, starting transfers between devices, swap(): return lax.ppermute(value, axis, [(i, i ^ bit) for i in range(n)])  82 us
    ppermute x15, waiting for transfers between devices, swap(): return lax.ppermute(value, axis, [(i, i ^ bit) for i in range(n)])  56.3 us
    all_to_all x5, starting transfers between devices, exchange(): return lax.all_to_all(parts, axis, split_axis=0, concat_axis=0, tiled=True)  36.7 us
    ppermute x3, waiting for transfers between devices, shift(): return lax.ppermute(value, axis, [(i, (i + step) % n) for i in range(n)])  16.3 us
    all_to_all x1, blocking collectives, exchange(): return lax.all_to_all(parts, axis, split_axis=0, concat_axis=0, tiled=True)  15.6 us
    ppermute x3, starting transfers between devices, shift(): return lax.ppermute(value, axis, [(i, (i + step) % n) for i in range(n)])  10.4 us
    all_to_all x5, waiting for transfers between devices, exchange(): return lax.all_to_all(parts, axis, split_axis=0, concat_axis=0, tiled=True)  7.79 us
    pallas_call x1, Pallas kernels, both_parts(): pl.pallas_call(both_kernel, grid=(wide // tile,), out_shape=jax.ShapeDtyp...  7.55 us
  transfers between devices with their start and end apart: 23, of which 15 were waited for; matrix products, arithmetic and copies ran while one was open for 2% of the time, Pallas kernels for 2%

profile of v6, /device:TPU:2, one launch (start us, length us, event | category | flops | bytes accessed | tf_op | source)
XLA Modules:
  0.0 258.3 jit_solution(15775782647893903202)
XLA Ops:
  0.0 2.1 broadcast_in_dim.40
  2.1 9.4 %all-to-all-start = ((bf16[4,128,1024]{2,1,0:T(8,128)(2,1)}), bf16[4,128,1024]{2,1,0:T(8,128)(2,1)S(1)}, u32[]{:S(2)}, u32[]{:S(2)}) async-start(bf16[4,128,1024]{2,1,0:T(8,128)(2,1)} %broadcast_in_dim.40), calls=%async_computation | async-start | bytes 2097152 | tf_op jit(solution)/shard_map/all_to_all | solution.py:39
  11.6 1.9 collective-permute-start.10
  13.6 8.4 %collective-permute-done.10 = bf16[128,1792]{1,0:T(8,128)(2,1)S(1)} collective-permute-done((bf16[128,1792]{1,0:T(8,128)(2,1)S(1)}, bf16[128,1792]{1,0:T(8,128)(2,1)S(1)}, u32[]{:S(2)}, u32[]{:S(2)}) %collective-permute-start.10) | collective-permute-done | bytes 458784 | tf_op jit(solution)/shard_map/ppermute | solution.py:31
  22.1 2.1 broadcast_in_dim.44
  24.2 5.1 %all-to-all-start.2 = ((bf16[4,256,1792]{2,1,0:T(8,128)(2,1)}), bf16[4,256,1792]{2,1,0:T(8,128)(2,1)}, u32[]{:S(2)}, u32[]{:S(2)}) async-start(bf16[4,256,1792]{2,1,0:T(8,128)(2,1)} %broadcast_in_dim.44), calls=%async_computation.2 | async-start | bytes 7340032 | tf_op jit(solution)/shard_map/all_to_all | solution.py:39
  29.4 1.9 collective-permute-start.3
  31.3 8.8 %collective-permute-start = (bf16[1,176,128]{2,1,0:T(8,128)(2,1)S(1)}, bf16[1,176,128]{2,1,0:T(8,128)(2,1)S(1)}, u32[]{:S(2)}, u32[]{:S(2)}) collective-permute-start(bf16[1,176,128]{2,1,0:T(8,128)(2,1)S(1)} %bitcast.55), channel_id=1, source_target_pairs={{0,32},{8,40},{16,48},{24,56},{32,0},{40,8},{48,16},{56,24},{1,33}... | collective-permute-start | bytes 135176 | tf_op jit(solution)/shard_map/ppermute | solution.py:31
  40.1 2.3 collective-permute-done
  42.4 5.5 %collective-permute-start.1 = (bf16[2,176,128]{2,1,0:T(8,128)(2,1)S(1)}, bf16[2,176,128]{2,1,0:T(8,128)(2,1)S(1)}, u32[]{:S(2)}, u32[]{:S(2)}) collective-permute-start(bf16[2,176,128]{2,1,0:T(8,128)(2,1)S(1)} %pad_maximum_fusion.7), channel_id=1, source_target_pairs={{0,16},{8,24},{16,0},{24,8},{32,48},{40,56},{48,32},{56,40},{1,17}... | collective-permute-start | bytes 270344 | tf_op jit(solution)/shard_map/ppermute | solution.py:31
  48.7 3.9 %collective-permute-done.1 = bf16[2,176,128]{2,1,0:T(8,128)(2,1)S(1)} collective-permute-done((bf16[2,176,128]{2,1,0:T(8,128)(2,1)S(1)}, bf16[2,176,128]{2,1,0:T(8,128)(2,1)S(1)}, u32[]{:S(2)}, u32[]{:S(2)}) %collective-permute-start.1) | collective-permute-done | bytes 90144 | tf_op jit(solution)/shard_map/ppermute | solution.py:31
  52.7 2.6 %collective-permute-start.2 = (bf16[4,176,128]{2,1,0:T(8,128)(2,1)S(1)}, bf16[4,176,128]{2,1,0:T(8,128)(2,1)S(1)}, u32[]{:S(2)}, u32[]{:S(2)}) collective-permute-start(bf16[4,176,128]{2,1,0:T(8,128)(2,1)S(1)} %pad_maximum_fusion.5), channel_id=1, source_target_pairs={{0,8},{8,0},{16,24},{24,16},{32,40},{40,32},{48,56},{56,48},{1,9},... | collective-permute-start | bytes 540680 | tf_op jit(solution)/shard_map/ppermute | solution.py:31
  55.3 4.7 %collective-permute-done.2 = bf16[4,176,128]{2,1,0:T(8,128)(2,1)S(1)} collective-permute-done((bf16[4,176,128]{2,1,0:T(8,128)(2,1)S(1)}, bf16[4,176,128]{2,1,0:T(8,128)(2,1)S(1)}, u32[]{:S(2)}, u32[]{:S(2)}) %collective-permute-start.2) | collective-permute-done | bytes 180256 | tf_op jit(solution)/shard_map/ppermute | solution.py:31
  60.8 1.0 copy-done.2
  61.9 3.0 %proj_mm.1 = (bf16[352,128]{1,0:T(8,128)(2,1)}, bf16[352,128]{1,0:T(8,128)(2,1)}, bf16[352,128]{1,0:T(8,128)(2,1)}, bf16[352,128]{1,0:T(8,128)(2,1)}) custom-call(s32[5]{0:T(128)} %stack.49.at, bf16[8,176,128]{2,1,0:T(8,128)(2,1)} %pad_maximum_fusion.3.x, bf16[512,1024]{1,0:T(8,128)(2,1)} %bitcast.51, bf16[512,1024]{1,0:T(8,128)(2,1)} %copy-done.2), custom_call_target="tpu_custom_call" | custom-call | flops 369098752 | bytes 3145728 | tf_op jit(solution)/shard_map/proj_mm/pallas_call | solution.py:99
  64.8 3.5 %collective-permute-start.4 = (bf16[352,128]{1,0:T(8,128)(2,1)}, bf16[352,128]{1,0:T(8,128)(2,1)S(1)}, u32[]{:S(2)}, u32[]{:S(2)}) collective-permute-start(bf16[352,128]{1,0:T(8,128)(2,1)} %get-tuple-element.10), channel_id=1, source_target_pairs={{0,1},{1,0},{2,3},{3,2},{4,5},{5,4},{6,7},{7,6},{8,9},{9,8},{10,11... | collective-permute-start | bytes 270344 | tf_op jit(solution)/shard_map/ppermute | solution.py:31
  68.3 4.8 %collective-permute-start.5 = (bf16[352,128]{1,0:T(8,128)(2,1)}, bf16[352,128]{1,0:T(8,128)(2,1)S(1)}, u32[]{:S(2)}, u32[]{:S(2)}) collective-permute-start(bf16[352,128]{1,0:T(8,128)(2,1)} %get-tuple-element.11), channel_id=1, source_target_pairs={{0,2},{1,3},{2,0},{3,1},{4,6},{5,7},{6,4},{7,5},{8,10},{9,11},{10,... | collective-permute-start | bytes 270344 | tf_op jit(solution)/shard_map/ppermute | solution.py:31
  73.1 2.1 collective-permute-start.6
  75.3 1.2 collective-permute-done.5
  76.4 4.5 %collective-permute-done.6 = bf16[352,128]{1,0:T(8,128)(2,1)S(1)} collective-permute-done((bf16[352,128]{1,0:T(8,128)(2,1)}, bf16[352,128]{1,0:T(8,128)(2,1)S(1)}, u32[]{:S(2)}, u32[]{:S(2)}) %collective-permute-start.6) | collective-permute-done | bytes 90144 | tf_op jit(solution)/shard_map/ppermute | solution.py:31
  82.0 1.9 collective-permute-start.11
  84.0 14.7 %collective-permute-start.7 = (bf16[360,128]{1,0:T(8,128)(2,1)S(1)}, bf16[360,128]{1,0:T(8,128)(2,1)S(1)}, u32[]{:S(2)}, u32[]{:S(2)}) collective-permute-start(bf16[360,128]{1,0:T(8,128)(2,1)S(1)} %pad_maximum_fusion.6), channel_id=1, source_target_pairs={{0,4},{4,0},{1,5},{5,1},{2,6},{6,2},{3,7},{7,3},{8,12},{12,8},{9,1... | collective-permute-start | bytes 276488 | tf_op jit(solution)/shard_map/ppermute | solution.py:31
  98.8 3.5 %collective-permute-done.7 = bf16[360,128]{1,0:T(8,128)(2,1)S(1)} collective-permute-done((bf16[360,128]{1,0:T(8,128)(2,1)S(1)}, bf16[360,128]{1,0:T(8,128)(2,1)S(1)}, u32[]{:S(2)}, u32[]{:S(2)}) %collective-permute-start.7) | collective-permute-done | bytes 92192 | tf_op jit(solution)/shard_map/ppermute | solution.py:31
  102.4 1.0 fusion
  103.9 15.6 %all_to_all.30.x = bf16[8,360,128]{2,1,0:T(8,128)(2,1)} all-to-all(bf16[8,360,128]{2,1,0:T(8,128)(2,1)S(1)} %broadcast_in_dim.43), channel_id=1, replica_groups=mesh['x'=4,'c'=2,'zq'=4,'zp'=2,'zh'=2,'y'=4] {'zp','y'}, dimensions={0} | all-to-all | bytes 1474560 | tf_op jit(solution)/shard_map/all_to_all | solution.py:39
  119.5 7.6 %both_mm.1 = bf16[4,48,1792]{2,1,0:T(8,128)(2,1)} custom-call(s32[5]{0:T(128)} %stack.49.at, bf16[8,360,128]{2,1,0:T(8,128)(2,1)} %all_to_all.30.x, bf16[1024,1792]{1,0:T(8,128)(2,1)} %bitcast.17.own, bf16[1024,1792]{1,0:T(8,128)(2,1)} %collective-permute-done.11.other), custom_call_target="tpu_custom_call" | custom-call | flops 1291845632 | bytes 9437184 | tf_op jit(solution)/shard_map/both_mm/pallas_call | solution.py:134
  127.1 13.1 %all-to-all-start.3 = ((bf16[4,48,1792]{2,1,0:T(8,128)(2,1)}), bf16[4,48,1792]{2,1,0:T(8,128)(2,1)S(1)}, u32[]{:S(2)}, u32[]{:S(2)}) async-start(bf16[4,48,1792]{2,1,0:T(8,128)(2,1)} %both_mm.1), calls=%async_computation.3 | async-start | bytes 1376256 | tf_op jit(solution)/shard_map/all_to_all | solution.py:39
  140.9 4.8 %collective-permute-start.8 = (f32[2,128]{1,0:T(2,128)S(1)}, f32[2,128]{1,0:T(2,128)S(1)}, u32[]{:S(2)}, u32[]{:S(2)}) collective-permute-start(f32[2,128]{1,0:T(2,128)S(1)} %slice_add_fusion.1), channel_id=1, source_target_pairs={{0,16},{16,0},{32,48},{48,32},{1,17},{17,1},{33,49},{49,33},{2,18}... | collective-permute-start | bytes 3080 | tf_op jit(solution)/shard_map/ppermute | solution.py:31
  145.8 8.5 %collective-permute-done.8 = f32[2,128]{1,0:T(2,128)S(1)} collective-permute-done((f32[2,128]{1,0:T(2,128)S(1)}, f32[2,128]{1,0:T(2,128)S(1)}, u32[]{:S(2)}, u32[]{:S(2)}) %collective-permute-start.8) | collective-permute-done | bytes 1056 | tf_op jit(solution)/shard_map/ppermute | solution.py:31
  154.3 17.2 %collective-permute-start.9 = (f32[2,128]{1,0:T(2,128)S(1)}, f32[2,128]{1,0:T(2,128)S(1)}, u32[]{:S(2)}, u32[]{:S(2)}) collective-permute-start(f32[2,128]{1,0:T(2,128)S(1)} %fusion.18), channel_id=1, source_target_pairs={{0,32},{16,48},{32,0},{48,16},{1,33},{17,49},{33,1},{49,17},{2,34}... | collective-permute-start | bytes 3080 | tf_op jit(solution)/shard_map/ppermute | solution.py:31
  171.5 3.1 %collective-permute-done.9 = f32[2,128]{1,0:T(2,128)S(1)} collective-permute-done((f32[2,128]{1,0:T(2,128)S(1)}, f32[2,128]{1,0:T(2,128)S(1)}, u32[]{:S(2)}, u32[]{:S(2)}) %collective-permute-start.9) | collective-permute-done | bytes 1056 | tf_op jit(solution)/shard_map/ppermute | solution.py:31
  175.6 5.6 %all-to-all-start.4 = ((bf16[4,48,896]{2,1,0:T(8,128)(2,1)}), bf16[4,48,896]{2,1,0:T(8,128)(2,1)S(1)}, u32[]{:S(2)}, u32[]{:S(2)}) async-start(bf16[4,48,896]{2,1,0:T(8,128)(2,1)} %broadcast_in_dim.45), calls=%async_computation.4 | async-start | bytes 688128 | tf_op jit(solution)/shard_map/all_to_all | solution.py:39
  181.3 3.4 %collective-permute-start.13 = (bf16[224,1024]{1,0:T(8,128)(2,1)S(1)}, bf16[224,1024]{1,0:T(8,128)(2,1)S(1)}, u32[]{:S(2)}, u32[]{:S(2)}) collective-permute-start(bf16[224,1024]{1,0:T(8,128)(2,1)S(1)} %copy-done.3), channel_id=1, source_target_pairs={{0,128},{128,256},{256,384},{384,0},{1,129},{129,257},{257,385},{3... | collective-permute-start | bytes 1376264 | tf_op jit(solution)/shard_map/ppermute | solution.py:26
  184.7 2.6 %collective-permute-start.14 = (bf16[224,1024]{1,0:T(8,128)(2,1)S(1)}, bf16[224,1024]{1,0:T(8,128)(2,1)S(1)}, u32[]{:S(2)}, u32[]{:S(2)}) collective-permute-start(bf16[224,1024]{1,0:T(8,128)(2,1)S(1)} %copy-done.3), channel_id=1, source_target_pairs={{0,256},{128,384},{256,0},{384,128},{1,257},{129,385},{257,1},{385... | collective-permute-start | bytes 1376264 | tf_op jit(solution)/shard_map/ppermute | solution.py:26
  187.2 4.5 %collective-permute-start.15 = (bf16[224,1024]{1,0:T(8,128)(2,1)S(1)}, bf16[224,1024]{1,0:T(8,128)(2,1)S(1)}, u32[]{:S(2)}, u32[]{:S(2)}) collective-permute-start(bf16[224,1024]{1,0:T(8,128)(2,1)S(1)} %copy-done.3), channel_id=1, source_target_pairs={{0,384},{128,0},{256,128},{384,256},{1,385},{129,1},{257,129},{385... | collective-permute-start | bytes 1376264 | tf_op jit(solution)/shard_map/ppermute | solution.py:26
  191.7 4.8 %collective-permute-done.13.refs_1_ = bf16[224,1024]{1,0:T(8,128)(2,1)S(1)} collective-permute-done((bf16[224,1024]{1,0:T(8,128)(2,1)S(1)}, bf16[224,1024]{1,0:T(8,128)(2,1)S(1)}, u32[]{:S(2)}, u32[]{:S(2)}) %collective-permute-start.13) | collective-permute-done | bytes 458784 | tf_op jit(solution)/shard_map/ppermute | solution.py:26
  196.5 4.9 %collective-permute-done.14.refs_2_ = bf16[224,1024]{1,0:T(8,128)(2,1)S(1)} collective-permute-done((bf16[224,1024]{1,0:T(8,128)(2,1)S(1)}, bf16[224,1024]{1,0:T(8,128)(2,1)S(1)}, u32[]{:S(2)}, u32[]{:S(2)}) %collective-permute-start.14) | collective-permute-done | bytes 458784 | tf_op jit(solution)/shard_map/ppermute | solution.py:26
  201.4 6.6 %collective-permute-done.15.refs_3_ = bf16[224,1024]{1,0:T(8,128)(2,1)S(1)} collective-permute-done((bf16[224,1024]{1,0:T(8,128)(2,1)S(1)}, bf16[224,1024]{1,0:T(8,128)(2,1)S(1)}, u32[]{:S(2)}, u32[]{:S(2)}) %collective-permute-start.15) | collective-permute-done | bytes 458784 | tf_op jit(solution)/shard_map/ppermute | solution.py:26
  208.8 2.8 %stack.57.own = bf16[896,1024]{1,0:T(8,128)(2,1)} custom-call(bf16[224,1024]{1,0:T(8,128)(2,1)} %refs_0_.1, bf16[224,1024]{1,0:T(8,128)(2,1)} %copy-done.4, bf16[224,1024]{1,0:T(8,128)(2,1)} %copy-done.5, bf16[224,1024]{1,0:T(8,128)(2,1)} %copy-done.6), custom_call_target="tpu_custom_call" | custom-call | tf_op jit(solution)/shard_map/stack/pallas_call | solution.py:63
  211.6 1.9 collective-permute-start.16
  213.6 2.3 collective-permute-start.12
  215.9 9.4 %collective-permute-done.12 = bf16[176,896]{1,0:T(8,128)(2,1)S(1)} collective-permute-done((bf16[176,896]{1,0:T(8,128)(2,1)S(1)}, bf16[176,896]{1,0:T(8,128)(2,1)S(1)}, u32[]{:S(2)}, u32[]{:S(2)}) %collective-permute-start.12) | collective-permute-done | bytes 315424 | tf_op jit(solution)/shard_map/ppermute | solution.py:31
  226.4 1.2 copy-done.1
  227.6 4.1 %down_mm.1 = bf16[4,352,128]{2,1,0:T(8,128)(2,1)} custom-call(s32[5]{0:T(128)} %stack.49.at, bf16[176,1792]{1,0:T(8,128)(2,1)} %pad_maximum_fusion.1.x, bf16[896,1024]{1,0:T(8,128)(2,1)} %stack.57.own, bf16[896,1024]{1,0:T(8,128)(2,1)} %copy-done.1), custom_call_target="tpu_custom_call" | custom-call | flops 645922816 | bytes 5242880 | tf_op jit(solution)/shard_map/down_mm/pallas_call | solution.py:166
  231.7 3.5 %all-to-all-start.5 = ((bf16[4,352,128]{2,1,0:T(8,128)(2,1)}), bf16[4,352,128]{2,1,0:T(8,128)(2,1)S(1)}, u32[]{:S(2)}, u32[]{:S(2)}) async-start(bf16[4,352,128]{2,1,0:T(8,128)(2,1)} %down_mm.1), calls=%async_computation.5 | async-start | bytes 720896 | tf_op jit(solution)/shard_map/all_to_all | solution.py:39
  235.1 7.8 %all-to-all-done.5 = bf16[4,352,128]{2,1,0:T(8,128)(2,1)S(1)} async-done(((bf16[4,352,128]{2,1,0:T(8,128)(2,1)}), bf16[4,352,128]{2,1,0:T(8,128)(2,1)S(1)}, u32[]{:S(2)}, u32[]{:S(2)}) %all-to-all-start.5) | async-done | bytes 360480 | tf_op jit(solution)/shard_map/all_to_all | solution.py:39
  243.0 8.0 %collective-permute-start.17 = (bf16[176,128]{1,0:T(8,128)(2,1)S(1)}, bf16[176,128]{1,0:T(8,128)(2,1)S(1)}, u32[]{:S(2)}, u32[]{:S(2)}) collective-permute-start(bf16[176,128]{1,0:T(8,128)(2,1)S(1)} %fusion.4), channel_id=1, source_target_pairs={{0,4},{4,0},{1,5},{5,1},{2,6},{6,2},{3,7},{7,3},{8,12},{12,8},{9,1... | collective-permute-start | bytes 135176 | tf_op jit(solution)/shard_map/ppermute | solution.py:31
  251.0 6.7 %collective-permute-done.17 = bf16[176,128]{1,0:T(8,128)(2,1)S(1)} collective-permute-done((bf16[176,128]{1,0:T(8,128)(2,1)S(1)}, bf16[176,128]{1,0:T(8,128)(2,1)S(1)}, u32[]{:S(2)}, u32[]{:S(2)}) %collective-permute-start.17) | collective-permute-done | bytes 45088 | tf_op jit(solution)/shard_map/ppermute | solution.py:31
  (73 shorter events, 7.8 us)
Async XLA Ops:
  0.0 11.5 %copy-start.8 = (bf16[128,1792]{1,0:T(8,128)(2,1)S(1)}, bf16[128,1792]{1,0:T(8,128)(2,1)}, u32[]{:S(2)}) copy-start(bf16[128,1792]{1,0:T(8,128)(2,1)} %param.11) | copy-start | bytes 1376260
  0.0 11.5 %copy-start.7 = (bf16[128,1792]{1,0:T(8,128)(2,1)S(1)}, bf16[128,1792]{1,0:T(8,128)(2,1)}, u32[]{:S(2)}) copy-start(bf16[128,1792]{1,0:T(8,128)(2,1)} %param.12) | copy-start | bytes 1376260
  2.1 19.9 %all-to-all-start = ((bf16[4,128,1024]{2,1,0:T(8,128)(2,1)}), bf16[4,128,1024]{2,1,0:T(8,128)(2,1)S(1)}, u32[]{:S(2)}, u32[]{:S(2)}) async-start(bf16[4,128,1024]{2,1,0:T(8,128)(2,1)} %broadcast_in_dim.40), calls=%async_computation | async-start | bytes 2097152 | tf_op jit(solution)/shard_map/all_to_all | solution.py:39
  11.6 10.4 %collective-permute-start.10 = (bf16[128,1792]{1,0:T(8,128)(2,1)S(1)}, bf16[128,1792]{1,0:T(8,128)(2,1)S(1)}, u32[]{:S(2)}, u32[]{:S(2)}) collective-permute-start(bf16[128,1792]{1,0:T(8,128)(2,1)S(1)} %pad_maximum_fusion.2), channel_id=1, source_target_pairs={{0,8},{8,0},{1,9},{9,1},{2,10},{10,2},{3,11},{11,3},{4,12},{12,4},... | collective-permute-start | bytes 1376264 | tf_op jit(solution)/shard_map/ppermute | solution.py:31
  22.1 7.3 %copy-start = (bf16[4,128,1024]{2,1,0:T(8,128)(2,1)}, bf16[4,128,1024]{2,1,0:T(8,128)(2,1)S(1)}, u32[]{:S(2)}) copy-start(bf16[4,128,1024]{2,1,0:T(8,128)(2,1)S(1)} %all-to-all-done) | copy-start | bytes 3145732
  24.2 7.1 %copy-start.9 = (bf16[176,128]{1,0:T(8,128)(2,1)S(1)}, bf16[176,128]{1,0:T(8,128)(2,1)}, u32[]{:S(2)}) copy-start(bf16[176,128]{1,0:T(8,128)(2,1)} %param.7) | copy-start | bytes 135172
  24.2 23.8 %copy-start.10 = (bf16[176,128]{1,0:T(8,128)(2,1)S(1)}, bf16[176,128]{1,0:T(8,128)(2,1)}, u32[]{:S(2)}) copy-start(bf16[176,128]{1,0:T(8,128)(2,1)} %param.8) | copy-start | bytes 135172
  24.2 31.1 %copy-start.11 = (f32[128]{0:T(128)S(1)}, f32[128]{0:T(128)}, u32[]{:S(2)}) copy-start(f32[128]{0:T(128)} %param.10) | copy-start | bytes 1540
  24.2 57.8 %all-to-all-start.2 = ((bf16[4,256,1792]{2,1,0:T(8,128)(2,1)}), bf16[4,256,1792]{2,1,0:T(8,128)(2,1)}, u32[]{:S(2)}, u32[]{:S(2)}) async-start(bf16[4,256,1792]{2,1,0:T(8,128)(2,1)} %broadcast_in_dim.44), calls=%async_computation.2 | async-start | bytes 7340032 | tf_op jit(solution)/shard_map/all_to_all | solution.py:39
  29.4 31.4 %collective-permute-start.3 = (bf16[512,1024]{1,0:T(8,128)(2,1)S(1)}, bf16[512,1024]{1,0:T(8,128)(2,1)S(1)}, u32[]{:S(2)}, u32[]{:S(2)}) collective-permute-start(bf16[512,1024]{1,0:T(8,128)(2,1)S(1)} %bitcast.50), channel_id=1, source_target_pairs={{0,64},{64,0},{1,65},{65,1},{2,66},{66,2},{3,67},{67,3},{4,68},{68... | collective-permute-start | bytes 3145736 | tf_op jit(solution)/shard_map/ppermute | solution.py:31
  31.3 11.1 %collective-permute-start = (bf16[1,176,128]{2,1,0:T(8,128)(2,1)S(1)}, bf16[1,176,128]{2,1,0:T(8,128)(2,1)S(1)}, u32[]{:S(2)}, u32[]{:S(2)}) collective-permute-start(bf16[1,176,128]{2,1,0:T(8,128)(2,1)S(1)} %bitcast.55), channel_id=1, source_target_pairs={{0,32},{8,40},{16,48},{24,56},{32,0},{40,8},{48,16},{56,24},{1,33}... | collective-permute-start | bytes 135176 | tf_op jit(solution)/shard_map/ppermute | solution.py:31
  42.4 10.2 %collective-permute-start.1 = (bf16[2,176,128]{2,1,0:T(8,128)(2,1)S(1)}, bf16[2,176,128]{2,1,0:T(8,128)(2,1)S(1)}, u32[]{:S(2)}, u32[]{:S(2)}) collective-permute-start(bf16[2,176,128]{2,1,0:T(8,128)(2,1)S(1)} %pad_maximum_fusion.7), channel_id=1, source_target_pairs={{0,16},{8,24},{16,0},{24,8},{32,48},{40,56},{48,32},{56,40},{1,17}... | collective-permute-start | bytes 270344 | tf_op jit(solution)/shard_map/ppermute | solution.py:31
  52.7 7.4 %collective-permute-start.2 = (bf16[4,176,128]{2,1,0:T(8,128)(2,1)S(1)}, bf16[4,176,128]{2,1,0:T(8,128)(2,1)S(1)}, u32[]{:S(2)}, u32[]{:S(2)}) collective-permute-start(bf16[4,176,128]{2,1,0:T(8,128)(2,1)S(1)} %pad_maximum_fusion.5), channel_id=1, source_target_pairs={{0,8},{8,0},{16,24},{24,16},{32,40},{40,32},{48,56},{56,48},{1,9},... | collective-permute-start | bytes 540680 | tf_op jit(solution)/shard_map/ppermute | solution.py:31
  60.8 1.0 copy-start.2
  64.8 10.5 %collective-permute-start.4 = (bf16[352,128]{1,0:T(8,128)(2,1)}, bf16[352,128]{1,0:T(8,128)(2,1)S(1)}, u32[]{:S(2)}, u32[]{:S(2)}) collective-permute-start(bf16[352,128]{1,0:T(8,128)(2,1)} %get-tuple-element.10), channel_id=1, source_target_pairs={{0,1},{1,0},{2,3},{3,2},{4,5},{5,4},{6,7},{7,6},{8,9},{9,8},{10,11... | collective-permute-start | bytes 270344 | tf_op jit(solution)/shard_map/ppermute | solution.py:31
  68.3 8.1 %collective-permute-start.5 = (bf16[352,128]{1,0:T(8,128)(2,1)}, bf16[352,128]{1,0:T(8,128)(2,1)S(1)}, u32[]{:S(2)}, u32[]{:S(2)}) collective-permute-start(bf16[352,128]{1,0:T(8,128)(2,1)} %get-tuple-element.11), channel_id=1, source_target_pairs={{0,2},{1,3},{2,0},{3,1},{4,6},{5,7},{6,4},{7,5},{8,10},{9,11},{10,... | collective-permute-start | bytes 270344 | tf_op jit(solution)/shard_map/ppermute | solution.py:31
  73.1 7.8 %collective-permute-start.6 = (bf16[352,128]{1,0:T(8,128)(2,1)}, bf16[352,128]{1,0:T(8,128)(2,1)S(1)}, u32[]{:S(2)}, u32[]{:S(2)}) collective-permute-start(bf16[352,128]{1,0:T(8,128)(2,1)} %get-tuple-element.12), channel_id=1, source_target_pairs={{0,3},{1,2},{2,1},{3,0},{4,7},{5,6},{6,5},{7,4},{8,11},{9,10},{10,... | collective-permute-start | bytes 270344 | tf_op jit(solution)/shard_map/ppermute | solution.py:31
  82.0 37.5 %collective-permute-start.11 = (bf16[1024,1792]{1,0:T(8,128)(2,1)}, bf16[1024,1792]{1,0:T(8,128)(2,1)}, u32[]{:S(2)}, u32[]{:S(2)}) collective-permute-start(bf16[1024,1792]{1,0:T(8,128)(2,1)} %bitcast.17.own), channel_id=1, source_target_pairs={{0,64},{64,0},{1,65},{65,1},{2,66},{66,2},{3,67},{67,3},{4,68},{68... | collective-permute-start | bytes 11010056 | tf_op jit(solution)/shard_map/ppermute | solution.py:31
  84.0 18.3 %collective-permute-start.7 = (bf16[360,128]{1,0:T(8,128)(2,1)S(1)}, bf16[360,128]{1,0:T(8,128)(2,1)S(1)}, u32[]{:S(2)}, u32[]{:S(2)}) collective-permute-start(bf16[360,128]{1,0:T(8,128)(2,1)S(1)} %pad_maximum_fusion.6), channel_id=1, source_target_pairs={{0,4},{4,0},{1,5},{5,1},{2,6},{6,2},{3,7},{7,3},{8,12},{12,8},{9,1... | collective-permute-start | bytes 276488 | tf_op jit(solution)/shard_map/ppermute | solution.py:31
  127.1 54.2 %copy-start.3 = (bf16[224,1024]{1,0:T(8,128)(2,1)S(1)}, bf16[224,1024]{1,0:T(8,128)(2,1)}, u32[]{:S(2)}) copy-start(bf16[224,1024]{1,0:T(8,128)(2,1)} %refs_0_.1) | copy-start | bytes 1376260
  127.1 47.6 %all-to-all-start.3 = ((bf16[4,48,1792]{2,1,0:T(8,128)(2,1)}), bf16[4,48,1792]{2,1,0:T(8,128)(2,1)S(1)}, u32[]{:S(2)}, u32[]{:S(2)}) async-start(bf16[4,48,1792]{2,1,0:T(8,128)(2,1)} %both_mm.1), calls=%async_computation.3 | async-start | bytes 1376256 | tf_op jit(solution)/shard_map/all_to_all | solution.py:39
  140.9 13.4 %collective-permute-start.8 = (f32[2,128]{1,0:T(2,128)S(1)}, f32[2,128]{1,0:T(2,128)S(1)}, u32[]{:S(2)}, u32[]{:S(2)}) collective-permute-start(f32[2,128]{1,0:T(2,128)S(1)} %slice_add_fusion.1), channel_id=1, source_target_pairs={{0,16},{16,0},{32,48},{48,32},{1,17},{17,1},{33,49},{49,33},{2,18}... | collective-permute-start | bytes 3080 | tf_op jit(solution)/shard_map/ppermute | solution.py:31
  154.3 20.3 %collective-permute-start.9 = (f32[2,128]{1,0:T(2,128)S(1)}, f32[2,128]{1,0:T(2,128)S(1)}, u32[]{:S(2)}, u32[]{:S(2)}) collective-permute-start(f32[2,128]{1,0:T(2,128)S(1)} %fusion.18), channel_id=1, source_target_pairs={{0,32},{16,48},{32,0},{48,16},{1,33},{17,49},{33,1},{49,17},{2,34}... | collective-permute-start | bytes 3080 | tf_op jit(solution)/shard_map/ppermute | solution.py:31
  175.6 37.9 %all-to-all-start.4 = ((bf16[4,48,896]{2,1,0:T(8,128)(2,1)}), bf16[4,48,896]{2,1,0:T(8,128)(2,1)S(1)}, u32[]{:S(2)}, u32[]{:S(2)}) async-start(bf16[4,48,896]{2,1,0:T(8,128)(2,1)} %broadcast_in_dim.45), calls=%async_computation.4 | async-start | bytes 688128 | tf_op jit(solution)/shard_map/all_to_all | solution.py:39
  181.3 15.3 %collective-permute-start.13 = (bf16[224,1024]{1,0:T(8,128)(2,1)S(1)}, bf16[224,1024]{1,0:T(8,128)(2,1)S(1)}, u32[]{:S(2)}, u32[]{:S(2)}) collective-permute-start(bf16[224,1024]{1,0:T(8,128)(2,1)S(1)} %copy-done.3), channel_id=1, source_target_pairs={{0,128},{128,256},{256,384},{384,0},{1,129},{129,257},{257,385},{3... | collective-permute-start | bytes 1376264 | tf_op jit(solution)/shard_map/ppermute | solution.py:26
  184.7 16.8 %collective-permute-start.14 = (bf16[224,1024]{1,0:T(8,128)(2,1)S(1)}, bf16[224,1024]{1,0:T(8,128)(2,1)S(1)}, u32[]{:S(2)}, u32[]{:S(2)}) collective-permute-start(bf16[224,1024]{1,0:T(8,128)(2,1)S(1)} %copy-done.3), channel_id=1, source_target_pairs={{0,256},{128,384},{256,0},{384,128},{1,257},{129,385},{257,1},{385... | collective-permute-start | bytes 1376264 | tf_op jit(solution)/shard_map/ppermute | solution.py:26
  187.2 20.8 %collective-permute-start.15 = (bf16[224,1024]{1,0:T(8,128)(2,1)S(1)}, bf16[224,1024]{1,0:T(8,128)(2,1)S(1)}, u32[]{:S(2)}, u32[]{:S(2)}) collective-permute-start(bf16[224,1024]{1,0:T(8,128)(2,1)S(1)} %copy-done.3), channel_id=1, source_target_pairs={{0,384},{128,0},{256,128},{384,256},{1,385},{129,1},{257,129},{385... | collective-permute-start | bytes 1376264 | tf_op jit(solution)/shard_map/ppermute | solution.py:26
  196.5 11.5 %copy-start.4 = (bf16[224,1024]{1,0:T(8,128)(2,1)}, bf16[224,1024]{1,0:T(8,128)(2,1)S(1)}, u32[]{:S(2)}) copy-start(bf16[224,1024]{1,0:T(8,128)(2,1)S(1)} %collective-permute-done.13.refs_1_) | copy-start | bytes 1376260
  201.4 6.6 %copy-start.5 = (bf16[224,1024]{1,0:T(8,128)(2,1)}, bf16[224,1024]{1,0:T(8,128)(2,1)S(1)}, u32[]{:S(2)}) copy-start(bf16[224,1024]{1,0:T(8,128)(2,1)S(1)} %collective-permute-done.14.refs_2_) | copy-start | bytes 1376260
  208.0 0.8 copy-start.6
  211.6 14.8 %collective-permute-start.16 = (bf16[896,1024]{1,0:T(8,128)(2,1)}, bf16[896,1024]{1,0:T(8,128)(2,1)S(1)}, u32[]{:S(2)}, u32[]{:S(2)}) collective-permute-start(bf16[896,1024]{1,0:T(8,128)(2,1)} %stack.57.own), channel_id=1, source_target_pairs={{0,64},{64,0},{1,65},{65,1},{2,66},{66,2},{3,67},{67,3},{4,68},{68... | collective-permute-start | bytes 5505032 | tf_op jit(solution)/shard_map/ppermute | solution.py:31
  213.6 11.7 %collective-permute-start.12 = (bf16[176,896]{1,0:T(8,128)(2,1)S(1)}, bf16[176,896]{1,0:T(8,128)(2,1)S(1)}, u32[]{:S(2)}, u32[]{:S(2)}) collective-permute-start(bf16[176,896]{1,0:T(8,128)(2,1)S(1)} %pad_maximum_fusion.4), channel_id=1, source_target_pairs={{0,8},{8,0},{1,9},{9,1},{2,10},{10,2},{3,11},{11,3},{4,12},{12,4},... | collective-permute-start | bytes 946184 | tf_op jit(solution)/shard_map/ppermute | solution.py:31
  226.4 1.2 copy-start.1
  231.7 11.2 %all-to-all-start.5 = ((bf16[4,352,128]{2,1,0:T(8,128)(2,1)}), bf16[4,352,128]{2,1,0:T(8,128)(2,1)S(1)}, u32[]{:S(2)}, u32[]{:S(2)}) async-start(bf16[4,352,128]{2,1,0:T(8,128)(2,1)} %down_mm.1), calls=%async_computation.5 | async-start | bytes 720896 | tf_op jit(solution)/shard_map/all_to_all | solution.py:39
  243.0 14.7 %collective-permute-start.17 = (bf16[176,128]{1,0:T(8,128)(2,1)S(1)}, bf16[176,128]{1,0:T(8,128)(2,1)S(1)}, u32[]{:S(2)}, u32[]{:S(2)}) collective-permute-start(bf16[176,128]{1,0:T(8,128)(2,1)S(1)} %fusion.4), channel_id=1, source_target_pairs={{0,4},{4,0},{1,5},{5,1},{2,6},{6,2},{3,7},{7,3},{8,12},{12,8},{9,1... | collective-permute-start | bytes 135176 | tf_op jit(solution)/shard_map/ppermute | solution.py:31

commit v7 on v6

--- a/solution.py
+++ b/solution.py
@@ -81,10 +81,13 @@
         offs = [(2 * k + core) ^ zl for k in range(4)]
         return [x[((off >> 2) & 1) | (off & 2) | ((off & 1) << 2)] for off in offs]
 
-    mine = jnp.concatenate(blocks(ci), axis=1)
+    *outs, parts, buffer, sem = outs
+    copy = pltpu.make_async_copy(other, buffer, sem)
+    copy.start()
+    part = dot(jnp.concatenate(blocks(ci), axis=1), own[...])
     theirs = jnp.concatenate(blocks(1 - ci), axis=1)
-    part = (dot(mine, own[...]) + dot(theirs, other[...])).astype(BF)
-    *outs, parts = outs
+    copy.wait()
+    part = (part + dot(theirs, buffer[...])).astype(BF)
     for zh in range(2):
         for y in range(4):
             n = (zh * 4 + y) * 128
@@ -95,13 +98,17 @@
 
 def proj_parts(at, x, own, other):
     rows = x.shape[1]
-    vmem = pl.BlockSpec(memory_space=pltpu.VMEM)
+    vmem, hbm = pl.BlockSpec(memory_space=pltpu.VMEM), pl.BlockSpec(memory_space=pltpu.HBM)
     return pl.pallas_call(
         proj_kernel,
         out_shape=[jax.ShapeDtypeStruct((2 * rows, 128), BF)] * 4,
-        in_specs=[pl.BlockSpec(memory_space=pltpu.SMEM), vmem, vmem, vmem],
+        in_specs=[pl.BlockSpec(memory_space=pltpu.SMEM), vmem, vmem, hbm],
         out_specs=[vmem] * 4,
-        scratch_shapes=[pltpu.VMEM((4, 2 * rows, 128), BF)],
+        scratch_shapes=[
+            pltpu.VMEM((4, 2 * rows, 128), BF),
+            pltpu.VMEM(other.shape, BF),
+            pltpu.SemaphoreType.DMA(()),
+        ],
         cost_estimate=pl.CostEstimate(
             flops=2 * rows * 1024 * 1024, bytes_accessed=3 << 20, transcendentals=0
         ),
@@ -125,16 +132,30 @@
     for q in range(4):
         out[q] = part[STARTS_OF[q] : STARTS_OF[q] + TOP]
 
+    @pl.when(pl.program_id(0) == pl.num_programs(0) - 1)
+    def _():
+        squares = sum(x[k, pl.ds(2 * rows, 4)].astype(F32) for k in range(8))
+        squares = jnp.concatenate([squares[k : k + 1] + squares[k + 2 : k + 3] for k in (0, 1)], 1)
+        lane = lax.broadcasted_iota(jnp.int32, (TOP, 256), 1)
+        row = lax.broadcasted_iota(jnp.int32, (TOP, 256), 0)
+        for q in range(4):
+            own_lane = jnp.where(lane == row + STARTS_OF[q], squares, 0.0)
+            total = jnp.sum(own_lane, axis=1, keepdims=True)
+            high = total.astype(BF).astype(F32)
+            place = lane[:, :128]
+            tail = jnp.where(place == 0, high, jnp.where(place == 1, total - high, 0.0))
+            out[q, :, out.shape[2] - 128 :] = tail.astype(BF)
+
 
 def both_parts(at, x, own, other):
     depth, wide = own.shape
-    tile = 256
+    tile = (wide + 128) // 3
     vmem = pl.BlockSpec(memory_space=pltpu.VMEM)
     weights = pl.BlockSpec((depth, tile), lambda n: (0, n))
     return pl.pallas_call(
         both_kernel,
-        grid=(wide // tile,),
-        out_shape=jax.ShapeDtypeStruct((4, TOP, wide), BF),
+        grid=(3,),
+        out_shape=jax.ShapeDtypeStruct((4, TOP, 3 * tile), BF),
         in_specs=[pl.BlockSpec(memory_space=pltpu.SMEM), vmem, weights, weights],
         out_specs=pl.BlockSpec((4, TOP, tile), lambda n: (0, 0, n)),
         cost_estimate=pl.CostEstimate(
@@ -144,36 +165,44 @@
     )(at, x, own, other)
 
 
-def down_kernel(at, x, own, other, out, whole):
-    ci, xi = at[0], at[4]
+def down_kernel(at, near, far, own, other, out, whole, sems):
+    ci, zp, xi = at[0], at[1], at[4]
     height = own.shape[0] // 4
-    rows = x.shape[0]
-    for ref, core in ((own, ci), (other, 1 - ci)):
-        for k in range(4):
-            b = ((xi + 4 - k) & 3) * 2 + core
-            to = pl.ds(pl.multiple_of(b * height, 16), height)
-            whole[to] = ref[k * height : (k + 1) * height]
-    part = dot(x[...], whole[...]).astype(BF)
-    for zh in range(2):
-        for y in range(4):
-            n = (zh * 4 + y) * 128
-            out[y, zh * rows : (zh + 1) * rows] = part[:, n : n + 128]
-
-
-def down_parts(at, x, own, other):
-    rows, depth = x.shape
-    vmem = pl.BlockSpec(memory_space=pltpu.VMEM)
+    half = near.shape[1]
+
+    def place(k, core):
+        b = ((xi + 4 - k) & 3) * 2 + core
+        return pl.ds(pl.multiple_of(b * height, 16), height)
+
+    copies = []
+    for k in range(4):
+        source = other.at[pl.ds(k * height, height)]
+        copies.append(pltpu.make_async_copy(source, whole.at[place(k, 1 - ci)], sems.at[k]))
+        copies[k].start()
+    for k in range(4):
+        whole[place(k, ci)] = own[k * height : (k + 1) * height]
+    for copy in copies:
+        copy.wait()
+    part = dot(near[...], whole[pl.ds(pl.multiple_of(zp * half, 16), half)])
+    part = part + dot(far[...], whole[pl.ds(pl.multiple_of((1 - zp) * half, 16), half)])
+    for n in range(8):
+        out[n] = part[:, n * 128 : (n + 1) * 128].astype(BF)
+
+
+def down_parts(at, near, far, own, other):
+    rows, half = near.shape
+    vmem, hbm = pl.BlockSpec(memory_space=pltpu.VMEM), pl.BlockSpec(memory_space=pltpu.HBM)
     return pl.pallas_call(
         down_kernel,
-        out_shape=jax.ShapeDtypeStruct((4, 2 * rows, 128), BF),
-        in_specs=[pl.BlockSpec(memory_space=pltpu.SMEM), vmem, vmem, vmem],
+        out_shape=jax.ShapeDtypeStruct((8, rows, 128), BF),
+        in_specs=[pl.BlockSpec(memory_space=pltpu.SMEM), vmem, vmem, vmem, hbm],
         out_specs=vmem,
-        scratch_shapes=[pltpu.VMEM((depth, 1024), BF)],
+        scratch_shapes=[pltpu.VMEM((2 * half, 1024), BF), pltpu.SemaphoreType.DMA((4,))],
         cost_estimate=pl.CostEstimate(
-            flops=2 * rows * depth * 1024, bytes_accessed=5 << 20, transcendentals=0
+            flops=4 * rows * half * 1024, bytes_accessed=5 << 20, transcendentals=0
         ),
         name="down_mm",
-    )(at, x, own, other)
+    )(at, near, far, own, other)
 
 
 def exact(value):
@@ -226,28 +255,21 @@
     high = exact(squares)
     tail = jnp.concatenate([high, squares - high, jnp.zeros((4, 128), F32)]).astype(BF)
     model = from_everyone(jnp.concatenate([scaled2, tail]), ("zp", "y"))
-    squares = model[:, 2 * rows : 2 * rows + 4].astype(F32).sum(axis=0)
-    squares = squares[:2] + squares[2:]
-
     parts = exchange(both_parts(at, model, both_own, both_other), "zq")
-    squares = squares + swap(squares, "zq", 1)
-    squares = squares + swap(squares, "zq", 2)
-    start = 40 * zq + 8 * jnp.minimum(zq, 1)
-    squares = lax.dynamic_slice_in_dim(squares.reshape(256), start, TOP, 0)
+    sums = parts.astype(F32).sum(axis=0)
+    squares = sums[:, 2 * ffw] + sums[:, 2 * ffw + 1]
     inverse = lax.rsqrt(squares / D + 1e-05)[:, None]
-    sums = parts.astype(F32).sum(axis=0)
-    gate_sum, up_sum = inverse * sums[:, :ffw], inverse * sums[:, ffw:]
+    gate_sum, up_sum = inverse * sums[:, :ffw], inverse * sums[:, ffw : 2 * ffw]
     hidden = (jax.nn.silu(gate_sum) * up_sum).astype(BF)
     hidden = from_everyone(hidden, "zq")
     hidden = [hidden[q, TOP - (end - begin) :] for q, begin, end in SPANS]
     hidden = jnp.concatenate(hidden)
-    hidden = jnp.concatenate(in_bits(hidden, swap(hidden, "zp", 1), zp), axis=1)
-
-    part = down_parts(at, hidden, down_own, down_other)
-    near = exchange(part, "y").astype(F32).sum(axis=0).reshape(2, rows, 128)
-    far = swap(pick(near, 1 - zh).astype(BF), "zh", 1)
+    facing = swap(hidden, "zp", 1)
+
+    part = down_parts(at, hidden, facing, down_own, down_other)
+    down_sum = exchange(part, ("zh", "y")).astype(F32).sum(axis=0)
     stream = pick(stream2.reshape(2, rows, 128), zh)
-    return (stream + pick(near, zh) + far.astype(F32)).astype(BF)
+    return (stream + down_sum).astype(BF)
 
 
 def solution(mesh):

time: 260 us -> 250 us (0.962)
  the two profiles are of different devices: /device:TPU:2 before, /device:TPU:38 now
where the time goes in v7:
time: 250 us; the launch traced here: 249 us
  starting transfers between devices  107 us (43%)
  waiting for transfers between devices  92.9 us (37%)
  Pallas kernels  17.5 us (7%)
  blocking collectives  16.9 us (7%)
  local copies, waits for them, and re-layouts  9.62 us (4%)
  other arithmetic  4.46 us (2%)
    all_to_all x5, waiting for transfers between devices, exchange(): return lax.all_to_all(parts, axis, split_axis=0, concat_axis=0, tiled=True)  62 us
    ppermute x12, starting transfers between devices, swap(): return lax.ppermute(value, axis, [(i, i ^ bit) for i in range(n)])  57.4 us
    all_to_all x5, starting transfers between devices, exchange(): return lax.all_to_all(parts, axis, split_axis=0, concat_axis=0, tiled=True)  41.1 us
    ppermute x12, waiting for transfers between devices, swap(): return lax.ppermute(value, axis, [(i, i ^ bit) for i in range(n)])  31 us
    all_to_all x1, blocking collectives, exchange(): return lax.all_to_all(parts, axis, split_axis=0, concat_axis=0, tiled=True)  16.9 us
    ppermute x3, starting transfers between devices, shift(): return lax.ppermute(value, axis, [(i, (i + step) % n) for i in range(n)])  8.8 us
    pallas_call x1, Pallas kernels, both_parts(): pl.pallas_call(both_kernel, grid=(3,), out_shape=jax.ShapeDtypeStruct((4,...  6.03 us
    broadcast_in_dim x4, local copies, waits for them, and re-layouts, from_everyone(): copies = jnp.broadcast_to(value, (size_of(axis), *value.shape))  5.13 us
  transfers between devices with their start and end apart: 20, of which 11 were waited for; matrix products, arithmetic and copies ran while one was open for 2% of the time, Pallas kernels for 3%

profile of v7, /device:TPU:38, one launch (start us, length us, event | category | flops | bytes accessed | tf_op | source)
XLA Modules:
  0.0 249.3 jit_solution(16697841560601406284)
XLA Ops:
  0.0 2.1 broadcast_in_dim.40
  2.2 4.8 %all-to-all-start = ((bf16[4,128,1024]{2,1,0:T(8,128)(2,1)}), bf16[4,128,1024]{2,1,0:T(8,128)(2,1)S(1)}, u32[]{:S(2)}, u32[]{:S(2)}) async-start(bf16[4,128,1024]{2,1,0:T(8,128)(2,1)} %broadcast_in_dim.40), calls=%async_computation | async-start | bytes 2097152 | tf_op jit(solution)/shard_map/all_to_all | solution.py:39
  7.1 6.6 %collective-permute-start.8 = (bf16[128,1792]{1,0:T(8,128)(2,1)S(1)}, bf16[128,1792]{1,0:T(8,128)(2,1)S(1)}, u32[]{:S(2)}, u32[]{:S(2)}) collective-permute-start(bf16[128,1792]{1,0:T(8,128)(2,1)S(1)} %pad_maximum_fusion.1), channel_id=1, source_target_pairs={{0,8},{8,0},{1,9},{9,1},{2,10},{10,2},{3,11},{11,3},{4,12},{12,4},... | collective-permute-start | bytes 1376264 | tf_op jit(solution)/shard_map/ppermute | solution.py:31
  13.6 7.0 %collective-permute-done.8 = bf16[128,1792]{1,0:T(8,128)(2,1)S(1)} collective-permute-done((bf16[128,1792]{1,0:T(8,128)(2,1)S(1)}, bf16[128,1792]{1,0:T(8,128)(2,1)S(1)}, u32[]{:S(2)}, u32[]{:S(2)}) %collective-permute-start.8) | collective-permute-done | bytes 458784 | tf_op jit(solution)/shard_map/ppermute | solution.py:31
  20.7 2.1 broadcast_in_dim.44
  22.9 6.1 %all-to-all-start.2 = ((bf16[4,256,1792]{2,1,0:T(8,128)(2,1)}), bf16[4,256,1792]{2,1,0:T(8,128)(2,1)}, u32[]{:S(2)}, u32[]{:S(2)}) async-start(bf16[4,256,1792]{2,1,0:T(8,128)(2,1)} %broadcast_in_dim.44), calls=%async_computation.2 | async-start | bytes 7340032 | tf_op jit(solution)/shard_map/all_to_all | solution.py:39
  29.0 1.9 collective-permute-start.3
  30.9 9.1 %collective-permute-start = (bf16[1,176,128]{2,1,0:T(8,128)(2,1)S(1)}, bf16[1,176,128]{2,1,0:T(8,128)(2,1)S(1)}, u32[]{:S(2)}, u32[]{:S(2)}) collective-permute-start(bf16[1,176,128]{2,1,0:T(8,128)(2,1)S(1)} %bitcast.48), channel_id=1, source_target_pairs={{0,32},{8,40},{16,48},{24,56},{32,0},{40,8},{48,16},{56,24},{1,33}... | collective-permute-start | bytes 135176 | tf_op jit(solution)/shard_map/ppermute | solution.py:31
  40.1 2.3 collective-permute-done
  42.4 6.0 %collective-permute-start.1 = (bf16[2,176,128]{2,1,0:T(8,128)(2,1)S(1)}, bf16[2,176,128]{2,1,0:T(8,128)(2,1)S(1)}, u32[]{:S(2)}, u32[]{:S(2)}) collective-permute-start(bf16[2,176,128]{2,1,0:T(8,128)(2,1)S(1)} %pad_maximum_fusion.6), channel_id=1, source_target_pairs={{0,16},{8,24},{16,0},{24,8},{32,48},{40,56},{48,32},{56,40},{1,17}... | collective-permute-start | bytes 270344 | tf_op jit(solution)/shard_map/ppermute | solution.py:31
  48.5 0.6 stack.49.at
  49.1 2.3 collective-permute-done.1
  51.4 3.2 %collective-permute-start.2 = (bf16[4,176,128]{2,1,0:T(8,128)(2,1)S(1)}, bf16[4,176,128]{2,1,0:T(8,128)(2,1)S(1)}, u32[]{:S(2)}, u32[]{:S(2)}) collective-permute-start(bf16[4,176,128]{2,1,0:T(8,128)(2,1)S(1)} %pad_maximum_fusion.4), channel_id=1, source_target_pairs={{0,8},{8,0},{16,24},{24,16},{32,40},{40,32},{48,56},{56,48},{1,9},... | collective-permute-start | bytes 540680 | tf_op jit(solution)/shard_map/ppermute | solution.py:31
  54.7 5.1 %collective-permute-done.2 = bf16[4,176,128]{2,1,0:T(8,128)(2,1)S(1)} collective-permute-done((bf16[4,176,128]{2,1,0:T(8,128)(2,1)S(1)}, bf16[4,176,128]{2,1,0:T(8,128)(2,1)S(1)}, u32[]{:S(2)}, u32[]{:S(2)}) %collective-permute-start.2) | collective-permute-done | bytes 180256 | tf_op jit(solution)/shard_map/ppermute | solution.py:31
  59.8 0.8 pad_maximum_fusion.2.x
  60.6 1.0 copy-done.3
  61.6 3.9 %proj_mm.1 = (bf16[352,128]{1,0:T(8,128)(2,1)}, bf16[352,128]{1,0:T(8,128)(2,1)}, bf16[352,128]{1,0:T(8,128)(2,1)}, bf16[352,128]{1,0:T(8,128)(2,1)}) custom-call(s32[5]{0:T(128)} %stack.49.at, bf16[8,176,128]{2,1,0:T(8,128)(2,1)} %pad_maximum_fusion.2.x, bf16[512,1024]{1,0:T(8,128)(2,1)} %bitcast.46, bf16[512,1024]{1,0:T(8,128)(2,1)} %copy-done.3), custom_call_target="tpu_custom_call" | custom-call | flops 369098752 | bytes 3145728 | tf_op jit(solution)/shard_map/proj_mm/pallas_call | solution.py:102
  65.5 4.9 %collective-permute-start.6 = (bf16[352,128]{1,0:T(8,128)(2,1)}, bf16[352,128]{1,0:T(8,128)(2,1)S(1)}, u32[]{:S(2)}, u32[]{:S(2)}) collective-permute-start(bf16[352,128]{1,0:T(8,128)(2,1)} %get-tuple-element.12), channel_id=1, source_target_pairs={{0,3},{1,2},{2,1},{3,0},{4,7},{5,6},{6,5},{7,4},{8,11},{9,10},{10,... | collective-permute-start | bytes 270344 | tf_op jit(solution)/shard_map/ppermute | solution.py:31
  70.4 2.5 %collective-permute-start.5 = (bf16[352,128]{1,0:T(8,128)(2,1)}, bf16[352,128]{1,0:T(8,128)(2,1)S(1)}, u32[]{:S(2)}, u32[]{:S(2)}) collective-permute-start(bf16[352,128]{1,0:T(8,128)(2,1)} %get-tuple-element.11), channel_id=1, source_target_pairs={{0,2},{1,3},{2,0},{3,1},{4,6},{5,7},{6,4},{7,5},{8,10},{9,11},{10,... | collective-permute-start | bytes 270344 | tf_op jit(solution)/shard_map/ppermute | solution.py:31
  73.0 2.4 collective-permute-start.4
  75.4 3.8 %collective-permute-done.5 = bf16[352,128]{1,0:T(8,128)(2,1)S(1)} collective-permute-done((bf16[352,128]{1,0:T(8,128)(2,1)}, bf16[352,128]{1,0:T(8,128)(2,1)S(1)}, u32[]{:S(2)}, u32[]{:S(2)}) %collective-permute-start.5) | collective-permute-done | bytes 90144 | tf_op jit(solution)/shard_map/ppermute | solution.py:31
  79.1 0.5 collective-permute-done.4
  79.6 1.0 fusion.20
  80.6 1.9 collective-permute-start.9
  82.6 13.0 %collective-permute-start.7 = (bf16[360,128]{1,0:T(8,128)(2,1)S(1)}, bf16[360,128]{1,0:T(8,128)(2,1)S(1)}, u32[]{:S(2)}, u32[]{:S(2)}) collective-permute-start(bf16[360,128]{1,0:T(8,128)(2,1)S(1)} %pad_maximum_fusion.5), channel_id=1, source_target_pairs={{0,4},{4,0},{1,5},{5,1},{2,6},{6,2},{3,7},{7,3},{8,12},{12,8},{9,1... | collective-permute-start | bytes 276488 | tf_op jit(solution)/shard_map/ppermute | solution.py:31
  95.7 3.4 %collective-permute-done.7 = bf16[360,128]{1,0:T(8,128)(2,1)S(1)} collective-permute-done((bf16[360,128]{1,0:T(8,128)(2,1)S(1)}, bf16[360,128]{1,0:T(8,128)(2,1)S(1)}, u32[]{:S(2)}, u32[]{:S(2)}) %collective-permute-start.7) | collective-permute-done | bytes 92192 | tf_op jit(solution)/shard_map/ppermute | solution.py:31
  99.2 1.0 fusion
  100.7 16.9 %all_to_all.30.x = bf16[8,360,128]{2,1,0:T(8,128)(2,1)} all-to-all(bf16[8,360,128]{2,1,0:T(8,128)(2,1)S(1)} %broadcast_in_dim.43), channel_id=1, replica_groups=mesh['x'=4,'c'=2,'zq'=4,'zp'=2,'zh'=2,'y'=4] {'zp','y'}, dimensions={0} | all-to-all | bytes 1474560 | tf_op jit(solution)/shard_map/all_to_all | solution.py:39
  117.7 6.0 %both_mm.1 = bf16[4,48,1920]{2,1,0:T(8,128)(2,1)} custom-call(s32[5]{0:T(128)} %stack.49.at, bf16[8,360,128]{2,1,0:T(8,128)(2,1)} %all_to_all.30.x, bf16[1024,1792]{1,0:T(8,128)(2,1)} %bitcast.17.own, bf16[1024,1792]{1,0:T(8,128)(2,1)} %collective-permute-done.9.other), custom_call_target="tpu_custom_call" | custom-call | flops 1291845632 | bytes 9437184 | tf_op jit(solution)/shard_map/both_mm/pallas_call | solution.py:155
  123.7 13.1 %all-to-all-start.3 = ((bf16[4,48,1920]{2,1,0:T(8,128)(2,1)}), bf16[4,48,1920]{2,1,0:T(8,128)(2,1)S(1)}, u32[]{:S(2)}, u32[]{:S(2)}) async-start(bf16[4,48,1920]{2,1,0:T(8,128)(2,1)} %both_mm.1), calls=%async_computation.3 | async-start | bytes 1474560 | tf_op jit(solution)/shard_map/all_to_all | solution.py:39
  136.8 2.1 collective-permute-start.11
  138.9 4.8 %collective-permute-start.12 = (bf16[224,1024]{1,0:T(8,128)(2,1)S(1)}, bf16[224,1024]{1,0:T(8,128)(2,1)S(1)}, u32[]{:S(2)}, u32[]{:S(2)}) collective-permute-start(bf16[224,1024]{1,0:T(8,128)(2,1)S(1)} %copy-done.4), channel_id=1, source_target_pairs={{0,256},{128,384},{256,0},{384,128},{1,257},{129,385},{257,1},{385... | collective-permute-start | bytes 1376264 | tf_op jit(solution)/shard_map/ppermute | solution.py:26
  143.7 1.9 collective-permute-start.13
  145.6 24.1 %all-to-all-done.3 = bf16[4,48,1920]{2,1,0:T(8,128)(2,1)S(1)} async-done(((bf16[4,48,1920]{2,1,0:T(8,128)(2,1)}), bf16[4,48,1920]{2,1,0:T(8,128)(2,1)S(1)}, u32[]{:S(2)}, u32[]{:S(2)}) %all-to-all-start.3) | async-done | bytes 737312 | tf_op jit(solution)/shard_map/all_to_all | solution.py:39
  170.1 0.8 broadcast_in_dim.45
  170.9 7.4 %all-to-all-start.4 = ((bf16[4,48,896]{2,1,0:T(8,128)(2,1)}), bf16[4,48,896]{2,1,0:T(8,128)(2,1)S(1)}, u32[]{:S(2)}, u32[]{:S(2)}) async-start(bf16[4,48,896]{2,1,0:T(8,128)(2,1)} %broadcast_in_dim.45), calls=%async_computation.4 | async-start | bytes 688128 | tf_op jit(solution)/shard_map/all_to_all | solution.py:39
  178.4 0.7 copy-done.5
  179.3 0.8 copy-done.7
  180.0 2.8 %stack.57.own = bf16[896,1024]{1,0:T(8,128)(2,1)} custom-call(bf16[224,1024]{1,0:T(8,128)(2,1)} %refs_0_.1, bf16[224,1024]{1,0:T(8,128)(2,1)} %copy-done.5, bf16[224,1024]{1,0:T(8,128)(2,1)} %copy-done.6, bf16[224,1024]{1,0:T(8,128)(2,1)} %copy-done.7), custom_call_target="tpu_custom_call" | custom-call | tf_op jit(solution)/shard_map/stack/pallas_call | solution.py:63
  182.8 1.9 collective-permute-start.14
  184.7 12.8 %all-to-all-done.4 = bf16[4,48,896]{2,1,0:T(8,128)(2,1)S(1)} async-done(((bf16[4,48,896]{2,1,0:T(8,128)(2,1)}), bf16[4,48,896]{2,1,0:T(8,128)(2,1)S(1)}, u32[]{:S(2)}, u32[]{:S(2)}) %all-to-all-start.4) | async-done | bytes 344096 | tf_op jit(solution)/shard_map/all_to_all | solution.py:39
  197.6 4.0 %collective-permute-start.10 = (bf16[176,896]{1,0:T(8,128)(2,1)S(1)}, bf16[176,896]{1,0:T(8,128)(2,1)S(1)}, u32[]{:S(2)}, u32[]{:S(2)}) collective-permute-start(bf16[176,896]{1,0:T(8,128)(2,1)S(1)} %pad_maximum_fusion.3.near), channel_id=1, source_target_pairs={{0,8},{8,0},{1,9},{9,1},{2,10},{10,2},{3,11},{11,3},{4,12},{12,4},... | collective-permute-start | bytes 946184 | tf_op jit(solution)/shard_map/ppermute | solution.py:31
  201.6 6.6 %collective-permute-done.10.far = bf16[176,896]{1,0:T(8,128)(2,1)S(1)} collective-permute-done((bf16[176,896]{1,0:T(8,128)(2,1)S(1)}, bf16[176,896]{1,0:T(8,128)(2,1)S(1)}, u32[]{:S(2)}, u32[]{:S(2)}) %collective-permute-start.10) | collective-permute-done | bytes 315424 | tf_op jit(solution)/shard_map/ppermute | solution.py:31
  208.3 0.7 copy-done.11
  209.0 4.8 %down_mm.1 = bf16[8,176,128]{2,1,0:T(8,128)(2,1)} custom-call(s32[5]{0:T(128)} %stack.49.at, bf16[176,896]{1,0:T(8,128)(2,1)} %copy-done.2, bf16[176,896]{1,0:T(8,128)(2,1)} %copy-done.11, bf16[896,1024]{1,0:T(8,128)(2,1)} %stack.57.own, bf16[896,1024]{1,0:T(8,128)(2,1)} %copy-done.1), custom_call_target="tpu_custom_call" | custom-call | flops 645922816 | bytes 5242880 | tf_op jit(solution)/shard_map/down_mm/pallas_call | solution.py:195
  213.9 9.7 %all-to-all-start.5 = ((bf16[8,176,128]{2,1,0:T(8,128)(2,1)}), bf16[8,176,128]{2,1,0:T(8,128)(2,1)S(1)}, u32[]{:S(2)}, u32[]{:S(2)}) async-start(bf16[8,176,128]{2,1,0:T(8,128)(2,1)} %down_mm.1), calls=%async_computation.5 | async-start | bytes 720896 | tf_op jit(solution)/shard_map/all_to_all | solution.py:39
  223.5 25.0 %all-to-all-done.5 = bf16[8,176,128]{2,1,0:T(8,128)(2,1)S(1)} async-done(((bf16[8,176,128]{2,1,0:T(8,128)(2,1)}), bf16[8,176,128]{2,1,0:T(8,128)(2,1)S(1)}, u32[]{:S(2)}, u32[]{:S(2)}) %all-to-all-start.5) | async-done | bytes 360480 | tf_op jit(solution)/shard_map/all_to_all | solution.py:39
  248.6 0.6 fusion.3
  (64 shorter events, 1.8 us)
Async XLA Ops:
  0.0 6.9 %copy-start.8 = (bf16[128,1792]{1,0:T(8,128)(2,1)S(1)}, bf16[128,1792]{1,0:T(8,128)(2,1)}, u32[]{:S(2)}) copy-start(bf16[128,1792]{1,0:T(8,128)(2,1)} %param.12) | copy-start | bytes 1376260
  0.0 6.9 %copy-start.9 = (bf16[128,1792]{1,0:T(8,128)(2,1)S(1)}, bf16[128,1792]{1,0:T(8,128)(2,1)}, u32[]{:S(2)}) copy-start(bf16[128,1792]{1,0:T(8,128)(2,1)} %param.11) | copy-start | bytes 1376260
  2.2 18.6 %all-to-all-start = ((bf16[4,128,1024]{2,1,0:T(8,128)(2,1)}), bf16[4,128,1024]{2,1,0:T(8,128)(2,1)S(1)}, u32[]{:S(2)}, u32[]{:S(2)}) async-start(bf16[4,128,1024]{2,1,0:T(8,128)(2,1)} %broadcast_in_dim.40), calls=%async_computation | async-start | bytes 2097152 | tf_op jit(solution)/shard_map/all_to_all | solution.py:39
  7.1 13.6 %collective-permute-start.8 = (bf16[128,1792]{1,0:T(8,128)(2,1)S(1)}, bf16[128,1792]{1,0:T(8,128)(2,1)S(1)}, u32[]{:S(2)}, u32[]{:S(2)}) collective-permute-start(bf16[128,1792]{1,0:T(8,128)(2,1)S(1)} %pad_maximum_fusion.1), channel_id=1, source_target_pairs={{0,8},{8,0},{1,9},{9,1},{2,10},{10,2},{3,11},{11,3},{4,12},{12,4},... | collective-permute-start | bytes 1376264 | tf_op jit(solution)/shard_map/ppermute | solution.py:31
  20.7 8.3 %copy-start = (bf16[4,128,1024]{2,1,0:T(8,128)(2,1)}, bf16[4,128,1024]{2,1,0:T(8,128)(2,1)S(1)}, u32[]{:S(2)}) copy-start(bf16[4,128,1024]{2,1,0:T(8,128)(2,1)S(1)} %all-to-all-done) | copy-start | bytes 3145732
  22.9 8.1 %copy-start.10 = (bf16[176,128]{1,0:T(8,128)(2,1)S(1)}, bf16[176,128]{1,0:T(8,128)(2,1)}, u32[]{:S(2)}) copy-start(bf16[176,128]{1,0:T(8,128)(2,1)} %param.7) | copy-start | bytes 135172
  22.9 17.2 %copy-start.12 = (bf16[176,128]{1,0:T(8,128)(2,1)S(1)}, bf16[176,128]{1,0:T(8,128)(2,1)}, u32[]{:S(2)}) copy-start(bf16[176,128]{1,0:T(8,128)(2,1)} %param.8) | copy-start | bytes 135172
  22.9 31.8 %copy-start.13 = (f32[128]{0:T(128)S(1)}, f32[128]{0:T(128)}, u32[]{:S(2)}) copy-start(f32[128]{0:T(128)} %param.10) | copy-start | bytes 1540
  22.9 57.7 %all-to-all-start.2 = ((bf16[4,256,1792]{2,1,0:T(8,128)(2,1)}), bf16[4,256,1792]{2,1,0:T(8,128)(2,1)}, u32[]{:S(2)}, u32[]{:S(2)}) async-start(bf16[4,256,1792]{2,1,0:T(8,128)(2,1)} %broadcast_in_dim.44), calls=%async_computation.2 | async-start | bytes 7340032 | tf_op jit(solution)/shard_map/all_to_all | solution.py:39
  29.0 31.6 %collective-permute-start.3 = (bf16[512,1024]{1,0:T(8,128)(2,1)S(1)}, bf16[512,1024]{1,0:T(8,128)(2,1)S(1)}, u32[]{:S(2)}, u32[]{:S(2)}) collective-permute-start(bf16[512,1024]{1,0:T(8,128)(2,1)S(1)} %bitcast.45), channel_id=1, source_target_pairs={{0,64},{64,0},{1,65},{65,1},{2,66},{66,2},{3,67},{67,3},{4,68},{68... | collective-permute-start | bytes 3145736 | tf_op jit(solution)/shard_map/ppermute | solution.py:31
  30.9 11.4 %collective-permute-start = (bf16[1,176,128]{2,1,0:T(8,128)(2,1)S(1)}, bf16[1,176,128]{2,1,0:T(8,128)(2,1)S(1)}, u32[]{:S(2)}, u32[]{:S(2)}) collective-permute-start(bf16[1,176,128]{2,1,0:T(8,128)(2,1)S(1)} %bitcast.48), channel_id=1, source_target_pairs={{0,32},{8,40},{16,48},{24,56},{32,0},{40,8},{48,16},{56,24},{1,33}... | collective-permute-start | bytes 135176 | tf_op jit(solution)/shard_map/ppermute | solution.py:31
  42.4 9.0 %collective-permute-start.1 = (bf16[2,176,128]{2,1,0:T(8,128)(2,1)S(1)}, bf16[2,176,128]{2,1,0:T(8,128)(2,1)S(1)}, u32[]{:S(2)}, u32[]{:S(2)}) collective-permute-start(bf16[2,176,128]{2,1,0:T(8,128)(2,1)S(1)} %pad_maximum_fusion.6), channel_id=1, source_target_pairs={{0,16},{8,24},{16,0},{24,8},{32,48},{40,56},{48,32},{56,40},{1,17}... | collective-permute-start | bytes 270344 | tf_op jit(solution)/shard_map/ppermute | solution.py:31
  51.4 8.4 %collective-permute-start.2 = (bf16[4,176,128]{2,1,0:T(8,128)(2,1)S(1)}, bf16[4,176,128]{2,1,0:T(8,128)(2,1)S(1)}, u32[]{:S(2)}, u32[]{:S(2)}) collective-permute-start(bf16[4,176,128]{2,1,0:T(8,128)(2,1)S(1)} %pad_maximum_fusion.4), channel_id=1, source_target_pairs={{0,8},{8,0},{16,24},{24,16},{32,40},{40,32},{48,56},{56,48},{1,9},... | collective-permute-start | bytes 540680 | tf_op jit(solution)/shard_map/ppermute | solution.py:31
  60.6 1.1 copy-start.3
  65.5 9.9 %collective-permute-start.6 = (bf16[352,128]{1,0:T(8,128)(2,1)}, bf16[352,128]{1,0:T(8,128)(2,1)S(1)}, u32[]{:S(2)}, u32[]{:S(2)}) collective-permute-start(bf16[352,128]{1,0:T(8,128)(2,1)} %get-tuple-element.12), channel_id=1, source_target_pairs={{0,3},{1,2},{2,1},{3,0},{4,7},{5,6},{6,5},{7,4},{8,11},{9,10},{10,... | collective-permute-start | bytes 270344 | tf_op jit(solution)/shard_map/ppermute | solution.py:31
  70.4 8.7 %collective-permute-start.5 = (bf16[352,128]{1,0:T(8,128)(2,1)}, bf16[352,128]{1,0:T(8,128)(2,1)S(1)}, u32[]{:S(2)}, u32[]{:S(2)}) collective-permute-start(bf16[352,128]{1,0:T(8,128)(2,1)} %get-tuple-element.11), channel_id=1, source_target_pairs={{0,2},{1,3},{2,0},{3,1},{4,6},{5,7},{6,4},{7,5},{8,10},{9,11},{10,... | collective-permute-start | bytes 270344 | tf_op jit(solution)/shard_map/ppermute | solution.py:31
  73.0 6.6 %collective-permute-start.4 = (bf16[352,128]{1,0:T(8,128)(2,1)}, bf16[352,128]{1,0:T(8,128)(2,1)S(1)}, u32[]{:S(2)}, u32[]{:S(2)}) collective-permute-start(bf16[352,128]{1,0:T(8,128)(2,1)} %get-tuple-element.10), channel_id=1, source_target_pairs={{0,1},{1,0},{2,3},{3,2},{4,5},{5,4},{6,7},{7,6},{8,9},{9,8},{10,11... | collective-permute-start | bytes 270344 | tf_op jit(solution)/shard_map/ppermute | solution.py:31
  80.6 37.0 %collective-permute-start.9 = (bf16[1024,1792]{1,0:T(8,128)(2,1)}, bf16[1024,1792]{1,0:T(8,128)(2,1)}, u32[]{:S(2)}, u32[]{:S(2)}) collective-permute-start(bf16[1024,1792]{1,0:T(8,128)(2,1)} %bitcast.17.own), channel_id=1, source_target_pairs={{0,64},{64,0},{1,65},{65,1},{2,66},{66,2},{3,67},{67,3},{4,68},{68... | collective-permute-start | bytes 11010056 | tf_op jit(solution)/shard_map/ppermute | solution.py:31
  82.6 16.5 %collective-permute-start.7 = (bf16[360,128]{1,0:T(8,128)(2,1)S(1)}, bf16[360,128]{1,0:T(8,128)(2,1)S(1)}, u32[]{:S(2)}, u32[]{:S(2)}) collective-permute-start(bf16[360,128]{1,0:T(8,128)(2,1)S(1)} %pad_maximum_fusion.5), channel_id=1, source_target_pairs={{0,4},{4,0},{1,5},{5,1},{2,6},{6,2},{3,7},{7,3},{8,12},{12,8},{9,1... | collective-permute-start | bytes 276488 | tf_op jit(solution)/shard_map/ppermute | solution.py:31
  117.6 19.1 %copy-start.4 = (bf16[224,1024]{1,0:T(8,128)(2,1)S(1)}, bf16[224,1024]{1,0:T(8,128)(2,1)}, u32[]{:S(2)}) copy-start(bf16[224,1024]{1,0:T(8,128)(2,1)} %refs_0_.1) | copy-start | bytes 1376260
  123.7 46.0 %all-to-all-start.3 = ((bf16[4,48,1920]{2,1,0:T(8,128)(2,1)}), bf16[4,48,1920]{2,1,0:T(8,128)(2,1)S(1)}, u32[]{:S(2)}, u32[]{:S(2)}) async-start(bf16[4,48,1920]{2,1,0:T(8,128)(2,1)} %both_mm.1), calls=%async_computation.3 | async-start | bytes 1474560 | tf_op jit(solution)/shard_map/all_to_all | solution.py:39
  136.8 41.5 %collective-permute-start.11 = (bf16[224,1024]{1,0:T(8,128)(2,1)S(1)}, bf16[224,1024]{1,0:T(8,128)(2,1)S(1)}, u32[]{:S(2)}, u32[]{:S(2)}) collective-permute-start(bf16[224,1024]{1,0:T(8,128)(2,1)S(1)} %copy-done.4), channel_id=1, source_target_pairs={{0,128},{128,256},{256,384},{384,0},{1,129},{129,257},{257,385},{3... | collective-permute-start | bytes 1376264 | tf_op jit(solution)/shard_map/ppermute | solution.py:26
  138.9 39.4 %collective-permute-start.12 = (bf16[224,1024]{1,0:T(8,128)(2,1)S(1)}, bf16[224,1024]{1,0:T(8,128)(2,1)S(1)}, u32[]{:S(2)}, u32[]{:S(2)}) collective-permute-start(bf16[224,1024]{1,0:T(8,128)(2,1)S(1)} %copy-done.4), channel_id=1, source_target_pairs={{0,256},{128,384},{256,0},{384,128},{1,257},{129,385},{257,1},{385... | collective-permute-start | bytes 1376264 | tf_op jit(solution)/shard_map/ppermute | solution.py:26
  143.7 34.7 %collective-permute-start.13 = (bf16[224,1024]{1,0:T(8,128)(2,1)S(1)}, bf16[224,1024]{1,0:T(8,128)(2,1)S(1)}, u32[]{:S(2)}, u32[]{:S(2)}) collective-permute-start(bf16[224,1024]{1,0:T(8,128)(2,1)S(1)} %copy-done.4), channel_id=1, source_target_pairs={{0,384},{128,0},{256,128},{384,256},{1,385},{129,1},{257,129},{385... | collective-permute-start | bytes 1376264 | tf_op jit(solution)/shard_map/ppermute | solution.py:26
  170.9 26.6 %all-to-all-start.4 = ((bf16[4,48,896]{2,1,0:T(8,128)(2,1)}), bf16[4,48,896]{2,1,0:T(8,128)(2,1)S(1)}, u32[]{:S(2)}, u32[]{:S(2)}) async-start(bf16[4,48,896]{2,1,0:T(8,128)(2,1)} %broadcast_in_dim.45), calls=%async_computation.4 | async-start | bytes 688128 | tf_op jit(solution)/shard_map/all_to_all | solution.py:39
  178.3 0.8 copy-start.5
  178.3 0.9 copy-start.6
  179.3 0.8 copy-start.7
  182.8 18.8 %collective-permute-start.14 = (bf16[896,1024]{1,0:T(8,128)(2,1)}, bf16[896,1024]{1,0:T(8,128)(2,1)S(1)}, u32[]{:S(2)}, u32[]{:S(2)}) collective-permute-start(bf16[896,1024]{1,0:T(8,128)(2,1)} %stack.57.own), channel_id=1, source_target_pairs={{0,64},{64,0},{1,65},{65,1},{2,66},{66,2},{3,67},{67,3},{4,68},{68... | collective-permute-start | bytes 5505032 | tf_op jit(solution)/shard_map/ppermute | solution.py:31
  197.6 10.7 %copy-start.2 = (bf16[176,896]{1,0:T(8,128)(2,1)}, bf16[176,896]{1,0:T(8,128)(2,1)S(1)}, u32[]{:S(2)}) copy-start(bf16[176,896]{1,0:T(8,128)(2,1)S(1)} %pad_maximum_fusion.3.near) | copy-start | bytes 946180
  197.6 10.6 %collective-permute-start.10 = (bf16[176,896]{1,0:T(8,128)(2,1)S(1)}, bf16[176,896]{1,0:T(8,128)(2,1)S(1)}, u32[]{:S(2)}, u32[]{:S(2)}) collective-permute-start(bf16[176,896]{1,0:T(8,128)(2,1)S(1)} %pad_maximum_fusion.3.near), channel_id=1, source_target_pairs={{0,8},{8,0},{1,9},{9,1},{2,10},{10,2},{3,11},{11,3},{4,12},{12,4},... | collective-permute-start | bytes 946184 | tf_op jit(solution)/shard_map/ppermute | solution.py:31
  201.6 6.6 %copy-start.1 = (bf16[896,1024]{1,0:T(8,128)(2,1)}, bf16[896,1024]{1,0:T(8,128)(2,1)S(1)}, u32[]{:S(2)}) copy-start(bf16[896,1024]{1,0:T(8,128)(2,1)S(1)} %collective-permute-done.14.other) | copy-start | bytes 5505028
  208.3 0.7 copy-start.11
  213.9 34.7 %all-to-all-start.5 = ((bf16[8,176,128]{2,1,0:T(8,128)(2,1)}), bf16[8,176,128]{2,1,0:T(8,128)(2,1)S(1)}, u32[]{:S(2)}, u32[]{:S(2)}) async-start(bf16[8,176,128]{2,1,0:T(8,128)(2,1)} %down_mm.1), calls=%async_computation.5 | async-start | bytes 720896 | tf_op jit(solution)/shard_map/all_to_all | solution.py:39

commit v8 on v6

--- a/solution.py
+++ b/solution.py
@@ -13,8 +13,6 @@
 AXES = ("x", "c", "zq", "zp", "zh", "y")
 ZL = ("zq", "zp")
 TOP = 48
-STARTS_OF = (0, 48, 88, 128)
-SPANS = ((0, 0, 48), (1, 48, 96), (2, 96, 136), (3, 136, 176))
 
 
 def size_of(axis):
@@ -109,8 +107,8 @@
     )(at, x, own, other)
 
 
-def both_kernel(at, x, own, other, out):
-    ci, zp = at[0], at[1]
+def both_kernel(at, x, own, other, send, keep):
+    ci, zp, bit = at[0], at[1], (at[2] >> 1) & 1
     rows = (x.shape[1] - 8) // 2
 
     def blocks(core):
@@ -121,59 +119,86 @@
                 parts.append(x[at_block, pl.ds((k // 2) * rows, rows)])
         return jnp.concatenate(parts, axis=1)
 
-    part = (dot(blocks(ci), own[...]) + dot(blocks(1 - ci), other[...])).astype(BF)
-    for q in range(4):
-        out[q] = part[STARTS_OF[q] : STARTS_OF[q] + TOP]
-
-
-def both_parts(at, x, own, other):
+    part = dot(blocks(ci), own[...]) + dot(blocks(1 - ci), other[...])
+    upper, lower = part[: rows // 2], part[rows // 2 :]
+    send[...] = jnp.where(bit == 0, lower, upper).astype(BF)
+    keep[...] = jnp.where(bit == 0, upper, lower)
+
+
+def both_parts(at, x, own, other, half):
     depth, wide = own.shape
-    tile = 256
+    tile = wide // 2
     vmem = pl.BlockSpec(memory_space=pltpu.VMEM)
     weights = pl.BlockSpec((depth, tile), lambda n: (0, n))
+    result = pl.BlockSpec((half, tile), lambda n: (0, n))
     return pl.pallas_call(
         both_kernel,
-        grid=(wide // tile,),
-        out_shape=jax.ShapeDtypeStruct((4, TOP, wide), BF),
+        grid=(2,),
+        out_shape=[jax.ShapeDtypeStruct((half, wide), kind) for kind in (BF, F32)],
         in_specs=[pl.BlockSpec(memory_space=pltpu.SMEM), vmem, weights, weights],
-        out_specs=pl.BlockSpec((4, TOP, tile), lambda n: (0, 0, n)),
+        out_specs=[result, result],
         cost_estimate=pl.CostEstimate(
-            flops=4 * 176 * depth * wide, bytes_accessed=9 << 20, transcendentals=0
+            flops=8 * half * depth * wide, bytes_accessed=9 << 20, transcendentals=0
         ),
         name="both_mm",
     )(at, x, own, other)
 
 
-def down_kernel(at, x, own, other, out, whole):
-    ci, xi = at[0], at[4]
+def near_kernel(at, x, own, other, part, rest, whole):
+    ci, zp, xi = at[0], at[1], at[4]
     height = own.shape[0] // 4
-    rows = x.shape[0]
+    half = x.shape[1]
     for ref, core in ((own, ci), (other, 1 - ci)):
         for k in range(4):
             b = ((xi + 4 - k) & 3) * 2 + core
             to = pl.ds(pl.multiple_of(b * height, 16), height)
             whole[to] = ref[k * height : (k + 1) * height]
-    part = dot(x[...], whole[...]).astype(BF)
+    part[...] = dot(x[...], whole[pl.ds(pl.multiple_of(zp * half, 16), half)])
+    rest[...] = whole[pl.ds(pl.multiple_of((1 - zp) * half, 16), half)]
+
+
+def far_kernel(x, part, rest, out):
+    rows = x.shape[0]
+    total = (part[...] + dot(x[...], rest[...])).astype(BF)
     for zh in range(2):
         for y in range(4):
             n = (zh * 4 + y) * 128
-            out[y, zh * rows : (zh + 1) * rows] = part[:, n : n + 128]
-
-
-def down_parts(at, x, own, other):
-    rows, depth = x.shape
-    vmem = pl.BlockSpec(memory_space=pltpu.VMEM)
-    return pl.pallas_call(
-        down_kernel,
+            out[y, zh * rows : (zh + 1) * rows] = total[:, n : n + 128]
+
+
+def near_part(at, x, own, other):
+    rows, half = x.shape
+    wide = own.shape[1]
+    vmem = pl.BlockSpec(memory_space=pltpu.VMEM)
+    return pl.pallas_call(
+        near_kernel,
+        out_shape=(
+            jax.ShapeDtypeStruct((rows, wide), F32),
+            jax.ShapeDtypeStruct((half, wide), BF),
+        ),
+        in_specs=[pl.BlockSpec(memory_space=pltpu.SMEM), vmem, vmem, vmem],
+        out_specs=(vmem, vmem),
+        scratch_shapes=[pltpu.VMEM((2 * half, wide), BF)],
+        cost_estimate=pl.CostEstimate(
+            flops=2 * rows * half * wide, bytes_accessed=5 << 20, transcendentals=0
+        ),
+        name="near_mm",
+    )(at, x, own, other)
+
+
+def down_parts(x, part, rest):
+    rows, half = x.shape
+    vmem = pl.BlockSpec(memory_space=pltpu.VMEM)
+    return pl.pallas_call(
+        far_kernel,
         out_shape=jax.ShapeDtypeStruct((4, 2 * rows, 128), BF),
-        in_specs=[pl.BlockSpec(memory_space=pltpu.SMEM), vmem, vmem, vmem],
+        in_specs=[vmem, vmem, vmem],
         out_specs=vmem,
-        scratch_shapes=[pltpu.VMEM((depth, 1024), BF)],
         cost_estimate=pl.CostEstimate(
-            flops=2 * rows * depth * 1024, bytes_accessed=5 << 20, transcendentals=0
-        ),
-        name="down_mm",
-    )(at, x, own, other)
+            flops=2 * rows * half * 1024, bytes_accessed=3 << 20, transcendentals=0
+        ),
+        name="far_mm",
+    )(x, part, rest)
 
 
 def exact(value):
@@ -229,21 +254,28 @@
     squares = model[:, 2 * rows : 2 * rows + 4].astype(F32).sum(axis=0)
     squares = squares[:2] + squares[2:]
 
-    parts = exchange(both_parts(at, model, both_own, both_other), "zq")
+    half, step = rows // 2, rows // 2 - TOP
+    bit1, bit2 = zq & 1, zq >> 1
+    send, keep = both_parts(at, model, both_own, both_other, half)
+    got = swap(send, "zq", 1)
     squares = squares + swap(squares, "zq", 1)
+    sums = keep + got.astype(F32)
+    sent = lax.dynamic_slice_in_dim(sums, step * (1 - bit2), TOP, 0).astype(BF)
+    got = swap(sent, "zq", 2)
     squares = squares + swap(squares, "zq", 2)
-    start = 40 * zq + 8 * jnp.minimum(zq, 1)
-    squares = lax.dynamic_slice_in_dim(squares.reshape(256), start, TOP, 0)
+    sums = lax.dynamic_slice_in_dim(sums, step * bit2, TOP, 0) + got.astype(F32)
+    squares = lax.dynamic_slice_in_dim(squares.reshape(256), half * bit1 + step * bit2, TOP, 0)
     inverse = lax.rsqrt(squares / D + 1e-05)[:, None]
-    sums = parts.astype(F32).sum(axis=0)
     gate_sum, up_sum = inverse * sums[:, :ffw], inverse * sums[:, ffw:]
     hidden = (jax.nn.silu(gate_sum) * up_sum).astype(BF)
-    hidden = from_everyone(hidden, "zq")
-    hidden = [hidden[q, TOP - (end - begin) :] for q, begin, end in SPANS]
-    hidden = jnp.concatenate(hidden)
-    hidden = jnp.concatenate(in_bits(hidden, swap(hidden, "zp", 1), zp), axis=1)
-
-    part = down_parts(at, hidden, down_own, down_other)
+    upper, lower = in_bits(hidden, swap(hidden, "zq", 2), bit2)
+    hidden = jnp.concatenate([upper, lower[2 * TOP - half :]])
+    hidden = jnp.concatenate(in_bits(hidden, swap(hidden, "zq", 1), bit1))
+    hidden, down_other = lax.optimization_barrier((hidden, down_other))
+    facing = swap(hidden, "zp", 1)
+
+    part, rest = near_part(at, hidden, down_own, down_other)
+    part = down_parts(facing, part, rest)
     near = exchange(part, "y").astype(F32).sum(axis=0).reshape(2, rows, 128)
     far = swap(pick(near, 1 - zh).astype(BF), "zh", 1)
     stream = pick(stream2.reshape(2, rows, 128), zh)

time: 260 us -> 236 us (0.908)
  the two profiles are of different devices: /device:TPU:2 before, /device:TPU:8 now
where the time goes in v8:
time: 236 us; the launch traced here: 235 us
  starting transfers between devices  110 us (47%)
  waiting for transfers between devices  90.7 us (38%)
  Pallas kernels  18.4 us (8%)
  local copies, waits for them, and re-layouts  9.9 us (4%)
  other arithmetic  5.6 us (2%)
    ppermute x19, waiting for transfers between devices, swap(): return lax.ppermute(value, axis, [(i, i ^ bit) for i in range(n)])  82.9 us
    ppermute x19, starting transfers between devices, swap(): return lax.ppermute(value, axis, [(i, i ^ bit) for i in range(n)])  78.9 us
    all_to_all x4, starting transfers between devices, exchange(): return lax.all_to_all(parts, axis, split_axis=0, concat_axis=0, tiled=True)  19.6 us
    ppermute x3, starting transfers between devices, shift(): return lax.ppermute(value, axis, [(i, (i + step) % n) for i in range(n)])  11.3 us
    all_to_all x4, waiting for transfers between devices, exchange(): return lax.all_to_all(parts, axis, split_axis=0, concat_axis=0, tiled=True)  6.58 us
    broadcast_in_dim x3, local copies, waits for them, and re-layouts, from_everyone(): copies = jnp.broadcast_to(value, (size_of(axis), *value.shape))  5.29 us
    pallas_call x1, Pallas kernels, both_parts(): pl.pallas_call(both_kernel, grid=(2,), out_shape=[jax.ShapeDtypeStruct((h...  5.12 us
  transfers between devices with their start and end apart: 26, of which 16 were waited for; matrix products, arithmetic and copies ran while one was open for 3% of the time, Pallas kernels for 7%

profile of v8, /device:TPU:8, one launch (start us, length us, event | category | flops | bytes accessed | tf_op | source)
XLA Modules:
  0.0 235.0 jit_solution(9403721742505783857)
XLA Ops:
  0.0 2.1 broadcast_in_dim.37
  2.1 4.3 %all-to-all-start = ((bf16[4,128,1024]{2,1,0:T(8,128)(2,1)}), bf16[4,128,1024]{2,1,0:T(8,128)(2,1)S(1)}, u32[]{:S(2)}, u32[]{:S(2)}) async-start(bf16[4,128,1024]{2,1,0:T(8,128)(2,1)} %broadcast_in_dim.37), calls=%async_computation | async-start | bytes 2097152 | tf_op jit(solution)/shard_map/all_to_all | solution.py:37
  6.6 3.8 %collective-permute-start.10 = (bf16[128,1792]{1,0:T(8,128)(2,1)S(1)}, bf16[128,1792]{1,0:T(8,128)(2,1)S(1)}, u32[]{:S(2)}, u32[]{:S(2)}) collective-permute-start(bf16[128,1792]{1,0:T(8,128)(2,1)S(1)} %pad_maximum_fusion.1), channel_id=1, source_target_pairs={{0,8},{8,0},{1,9},{9,1},{2,10},{10,2},{3,11},{11,3},{4,12},{12,4},... | collective-permute-start | bytes 1376264 | tf_op jit(solution)/shard_map/ppermute | solution.py:29
  10.4 10.2 %collective-permute-done.10 = bf16[128,1792]{1,0:T(8,128)(2,1)S(1)} collective-permute-done((bf16[128,1792]{1,0:T(8,128)(2,1)S(1)}, bf16[128,1792]{1,0:T(8,128)(2,1)S(1)}, u32[]{:S(2)}, u32[]{:S(2)}) %collective-permute-start.10) | collective-permute-done | bytes 458784 | tf_op jit(solution)/shard_map/ppermute | solution.py:29
  21.5 2.1 broadcast_in_dim.41
  23.6 4.9 %all-to-all-start.2 = ((bf16[4,256,1792]{2,1,0:T(8,128)(2,1)}), bf16[4,256,1792]{2,1,0:T(8,128)(2,1)}, u32[]{:S(2)}, u32[]{:S(2)}) async-start(bf16[4,256,1792]{2,1,0:T(8,128)(2,1)} %broadcast_in_dim.41), calls=%async_computation.2 | async-start | bytes 7340032 | tf_op jit(solution)/shard_map/all_to_all | solution.py:37
  28.5 1.9 collective-permute-start.3
  30.5 9.1 %collective-permute-start = (bf16[1,176,128]{2,1,0:T(8,128)(2,1)S(1)}, bf16[1,176,128]{2,1,0:T(8,128)(2,1)S(1)}, u32[]{:S(2)}, u32[]{:S(2)}) collective-permute-start(bf16[1,176,128]{2,1,0:T(8,128)(2,1)S(1)} %bitcast.47), channel_id=1, source_target_pairs={{0,32},{8,40},{16,48},{24,56},{32,0},{40,8},{48,16},{56,24},{1,33}... | collective-permute-start | bytes 135176 | tf_op jit(solution)/shard_map/ppermute | solution.py:29
  39.6 2.3 collective-permute-done
  41.9 5.5 %collective-permute-start.1 = (bf16[2,176,128]{2,1,0:T(8,128)(2,1)S(1)}, bf16[2,176,128]{2,1,0:T(8,128)(2,1)S(1)}, u32[]{:S(2)}, u32[]{:S(2)}) collective-permute-start(bf16[2,176,128]{2,1,0:T(8,128)(2,1)S(1)} %pad_maximum_fusion.7), channel_id=1, source_target_pairs={{0,16},{8,24},{16,0},{24,8},{32,48},{40,56},{48,32},{56,40},{1,17}... | collective-permute-start | bytes 270344 | tf_op jit(solution)/shard_map/ppermute | solution.py:29
  48.2 3.9 %collective-permute-done.1 = bf16[2,176,128]{2,1,0:T(8,128)(2,1)S(1)} collective-permute-done((bf16[2,176,128]{2,1,0:T(8,128)(2,1)S(1)}, bf16[2,176,128]{2,1,0:T(8,128)(2,1)S(1)}, u32[]{:S(2)}, u32[]{:S(2)}) %collective-permute-start.1) | collective-permute-done | bytes 90144 | tf_op jit(solution)/shard_map/ppermute | solution.py:29
  52.2 2.6 %collective-permute-start.2 = (bf16[4,176,128]{2,1,0:T(8,128)(2,1)S(1)}, bf16[4,176,128]{2,1,0:T(8,128)(2,1)S(1)}, u32[]{:S(2)}, u32[]{:S(2)}) collective-permute-start(bf16[4,176,128]{2,1,0:T(8,128)(2,1)S(1)} %pad_maximum_fusion.4), channel_id=1, source_target_pairs={{0,8},{8,0},{16,24},{24,16},{32,40},{40,32},{48,56},{56,48},{1,9},... | collective-permute-start | bytes 540680 | tf_op jit(solution)/shard_map/ppermute | solution.py:29
  54.8 4.7 %collective-permute-done.2 = bf16[4,176,128]{2,1,0:T(8,128)(2,1)S(1)} collective-permute-done((bf16[4,176,128]{2,1,0:T(8,128)(2,1)S(1)}, bf16[4,176,128]{2,1,0:T(8,128)(2,1)S(1)}, u32[]{:S(2)}, u32[]{:S(2)}) %collective-permute-start.2) | collective-permute-done | bytes 180256 | tf_op jit(solution)/shard_map/ppermute | solution.py:29
  61.3 3.0 %proj_mm.1 = (bf16[352,128]{1,0:T(8,128)(2,1)}, bf16[352,128]{1,0:T(8,128)(2,1)}, bf16[352,128]{1,0:T(8,128)(2,1)}, bf16[352,128]{1,0:T(8,128)(2,1)}) custom-call(s32[5]{0:T(128)} %stack.49.at, bf16[8,176,128]{2,1,0:T(8,128)(2,1)} %pad_maximum_fusion.2.x, bf16[512,1024]{1,0:T(8,128)(2,1)} %bitcast.43, bf16[512,1024]{1,0:T(8,128)(2,1)} %copy-done.4), custom_call_target="tpu_custom_call" | custom-call | flops 369098752 | bytes 3145728 | tf_op jit(solution)/shard_map/proj_mm/pallas_call | solution.py:97
  64.3 3.5 %collective-permute-start.6 = (bf16[352,128]{1,0:T(8,128)(2,1)}, bf16[352,128]{1,0:T(8,128)(2,1)S(1)}, u32[]{:S(2)}, u32[]{:S(2)}) collective-permute-start(bf16[352,128]{1,0:T(8,128)(2,1)} %get-tuple-element.18), channel_id=1, source_target_pairs={{0,3},{1,2},{2,1},{3,0},{4,7},{5,6},{6,5},{7,4},{8,11},{9,10},{10,... | collective-permute-start | bytes 270344 | tf_op jit(solution)/shard_map/ppermute | solution.py:29
  67.8 2.9 %collective-permute-start.5 = (bf16[352,128]{1,0:T(8,128)(2,1)}, bf16[352,128]{1,0:T(8,128)(2,1)S(1)}, u32[]{:S(2)}, u32[]{:S(2)}) collective-permute-start(bf16[352,128]{1,0:T(8,128)(2,1)} %get-tuple-element.17), channel_id=1, source_target_pairs={{0,2},{1,3},{2,0},{3,1},{4,6},{5,7},{6,4},{7,5},{8,10},{9,11},{10,... | collective-permute-start | bytes 270344 | tf_op jit(solution)/shard_map/ppermute | solution.py:29
  70.7 3.5 %collective-permute-start.4 = (bf16[352,128]{1,0:T(8,128)(2,1)}, bf16[352,128]{1,0:T(8,128)(2,1)S(1)}, u32[]{:S(2)}, u32[]{:S(2)}) collective-permute-start(bf16[352,128]{1,0:T(8,128)(2,1)} %get-tuple-element.16), channel_id=1, source_target_pairs={{0,1},{1,0},{2,3},{3,2},{4,5},{5,4},{6,7},{7,6},{8,9},{9,8},{10,11... | collective-permute-start | bytes 270344 | tf_op jit(solution)/shard_map/ppermute | solution.py:29
  74.2 2.6 %collective-permute-done.5 = bf16[352,128]{1,0:T(8,128)(2,1)S(1)} collective-permute-done((bf16[352,128]{1,0:T(8,128)(2,1)}, bf16[352,128]{1,0:T(8,128)(2,1)S(1)}, u32[]{:S(2)}, u32[]{:S(2)}) %collective-permute-start.5) | collective-permute-done | bytes 90144 | tf_op jit(solution)/shard_map/ppermute | solution.py:29
  78.3 14.7 %collective-permute-start.7 = (bf16[360,128]{1,0:T(8,128)(2,1)S(1)}, bf16[360,128]{1,0:T(8,128)(2,1)S(1)}, u32[]{:S(2)}, u32[]{:S(2)}) collective-permute-start(bf16[360,128]{1,0:T(8,128)(2,1)S(1)} %pad_maximum_fusion.6), channel_id=1, source_target_pairs={{0,4},{4,0},{1,5},{5,1},{2,6},{6,2},{3,7},{7,3},{8,12},{12,8},{9,1... | collective-permute-start | bytes 276488 | tf_op jit(solution)/shard_map/ppermute | solution.py:29
  93.1 1.9 collective-permute-start.11
  95.1 2.5 %collective-permute-done.7 = bf16[360,128]{1,0:T(8,128)(2,1)S(1)} collective-permute-done((bf16[360,128]{1,0:T(8,128)(2,1)S(1)}, bf16[360,128]{1,0:T(8,128)(2,1)S(1)}, u32[]{:S(2)}, u32[]{:S(2)}) %collective-permute-start.7) | collective-permute-done | bytes 92192 | tf_op jit(solution)/shard_map/ppermute | solution.py:29
  97.7 1.1 fusion
  100.2 5.6 %all-to-all-start.1 = ((bf16[8,360,128]{2,1,0:T(8,128)(2,1)}), bf16[8,360,128]{2,1,0:T(8,128)(2,1)S(1)}, u32[]{:S(2)}, u32[]{:S(2)}) async-start(bf16[8,360,128]{2,1,0:T(8,128)(2,1)} %broadcast_in_dim.40), calls=%async_computation.1 | async-start | bytes 1474560 | tf_op jit(solution)/shard_map/all_to_all | solution.py:37
  105.8 3.3 %collective-permute-start.16 = (bf16[224,1024]{1,0:T(8,128)(2,1)S(1)}, bf16[224,1024]{1,0:T(8,128)(2,1)S(1)}, u32[]{:S(2)}, u32[]{:S(2)}) collective-permute-start(bf16[224,1024]{1,0:T(8,128)(2,1)S(1)} %copy-done.6), channel_id=1, source_target_pairs={{0,128},{128,256},{256,384},{384,0},{1,129},{129,257},{257,385},{3... | collective-permute-start | bytes 1376264 | tf_op jit(solution)/shard_map/ppermute | solution.py:24
  109.1 5.1 %collective-permute-start.17 = (bf16[224,1024]{1,0:T(8,128)(2,1)S(1)}, bf16[224,1024]{1,0:T(8,128)(2,1)S(1)}, u32[]{:S(2)}, u32[]{:S(2)}) collective-permute-start(bf16[224,1024]{1,0:T(8,128)(2,1)S(1)} %copy-done.6), channel_id=1, source_target_pairs={{0,256},{128,384},{256,0},{384,128},{1,257},{129,385},{257,1},{385... | collective-permute-start | bytes 1376264 | tf_op jit(solution)/shard_map/ppermute | solution.py:24
  114.2 2.9 %collective-permute-start.18 = (bf16[224,1024]{1,0:T(8,128)(2,1)S(1)}, bf16[224,1024]{1,0:T(8,128)(2,1)S(1)}, u32[]{:S(2)}, u32[]{:S(2)}) collective-permute-start(bf16[224,1024]{1,0:T(8,128)(2,1)S(1)} %copy-done.6), channel_id=1, source_target_pairs={{0,384},{128,0},{256,128},{384,256},{1,385},{129,1},{257,129},{385... | collective-permute-start | bytes 1376264 | tf_op jit(solution)/shard_map/ppermute | solution.py:24
  118.1 5.1 %both_mm.1 = (bf16[88,1792]{1,0:T(8,128)(2,1)}, f32[88,1792]{1,0:T(8,128)}) custom-call(s32[5]{0:T(128)} %stack.49.at, bf16[8,360,128]{2,1,0:T(8,128)(2,1)} %copy-done.1, bf16[1024,1792]{1,0:T(8,128)(2,1)} %bitcast.17.own, bf16[1024,1792]{1,0:T(8,128)(2,1)} %collective-permute-done.11.other), custom_call_target="tpu_custom_call" | custom-call | flops 1291845632 | bytes 9437184 | tf_op jit(solution)/shard_map/both_mm/pallas_call | solution.py:134
  123.2 5.0 %collective-permute-start.12 = (bf16[88,1792]{1,0:T(8,128)(2,1)}, bf16[88,1792]{1,0:T(8,128)(2,1)}, u32[]{:S(2)}, u32[]{:S(2)}) collective-permute-start(bf16[88,1792]{1,0:T(8,128)(2,1)} %get-tuple-element.20), channel_id=1, source_target_pairs={{0,16},{16,0},{32,48},{48,32},{1,17},{17,1},{33,49},{49,33},{2,18}... | collective-permute-start | bytes 946184 | tf_op jit(solution)/shard_map/ppermute | solution.py:29
  128.3 1.9 collective-permute-start.8
  130.2 1.2 collective-permute-done.18.refs_3_
  132.2 2.8 %stack.57.own = bf16[896,1024]{1,0:T(8,128)(2,1)} custom-call(bf16[224,1024]{1,0:T(8,128)(2,1)} %refs_0_.1, bf16[224,1024]{1,0:T(8,128)(2,1)} %copy-done.7, bf16[224,1024]{1,0:T(8,128)(2,1)} %copy-done.8, bf16[224,1024]{1,0:T(8,128)(2,1)} %copy-done.9), custom_call_target="tpu_custom_call" | custom-call | tf_op jit(solution)/shard_map/stack/pallas_call | solution.py:61
  135.0 1.9 collective-permute-start.19
  137.0 2.7 %collective-permute-done.8 = f32[2,128]{1,0:T(2,128)S(1)} collective-permute-done((f32[2,128]{1,0:T(2,128)S(1)}, f32[2,128]{1,0:T(2,128)S(1)}, u32[]{:S(2)}, u32[]{:S(2)}) %collective-permute-start.8) | collective-permute-done | bytes 1056 | tf_op jit(solution)/shard_map/ppermute | solution.py:29
  139.7 7.1 %collective-permute-start.9 = (f32[2,128]{1,0:T(2,128)S(1)}, f32[2,128]{1,0:T(2,128)S(1)}, u32[]{:S(2)}, u32[]{:S(2)}) collective-permute-start(f32[2,128]{1,0:T(2,128)S(1)} %fusion.18), channel_id=1, source_target_pairs={{0,32},{16,48},{32,0},{48,16},{1,33},{17,49},{33,1},{49,17},{2,34}... | collective-permute-start | bytes 3080 | tf_op jit(solution)/shard_map/ppermute | solution.py:29
  147.9 2.6 %collective-permute-start.13 = (bf16[48,1792]{1,0:T(8,128)(2,1)S(1)}, bf16[48,1792]{1,0:T(8,128)(2,1)S(1)}, u32[]{:S(2)}, u32[]{:S(2)}) collective-permute-start(bf16[48,1792]{1,0:T(8,128)(2,1)S(1)} %dynamic-slice_convert_fusion), channel_id=1, source_target_pairs={{0,32},{16,48},{32,0},{48,16},{1,33},{17,49},{33,1},{49,17},{2,34}... | collective-permute-start | bytes 516104 | tf_op jit(solution)/shard_map/ppermute | solution.py:29
  150.6 20.5 %collective-permute-done.13 = bf16[48,1792]{1,0:T(8,128)(2,1)S(1)} collective-permute-done((bf16[48,1792]{1,0:T(8,128)(2,1)S(1)}, bf16[48,1792]{1,0:T(8,128)(2,1)S(1)}, u32[]{:S(2)}, u32[]{:S(2)}) %collective-permute-start.13) | collective-permute-done | bytes 172064 | tf_op jit(solution)/shard_map/ppermute | solution.py:29
  171.3 1.9 collective-permute-start.14
  173.2 9.0 %collective-permute-done.14 = bf16[48,896]{1,0:T(8,128)(2,1)S(1)} collective-permute-done((bf16[48,896]{1,0:T(8,128)(2,1)S(1)}, bf16[48,896]{1,0:T(8,128)(2,1)S(1)}, u32[]{:S(2)}, u32[]{:S(2)}) %collective-permute-start.14) | collective-permute-done | bytes 86048 | tf_op jit(solution)/shard_map/ppermute | solution.py:29
  182.4 1.9 collective-permute-start.15
  184.3 8.1 %collective-permute-done.15 = bf16[88,896]{1,0:T(8,128)(2,1)S(1)} collective-permute-done((bf16[88,896]{1,0:T(8,128)(2,1)S(1)}, bf16[88,896]{1,0:T(8,128)(2,1)S(1)}, u32[]{:S(2)}, u32[]{:S(2)}) %collective-permute-start.15) | collective-permute-done | bytes 157728 | tf_op jit(solution)/shard_map/ppermute | solution.py:29
  192.6 1.9 collective-permute-start.20
  194.5 4.4 %near_mm.1 = (f32[176,1024]{1,0:T(8,128)}, bf16[896,1024]{1,0:T(8,128)(2,1)}) custom-call(s32[5]{0:T(128)} %stack.49.at, bf16[176,896]{1,0:T(8,128)(2,1)} %copy-done.3, bf16[896,1024]{1,0:T(8,128)(2,1)} %stack.57.own, bf16[896,1024]{1,0:T(8,128)(2,1)} %copy-done.2), custom_call_target="tpu_custom_call" | custom-call | flops 322961408 | bytes 5242880 | tf_op jit(solution)/shard_map/near_mm/pallas_call | solution.py:173
  198.9 4.9 %collective-permute-done.20.x = bf16[176,896]{1,0:T(8,128)(2,1)S(1)} collective-permute-done((bf16[176,896]{1,0:T(8,128)(2,1)S(1)}, bf16[176,896]{1,0:T(8,128)(2,1)S(1)}, u32[]{:S(2)}, u32[]{:S(2)}) %collective-permute-start.20) | collective-permute-done | bytes 315424 | tf_op jit(solution)/shard_map/ppermute | solution.py:29
  204.6 3.1 %far_mm.1 = bf16[4,352,128]{2,1,0:T(8,128)(2,1)} custom-call(bf16[176,896]{1,0:T(8,128)(2,1)} %copy-done.13, f32[176,1024]{1,0:T(8,128)} %get-tuple-element.23.part, bf16[896,1024]{1,0:T(8,128)(2,1)} %get-tuple-element.24.rest), custom_call_target="tpu_custom_call" | custom-call | flops 322961408 | bytes 3145728 | tf_op jit(solution)/shard_map/far_mm/pallas_call | solution.py:192
  207.7 4.8 %all-to-all-start.3 = ((bf16[4,352,128]{2,1,0:T(8,128)(2,1)}), bf16[4,352,128]{2,1,0:T(8,128)(2,1)S(1)}, u32[]{:S(2)}, u32[]{:S(2)}) async-start(bf16[4,352,128]{2,1,0:T(8,128)(2,1)} %far_mm.1), calls=%async_computation.3 | async-start | bytes 720896 | tf_op jit(solution)/shard_map/all_to_all | solution.py:37
  212.5 5.7 %all-to-all-done.3 = bf16[4,352,128]{2,1,0:T(8,128)(2,1)S(1)} async-done(((bf16[4,352,128]{2,1,0:T(8,128)(2,1)}), bf16[4,352,128]{2,1,0:T(8,128)(2,1)S(1)}, u32[]{:S(2)}, u32[]{:S(2)}) %all-to-all-start.3) | async-done | bytes 360480 | tf_op jit(solution)/shard_map/all_to_all | solution.py:37
  218.3 5.1 %collective-permute-start.21 = (bf16[176,128]{1,0:T(8,128)(2,1)S(1)}, bf16[176,128]{1,0:T(8,128)(2,1)S(1)}, u32[]{:S(2)}, u32[]{:S(2)}) collective-permute-start(bf16[176,128]{1,0:T(8,128)(2,1)S(1)} %fusion.4), channel_id=1, source_target_pairs={{0,4},{4,0},{1,5},{5,1},{2,6},{6,2},{3,7},{7,3},{8,12},{12,8},{9,1... | collective-permute-start | bytes 135176 | tf_op jit(solution)/shard_map/ppermute | solution.py:29
  223.5 10.8 %collective-permute-done.21 = bf16[176,128]{1,0:T(8,128)(2,1)S(1)} collective-permute-done((bf16[176,128]{1,0:T(8,128)(2,1)S(1)}, bf16[176,128]{1,0:T(8,128)(2,1)S(1)}, u32[]{:S(2)}, u32[]{:S(2)}) %collective-permute-start.21) | collective-permute-done | bytes 45088 | tf_op jit(solution)/shard_map/ppermute | solution.py:29
  (88 shorter events, 11.5 us)
Async XLA Ops:
  0.0 6.4 %copy-start.10 = (bf16[128,1792]{1,0:T(8,128)(2,1)S(1)}, bf16[128,1792]{1,0:T(8,128)(2,1)}, u32[]{:S(2)}) copy-start(bf16[128,1792]{1,0:T(8,128)(2,1)} %param.12) | copy-start | bytes 1376260
  0.0 6.4 %copy-start.11 = (bf16[128,1792]{1,0:T(8,128)(2,1)S(1)}, bf16[128,1792]{1,0:T(8,128)(2,1)}, u32[]{:S(2)}) copy-start(bf16[128,1792]{1,0:T(8,128)(2,1)} %param.11) | copy-start | bytes 1376260
  2.1 19.4 %all-to-all-start = ((bf16[4,128,1024]{2,1,0:T(8,128)(2,1)}), bf16[4,128,1024]{2,1,0:T(8,128)(2,1)S(1)}, u32[]{:S(2)}, u32[]{:S(2)}) async-start(bf16[4,128,1024]{2,1,0:T(8,128)(2,1)} %broadcast_in_dim.37), calls=%async_computation | async-start | bytes 2097152 | tf_op jit(solution)/shard_map/all_to_all | solution.py:37
  6.6 14.1 %collective-permute-start.10 = (bf16[128,1792]{1,0:T(8,128)(2,1)S(1)}, bf16[128,1792]{1,0:T(8,128)(2,1)S(1)}, u32[]{:S(2)}, u32[]{:S(2)}) collective-permute-start(bf16[128,1792]{1,0:T(8,128)(2,1)S(1)} %pad_maximum_fusion.1), channel_id=1, source_target_pairs={{0,8},{8,0},{1,9},{9,1},{2,10},{10,2},{3,11},{11,3},{4,12},{12,4},... | collective-permute-start | bytes 1376264 | tf_op jit(solution)/shard_map/ppermute | solution.py:29
  21.5 7.0 %copy-start = (bf16[4,128,1024]{2,1,0:T(8,128)(2,1)}, bf16[4,128,1024]{2,1,0:T(8,128)(2,1)S(1)}, u32[]{:S(2)}) copy-start(bf16[4,128,1024]{2,1,0:T(8,128)(2,1)S(1)} %all-to-all-done) | copy-start | bytes 3145732
  23.6 6.8 %copy-start.12 = (bf16[176,128]{1,0:T(8,128)(2,1)S(1)}, bf16[176,128]{1,0:T(8,128)(2,1)}, u32[]{:S(2)}) copy-start(bf16[176,128]{1,0:T(8,128)(2,1)} %param.7) | copy-start | bytes 135172
  23.6 16.0 %copy-start.14 = (bf16[176,128]{1,0:T(8,128)(2,1)S(1)}, bf16[176,128]{1,0:T(8,128)(2,1)}, u32[]{:S(2)}) copy-start(bf16[176,128]{1,0:T(8,128)(2,1)} %param.8) | copy-start | bytes 135172
  23.6 31.2 %copy-start.15 = (f32[128]{0:T(128)S(1)}, f32[128]{0:T(128)}, u32[]{:S(2)}) copy-start(f32[128]{0:T(128)} %param.10) | copy-start | bytes 1540
  23.6 69.4 %all-to-all-start.2 = ((bf16[4,256,1792]{2,1,0:T(8,128)(2,1)}), bf16[4,256,1792]{2,1,0:T(8,128)(2,1)}, u32[]{:S(2)}, u32[]{:S(2)}) async-start(bf16[4,256,1792]{2,1,0:T(8,128)(2,1)} %broadcast_in_dim.41), calls=%async_computation.2 | async-start | bytes 7340032 | tf_op jit(solution)/shard_map/all_to_all | solution.py:37
  28.5 31.8 %collective-permute-start.3 = (bf16[512,1024]{1,0:T(8,128)(2,1)S(1)}, bf16[512,1024]{1,0:T(8,128)(2,1)S(1)}, u32[]{:S(2)}, u32[]{:S(2)}) collective-permute-start(bf16[512,1024]{1,0:T(8,128)(2,1)S(1)} %bitcast.42), channel_id=1, source_target_pairs={{0,64},{64,0},{1,65},{65,1},{2,66},{66,2},{3,67},{67,3},{4,68},{68... | collective-permute-start | bytes 3145736 | tf_op jit(solution)/shard_map/ppermute | solution.py:29
  30.5 11.4 %collective-permute-start = (bf16[1,176,128]{2,1,0:T(8,128)(2,1)S(1)}, bf16[1,176,128]{2,1,0:T(8,128)(2,1)S(1)}, u32[]{:S(2)}, u32[]{:S(2)}) collective-permute-start(bf16[1,176,128]{2,1,0:T(8,128)(2,1)S(1)} %bitcast.47), channel_id=1, source_target_pairs={{0,32},{8,40},{16,48},{24,56},{32,0},{40,8},{48,16},{56,24},{1,33}... | collective-permute-start | bytes 135176 | tf_op jit(solution)/shard_map/ppermute | solution.py:29
  41.9 10.2 %collective-permute-start.1 = (bf16[2,176,128]{2,1,0:T(8,128)(2,1)S(1)}, bf16[2,176,128]{2,1,0:T(8,128)(2,1)S(1)}, u32[]{:S(2)}, u32[]{:S(2)}) collective-permute-start(bf16[2,176,128]{2,1,0:T(8,128)(2,1)S(1)} %pad_maximum_fusion.7), channel_id=1, source_target_pairs={{0,16},{8,24},{16,0},{24,8},{32,48},{40,56},{48,32},{56,40},{1,17}... | collective-permute-start | bytes 270344 | tf_op jit(solution)/shard_map/ppermute | solution.py:29
  52.2 7.4 %collective-permute-start.2 = (bf16[4,176,128]{2,1,0:T(8,128)(2,1)S(1)}, bf16[4,176,128]{2,1,0:T(8,128)(2,1)S(1)}, u32[]{:S(2)}, u32[]{:S(2)}) collective-permute-start(bf16[4,176,128]{2,1,0:T(8,128)(2,1)S(1)} %pad_maximum_fusion.4), channel_id=1, source_target_pairs={{0,8},{8,0},{16,24},{24,16},{32,40},{40,32},{48,56},{56,48},{1,9},... | collective-permute-start | bytes 540680 | tf_op jit(solution)/shard_map/ppermute | solution.py:29
  60.3 1.0 copy-start.4
  64.3 9.8 %collective-permute-start.6 = (bf16[352,128]{1,0:T(8,128)(2,1)}, bf16[352,128]{1,0:T(8,128)(2,1)S(1)}, u32[]{:S(2)}, u32[]{:S(2)}) collective-permute-start(bf16[352,128]{1,0:T(8,128)(2,1)} %get-tuple-element.18), channel_id=1, source_target_pairs={{0,3},{1,2},{2,1},{3,0},{4,7},{5,6},{6,5},{7,4},{8,11},{9,10},{10,... | collective-permute-start | bytes 270344 | tf_op jit(solution)/shard_map/ppermute | solution.py:29
  67.8 9.0 %collective-permute-start.5 = (bf16[352,128]{1,0:T(8,128)(2,1)}, bf16[352,128]{1,0:T(8,128)(2,1)S(1)}, u32[]{:S(2)}, u32[]{:S(2)}) collective-permute-start(bf16[352,128]{1,0:T(8,128)(2,1)} %get-tuple-element.17), channel_id=1, source_target_pairs={{0,2},{1,3},{2,0},{3,1},{4,6},{5,7},{6,4},{7,5},{8,10},{9,11},{10,... | collective-permute-start | bytes 270344 | tf_op jit(solution)/shard_map/ppermute | solution.py:29
  70.7 6.6 %collective-permute-start.4 = (bf16[352,128]{1,0:T(8,128)(2,1)}, bf16[352,128]{1,0:T(8,128)(2,1)S(1)}, u32[]{:S(2)}, u32[]{:S(2)}) collective-permute-start(bf16[352,128]{1,0:T(8,128)(2,1)} %get-tuple-element.16), channel_id=1, source_target_pairs={{0,1},{1,0},{2,3},{3,2},{4,5},{5,4},{6,7},{7,6},{8,9},{9,8},{10,11... | collective-permute-start | bytes 270344 | tf_op jit(solution)/shard_map/ppermute | solution.py:29
  78.3 19.3 %collective-permute-start.7 = (bf16[360,128]{1,0:T(8,128)(2,1)S(1)}, bf16[360,128]{1,0:T(8,128)(2,1)S(1)}, u32[]{:S(2)}, u32[]{:S(2)}) collective-permute-start(bf16[360,128]{1,0:T(8,128)(2,1)S(1)} %pad_maximum_fusion.6), channel_id=1, source_target_pairs={{0,4},{4,0},{1,5},{5,1},{2,6},{6,2},{3,7},{7,3},{8,12},{12,8},{9,1... | collective-permute-start | bytes 276488 | tf_op jit(solution)/shard_map/ppermute | solution.py:29
  93.1 24.1 %collective-permute-start.11 = (bf16[1024,1792]{1,0:T(8,128)(2,1)}, bf16[1024,1792]{1,0:T(8,128)(2,1)}, u32[]{:S(2)}, u32[]{:S(2)}) collective-permute-start(bf16[1024,1792]{1,0:T(8,128)(2,1)} %bitcast.17.own), channel_id=1, source_target_pairs={{0,64},{64,0},{1,65},{65,1},{2,66},{66,2},{3,67},{67,3},{4,68},{68... | collective-permute-start | bytes 11010056 | tf_op jit(solution)/shard_map/ppermute | solution.py:29
  97.6 8.2 %copy-start.6 = (bf16[224,1024]{1,0:T(8,128)(2,1)S(1)}, bf16[224,1024]{1,0:T(8,128)(2,1)}, u32[]{:S(2)}) copy-start(bf16[224,1024]{1,0:T(8,128)(2,1)} %refs_0_.1) | copy-start | bytes 1376260
  100.2 17.0 %all-to-all-start.1 = ((bf16[8,360,128]{2,1,0:T(8,128)(2,1)}), bf16[8,360,128]{2,1,0:T(8,128)(2,1)S(1)}, u32[]{:S(2)}, u32[]{:S(2)}) async-start(bf16[8,360,128]{2,1,0:T(8,128)(2,1)} %broadcast_in_dim.40), calls=%async_computation.1 | async-start | bytes 1474560 | tf_op jit(solution)/shard_map/all_to_all | solution.py:37
  105.8 24.4 %collective-permute-start.16 = (bf16[224,1024]{1,0:T(8,128)(2,1)S(1)}, bf16[224,1024]{1,0:T(8,128)(2,1)S(1)}, u32[]{:S(2)}, u32[]{:S(2)}) collective-permute-start(bf16[224,1024]{1,0:T(8,128)(2,1)S(1)} %copy-done.6), channel_id=1, source_target_pairs={{0,128},{128,256},{256,384},{384,0},{1,129},{129,257},{257,385},{3... | collective-permute-start | bytes 1376264 | tf_op jit(solution)/shard_map/ppermute | solution.py:24
  109.1 21.1 %collective-permute-start.17 = (bf16[224,1024]{1,0:T(8,128)(2,1)S(1)}, bf16[224,1024]{1,0:T(8,128)(2,1)S(1)}, u32[]{:S(2)}, u32[]{:S(2)}) collective-permute-start(bf16[224,1024]{1,0:T(8,128)(2,1)S(1)} %copy-done.6), channel_id=1, source_target_pairs={{0,256},{128,384},{256,0},{384,128},{1,257},{129,385},{257,1},{385... | collective-permute-start | bytes 1376264 | tf_op jit(solution)/shard_map/ppermute | solution.py:24
  114.2 17.2 %collective-permute-start.18 = (bf16[224,1024]{1,0:T(8,128)(2,1)S(1)}, bf16[224,1024]{1,0:T(8,128)(2,1)S(1)}, u32[]{:S(2)}, u32[]{:S(2)}) collective-permute-start(bf16[224,1024]{1,0:T(8,128)(2,1)S(1)} %copy-done.6), channel_id=1, source_target_pairs={{0,384},{128,0},{256,128},{384,256},{1,385},{129,1},{257,129},{385... | collective-permute-start | bytes 1376264 | tf_op jit(solution)/shard_map/ppermute | solution.py:24
  117.1 1.0 copy-start.1
  123.2 23.6 %collective-permute-start.12 = (bf16[88,1792]{1,0:T(8,128)(2,1)}, bf16[88,1792]{1,0:T(8,128)(2,1)}, u32[]{:S(2)}, u32[]{:S(2)}) collective-permute-start(bf16[88,1792]{1,0:T(8,128)(2,1)} %get-tuple-element.20), channel_id=1, source_target_pairs={{0,16},{16,0},{32,48},{48,32},{1,17},{17,1},{33,49},{49,33},{2,18}... | collective-permute-start | bytes 946184 | tf_op jit(solution)/shard_map/ppermute | solution.py:29
  128.3 11.4 %collective-permute-start.8 = (f32[2,128]{1,0:T(2,128)S(1)}, f32[2,128]{1,0:T(2,128)S(1)}, u32[]{:S(2)}, u32[]{:S(2)}) collective-permute-start(f32[2,128]{1,0:T(2,128)S(1)} %slice_add_fusion.1), channel_id=1, source_target_pairs={{0,16},{16,0},{32,48},{48,32},{1,17},{17,1},{33,49},{49,33},{2,18}... | collective-permute-start | bytes 3080 | tf_op jit(solution)/shard_map/ppermute | solution.py:29
  130.2 16.7 %copy-start.5 = (f32[88,1792]{1,0:T(8,128)S(1)}, f32[88,1792]{1,0:T(8,128)}, u32[]{:S(2)}) copy-start(f32[88,1792]{1,0:T(8,128)} %get-tuple-element.19) | copy-start | bytes 1892356
  130.2 1.2 copy-start.7
  130.2 1.2 copy-start.8
  131.4 0.8 copy-start.9
  135.0 57.5 %collective-permute-start.19 = (bf16[896,1024]{1,0:T(8,128)(2,1)}, bf16[896,1024]{1,0:T(8,128)(2,1)S(1)}, u32[]{:S(2)}, u32[]{:S(2)}) collective-permute-start(bf16[896,1024]{1,0:T(8,128)(2,1)} %stack.57.own), channel_id=1, source_target_pairs={{0,64},{64,0},{1,65},{65,1},{2,66},{66,2},{3,67},{67,3},{4,68},{68... | collective-permute-start | bytes 5505032 | tf_op jit(solution)/shard_map/ppermute | solution.py:29
  139.7 10.8 %collective-permute-start.9 = (f32[2,128]{1,0:T(2,128)S(1)}, f32[2,128]{1,0:T(2,128)S(1)}, u32[]{:S(2)}, u32[]{:S(2)}) collective-permute-start(f32[2,128]{1,0:T(2,128)S(1)} %fusion.18), channel_id=1, source_target_pairs={{0,32},{16,48},{32,0},{48,16},{1,33},{17,49},{33,1},{49,17},{2,34}... | collective-permute-start | bytes 3080 | tf_op jit(solution)/shard_map/ppermute | solution.py:29
  147.9 23.2 %collective-permute-start.13 = (bf16[48,1792]{1,0:T(8,128)(2,1)S(1)}, bf16[48,1792]{1,0:T(8,128)(2,1)S(1)}, u32[]{:S(2)}, u32[]{:S(2)}) collective-permute-start(bf16[48,1792]{1,0:T(8,128)(2,1)S(1)} %dynamic-slice_convert_fusion), channel_id=1, source_target_pairs={{0,32},{16,48},{32,0},{48,16},{1,33},{17,49},{33,1},{49,17},{2,34}... | collective-permute-start | bytes 516104 | tf_op jit(solution)/shard_map/ppermute | solution.py:29
  171.3 10.9 %collective-permute-start.14 = (bf16[48,896]{1,0:T(8,128)(2,1)S(1)}, bf16[48,896]{1,0:T(8,128)(2,1)S(1)}, u32[]{:S(2)}, u32[]{:S(2)}) collective-permute-start(bf16[48,896]{1,0:T(8,128)(2,1)S(1)} %fusion.2), channel_id=1, source_target_pairs={{0,32},{16,48},{32,0},{48,16},{1,33},{17,49},{33,1},{49,17},{2,34}... | collective-permute-start | bytes 258056 | tf_op jit(solution)/shard_map/ppermute | solution.py:29
  182.4 10.0 %collective-permute-start.15 = (bf16[88,896]{1,0:T(8,128)(2,1)S(1)}, bf16[88,896]{1,0:T(8,128)(2,1)S(1)}, u32[]{:S(2)}, u32[]{:S(2)}) collective-permute-start(bf16[88,896]{1,0:T(8,128)(2,1)S(1)} %pad_maximum_fusion.5), channel_id=1, source_target_pairs={{0,16},{16,0},{32,48},{48,32},{1,17},{17,1},{33,49},{49,33},{2,18}... | collective-permute-start | bytes 473096 | tf_op jit(solution)/shard_map/ppermute | solution.py:29
  192.6 2.0 copy-start.3
  192.6 2.0 copy-start.2
  192.6 11.3 %collective-permute-start.20 = (bf16[176,896]{1,0:T(8,128)(2,1)S(1)}, bf16[176,896]{1,0:T(8,128)(2,1)S(1)}, u32[]{:S(2)}, u32[]{:S(2)}) collective-permute-start(bf16[176,896]{1,0:T(8,128)(2,1)S(1)} %pad_maximum_fusion.3.x), channel_id=1, source_target_pairs={{0,8},{8,0},{1,9},{9,1},{2,10},{10,2},{3,11},{11,3},{4,12},{12,4},... | collective-permute-start | bytes 946184 | tf_op jit(solution)/shard_map/ppermute | solution.py:29
  203.8 0.7 copy-start.13
  207.7 10.5 %all-to-all-start.3 = ((bf16[4,352,128]{2,1,0:T(8,128)(2,1)}), bf16[4,352,128]{2,1,0:T(8,128)(2,1)S(1)}, u32[]{:S(2)}, u32[]{:S(2)}) async-start(bf16[4,352,128]{2,1,0:T(8,128)(2,1)} %far_mm.1), calls=%async_computation.3 | async-start | bytes 720896 | tf_op jit(solution)/shard_map/all_to_all | solution.py:37
  218.3 16.0 %collective-permute-start.21 = (bf16[176,128]{1,0:T(8,128)(2,1)S(1)}, bf16[176,128]{1,0:T(8,128)(2,1)S(1)}, u32[]{:S(2)}, u32[]{:S(2)}) collective-permute-start(bf16[176,128]{1,0:T(8,128)(2,1)S(1)} %fusion.4), channel_id=1, source_target_pairs={{0,4},{4,0},{1,5},{5,1},{2,6},{6,2},{3,7},{7,3},{8,12},{12,8},{9,1... | collective-permute-start | bytes 135176 | tf_op jit(solution)/shard_map/ppermute | solution.py:29

commit v9 on v8

--- a/solution.py
+++ b/solution.py
@@ -19,11 +19,6 @@
     return lax.axis_size(axis)
 
 
-def shift(value, axis, step):
-    n = size_of(axis)
-    return lax.ppermute(value, axis, [(i, (i + step) % n) for i in range(n)])
-
-
 def swap(value, axis, bit):
     n = size_of(axis)
     return lax.ppermute(value, axis, [(i, i ^ bit) for i in range(n)])
@@ -48,31 +43,17 @@
     return first, second
 
 
-def stack_kernel(*refs):
-    *ins, out = refs
-    height = ins[0].shape[0]
-    for k, ref in enumerate(ins):
-        out[k * height : (k + 1) * height] = ref[...]
-
-
-def stacked(parts):
-    height, width = parts[0].shape
-    vmem = pl.BlockSpec(memory_space=pltpu.VMEM)
-    return pl.pallas_call(
-        stack_kernel,
-        out_shape=jax.ShapeDtypeStruct((len(parts) * height, width), BF),
-        in_specs=[vmem] * len(parts),
-        out_specs=vmem,
-        name="stack",
-    )(*parts)
+def gathered(w):
+    own = lax.all_gather(w, "x", axis=0, tiled=True)
+    return own, swap(own, "c", 1)
 
 
 def dot(a, b):
     return jnp.dot(a, b, preferred_element_type=F32)
 
 
-def proj_kernel(at, x, own, other, *outs):
-    ci, zl, yi = at[0], at[2], at[3]
+def proj_kernel(at, x, own, other, out):
+    ci, zl = at[0], at[2]
     rows = x.shape[1]
 
     def blocks(core):
@@ -82,13 +63,10 @@
     mine = jnp.concatenate(blocks(ci), axis=1)
     theirs = jnp.concatenate(blocks(1 - ci), axis=1)
     part = (dot(mine, own[...]) + dot(theirs, other[...])).astype(BF)
-    *outs, parts = outs
     for zh in range(2):
         for y in range(4):
             n = (zh * 4 + y) * 128
-            parts[y, zh * rows : (zh + 1) * rows] = part[:, n : n + 128]
-    for k, out in enumerate(outs):
-        out[...] = parts[yi ^ k]
+            out[y, zh * rows : (zh + 1) * rows] = part[:, n : n + 128]
 
 
 def proj_parts(at, x, own, other):
@@ -96,10 +74,9 @@
     vmem = pl.BlockSpec(memory_space=pltpu.VMEM)
     return pl.pallas_call(
         proj_kernel,
-        out_shape=[jax.ShapeDtypeStruct((2 * rows, 128), BF)] * 4,
+        out_shape=jax.ShapeDtypeStruct((4, 2 * rows, 128), BF),
         in_specs=[pl.BlockSpec(memory_space=pltpu.SMEM), vmem, vmem, vmem],
-        out_specs=[vmem] * 4,
-        scratch_shapes=[pltpu.VMEM((4, 2 * rows, 128), BF)],
+        out_specs=vmem,
         cost_estimate=pl.CostEstimate(
             flops=2 * rows * 1024 * 1024, bytes_accessed=3 << 20, transcendentals=0
         ),
@@ -145,12 +122,12 @@
 
 
 def near_kernel(at, x, own, other, part, rest, whole):
-    ci, zp, xi = at[0], at[1], at[4]
+    ci, zp = at[0], at[1]
     height = own.shape[0] // 4
     half = x.shape[1]
     for ref, core in ((own, ci), (other, 1 - ci)):
         for k in range(4):
-            b = ((xi + 4 - k) & 3) * 2 + core
+            b = 2 * k + core
             to = pl.ds(pl.multiple_of(b * height, 16), height)
             whole[to] = ref[k * height : (k + 1) * height]
     part[...] = dot(x[...], whole[pl.ds(pl.multiple_of(zp * half, 16), half)])
@@ -206,15 +183,16 @@
 
 
 def on_device(attn_out, residual, proj_weight, norm_gain, gate_proj, up_proj, down_proj):
-    xi, ci, zh, yi = (lax.axis_index(name) for name in ("x", "c", "zh", "y"))
+    ci, zh = lax.axis_index("c"), lax.axis_index("zh")
     zq, zp = lax.axis_index("zq"), lax.axis_index("zp")
-    at = jnp.stack([ci, zp, 2 * zq + zp, yi, xi]).astype(jnp.int32)
+    at = jnp.stack([ci, zp, 2 * zq + zp]).astype(jnp.int32)
     rows = attn_out.shape[0]
     ffw = gate_proj.shape[1] // 2
 
     cols = attn_out[None]
     for bit in (4, 2, 1):
-        cols = jnp.concatenate([cols, swap(cols, ZL, bit)])
+        arrived = swap(cols, ZL, bit)
+        cols = jnp.concatenate([cols, arrived])
 
     def columns(which):
         halves = [lax.dynamic_slice_in_dim(w, which * ffw, ffw, 1) for w in (gate_proj, up_proj)]
@@ -222,14 +200,9 @@
 
     facing = swap(columns(1 - zp), "zp", 1)
     both = jnp.concatenate([columns(zp), facing])
-    both_own = from_everyone(both, "x").reshape(-1, 2 * ffw)
-    both_other = swap(both_own, "c", 1)
-    proj_own = from_everyone(proj_weight, "x").reshape(-1, proj_weight.shape[1])
-    proj_other = swap(proj_own, "c", 1)
-    ring = [1, 2, -1]
-    shards = [down_proj] + [shift(down_proj, "x", k) for k in ring]
-    down_own = stacked(shards)
-    down_other = swap(down_own, "c", 1)
+    proj_own, proj_other = gathered(proj_weight)
+    both_own, both_other = gathered(both)
+    down_own, down_other = gathered(down_proj)
 
     high = exact(norm_gain)
     mid = exact(norm_gain - high)
@@ -237,8 +210,7 @@
     gains = jnp.pad(jnp.stack([high, mid, low]), ((0, 5), (0, 0)))
 
     part = proj_parts(at, cols, proj_own, proj_other)
-    near = [part[0]] + [swap(part[k], "y", k) for k in (1, 2, 3)]
-    near = sum(p.astype(F32) for p in near).reshape(2, rows, 128)
+    near = exchange(part, "y").astype(F32).sum(axis=0).reshape(2, rows, 128)
     mine = jnp.arange(2)[:, None, None] == zh
     near = jnp.where(mine, near + residual.astype(F32), near).reshape(2 * rows, 128)
     far = swap(jnp.concatenate([near, gains]).astype(BF), "zh", 1).astype(F32)

time: 236 us -> 259 us (1.097)
  waiting for transfers between devices: 90.7 us -> 136 us
  starting transfers between devices: 110 us -> 82.2 us
  between operations: 0.61 us -> 13.6 us
  local copies, waits for them, and re-layouts: 9.9 us -> 5.31 us
  Pallas kernels: 18.4 us -> 15.6 us
    all_gather x0 -> x3, waiting for transfers between devices: none -> 39.2 us  [gathered(): own = lax.all_gather(w, 'x', axis=0, tiled=True)]
    all_to_all x4 -> x3, waiting for transfers between devices: 6.58 us -> 20.9 us  [exchange(): return lax.all_to_all(parts, axis, split_axis=0, concat_axis=0, tiled=True)]
    ppermute x3 -> x0, starting transfers between devices: 11.3 us -> none  [shift(): return lax.ppermute(value, axis, [(i, (i + step) % n) for i in range(n)])]
    ppermute x19 -> x16, starting transfers between devices: 78.9 us -> 68.9 us  [swap(): return lax.ppermute(value, axis, [(i, i ^ bit) for i in range(n)])]
    ppermute x19 -> x16, waiting for transfers between devices: 82.9 us -> 74.4 us  [swap(): return lax.ppermute(value, axis, [(i, i ^ bit) for i in range(n)])]
    all_to_all x4 -> x3, starting transfers between devices: 19.6 us -> 13.3 us  [exchange(): return lax.all_to_all(parts, axis, split_axis=0, concat_axis=0, tiled=True)]
    broadcast_in_dim x3 -> x1, local copies, waits for them, and re-layouts: 5.29 us -> 0.97 us  [from_everyone(): copies = jnp.broadcast_to(value, (size_of(axis), *value.shape))]
    pallas_call x2 -> x1, Pallas kernels: 5.78 us -> 2.96 us  [proj_parts(): pl.pallas_call(proj_kernel, out_shape=jax.ShapeDtypeStruct((4, 2 * rows,...]
  transfers between devices with their start and end apart: 26 -> 22, of which waited for: 16 -> 15; matrix products, arithmetic and copies ran while one was open for 3% -> 3% of each run, Pallas kernels for 7% -> 5%
where the time goes in v9:
time: 259 us; the launch traced here: 258 us
  waiting for transfers between devices  136 us (53%)
  starting transfers between devices  82.2 us (32%)
  Pallas kernels  15.6 us (6%)
  between operations  13.6 us (5%)
  other arithmetic  5.46 us (2%)
  local copies, waits for them, and re-layouts  5.31 us (2%)
    ppermute x16, waiting for transfers between devices, swap(): return lax.ppermute(value, axis, [(i, i ^ bit) for i in range(n)])  74.4 us
    ppermute x16, starting transfers between devices, swap(): return lax.ppermute(value, axis, [(i, i ^ bit) for i in range(n)])  68.9 us
    all_gather x3, waiting for transfers between devices, gathered(): own = lax.all_gather(w, 'x', axis=0, tiled=True)  39.2 us
    all_to_all x3, waiting for transfers between devices, exchange(): return lax.all_to_all(parts, axis, split_axis=0, concat_axis=0, tiled=True)  20.9 us
    all_to_all x3, starting transfers between devices, exchange(): return lax.all_to_all(parts, axis, split_axis=0, concat_axis=0, tiled=True)  13.3 us
  transfers between devices with their start and end apart: 22, of which 15 were waited for; matrix products, arithmetic and copies ran while one was open for 3% of the time, Pallas kernels for 5%

profile of v9, /device:TPU:8, one launch (start us, length us, event | category | flops | bytes accessed | tf_op | source)
XLA Modules:
  0.0 258.1 jit_solution(5262453384918537982)
XLA Ops:
  6.5 0.7 all-gather.4.cloned.1.call-update
  7.3 1.4 constant_dynamic-slice_fusion.2
  8.7 3.8 %collective-permute-start.7 = (bf16[128,1792]{1,0:T(8,128)(2,1)S(1)}, bf16[128,1792]{1,0:T(8,128)(2,1)S(1)}, u32[]{:S(2)}, u32[]{:S(2)}) collective-permute-start(bf16[128,1792]{1,0:T(8,128)(2,1)S(1)} %pad_maximum_fusion.1), channel_id=1, source_target_pairs={{0,8},{8,0},{1,9},{9,1},{2,10},{10,2},{3,11},{11,3},{4,12},{12,4},... | collective-permute-start | bytes 1376264 | tf_op jit(solution)/shard_map/ppermute | solution.py:24
  12.6 10.5 %collective-permute-done.7 = bf16[128,1792]{1,0:T(8,128)(2,1)S(1)} collective-permute-done((bf16[128,1792]{1,0:T(8,128)(2,1)S(1)}, bf16[128,1792]{1,0:T(8,128)(2,1)S(1)}, u32[]{:S(2)}, u32[]{:S(2)}) %collective-permute-start.7) | collective-permute-done | bytes 458784 | tf_op jit(solution)/shard_map/ppermute | solution.py:24
  23.1 1.0 pad_maximum_fusion
  24.1 21.5 %all-gather.4.cloned.1.call-done.own = bf16[512,1024]{1,0:T(8,128)(2,1)} async-done(((bf16[128,1024]{1,0:T(8,128)(2,1)}), bf16[512,1024]{1,0:T(8,128)(2,1)}) %all-gather.4.cloned.1.call-update) | async-done | bytes 1048592 | tf_op jit(solution)/shard_map/all_gather | solution.py:47
  45.6 1.9 collective-permute-start.3
  47.5 7.6 %collective-permute-start = (bf16[1,176,128]{2,1,0:T(8,128)(2,1)S(1)}, bf16[1,176,128]{2,1,0:T(8,128)(2,1)S(1)}, u32[]{:S(2)}, u32[]{:S(2)}) collective-permute-start(bf16[1,176,128]{2,1,0:T(8,128)(2,1)S(1)} %bitcast.41), channel_id=1, source_target_pairs={{0,32},{8,40},{16,48},{24,56},{32,0},{40,8},{48,16},{56,24},{1,33}... | collective-permute-start | bytes 135176 | tf_op jit(solution)/shard_map/ppermute | solution.py:24
  55.2 2.3 collective-permute-done
  57.5 5.5 %collective-permute-start.1 = (bf16[2,176,128]{2,1,0:T(8,128)(2,1)S(1)}, bf16[2,176,128]{2,1,0:T(8,128)(2,1)S(1)}, u32[]{:S(2)}, u32[]{:S(2)}) collective-permute-start(bf16[2,176,128]{2,1,0:T(8,128)(2,1)S(1)} %pad_maximum_fusion.7), channel_id=1, source_target_pairs={{0,16},{8,24},{16,0},{24,8},{32,48},{40,56},{48,32},{56,40},{1,17}... | collective-permute-start | bytes 270344 | tf_op jit(solution)/shard_map/ppermute | solution.py:24
  63.1 4.7 %collective-permute-done.1 = bf16[2,176,128]{2,1,0:T(8,128)(2,1)S(1)} collective-permute-done((bf16[2,176,128]{2,1,0:T(8,128)(2,1)S(1)}, bf16[2,176,128]{2,1,0:T(8,128)(2,1)S(1)}, u32[]{:S(2)}, u32[]{:S(2)}) %collective-permute-start.1) | collective-permute-done | bytes 90144 | tf_op jit(solution)/shard_map/ppermute | solution.py:24
  67.8 2.6 %collective-permute-start.2 = (bf16[4,176,128]{2,1,0:T(8,128)(2,1)S(1)}, bf16[4,176,128]{2,1,0:T(8,128)(2,1)S(1)}, u32[]{:S(2)}, u32[]{:S(2)}) collective-permute-start(bf16[4,176,128]{2,1,0:T(8,128)(2,1)S(1)} %pad_maximum_fusion.4), channel_id=1, source_target_pairs={{0,8},{8,0},{16,24},{24,16},{32,40},{40,32},{48,56},{56,48},{1,9},... | collective-permute-start | bytes 540680 | tf_op jit(solution)/shard_map/ppermute | solution.py:24
  71.2 4.0 %collective-permute-done.2 = bf16[4,176,128]{2,1,0:T(8,128)(2,1)S(1)} collective-permute-done((bf16[4,176,128]{2,1,0:T(8,128)(2,1)S(1)}, bf16[4,176,128]{2,1,0:T(8,128)(2,1)S(1)}, u32[]{:S(2)}, u32[]{:S(2)}) %collective-permute-start.2) | collective-permute-done | bytes 180256 | tf_op jit(solution)/shard_map/ppermute | solution.py:24
  75.2 0.8 pad_maximum_fusion.2.x
  76.0 1.0 copy-done.3
  77.0 3.0 %proj_mm.1 = bf16[4,352,128]{2,1,0:T(8,128)(2,1)} custom-call(s32[3]{0:T(128)} %pad_add_fusion.at, bf16[8,176,128]{2,1,0:T(8,128)(2,1)} %pad_maximum_fusion.2.x, bf16[512,1024]{1,0:T(8,128)(2,1)} %all-gather.4.cloned.1.call-done.own, bf16[512,1024]{1,0:T(8,128)(2,1)} %copy-done.3), custom_call_target="tpu_custom_call" | custom-call | flops 369098752 | bytes 3145728 | tf_op jit(solution)/shard_map/proj_mm/pallas_call | solution.py:75
  79.9 4.8 %all-to-all-start = ((bf16[4,352,128]{2,1,0:T(8,128)(2,1)}), bf16[4,352,128]{2,1,0:T(8,128)(2,1)S(1)}, u32[]{:S(2)}, u32[]{:S(2)}) async-start(bf16[4,352,128]{2,1,0:T(8,128)(2,1)} %proj_mm.1), calls=%async_computation | async-start | bytes 720896 | tf_op jit(solution)/shard_map/all_to_all | solution.py:32
  84.8 5.7 %all-to-all-done = bf16[4,352,128]{2,1,0:T(8,128)(2,1)S(1)} async-done(((bf16[4,352,128]{2,1,0:T(8,128)(2,1)}), bf16[4,352,128]{2,1,0:T(8,128)(2,1)S(1)}, u32[]{:S(2)}, u32[]{:S(2)}) %all-to-all-start) | async-done | bytes 360480 | tf_op jit(solution)/shard_map/all_to_all | solution.py:32
  90.7 14.7 %collective-permute-start.4 = (bf16[360,128]{1,0:T(8,128)(2,1)S(1)}, bf16[360,128]{1,0:T(8,128)(2,1)S(1)}, u32[]{:S(2)}, u32[]{:S(2)}) collective-permute-start(bf16[360,128]{1,0:T(8,128)(2,1)S(1)} %pad_maximum_fusion.6), channel_id=1, source_target_pairs={{0,4},{4,0},{1,5},{5,1},{2,6},{6,2},{3,7},{7,3},{8,12},{12,8},{9,1... | collective-permute-start | bytes 276488 | tf_op jit(solution)/shard_map/ppermute | solution.py:24
  105.4 1.9 collective-permute-start.8
  107.4 2.4 collective-permute-done.4
  110.4 1.0 broadcast_in_dim.33
  111.3 3.6 %all-to-all-start.1 = ((bf16[8,360,128]{2,1,0:T(8,128)(2,1)}), bf16[8,360,128]{2,1,0:T(8,128)(2,1)S(1)}, u32[]{:S(2)}, u32[]{:S(2)}) async-start(bf16[8,360,128]{2,1,0:T(8,128)(2,1)} %broadcast_in_dim.33), calls=%async_computation.1 | async-start | bytes 1474560 | tf_op jit(solution)/shard_map/all_to_all | solution.py:32
  115.0 0.7 all-gather.8.cloned.1.call-update
  115.7 9.4 %all-to-all-done.1.x = bf16[8,360,128]{2,1,0:T(8,128)(2,1)S(1)} async-done(((bf16[8,360,128]{2,1,0:T(8,128)(2,1)}), bf16[8,360,128]{2,1,0:T(8,128)(2,1)S(1)}, u32[]{:S(2)}, u32[]{:S(2)}) %all-to-all-start.1) | async-done | bytes 737312 | tf_op jit(solution)/shard_map/all_to_all | solution.py:32
  125.1 0.9 copy-done
  126.0 5.1 %both_mm.1 = (bf16[88,1792]{1,0:T(8,128)(2,1)}, f32[88,1792]{1,0:T(8,128)}) custom-call(s32[3]{0:T(128)} %pad_add_fusion.at, bf16[8,360,128]{2,1,0:T(8,128)(2,1)} %copy-done, bf16[1024,1792]{1,0:T(8,128)(2,1)} %all-gather.6.cloned.1.call-done.own, bf16[1024,1792]{1,0:T(8,128)(2,1)} %collective-permute-done.8.other), custom_call_target="tpu_custom_call" | custom-call | flops 1291845632 | bytes 9437184 | tf_op jit(solution)/shard_map/both_mm/pallas_call | solution.py:111
  131.1 3.8 %collective-permute-start.9 = (bf16[88,1792]{1,0:T(8,128)(2,1)}, bf16[88,1792]{1,0:T(8,128)(2,1)S(1)}, u32[]{:S(2)}, u32[]{:S(2)}) collective-permute-start(bf16[88,1792]{1,0:T(8,128)(2,1)} %get-tuple-element.12), channel_id=1, source_target_pairs={{0,16},{16,0},{32,48},{48,32},{1,17},{17,1},{33,49},{49,33},{2,18}... | collective-permute-start | bytes 946184 | tf_op jit(solution)/shard_map/ppermute | solution.py:24
  134.9 3.0 %collective-permute-start.5 = (f32[2,128]{1,0:T(2,128)S(1)}, f32[2,128]{1,0:T(2,128)S(1)}, u32[]{:S(2)}, u32[]{:S(2)}) collective-permute-start(f32[2,128]{1,0:T(2,128)S(1)} %slice_add_fusion.1), channel_id=1, source_target_pairs={{0,16},{16,0},{32,48},{48,32},{1,17},{17,1},{33,49},{49,33},{2,18}... | collective-permute-start | bytes 3080 | tf_op jit(solution)/shard_map/ppermute | solution.py:24
  137.9 17.6 %all-gather.8.cloned.1.call-done.own = bf16[896,1024]{1,0:T(8,128)(2,1)} async-done(((bf16[224,1024]{1,0:T(8,128)(2,1)}), bf16[896,1024]{1,0:T(8,128)(2,1)}) %all-gather.8.cloned.1.call-update) | async-done | bytes 1835024 | tf_op jit(solution)/shard_map/all_gather | solution.py:47
  155.5 1.9 collective-permute-start.13
  157.5 7.6 %collective-permute-start.6 = (f32[2,128]{1,0:T(2,128)S(1)}, f32[2,128]{1,0:T(2,128)S(1)}, u32[]{:S(2)}, u32[]{:S(2)}) collective-permute-start(f32[2,128]{1,0:T(2,128)S(1)} %fusion.18), channel_id=1, source_target_pairs={{0,32},{16,48},{32,0},{48,16},{1,33},{17,49},{33,1},{49,17},{2,34}... | collective-permute-start | bytes 3080 | tf_op jit(solution)/shard_map/ppermute | solution.py:24
  165.1 1.1 convert_add_fusion
  166.3 2.1 collective-permute-start.10
  168.5 21.1 %collective-permute-done.10 = bf16[48,1792]{1,0:T(8,128)(2,1)S(1)} collective-permute-done((bf16[48,1792]{1,0:T(8,128)(2,1)S(1)}, bf16[48,1792]{1,0:T(8,128)(2,1)S(1)}, u32[]{:S(2)}, u32[]{:S(2)}) %collective-permute-start.10) | collective-permute-done | bytes 172064 | tf_op jit(solution)/shard_map/ppermute | solution.py:24
  189.8 1.9 collective-permute-start.11
  191.8 8.7 %collective-permute-done.11 = bf16[48,896]{1,0:T(8,128)(2,1)S(1)} collective-permute-done((bf16[48,896]{1,0:T(8,128)(2,1)S(1)}, bf16[48,896]{1,0:T(8,128)(2,1)S(1)}, u32[]{:S(2)}, u32[]{:S(2)}) %collective-permute-start.11) | collective-permute-done | bytes 86048 | tf_op jit(solution)/shard_map/ppermute | solution.py:24
  200.7 1.9 collective-permute-start.12
  202.6 7.7 %collective-permute-done.12 = bf16[88,896]{1,0:T(8,128)(2,1)S(1)} collective-permute-done((bf16[88,896]{1,0:T(8,128)(2,1)S(1)}, bf16[88,896]{1,0:T(8,128)(2,1)S(1)}, u32[]{:S(2)}, u32[]{:S(2)}) %collective-permute-start.12) | collective-permute-done | bytes 157728 | tf_op jit(solution)/shard_map/ppermute | solution.py:24
  210.5 1.9 collective-permute-start.14
  212.4 4.4 %near_mm.1 = (f32[176,1024]{1,0:T(8,128)}, bf16[896,1024]{1,0:T(8,128)(2,1)}) custom-call(s32[3]{0:T(128)} %pad_add_fusion.at, bf16[176,896]{1,0:T(8,128)(2,1)} %copy-done.2, bf16[896,1024]{1,0:T(8,128)(2,1)} %all-gather.8.cloned.1.call-done.own, bf16[896,1024]{1,0:T(8,128)(2,1)} %copy-done.1), custom_call_target="tpu_custom_call" | custom-call | flops 322961408 | bytes 5242880 | tf_op jit(solution)/shard_map/near_mm/pallas_call | solution.py:150
  216.8 4.9 %collective-permute-done.14.x = bf16[176,896]{1,0:T(8,128)(2,1)S(1)} collective-permute-done((bf16[176,896]{1,0:T(8,128)(2,1)S(1)}, bf16[176,896]{1,0:T(8,128)(2,1)S(1)}, u32[]{:S(2)}, u32[]{:S(2)}) %collective-permute-start.14) | collective-permute-done | bytes 315424 | tf_op jit(solution)/shard_map/ppermute | solution.py:24
  221.7 0.7 copy-done.5
  222.4 3.1 %far_mm.1 = bf16[4,352,128]{2,1,0:T(8,128)(2,1)} custom-call(bf16[176,896]{1,0:T(8,128)(2,1)} %copy-done.5, f32[176,1024]{1,0:T(8,128)} %get-tuple-element.15.part, bf16[896,1024]{1,0:T(8,128)(2,1)} %get-tuple-element.16.rest), custom_call_target="tpu_custom_call" | custom-call | flops 322961408 | bytes 3145728 | tf_op jit(solution)/shard_map/far_mm/pallas_call | solution.py:169
  225.6 4.8 %all-to-all-start.2 = ((bf16[4,352,128]{2,1,0:T(8,128)(2,1)}), bf16[4,352,128]{2,1,0:T(8,128)(2,1)S(1)}, u32[]{:S(2)}, u32[]{:S(2)}) async-start(bf16[4,352,128]{2,1,0:T(8,128)(2,1)} %far_mm.1), calls=%async_computation.2 | async-start | bytes 720896 | tf_op jit(solution)/shard_map/all_to_all | solution.py:32
  230.4 5.7 %all-to-all-done.2 = bf16[4,352,128]{2,1,0:T(8,128)(2,1)S(1)} async-done(((bf16[4,352,128]{2,1,0:T(8,128)(2,1)}), bf16[4,352,128]{2,1,0:T(8,128)(2,1)S(1)}, u32[]{:S(2)}, u32[]{:S(2)}) %all-to-all-start.2) | async-done | bytes 360480 | tf_op jit(solution)/shard_map/all_to_all | solution.py:32
  236.2 6.6 %collective-permute-start.15 = (bf16[176,128]{1,0:T(8,128)(2,1)S(1)}, bf16[176,128]{1,0:T(8,128)(2,1)S(1)}, u32[]{:S(2)}, u32[]{:S(2)}) collective-permute-start(bf16[176,128]{1,0:T(8,128)(2,1)S(1)} %fusion.5), channel_id=1, source_target_pairs={{0,4},{4,0},{1,5},{5,1},{2,6},{6,2},{3,7},{7,3},{8,12},{12,8},{9,1... | collective-permute-start | bytes 135176 | tf_op jit(solution)/shard_map/ppermute | solution.py:24
  242.8 8.1 %collective-permute-done.15 = bf16[176,128]{1,0:T(8,128)(2,1)S(1)} collective-permute-done((bf16[176,128]{1,0:T(8,128)(2,1)S(1)}, bf16[176,128]{1,0:T(8,128)(2,1)S(1)}, u32[]{:S(2)}, u32[]{:S(2)}) %collective-permute-start.15) | collective-permute-done | bytes 45088 | tf_op jit(solution)/shard_map/ppermute | solution.py:24
  (65 shorter events, 3.1 us)
Async XLA Ops:
  6.5 39.1 %all-gather.4.cloned.1.call-start = ((), (), s32[]{:S(2)}) async-start(), calls=%async_computation.3 | async-start | bytes 1310720 | tf_op jit(solution)/shard_map/all_gather | solution.py:47
  7.3 98.1 %all-gather.6.cloned.1.call-start = ((), (), s32[]{:S(2)}) async-start(), calls=%async_computation.4 | async-start | bytes 4587520 | tf_op jit(solution)/shard_map/all_gather | solution.py:47
  8.7 38.8 %copy-start.4 = (bf16[176,128]{1,0:T(8,128)(2,1)S(1)}, bf16[176,128]{1,0:T(8,128)(2,1)}, u32[]{:S(2)}) copy-start(bf16[176,128]{1,0:T(8,128)(2,1)} %param.7) | copy-start | bytes 135172
  8.7 54.3 %copy-start.6 = (bf16[176,128]{1,0:T(8,128)(2,1)S(1)}, bf16[176,128]{1,0:T(8,128)(2,1)}, u32[]{:S(2)}) copy-start(bf16[176,128]{1,0:T(8,128)(2,1)} %param.8) | copy-start | bytes 135172
  8.7 14.3 %collective-permute-start.7 = (bf16[128,1792]{1,0:T(8,128)(2,1)S(1)}, bf16[128,1792]{1,0:T(8,128)(2,1)S(1)}, u32[]{:S(2)}, u32[]{:S(2)}) collective-permute-start(bf16[128,1792]{1,0:T(8,128)(2,1)S(1)} %pad_maximum_fusion.1), channel_id=1, source_target_pairs={{0,8},{8,0},{1,9},{9,1},{2,10},{10,2},{3,11},{11,3},{4,12},{12,4},... | collective-permute-start | bytes 1376264 | tf_op jit(solution)/shard_map/ppermute | solution.py:24
  45.6 30.4 %collective-permute-start.3 = (bf16[512,1024]{1,0:T(8,128)(2,1)}, bf16[512,1024]{1,0:T(8,128)(2,1)S(1)}, u32[]{:S(2)}, u32[]{:S(2)}) collective-permute-start(bf16[512,1024]{1,0:T(8,128)(2,1)} %all-gather.4.cloned.1.call-done.own), channel_id=1, source_target_pairs={{0,64},{64,0},{1,65},{65,1},{2,66},{66,2},{3,67},{67,3},{4,68},{68... | collective-permute-start | bytes 3145736 | tf_op jit(solution)/shard_map/ppermute | solution.py:24
  47.5 10.0 %collective-permute-start = (bf16[1,176,128]{2,1,0:T(8,128)(2,1)S(1)}, bf16[1,176,128]{2,1,0:T(8,128)(2,1)S(1)}, u32[]{:S(2)}, u32[]{:S(2)}) collective-permute-start(bf16[1,176,128]{2,1,0:T(8,128)(2,1)S(1)} %bitcast.41), channel_id=1, source_target_pairs={{0,32},{8,40},{16,48},{24,56},{32,0},{40,8},{48,16},{56,24},{1,33}... | collective-permute-start | bytes 135176 | tf_op jit(solution)/shard_map/ppermute | solution.py:24
  57.5 10.3 %collective-permute-start.1 = (bf16[2,176,128]{2,1,0:T(8,128)(2,1)S(1)}, bf16[2,176,128]{2,1,0:T(8,128)(2,1)S(1)}, u32[]{:S(2)}, u32[]{:S(2)}) collective-permute-start(bf16[2,176,128]{2,1,0:T(8,128)(2,1)S(1)} %pad_maximum_fusion.7), channel_id=1, source_target_pairs={{0,16},{8,24},{16,0},{24,8},{32,48},{40,56},{48,32},{56,40},{1,17}... | collective-permute-start | bytes 270344 | tf_op jit(solution)/shard_map/ppermute | solution.py:24
  67.8 7.4 %collective-permute-start.2 = (bf16[4,176,128]{2,1,0:T(8,128)(2,1)S(1)}, bf16[4,176,128]{2,1,0:T(8,128)(2,1)S(1)}, u32[]{:S(2)}, u32[]{:S(2)}) collective-permute-start(bf16[4,176,128]{2,1,0:T(8,128)(2,1)S(1)} %pad_maximum_fusion.4), channel_id=1, source_target_pairs={{0,8},{8,0},{16,24},{24,16},{32,40},{40,32},{48,56},{56,48},{1,9},... | collective-permute-start | bytes 540680 | tf_op jit(solution)/shard_map/ppermute | solution.py:24
  76.0 8.8 %copy-start.7 = (f32[128]{0:T(128)S(1)}, f32[128]{0:T(128)}, u32[]{:S(2)}) copy-start(f32[128]{0:T(128)} %param.10) | copy-start | bytes 1540
  76.0 1.0 copy-start.3
  79.9 10.6 %all-to-all-start = ((bf16[4,352,128]{2,1,0:T(8,128)(2,1)}), bf16[4,352,128]{2,1,0:T(8,128)(2,1)S(1)}, u32[]{:S(2)}, u32[]{:S(2)}) async-start(bf16[4,352,128]{2,1,0:T(8,128)(2,1)} %proj_mm.1), calls=%async_computation | async-start | bytes 720896 | tf_op jit(solution)/shard_map/all_to_all | solution.py:32
  90.7 19.1 %collective-permute-start.4 = (bf16[360,128]{1,0:T(8,128)(2,1)S(1)}, bf16[360,128]{1,0:T(8,128)(2,1)S(1)}, u32[]{:S(2)}, u32[]{:S(2)}) collective-permute-start(bf16[360,128]{1,0:T(8,128)(2,1)S(1)} %pad_maximum_fusion.6), channel_id=1, source_target_pairs={{0,4},{4,0},{1,5},{5,1},{2,6},{6,2},{3,7},{7,3},{8,12},{12,8},{9,1... | collective-permute-start | bytes 276488 | tf_op jit(solution)/shard_map/ppermute | solution.py:24
  105.4 19.8 %collective-permute-start.8 = (bf16[1024,1792]{1,0:T(8,128)(2,1)}, bf16[1024,1792]{1,0:T(8,128)(2,1)}, u32[]{:S(2)}, u32[]{:S(2)}) collective-permute-start(bf16[1024,1792]{1,0:T(8,128)(2,1)} %all-gather.6.cloned.1.call-done.own), channel_id=1, source_target_pairs={{0,64},{64,0},{1,65},{65,1},{2,66},{66,2},{3,67},{67,3},{4,68},{68... | collective-permute-start | bytes 11010056 | tf_op jit(solution)/shard_map/ppermute | solution.py:24
  111.3 13.8 %all-to-all-start.1 = ((bf16[8,360,128]{2,1,0:T(8,128)(2,1)}), bf16[8,360,128]{2,1,0:T(8,128)(2,1)S(1)}, u32[]{:S(2)}, u32[]{:S(2)}) async-start(bf16[8,360,128]{2,1,0:T(8,128)(2,1)} %broadcast_in_dim.33), calls=%async_computation.1 | async-start | bytes 1474560 | tf_op jit(solution)/shard_map/all_to_all | solution.py:32
  115.0 40.6 %all-gather.8.cloned.1.call-start = ((), (), s32[]{:S(2)}) async-start(), calls=%async_computation.5 | async-start | bytes 2293760 | tf_op jit(solution)/shard_map/all_gather | solution.py:47
  125.1 0.9 copy-start
  131.1 34.0 %collective-permute-start.9 = (bf16[88,1792]{1,0:T(8,128)(2,1)}, bf16[88,1792]{1,0:T(8,128)(2,1)S(1)}, u32[]{:S(2)}, u32[]{:S(2)}) collective-permute-start(bf16[88,1792]{1,0:T(8,128)(2,1)} %get-tuple-element.12), channel_id=1, source_target_pairs={{0,16},{16,0},{32,48},{48,32},{1,17},{17,1},{33,49},{49,33},{2,18}... | collective-permute-start | bytes 946184 | tf_op jit(solution)/shard_map/ppermute | solution.py:24
  134.9 22.5 %collective-permute-start.5 = (f32[2,128]{1,0:T(2,128)S(1)}, f32[2,128]{1,0:T(2,128)S(1)}, u32[]{:S(2)}, u32[]{:S(2)}) collective-permute-start(f32[2,128]{1,0:T(2,128)S(1)} %slice_add_fusion.1), channel_id=1, source_target_pairs={{0,16},{16,0},{32,48},{48,32},{1,17},{17,1},{33,49},{49,33},{2,18}... | collective-permute-start | bytes 3080 | tf_op jit(solution)/shard_map/ppermute | solution.py:24
  155.5 54.9 %collective-permute-start.13 = (bf16[896,1024]{1,0:T(8,128)(2,1)}, bf16[896,1024]{1,0:T(8,128)(2,1)S(1)}, u32[]{:S(2)}, u32[]{:S(2)}) collective-permute-start(bf16[896,1024]{1,0:T(8,128)(2,1)} %all-gather.8.cloned.1.call-done.own), channel_id=1, source_target_pairs={{0,64},{64,0},{1,65},{65,1},{2,66},{66,2},{3,67},{67,3},{4,68},{68... | collective-permute-start | bytes 5505032 | tf_op jit(solution)/shard_map/ppermute | solution.py:24
  157.5 11.0 %collective-permute-start.6 = (f32[2,128]{1,0:T(2,128)S(1)}, f32[2,128]{1,0:T(2,128)S(1)}, u32[]{:S(2)}, u32[]{:S(2)}) collective-permute-start(f32[2,128]{1,0:T(2,128)S(1)} %fusion.18), channel_id=1, source_target_pairs={{0,32},{16,48},{32,0},{48,16},{1,33},{17,49},{33,1},{49,17},{2,34}... | collective-permute-start | bytes 3080 | tf_op jit(solution)/shard_map/ppermute | solution.py:24
  166.3 23.4 %collective-permute-start.10 = (bf16[48,1792]{1,0:T(8,128)(2,1)S(1)}, bf16[48,1792]{1,0:T(8,128)(2,1)S(1)}, u32[]{:S(2)}, u32[]{:S(2)}) collective-permute-start(bf16[48,1792]{1,0:T(8,128)(2,1)S(1)} %dynamic-slice_convert_fusion), channel_id=1, source_target_pairs={{0,32},{16,48},{32,0},{48,16},{1,33},{17,49},{33,1},{49,17},{2,34}... | collective-permute-start | bytes 516104 | tf_op jit(solution)/shard_map/ppermute | solution.py:24
  189.8 10.6 %collective-permute-start.11 = (bf16[48,896]{1,0:T(8,128)(2,1)S(1)}, bf16[48,896]{1,0:T(8,128)(2,1)S(1)}, u32[]{:S(2)}, u32[]{:S(2)}) collective-permute-start(bf16[48,896]{1,0:T(8,128)(2,1)S(1)} %fusion.2), channel_id=1, source_target_pairs={{0,32},{16,48},{32,0},{48,16},{1,33},{17,49},{33,1},{49,17},{2,34}... | collective-permute-start | bytes 258056 | tf_op jit(solution)/shard_map/ppermute | solution.py:24
  200.7 9.7 %collective-permute-start.12 = (bf16[88,896]{1,0:T(8,128)(2,1)S(1)}, bf16[88,896]{1,0:T(8,128)(2,1)S(1)}, u32[]{:S(2)}, u32[]{:S(2)}) collective-permute-start(bf16[88,896]{1,0:T(8,128)(2,1)S(1)} %pad_maximum_fusion.5), channel_id=1, source_target_pairs={{0,16},{16,0},{32,48},{48,32},{1,17},{17,1},{33,49},{49,33},{2,18}... | collective-permute-start | bytes 473096 | tf_op jit(solution)/shard_map/ppermute | solution.py:24
  210.4 2.0 copy-start.2
  210.5 2.0 copy-start.1
  210.5 11.3 %collective-permute-start.14 = (bf16[176,896]{1,0:T(8,128)(2,1)S(1)}, bf16[176,896]{1,0:T(8,128)(2,1)S(1)}, u32[]{:S(2)}, u32[]{:S(2)}) collective-permute-start(bf16[176,896]{1,0:T(8,128)(2,1)S(1)} %pad_maximum_fusion.3.x), channel_id=1, source_target_pairs={{0,8},{8,0},{1,9},{9,1},{2,10},{10,2},{3,11},{11,3},{4,12},{12,4},... | collective-permute-start | bytes 946184 | tf_op jit(solution)/shard_map/ppermute | solution.py:24
  221.7 0.7 copy-start.5
  225.6 10.6 %all-to-all-start.2 = ((bf16[4,352,128]{2,1,0:T(8,128)(2,1)}), bf16[4,352,128]{2,1,0:T(8,128)(2,1)S(1)}, u32[]{:S(2)}, u32[]{:S(2)}) async-start(bf16[4,352,128]{2,1,0:T(8,128)(2,1)} %far_mm.1), calls=%async_computation.2 | async-start | bytes 720896 | tf_op jit(solution)/shard_map/all_to_all | solution.py:32
  236.2 14.7 %collective-permute-start.15 = (bf16[176,128]{1,0:T(8,128)(2,1)S(1)}, bf16[176,128]{1,0:T(8,128)(2,1)S(1)}, u32[]{:S(2)}, u32[]{:S(2)}) collective-permute-start(bf16[176,128]{1,0:T(8,128)(2,1)S(1)} %fusion.5), channel_id=1, source_target_pairs={{0,4},{4,0},{1,5},{5,1},{2,6},{6,2},{3,7},{7,3},{8,12},{12,8},{9,1... | collective-permute-start | bytes 135176 | tf_op jit(solution)/shard_map/ppermute | solution.py:24
Sparse Core Ops, SparseCore 0:
  9.4 36.1 all-gather.3
  47.7 51.9 all-gather.5
  117.8 37.6 all-gather.7

commit v10 on v9

--- a/solution.py
+++ b/solution.py
@@ -19,6 +19,11 @@
     return lax.axis_size(axis)
 
 
+def shift(value, axis, step):
+    n = size_of(axis)
+    return lax.ppermute(value, axis, [(i, (i + step) % n) for i in range(n)])
+
+
 def swap(value, axis, bit):
     n = size_of(axis)
     return lax.ppermute(value, axis, [(i, i ^ bit) for i in range(n)])
@@ -43,8 +48,29 @@
     return first, second
 
 
-def gathered(w):
-    own = lax.all_gather(w, "x", axis=0, tiled=True)
+def stack_kernel(*refs):
+    *ins, out = refs
+    height = ins[0].shape[0]
+    for k, ref in enumerate(ins):
+        out[k * height : (k + 1) * height] = ref[...]
+
+
+def stacked(parts):
+    height, width = parts[0].shape
+    vmem = pl.BlockSpec(memory_space=pltpu.VMEM)
+    return pl.pallas_call(
+        stack_kernel,
+        out_shape=jax.ShapeDtypeStruct((len(parts) * height, width), BF),
+        in_specs=[vmem] * len(parts),
+        out_specs=vmem,
+        name="stack",
+    )(*parts)
+
+
+def ring_gathered(w):
+    ring = [1, 2, -1]
+    shards = [w] + [shift(w, "x", k) for k in ring]
+    own = stacked(shards)
     return own, swap(own, "c", 1)
 
 
@@ -85,15 +111,17 @@
 
 
 def both_kernel(at, x, own, other, send, keep):
-    ci, zp, bit = at[0], at[1], (at[2] >> 1) & 1
+    ci, zp, bit, xi = at[0], at[1], (at[2] >> 1) & 1, at[3]
     rows = (x.shape[1] - 8) // 2
 
     def blocks(core):
         parts = []
         for k in range(4):
+            place = (xi + 4 - k) & 3
+            row = pl.multiple_of((place >> 1) * rows, 16)
             for turn in range(2):
-                at_block = (zp ^ turn) * 4 + (k % 2) * 2 + core
-                parts.append(x[at_block, pl.ds((k // 2) * rows, rows)])
+                at_block = (zp ^ turn) * 4 + (place & 1) * 2 + core
+                parts.append(x[at_block, pl.ds(row, rows)])
         return jnp.concatenate(parts, axis=1)
 
     part = dot(blocks(ci), own[...]) + dot(blocks(1 - ci), other[...])
@@ -122,12 +150,12 @@
 
 
 def near_kernel(at, x, own, other, part, rest, whole):
-    ci, zp = at[0], at[1]
+    ci, zp, xi = at[0], at[1], at[3]
     height = own.shape[0] // 4
     half = x.shape[1]
     for ref, core in ((own, ci), (other, 1 - ci)):
         for k in range(4):
-            b = 2 * k + core
+            b = ((xi + 4 - k) & 3) * 2 + core
             to = pl.ds(pl.multiple_of(b * height, 16), height)
             whole[to] = ref[k * height : (k + 1) * height]
     part[...] = dot(x[...], whole[pl.ds(pl.multiple_of(zp * half, 16), half)])
@@ -183,9 +211,9 @@
 
 
 def on_device(attn_out, residual, proj_weight, norm_gain, gate_proj, up_proj, down_proj):
-    ci, zh = lax.axis_index("c"), lax.axis_index("zh")
+    xi, ci, zh = (lax.axis_index(name) for name in ("x", "c", "zh"))
     zq, zp = lax.axis_index("zq"), lax.axis_index("zp")
-    at = jnp.stack([ci, zp, 2 * zq + zp]).astype(jnp.int32)
+    at = jnp.stack([ci, zp, 2 * zq + zp, xi]).astype(jnp.int32)
     rows = attn_out.shape[0]
     ffw = gate_proj.shape[1] // 2
 
@@ -200,9 +228,10 @@
 
     facing = swap(columns(1 - zp), "zp", 1)
     both = jnp.concatenate([columns(zp), facing])
-    proj_own, proj_other = gathered(proj_weight)
-    both_own, both_other = gathered(both)
-    down_own, down_other = gathered(down_proj)
+    both_own, both_other = ring_gathered(both)
+    proj_own = from_everyone(proj_weight, "x").reshape(-1, proj_weight.shape[1])
+    proj_other = swap(proj_own, "c", 1)
+    down_own, down_other = ring_gathered(down_proj)
 
     high = exact(norm_gain)
     mid = exact(norm_gain - high)
@@ -230,11 +259,10 @@
     bit1, bit2 = zq & 1, zq >> 1
     send, keep = both_parts(at, model, both_own, both_other, half)
     got = swap(send, "zq", 1)
-    squares = squares + swap(squares, "zq", 1)
+    squares = sum([swap(squares, "zq", k) for k in (1, 2, 3)], squares)
     sums = keep + got.astype(F32)
     sent = lax.dynamic_slice_in_dim(sums, step * (1 - bit2), TOP, 0).astype(BF)
     got = swap(sent, "zq", 2)
-    squares = squares + swap(squares, "zq", 2)
     sums = lax.dynamic_slice_in_dim(sums, step * bit2, TOP, 0) + got.astype(F32)
     squares = lax.dynamic_slice_in_dim(squares.reshape(256), half * bit1 + step * bit2, TOP, 0)
     inverse = lax.rsqrt(squares / D + 1e-05)[:, None]

time: 259 us -> 272 us (1.050)
  the two profiles are of different devices: /device:TPU:8 before, /device:TPU:6 now
where the time goes in v10:
time: 272 us; the launch traced here: 271 us
  starting transfers between devices  124 us (46%)
  waiting for transfers between devices  107 us (39%)
  Pallas kernels  22.6 us (8%)
  other arithmetic  9.53 us (4%)
  local copies, waits for them, and re-layouts  7.63 us (3%)
    ppermute x17, starting transfers between devices, swap(): return lax.ppermute(value, axis, [(i, i ^ bit) for i in range(n)])  81.1 us
    ppermute x17, waiting for transfers between devices, swap(): return lax.ppermute(value, axis, [(i, i ^ bit) for i in range(n)])  53.1 us
    ppermute x6, waiting for transfers between devices, shift(): return lax.ppermute(value, axis, [(i, (i + step) % n) for i in range(n)])  39.6 us
    all_to_all x4, starting transfers between devices, exchange(): return lax.all_to_all(parts, axis, split_axis=0, concat_axis=0, tiled=True)  26 us
    ppermute x6, starting transfers between devices, shift(): return lax.ppermute(value, axis, [(i, (i + step) % n) for i in range(n)])  17 us
    all_to_all x4, waiting for transfers between devices, exchange(): return lax.all_to_all(parts, axis, split_axis=0, concat_axis=0, tiled=True)  13.9 us
    pallas_call x2, Pallas kernels, stacked(): pl.pallas_call(stack_kernel, out_shape=jax.ShapeDtypeStruct((len(parts) *...  6.91 us
  transfers between devices with their start and end apart: 27, of which 15 were waited for; matrix products, arithmetic and copies ran while one was open for 4% of the time, Pallas kernels for 7%

profile of v10, /device:TPU:6, one launch (start us, length us, event | category | flops | bytes accessed | tf_op | source)
XLA Modules:
  0.0 271.0 jit_solution(12740849100176298600)
XLA Ops:
  0.0 2.1 broadcast_in_dim.34
  2.1 9.3 %all-to-all-start = ((bf16[4,128,1024]{2,1,0:T(8,128)(2,1)}), bf16[4,128,1024]{2,1,0:T(8,128)(2,1)S(1)}, u32[]{:S(2)}, u32[]{:S(2)}) async-start(bf16[4,128,1024]{2,1,0:T(8,128)(2,1)} %broadcast_in_dim.34), calls=%async_computation | async-start | bytes 2097152 | tf_op jit(solution)/shard_map/all_to_all | solution.py:37
  11.6 1.9 collective-permute-start.8
  13.5 6.7 %all-to-all-done = bf16[4,128,1024]{2,1,0:T(8,128)(2,1)S(1)} async-done(((bf16[4,128,1024]{2,1,0:T(8,128)(2,1)}), bf16[4,128,1024]{2,1,0:T(8,128)(2,1)S(1)}, u32[]{:S(2)}, u32[]{:S(2)}) %all-to-all-start) | async-done | bytes 1048608 | tf_op jit(solution)/shard_map/all_to_all | solution.py:37
  20.3 1.9 collective-permute-start.3
  22.2 8.8 %collective-permute-start = (bf16[1,176,128]{2,1,0:T(8,128)(2,1)S(1)}, bf16[1,176,128]{2,1,0:T(8,128)(2,1)S(1)}, u32[]{:S(2)}, u32[]{:S(2)}) collective-permute-start(bf16[1,176,128]{2,1,0:T(8,128)(2,1)S(1)} %bitcast.45), channel_id=1, source_target_pairs={{0,32},{8,40},{16,48},{24,56},{32,0},{40,8},{48,16},{56,24},{1,33}... | collective-permute-start | bytes 135176 | tf_op jit(solution)/shard_map/ppermute | solution.py:29
  31.0 2.3 collective-permute-done
  33.9 5.5 %collective-permute-start.1 = (bf16[2,176,128]{2,1,0:T(8,128)(2,1)}, bf16[2,176,128]{2,1,0:T(8,128)(2,1)}, u32[]{:S(2)}, u32[]{:S(2)}) collective-permute-start(bf16[2,176,128]{2,1,0:T(8,128)(2,1)} %pad_maximum_fusion.7), channel_id=1, source_target_pairs={{0,16},{8,24},{16,0},{24,8},{32,48},{40,56},{48,32},{56,40},{1,17}... | collective-permute-start | bytes 270344 | tf_op jit(solution)/shard_map/ppermute | solution.py:29
  41.3 4.0 %collective-permute-start.9 = (bf16[256,1792]{1,0:T(8,128)(2,1)S(1)}, bf16[256,1792]{1,0:T(8,128)(2,1)}, u32[]{:S(2)}, u32[]{:S(2)}) collective-permute-start(bf16[256,1792]{1,0:T(8,128)(2,1)S(1)} %pad_maximum_fusion.refs_0_), channel_id=1, source_target_pairs={{0,128},{128,256},{256,384},{384,0},{1,129},{129,257},{257,385},{3... | collective-permute-start | bytes 2752520 | tf_op jit(solution)/shard_map/ppermute | solution.py:24
  45.2 1.9 collective-permute-start.10
  47.2 3.3 %collective-permute-start.11 = (bf16[256,1792]{1,0:T(8,128)(2,1)S(1)}, bf16[256,1792]{1,0:T(8,128)(2,1)}, u32[]{:S(2)}, u32[]{:S(2)}) collective-permute-start(bf16[256,1792]{1,0:T(8,128)(2,1)S(1)} %pad_maximum_fusion.refs_0_), channel_id=1, source_target_pairs={{0,384},{128,0},{256,128},{384,256},{1,385},{129,1},{257,129},{385... | collective-permute-start | bytes 2752520 | tf_op jit(solution)/shard_map/ppermute | solution.py:24
  52.2 4.3 %collective-permute-start.2 = (bf16[4,176,128]{2,1,0:T(8,128)(2,1)S(1)}, bf16[4,176,128]{2,1,0:T(8,128)(2,1)S(1)}, u32[]{:S(2)}, u32[]{:S(2)}) collective-permute-start(bf16[4,176,128]{2,1,0:T(8,128)(2,1)S(1)} %pad_maximum_fusion.4), channel_id=1, source_target_pairs={{0,8},{8,0},{16,24},{24,16},{32,40},{40,32},{48,56},{56,48},{1,9},... | collective-permute-start | bytes 540680 | tf_op jit(solution)/shard_map/ppermute | solution.py:29
  57.4 2.6 collective-permute-done.2
  62.7 3.0 %proj_mm.1 = bf16[4,352,128]{2,1,0:T(8,128)(2,1)} custom-call(s32[4]{0:T(128)} %pad_add_fusion.at, bf16[8,176,128]{2,1,0:T(8,128)(2,1)} %pad_maximum_fusion.2.x, bf16[512,1024]{1,0:T(8,128)(2,1)} %bitcast.41, bf16[512,1024]{1,0:T(8,128)(2,1)} %copy-done.5), custom_call_target="tpu_custom_call" | custom-call | flops 369098752 | bytes 3145728 | tf_op jit(solution)/shard_map/proj_mm/pallas_call | solution.py:101
  65.7 4.5 %all-to-all-start.1 = ((bf16[4,352,128]{2,1,0:T(8,128)(2,1)}), bf16[4,352,128]{2,1,0:T(8,128)(2,1)S(1)}, u32[]{:S(2)}, u32[]{:S(2)}) async-start(bf16[4,352,128]{2,1,0:T(8,128)(2,1)} %proj_mm.1), calls=%async_computation.1 | async-start | bytes 720896 | tf_op jit(solution)/shard_map/all_to_all | solution.py:37
  70.2 14.2 %collective-permute-done.9.refs_1_ = bf16[256,1792]{1,0:T(8,128)(2,1)} collective-permute-done((bf16[256,1792]{1,0:T(8,128)(2,1)S(1)}, bf16[256,1792]{1,0:T(8,128)(2,1)}, u32[]{:S(2)}, u32[]{:S(2)}) %collective-permute-start.9) | collective-permute-done | bytes 917536 | tf_op jit(solution)/shard_map/ppermute | solution.py:24
  84.5 5.7 %collective-permute-done.11.refs_3_ = bf16[256,1792]{1,0:T(8,128)(2,1)} collective-permute-done((bf16[256,1792]{1,0:T(8,128)(2,1)S(1)}, bf16[256,1792]{1,0:T(8,128)(2,1)}, u32[]{:S(2)}, u32[]{:S(2)}) %collective-permute-start.11) | collective-permute-done | bytes 917536 | tf_op jit(solution)/shard_map/ppermute | solution.py:24
  90.2 4.0 %stack.54.own = bf16[1024,1792]{1,0:T(8,128)(2,1)} custom-call(bf16[256,1792]{1,0:T(8,128)(2,1)} %copy-done.1, bf16[256,1792]{1,0:T(8,128)(2,1)} %collective-permute-done.9.refs_1_, bf16[256,1792]{1,0:T(8,128)(2,1)} %collective-permute-done.10.refs_2_, bf16[256,1792]{1,0:T(8,128)(2,1)} %collective-permute-done.11.refs_3_), custom_call_target="tpu_custom_call" | custom-call | tf_op jit(solution)/shard_map/stack/pallas_call | solution.py:61
  94.2 1.9 collective-permute-start.12
  96.3 11.7 %collective-permute-start.4 = (bf16[360,128]{1,0:T(8,128)(2,1)S(1)}, bf16[360,128]{1,0:T(8,128)(2,1)S(1)}, u32[]{:S(2)}, u32[]{:S(2)}) collective-permute-start(bf16[360,128]{1,0:T(8,128)(2,1)S(1)} %pad_maximum_fusion.6), channel_id=1, source_target_pairs={{0,4},{4,0},{1,5},{5,1},{2,6},{6,2},{3,7},{7,3},{8,12},{12,8},{9,1... | collective-permute-start | bytes 276488 | tf_op jit(solution)/shard_map/ppermute | solution.py:29
  108.1 4.2 %collective-permute-done.4 = bf16[360,128]{1,0:T(8,128)(2,1)S(1)} collective-permute-done((bf16[360,128]{1,0:T(8,128)(2,1)S(1)}, bf16[360,128]{1,0:T(8,128)(2,1)S(1)}, u32[]{:S(2)}, u32[]{:S(2)}) %collective-permute-start.4) | collective-permute-done | bytes 92192 | tf_op jit(solution)/shard_map/ppermute | solution.py:29
  113.8 7.8 %all-to-all-start.2 = ((bf16[8,360,128]{2,1,0:T(8,128)(2,1)}), bf16[8,360,128]{2,1,0:T(8,128)(2,1)S(1)}, u32[]{:S(2)}, u32[]{:S(2)}) async-start(bf16[8,360,128]{2,1,0:T(8,128)(2,1)} %broadcast_in_dim.37), calls=%async_computation.2 | async-start | bytes 1474560 | tf_op jit(solution)/shard_map/all_to_all | solution.py:37
  121.6 2.5 collective-permute-start.17
  124.1 2.2 collective-permute-start.18
  126.3 3.0 %collective-permute-start.19 = (bf16[224,1024]{1,0:T(8,128)(2,1)S(1)}, bf16[224,1024]{1,0:T(8,128)(2,1)S(1)}, u32[]{:S(2)}, u32[]{:S(2)}) collective-permute-start(bf16[224,1024]{1,0:T(8,128)(2,1)S(1)} %copy-done.6), channel_id=1, source_target_pairs={{0,384},{128,0},{256,128},{384,256},{1,385},{129,1},{257,129},{385... | collective-permute-start | bytes 1376264 | tf_op jit(solution)/shard_map/ppermute | solution.py:24
  129.4 7.5 %collective-permute-done.17.refs_1_ = bf16[224,1024]{1,0:T(8,128)(2,1)S(1)} collective-permute-done((bf16[224,1024]{1,0:T(8,128)(2,1)S(1)}, bf16[224,1024]{1,0:T(8,128)(2,1)S(1)}, u32[]{:S(2)}, u32[]{:S(2)}) %collective-permute-start.17) | collective-permute-done | bytes 458784 | tf_op jit(solution)/shard_map/ppermute | solution.py:24
  136.9 4.1 %collective-permute-done.18.refs_2_ = bf16[224,1024]{1,0:T(8,128)(2,1)S(1)} collective-permute-done((bf16[224,1024]{1,0:T(8,128)(2,1)S(1)}, bf16[224,1024]{1,0:T(8,128)(2,1)S(1)}, u32[]{:S(2)}, u32[]{:S(2)}) %collective-permute-start.18) | collective-permute-done | bytes 458784 | tf_op jit(solution)/shard_map/ppermute | solution.py:24
  141.0 8.1 %collective-permute-done.19.refs_3_ = bf16[224,1024]{1,0:T(8,128)(2,1)S(1)} collective-permute-done((bf16[224,1024]{1,0:T(8,128)(2,1)S(1)}, bf16[224,1024]{1,0:T(8,128)(2,1)S(1)}, u32[]{:S(2)}, u32[]{:S(2)}) %collective-permute-start.19) | collective-permute-done | bytes 458784 | tf_op jit(solution)/shard_map/ppermute | solution.py:24
  149.9 2.9 %stack.55.own = bf16[896,1024]{1,0:T(8,128)(2,1)} custom-call(bf16[224,1024]{1,0:T(8,128)(2,1)} %refs_0_.1, bf16[224,1024]{1,0:T(8,128)(2,1)} %copy-done.7, bf16[224,1024]{1,0:T(8,128)(2,1)} %copy-done.8, bf16[224,1024]{1,0:T(8,128)(2,1)} %copy-done.9), custom_call_target="tpu_custom_call" | custom-call | tf_op jit(solution)/shard_map/stack/pallas_call | solution.py:61
  152.8 1.9 collective-permute-start.20
  155.5 5.1 %both_mm.1 = (bf16[88,1792]{1,0:T(8,128)(2,1)}, f32[88,1792]{1,0:T(8,128)}) custom-call(s32[4]{0:T(128)} %pad_add_fusion.at, bf16[8,360,128]{2,1,0:T(8,128)(2,1)} %copy-done.2, bf16[1024,1792]{1,0:T(8,128)(2,1)} %stack.54.own, bf16[1024,1792]{1,0:T(8,128)(2,1)} %collective-permute-done.12.other), custom_call_target="tpu_custom_call" | custom-call | flops 1291845632 | bytes 9437184 | tf_op jit(solution)/shard_map/both_mm/pallas_call | solution.py:139
  163.3 14.7 %collective-permute-start.7 = (f32[2,128]{1,0:T(2,128)S(1)}, f32[2,128]{1,0:T(2,128)S(1)}, u32[]{:S(2)}, u32[]{:S(2)}) collective-permute-start(f32[2,128]{1,0:T(2,128)S(1)} %slice_add_fusion.1), channel_id=1, source_target_pairs={{0,48},{16,32},{32,16},{48,0},{1,49},{17,33},{33,17},{49,1},{2,50}... | collective-permute-start | bytes 3080 | tf_op jit(solution)/shard_map/ppermute | solution.py:29
  178.0 1.9 collective-permute-start.6
  180.0 2.5 collective-permute-start.5
  183.6 10.2 %collective-permute-start.14 = (bf16[48,1792]{1,0:T(8,128)(2,1)S(1)}, bf16[48,1792]{1,0:T(8,128)(2,1)S(1)}, u32[]{:S(2)}, u32[]{:S(2)}) collective-permute-start(bf16[48,1792]{1,0:T(8,128)(2,1)S(1)} %dynamic-slice_convert_fusion), channel_id=1, source_target_pairs={{0,32},{16,48},{32,0},{48,16},{1,33},{17,49},{33,1},{49,17},{2,34}... | collective-permute-start | bytes 516104 | tf_op jit(solution)/shard_map/ppermute | solution.py:29
  194.0 13.6 %collective-permute-done.14 = bf16[48,1792]{1,0:T(8,128)(2,1)S(1)} collective-permute-done((bf16[48,1792]{1,0:T(8,128)(2,1)S(1)}, bf16[48,1792]{1,0:T(8,128)(2,1)S(1)}, u32[]{:S(2)}, u32[]{:S(2)}) %collective-permute-start.14) | collective-permute-done | bytes 172064 | tf_op jit(solution)/shard_map/ppermute | solution.py:29
  207.8 1.9 collective-permute-start.15
  209.7 10.2 %collective-permute-done.15 = bf16[48,896]{1,0:T(8,128)(2,1)S(1)} collective-permute-done((bf16[48,896]{1,0:T(8,128)(2,1)S(1)}, bf16[48,896]{1,0:T(8,128)(2,1)S(1)}, u32[]{:S(2)}, u32[]{:S(2)}) %collective-permute-start.15) | collective-permute-done | bytes 86048 | tf_op jit(solution)/shard_map/ppermute | solution.py:29
  220.1 1.9 collective-permute-start.16
  222.0 7.2 %collective-permute-done.16 = bf16[88,896]{1,0:T(8,128)(2,1)S(1)} collective-permute-done((bf16[88,896]{1,0:T(8,128)(2,1)S(1)}, bf16[88,896]{1,0:T(8,128)(2,1)S(1)}, u32[]{:S(2)}, u32[]{:S(2)}) %collective-permute-start.16) | collective-permute-done | bytes 157728 | tf_op jit(solution)/shard_map/ppermute | solution.py:29
  229.4 1.9 collective-permute-start.21
  231.3 4.4 %near_mm.1 = (f32[176,1024]{1,0:T(8,128)}, bf16[896,1024]{1,0:T(8,128)(2,1)}) custom-call(s32[4]{0:T(128)} %pad_add_fusion.at, bf16[176,896]{1,0:T(8,128)(2,1)} %copy-done.4, bf16[896,1024]{1,0:T(8,128)(2,1)} %stack.55.own, bf16[896,1024]{1,0:T(8,128)(2,1)} %copy-done.3), custom_call_target="tpu_custom_call" | custom-call | flops 322961408 | bytes 5242880 | tf_op jit(solution)/shard_map/near_mm/pallas_call | solution.py:178
  235.8 4.4 %collective-permute-done.21.x = bf16[176,896]{1,0:T(8,128)(2,1)S(1)} collective-permute-done((bf16[176,896]{1,0:T(8,128)(2,1)S(1)}, bf16[176,896]{1,0:T(8,128)(2,1)S(1)}, u32[]{:S(2)}, u32[]{:S(2)}) %collective-permute-start.21) | collective-permute-done | bytes 315424 | tf_op jit(solution)/shard_map/ppermute | solution.py:29
  240.9 3.1 %far_mm.1 = bf16[4,352,128]{2,1,0:T(8,128)(2,1)} custom-call(bf16[176,896]{1,0:T(8,128)(2,1)} %copy-done.15, f32[176,1024]{1,0:T(8,128)} %get-tuple-element.15.part, bf16[896,1024]{1,0:T(8,128)(2,1)} %get-tuple-element.16.rest), custom_call_target="tpu_custom_call" | custom-call | flops 322961408 | bytes 3145728 | tf_op jit(solution)/shard_map/far_mm/pallas_call | solution.py:197
  244.0 4.4 %all-to-all-start.3 = ((bf16[4,352,128]{2,1,0:T(8,128)(2,1)}), bf16[4,352,128]{2,1,0:T(8,128)(2,1)S(1)}, u32[]{:S(2)}, u32[]{:S(2)}) async-start(bf16[4,352,128]{2,1,0:T(8,128)(2,1)} %far_mm.1), calls=%async_computation.3 | async-start | bytes 720896 | tf_op jit(solution)/shard_map/all_to_all | solution.py:37
  248.4 7.2 %all-to-all-done.3 = bf16[4,352,128]{2,1,0:T(8,128)(2,1)S(1)} async-done(((bf16[4,352,128]{2,1,0:T(8,128)(2,1)}), bf16[4,352,128]{2,1,0:T(8,128)(2,1)S(1)}, u32[]{:S(2)}, u32[]{:S(2)}) %all-to-all-start.3) | async-done | bytes 360480 | tf_op jit(solution)/shard_map/all_to_all | solution.py:37
  255.7 6.1 %collective-permute-start.22 = (bf16[176,128]{1,0:T(8,128)(2,1)S(1)}, bf16[176,128]{1,0:T(8,128)(2,1)S(1)}, u32[]{:S(2)}, u32[]{:S(2)}) collective-permute-start(bf16[176,128]{1,0:T(8,128)(2,1)S(1)} %fusion.5), channel_id=1, source_target_pairs={{0,4},{4,0},{1,5},{5,1},{2,6},{6,2},{3,7},{7,3},{8,12},{12,8},{9,1... | collective-permute-start | bytes 135176 | tf_op jit(solution)/shard_map/ppermute | solution.py:29
  261.8 8.5 %collective-permute-done.22 = bf16[176,128]{1,0:T(8,128)(2,1)S(1)} collective-permute-done((bf16[176,128]{1,0:T(8,128)(2,1)S(1)}, bf16[176,128]{1,0:T(8,128)(2,1)S(1)}, u32[]{:S(2)}, u32[]{:S(2)}) %collective-permute-start.22) | collective-permute-done | bytes 45088 | tf_op jit(solution)/shard_map/ppermute | solution.py:29
  (92 shorter events, 17.0 us)
Async XLA Ops:
  0.0 11.4 %copy-start.11 = (bf16[128,1792]{1,0:T(8,128)(2,1)S(1)}, bf16[128,1792]{1,0:T(8,128)(2,1)}, u32[]{:S(2)}) copy-start(bf16[128,1792]{1,0:T(8,128)(2,1)} %param.12) | copy-start | bytes 1376260
  0.0 11.4 %copy-start.12 = (bf16[128,1792]{1,0:T(8,128)(2,1)S(1)}, bf16[128,1792]{1,0:T(8,128)(2,1)}, u32[]{:S(2)}) copy-start(bf16[128,1792]{1,0:T(8,128)(2,1)} %param.11) | copy-start | bytes 1376260
  2.1 18.1 %all-to-all-start = ((bf16[4,128,1024]{2,1,0:T(8,128)(2,1)}), bf16[4,128,1024]{2,1,0:T(8,128)(2,1)S(1)}, u32[]{:S(2)}, u32[]{:S(2)}) async-start(bf16[4,128,1024]{2,1,0:T(8,128)(2,1)} %broadcast_in_dim.34), calls=%async_computation | async-start | bytes 2097152 | tf_op jit(solution)/shard_map/all_to_all | solution.py:37
  11.4 10.7 %copy-start.13 = (bf16[176,128]{1,0:T(8,128)(2,1)S(1)}, bf16[176,128]{1,0:T(8,128)(2,1)}, u32[]{:S(2)}) copy-start(bf16[176,128]{1,0:T(8,128)(2,1)} %param.7) | copy-start | bytes 135172
  11.6 27.8 %collective-permute-start.8 = (bf16[128,1792]{1,0:T(8,128)(2,1)S(1)}, bf16[128,1792]{1,0:T(8,128)(2,1)S(1)}, u32[]{:S(2)}, u32[]{:S(2)}) collective-permute-start(bf16[128,1792]{1,0:T(8,128)(2,1)S(1)} %pad_maximum_fusion.1), channel_id=1, source_target_pairs={{0,8},{8,0},{1,9},{9,1},{2,10},{10,2},{3,11},{11,3},{4,12},{12,4},... | collective-permute-start | bytes 1376264 | tf_op jit(solution)/shard_map/ppermute | solution.py:29
  20.3 41.5 %copy-start = (bf16[4,128,1024]{2,1,0:T(8,128)(2,1)}, bf16[4,128,1024]{2,1,0:T(8,128)(2,1)S(1)}, u32[]{:S(2)}) copy-start(bf16[4,128,1024]{2,1,0:T(8,128)(2,1)S(1)} %all-to-all-done) | copy-start | bytes 3145732
  20.3 41.5 %collective-permute-start.3 = (bf16[512,1024]{1,0:T(8,128)(2,1)S(1)}, bf16[512,1024]{1,0:T(8,128)(2,1)S(1)}, u32[]{:S(2)}, u32[]{:S(2)}) collective-permute-start(bf16[512,1024]{1,0:T(8,128)(2,1)S(1)} %bitcast.40), channel_id=1, source_target_pairs={{0,64},{64,0},{1,65},{65,1},{2,66},{66,2},{3,67},{67,3},{4,68},{68... | collective-permute-start | bytes 3145736 | tf_op jit(solution)/shard_map/ppermute | solution.py:29
  22.2 11.1 %collective-permute-start = (bf16[1,176,128]{2,1,0:T(8,128)(2,1)S(1)}, bf16[1,176,128]{2,1,0:T(8,128)(2,1)S(1)}, u32[]{:S(2)}, u32[]{:S(2)}) collective-permute-start(bf16[1,176,128]{2,1,0:T(8,128)(2,1)S(1)} %bitcast.45), channel_id=1, source_target_pairs={{0,32},{8,40},{16,48},{24,56},{32,0},{40,8},{48,16},{56,24},{1,33}... | collective-permute-start | bytes 135176 | tf_op jit(solution)/shard_map/ppermute | solution.py:29
  33.3 6.1 %copy-start.14 = (bf16[1,176,128]{2,1,0:T(8,128)(2,1)}, bf16[1,176,128]{2,1,0:T(8,128)(2,1)S(1)}, u32[]{:S(2)}) copy-start(bf16[1,176,128]{2,1,0:T(8,128)(2,1)S(1)} %collective-permute-done) | copy-start | bytes 135172
  33.9 17.4 %collective-permute-start.1 = (bf16[2,176,128]{2,1,0:T(8,128)(2,1)}, bf16[2,176,128]{2,1,0:T(8,128)(2,1)}, u32[]{:S(2)}, u32[]{:S(2)}) collective-permute-start(bf16[2,176,128]{2,1,0:T(8,128)(2,1)} %pad_maximum_fusion.7), channel_id=1, source_target_pairs={{0,16},{8,24},{16,0},{24,8},{32,48},{40,56},{48,32},{56,40},{1,17}... | collective-permute-start | bytes 270344 | tf_op jit(solution)/shard_map/ppermute | solution.py:29
  39.4 0.8 copy-start.10
  41.3 24.5 %copy-start.1 = (bf16[256,1792]{1,0:T(8,128)(2,1)}, bf16[256,1792]{1,0:T(8,128)(2,1)S(1)}, u32[]{:S(2)}) copy-start(bf16[256,1792]{1,0:T(8,128)(2,1)S(1)} %pad_maximum_fusion.refs_0_) | copy-start | bytes 2752516
  41.3 43.2 %collective-permute-start.9 = (bf16[256,1792]{1,0:T(8,128)(2,1)S(1)}, bf16[256,1792]{1,0:T(8,128)(2,1)}, u32[]{:S(2)}, u32[]{:S(2)}) collective-permute-start(bf16[256,1792]{1,0:T(8,128)(2,1)S(1)} %pad_maximum_fusion.refs_0_), channel_id=1, source_target_pairs={{0,128},{128,256},{256,384},{384,0},{1,129},{129,257},{257,385},{3... | collective-permute-start | bytes 2752520 | tf_op jit(solution)/shard_map/ppermute | solution.py:24
  45.2 39.2 %collective-permute-start.10 = (bf16[256,1792]{1,0:T(8,128)(2,1)S(1)}, bf16[256,1792]{1,0:T(8,128)(2,1)}, u32[]{:S(2)}, u32[]{:S(2)}) collective-permute-start(bf16[256,1792]{1,0:T(8,128)(2,1)S(1)} %pad_maximum_fusion.refs_0_), channel_id=1, source_target_pairs={{0,256},{128,384},{256,0},{384,128},{1,257},{129,385},{257,1},{385... | collective-permute-start | bytes 2752520 | tf_op jit(solution)/shard_map/ppermute | solution.py:24
  47.2 43.0 %collective-permute-start.11 = (bf16[256,1792]{1,0:T(8,128)(2,1)S(1)}, bf16[256,1792]{1,0:T(8,128)(2,1)}, u32[]{:S(2)}, u32[]{:S(2)}) collective-permute-start(bf16[256,1792]{1,0:T(8,128)(2,1)S(1)} %pad_maximum_fusion.refs_0_), channel_id=1, source_target_pairs={{0,384},{128,0},{256,128},{384,256},{1,385},{129,1},{257,129},{385... | collective-permute-start | bytes 2752520 | tf_op jit(solution)/shard_map/ppermute | solution.py:24
  52.2 7.8 %collective-permute-start.2 = (bf16[4,176,128]{2,1,0:T(8,128)(2,1)S(1)}, bf16[4,176,128]{2,1,0:T(8,128)(2,1)S(1)}, u32[]{:S(2)}, u32[]{:S(2)}) collective-permute-start(bf16[4,176,128]{2,1,0:T(8,128)(2,1)S(1)} %pad_maximum_fusion.4), channel_id=1, source_target_pairs={{0,8},{8,0},{16,24},{24,16},{32,40},{40,32},{48,56},{56,48},{1,9},... | collective-permute-start | bytes 540680 | tf_op jit(solution)/shard_map/ppermute | solution.py:29
  61.8 8.5 %copy-start.16 = (f32[128]{0:T(128)S(1)}, f32[128]{0:T(128)}, u32[]{:S(2)}) copy-start(f32[128]{0:T(128)} %param.10) | copy-start | bytes 1540
  61.8 1.0 copy-start.5
  65.7 30.4 %all-to-all-start.1 = ((bf16[4,352,128]{2,1,0:T(8,128)(2,1)}), bf16[4,352,128]{2,1,0:T(8,128)(2,1)S(1)}, u32[]{:S(2)}, u32[]{:S(2)}) async-start(bf16[4,352,128]{2,1,0:T(8,128)(2,1)} %proj_mm.1), calls=%async_computation.1 | async-start | bytes 720896 | tf_op jit(solution)/shard_map/all_to_all | solution.py:37
  94.2 60.5 %collective-permute-start.12 = (bf16[1024,1792]{1,0:T(8,128)(2,1)}, bf16[1024,1792]{1,0:T(8,128)(2,1)}, u32[]{:S(2)}, u32[]{:S(2)}) collective-permute-start(bf16[1024,1792]{1,0:T(8,128)(2,1)} %stack.54.own), channel_id=1, source_target_pairs={{0,64},{64,0},{1,65},{65,1},{2,66},{66,2},{3,67},{67,3},{4,68},{68... | collective-permute-start | bytes 11010056 | tf_op jit(solution)/shard_map/ppermute | solution.py:29
  96.3 16.0 %collective-permute-start.4 = (bf16[360,128]{1,0:T(8,128)(2,1)S(1)}, bf16[360,128]{1,0:T(8,128)(2,1)S(1)}, u32[]{:S(2)}, u32[]{:S(2)}) collective-permute-start(bf16[360,128]{1,0:T(8,128)(2,1)S(1)} %pad_maximum_fusion.6), channel_id=1, source_target_pairs={{0,4},{4,0},{1,5},{5,1},{2,6},{6,2},{3,7},{7,3},{8,12},{12,8},{9,1... | collective-permute-start | bytes 276488 | tf_op jit(solution)/shard_map/ppermute | solution.py:29
  108.1 13.5 %copy-start.6 = (bf16[224,1024]{1,0:T(8,128)(2,1)S(1)}, bf16[224,1024]{1,0:T(8,128)(2,1)}, u32[]{:S(2)}) copy-start(bf16[224,1024]{1,0:T(8,128)(2,1)} %refs_0_.1) | copy-start | bytes 1376260
  113.8 40.9 %all-to-all-start.2 = ((bf16[8,360,128]{2,1,0:T(8,128)(2,1)}), bf16[8,360,128]{2,1,0:T(8,128)(2,1)S(1)}, u32[]{:S(2)}, u32[]{:S(2)}) async-start(bf16[8,360,128]{2,1,0:T(8,128)(2,1)} %broadcast_in_dim.37), calls=%async_computation.2 | async-start | bytes 1474560 | tf_op jit(solution)/shard_map/all_to_all | solution.py:37
  121.6 15.3 %collective-permute-start.17 = (bf16[224,1024]{1,0:T(8,128)(2,1)S(1)}, bf16[224,1024]{1,0:T(8,128)(2,1)S(1)}, u32[]{:S(2)}, u32[]{:S(2)}) collective-permute-start(bf16[224,1024]{1,0:T(8,128)(2,1)S(1)} %copy-done.6), channel_id=1, source_target_pairs={{0,128},{128,256},{256,384},{384,0},{1,129},{129,257},{257,385},{3... | collective-permute-start | bytes 1376264 | tf_op jit(solution)/shard_map/ppermute | solution.py:24
  124.1 16.8 %collective-permute-start.18 = (bf16[224,1024]{1,0:T(8,128)(2,1)S(1)}, bf16[224,1024]{1,0:T(8,128)(2,1)S(1)}, u32[]{:S(2)}, u32[]{:S(2)}) collective-permute-start(bf16[224,1024]{1,0:T(8,128)(2,1)S(1)} %copy-done.6), channel_id=1, source_target_pairs={{0,256},{128,384},{256,0},{384,128},{1,257},{129,385},{257,1},{385... | collective-permute-start | bytes 1376264 | tf_op jit(solution)/shard_map/ppermute | solution.py:24
  126.3 22.8 %collective-permute-start.19 = (bf16[224,1024]{1,0:T(8,128)(2,1)S(1)}, bf16[224,1024]{1,0:T(8,128)(2,1)S(1)}, u32[]{:S(2)}, u32[]{:S(2)}) collective-permute-start(bf16[224,1024]{1,0:T(8,128)(2,1)S(1)} %copy-done.6), channel_id=1, source_target_pairs={{0,384},{128,0},{256,128},{384,256},{1,385},{129,1},{257,129},{385... | collective-permute-start | bytes 1376264 | tf_op jit(solution)/shard_map/ppermute | solution.py:24
  136.9 12.2 %copy-start.7 = (bf16[224,1024]{1,0:T(8,128)(2,1)}, bf16[224,1024]{1,0:T(8,128)(2,1)S(1)}, u32[]{:S(2)}) copy-start(bf16[224,1024]{1,0:T(8,128)(2,1)S(1)} %collective-permute-done.17.refs_1_) | copy-start | bytes 1376260
  141.0 8.1 %copy-start.8 = (bf16[224,1024]{1,0:T(8,128)(2,1)}, bf16[224,1024]{1,0:T(8,128)(2,1)S(1)}, u32[]{:S(2)}) copy-start(bf16[224,1024]{1,0:T(8,128)(2,1)S(1)} %collective-permute-done.18.refs_2_) | copy-start | bytes 1376260
  149.1 0.8 copy-start.9
  152.8 76.6 %collective-permute-start.20 = (bf16[896,1024]{1,0:T(8,128)(2,1)}, bf16[896,1024]{1,0:T(8,128)(2,1)S(1)}, u32[]{:S(2)}, u32[]{:S(2)}) collective-permute-start(bf16[896,1024]{1,0:T(8,128)(2,1)} %stack.55.own), channel_id=1, source_target_pairs={{0,64},{64,0},{1,65},{65,1},{2,66},{66,2},{3,67},{67,3},{4,68},{68... | collective-permute-start | bytes 5505032 | tf_op jit(solution)/shard_map/ppermute | solution.py:29
  154.7 0.8 copy-start.2
  160.6 21.8 %collective-permute-start.13 = (bf16[88,1792]{1,0:T(8,128)(2,1)}, bf16[88,1792]{1,0:T(8,128)(2,1)S(1)}, u32[]{:S(2)}, u32[]{:S(2)}) collective-permute-start(bf16[88,1792]{1,0:T(8,128)(2,1)} %get-tuple-element.12), channel_id=1, source_target_pairs={{0,16},{16,0},{32,48},{48,32},{1,17},{17,1},{33,49},{49,33},{2,18}... | collective-permute-start | bytes 946184 | tf_op jit(solution)/shard_map/ppermute | solution.py:29
  163.3 30.6 %collective-permute-start.7 = (f32[2,128]{1,0:T(2,128)S(1)}, f32[2,128]{1,0:T(2,128)S(1)}, u32[]{:S(2)}, u32[]{:S(2)}) collective-permute-start(f32[2,128]{1,0:T(2,128)S(1)} %slice_add_fusion.1), channel_id=1, source_target_pairs={{0,48},{16,32},{32,16},{48,0},{1,49},{17,33},{33,17},{49,1},{2,50}... | collective-permute-start | bytes 3080 | tf_op jit(solution)/shard_map/ppermute | solution.py:29
  178.0 15.9 %collective-permute-start.6 = (f32[2,128]{1,0:T(2,128)S(1)}, f32[2,128]{1,0:T(2,128)S(1)}, u32[]{:S(2)}, u32[]{:S(2)}) collective-permute-start(f32[2,128]{1,0:T(2,128)S(1)} %slice_add_fusion.1), channel_id=1, source_target_pairs={{0,32},{16,48},{32,0},{48,16},{1,33},{17,49},{33,1},{49,17},{2,34}... | collective-permute-start | bytes 3080 | tf_op jit(solution)/shard_map/ppermute | solution.py:29
  180.0 13.9 %collective-permute-start.5 = (f32[2,128]{1,0:T(2,128)S(1)}, f32[2,128]{1,0:T(2,128)S(1)}, u32[]{:S(2)}, u32[]{:S(2)}) collective-permute-start(f32[2,128]{1,0:T(2,128)S(1)} %slice_add_fusion.1), channel_id=1, source_target_pairs={{0,16},{16,0},{32,48},{48,32},{1,17},{17,1},{33,49},{49,33},{2,18}... | collective-permute-start | bytes 3080 | tf_op jit(solution)/shard_map/ppermute | solution.py:29
  183.6 24.0 %collective-permute-start.14 = (bf16[48,1792]{1,0:T(8,128)(2,1)S(1)}, bf16[48,1792]{1,0:T(8,128)(2,1)S(1)}, u32[]{:S(2)}, u32[]{:S(2)}) collective-permute-start(bf16[48,1792]{1,0:T(8,128)(2,1)S(1)} %dynamic-slice_convert_fusion), channel_id=1, source_target_pairs={{0,32},{16,48},{32,0},{48,16},{1,33},{17,49},{33,1},{49,17},{2,34}... | collective-permute-start | bytes 516104 | tf_op jit(solution)/shard_map/ppermute | solution.py:29
  207.8 12.1 %collective-permute-start.15 = (bf16[48,896]{1,0:T(8,128)(2,1)S(1)}, bf16[48,896]{1,0:T(8,128)(2,1)S(1)}, u32[]{:S(2)}, u32[]{:S(2)}) collective-permute-start(bf16[48,896]{1,0:T(8,128)(2,1)S(1)} %fusion.2), channel_id=1, source_target_pairs={{0,32},{16,48},{32,0},{48,16},{1,33},{17,49},{33,1},{49,17},{2,34}... | collective-permute-start | bytes 258056 | tf_op jit(solution)/shard_map/ppermute | solution.py:29
  220.1 9.2 %collective-permute-start.16 = (bf16[88,896]{1,0:T(8,128)(2,1)S(1)}, bf16[88,896]{1,0:T(8,128)(2,1)S(1)}, u32[]{:S(2)}, u32[]{:S(2)}) collective-permute-start(bf16[88,896]{1,0:T(8,128)(2,1)S(1)} %pad_maximum_fusion.5), channel_id=1, source_target_pairs={{0,16},{16,0},{32,48},{48,32},{1,17},{17,1},{33,49},{49,33},{2,18}... | collective-permute-start | bytes 473096 | tf_op jit(solution)/shard_map/ppermute | solution.py:29
  229.3 2.0 copy-start.4
  229.4 2.0 copy-start.3
  229.4 10.8 %collective-permute-start.21 = (bf16[176,896]{1,0:T(8,128)(2,1)S(1)}, bf16[176,896]{1,0:T(8,128)(2,1)S(1)}, u32[]{:S(2)}, u32[]{:S(2)}) collective-permute-start(bf16[176,896]{1,0:T(8,128)(2,1)S(1)} %pad_maximum_fusion.3.x), channel_id=1, source_target_pairs={{0,8},{8,0},{1,9},{9,1},{2,10},{10,2},{3,11},{11,3},{4,12},{12,4},... | collective-permute-start | bytes 946184 | tf_op jit(solution)/shard_map/ppermute | solution.py:29
  240.2 0.7 copy-start.15
  244.0 11.6 %all-to-all-start.3 = ((bf16[4,352,128]{2,1,0:T(8,128)(2,1)}), bf16[4,352,128]{2,1,0:T(8,128)(2,1)S(1)}, u32[]{:S(2)}, u32[]{:S(2)}) async-start(bf16[4,352,128]{2,1,0:T(8,128)(2,1)} %far_mm.1), calls=%async_computation.3 | async-start | bytes 720896 | tf_op jit(solution)/shard_map/all_to_all | solution.py:37
  255.7 14.7 %collective-permute-start.22 = (bf16[176,128]{1,0:T(8,128)(2,1)S(1)}, bf16[176,128]{1,0:T(8,128)(2,1)S(1)}, u32[]{:S(2)}, u32[]{:S(2)}) collective-permute-start(bf16[176,128]{1,0:T(8,128)(2,1)S(1)} %fusion.5), channel_id=1, source_target_pairs={{0,4},{4,0},{1,5},{5,1},{2,6},{6,2},{3,7},{7,3},{8,12},{12,8},{9,1... | collective-permute-start | bytes 135176 | tf_op jit(solution)/shard_map/ppermute | solution.py:29

commit v11 on v10

--- a/solution.py
+++ b/solution.py
@@ -78,7 +78,8 @@
     return jnp.dot(a, b, preferred_element_type=F32)
 
 
-def proj_kernel(at, x, own, other, out):
+def proj_kernel(at, first, second, third, fourth, own, other, out, x):
+    x[0], x[1], x[2:4], x[4:8] = first[0], second[0], third[...], fourth[...]
     ci, zl = at[0], at[2]
     rows = x.shape[1]
 
@@ -95,19 +96,20 @@
             out[y, zh * rows : (zh + 1) * rows] = part[:, n : n + 128]
 
 
-def proj_parts(at, x, own, other):
-    rows = x.shape[1]
+def proj_parts(at, pieces, own, other):
+    rows = pieces[0].shape[1]
     vmem = pl.BlockSpec(memory_space=pltpu.VMEM)
     return pl.pallas_call(
         proj_kernel,
         out_shape=jax.ShapeDtypeStruct((4, 2 * rows, 128), BF),
-        in_specs=[pl.BlockSpec(memory_space=pltpu.SMEM), vmem, vmem, vmem],
+        in_specs=[pl.BlockSpec(memory_space=pltpu.SMEM)] + [vmem] * 6,
         out_specs=vmem,
+        scratch_shapes=[pltpu.VMEM((8, rows, 128), BF)],
         cost_estimate=pl.CostEstimate(
             flops=2 * rows * 1024 * 1024, bytes_accessed=3 << 20, transcendentals=0
         ),
         name="proj_mm",
-    )(at, x, own, other)
+    )(at, *pieces, own, other)
 
 
 def both_kernel(at, x, own, other, send, keep):
@@ -218,9 +220,10 @@
     ffw = gate_proj.shape[1] // 2
 
     cols = attn_out[None]
+    pieces = [cols]
     for bit in (4, 2, 1):
-        arrived = swap(cols, ZL, bit)
-        cols = jnp.concatenate([cols, arrived])
+        pieces.append(swap(cols, ZL, bit))
+        cols = jnp.concatenate(pieces)
 
     def columns(which):
         halves = [lax.dynamic_slice_in_dim(w, which * ffw, ffw, 1) for w in (gate_proj, up_proj)]
@@ -238,7 +241,8 @@
     low = norm_gain - high - mid
     gains = jnp.pad(jnp.stack([high, mid, low]), ((0, 5), (0, 0)))
 
-    part = proj_parts(at, cols, proj_own, proj_other)
+    part = proj_parts(at, pieces, proj_own, proj_other)
+    part, residual = lax.optimization_barrier((part, residual))
     near = exchange(part, "y").astype(F32).sum(axis=0).reshape(2, rows, 128)
     mine = jnp.arange(2)[:, None, None] == zh
     near = jnp.where(mine, near + residual.astype(F32), near).reshape(2 * rows, 128)

time: 272 us -> 261 us (0.960)
  starting transfers between devices: 124 us -> 114 us
  other arithmetic: 9.53 us -> 6.34 us
    ppermute x17, starting transfers between devices: 81.1 us -> 66.4 us  [swap(): return lax.ppermute(value, axis, [(i, i ^ bit) for i in range(n)])]
    ppermute x17, waiting for transfers between devices: 53.1 us -> 61.9 us  [swap(): return lax.ppermute(value, axis, [(i, i ^ bit) for i in range(n)])]
    ppermute x6, waiting for transfers between devices: 39.6 us -> 31.8 us  [shift(): return lax.ppermute(value, axis, [(i, (i + step) % n) for i in range(n)])]
    all_to_all x4, starting transfers between devices: 26 us -> 30.3 us  [exchange(): return lax.all_to_all(parts, axis, split_axis=0, concat_axis=0, tiled=True)]
  transfers between devices with their start and end apart: 27 -> 27, of which waited for: 15 -> 16; matrix products, arithmetic and copies ran while one was open for 4% -> 3% of each run, Pallas kernels for 7% -> 8%
where the time goes in v11:
time: 261 us; the launch traced here: 260 us
  starting transfers between devices  114 us (44%)
  waiting for transfers between devices  108 us (41%)
  Pallas kernels  22.7 us (9%)
  local copies, waits for them, and re-layouts  8.97 us (3%)
  other arithmetic  6.34 us (2%)
    ppermute x17, starting transfers between devices, swap(): return lax.ppermute(value, axis, [(i, i ^ bit) for i in range(n)])  66.4 us
    ppermute x17, waiting for transfers between devices, swap(): return lax.ppermute(value, axis, [(i, i ^ bit) for i in range(n)])  61.9 us
    ppermute x6, waiting for transfers between devices, shift(): return lax.ppermute(value, axis, [(i, (i + step) % n) for i in range(n)])  31.8 us
    all_to_all x4, starting transfers between devices, exchange(): return lax.all_to_all(parts, axis, split_axis=0, concat_axis=0, tiled=True)  30.3 us
    ppermute x6, starting transfers between devices, shift(): return lax.ppermute(value, axis, [(i, (i + step) % n) for i in range(n)])  17 us
    all_to_all x4, waiting for transfers between devices, exchange(): return lax.all_to_all(parts, axis, split_axis=0, concat_axis=0, tiled=True)  13.9 us
    pallas_call x2, Pallas kernels, stacked(): pl.pallas_call(stack_kernel, out_shape=jax.ShapeDtypeStruct((len(parts) *...  6.93 us
    unnamed x40, local copies, waits for them, and re-layouts  5.4 us
  transfers between devices with their start and end apart: 27, of which 16 were waited for; matrix products, arithmetic and copies ran while one was open for 3% of the time, Pallas kernels for 8%

profile of v11, /device:TPU:6, one launch (start us, length us, event | category | flops | bytes accessed | tf_op | source)
XLA Modules:
  0.0 260.1 jit_solution(6438903144249319510)
XLA Ops:
  0.0 2.1 broadcast_in_dim.34
  2.2 9.3 %all-to-all-start = ((bf16[4,128,1024]{2,1,0:T(8,128)(2,1)}), bf16[4,128,1024]{2,1,0:T(8,128)(2,1)S(1)}, u32[]{:S(2)}, u32[]{:S(2)}) async-start(bf16[4,128,1024]{2,1,0:T(8,128)(2,1)} %broadcast_in_dim.34), calls=%async_computation | async-start | bytes 2097152 | tf_op jit(solution)/shard_map/all_to_all | solution.py:37
  11.6 1.9 collective-permute-start.8
  13.5 6.7 %all-to-all-done = bf16[4,128,1024]{2,1,0:T(8,128)(2,1)S(1)} async-done(((bf16[4,128,1024]{2,1,0:T(8,128)(2,1)}), bf16[4,128,1024]{2,1,0:T(8,128)(2,1)S(1)}, u32[]{:S(2)}, u32[]{:S(2)}) %all-to-all-start) | async-done | bytes 1048608 | tf_op jit(solution)/shard_map/all_to_all | solution.py:37
  22.2 8.8 %collective-permute-start = (bf16[1,176,128]{2,1,0:T(8,128)(2,1)S(1)}, bf16[1,176,128]{2,1,0:T(8,128)(2,1)S(1)}, u32[]{:S(2)}, u32[]{:S(2)}) collective-permute-start(bf16[1,176,128]{2,1,0:T(8,128)(2,1)S(1)} %bitcast.46), channel_id=1, source_target_pairs={{0,32},{8,40},{16,48},{24,56},{32,0},{40,8},{48,16},{56,24},{1,33}... | collective-permute-start | bytes 135176 | tf_op jit(solution)/shard_map/ppermute | solution.py:29
  32.9 4.0 %collective-permute-start.9 = (bf16[256,1792]{1,0:T(8,128)(2,1)S(1)}, bf16[256,1792]{1,0:T(8,128)(2,1)}, u32[]{:S(2)}, u32[]{:S(2)}) collective-permute-start(bf16[256,1792]{1,0:T(8,128)(2,1)S(1)} %pad_maximum_fusion.refs_0_), channel_id=1, source_target_pairs={{0,128},{128,256},{256,384},{384,0},{1,129},{129,257},{257,385},{3... | collective-permute-start | bytes 2752520 | tf_op jit(solution)/shard_map/ppermute | solution.py:24
  36.8 1.9 collective-permute-start.10
  38.8 3.3 %collective-permute-start.11 = (bf16[256,1792]{1,0:T(8,128)(2,1)S(1)}, bf16[256,1792]{1,0:T(8,128)(2,1)}, u32[]{:S(2)}, u32[]{:S(2)}) collective-permute-start(bf16[256,1792]{1,0:T(8,128)(2,1)S(1)} %pad_maximum_fusion.refs_0_), channel_id=1, source_target_pairs={{0,384},{128,0},{256,128},{384,256},{1,385},{129,1},{257,129},{385... | collective-permute-start | bytes 2752520 | tf_op jit(solution)/shard_map/ppermute | solution.py:24
  42.7 5.2 %collective-permute-start.1 = (bf16[2,176,128]{2,1,0:T(8,128)(2,1)S(1)}, bf16[2,176,128]{2,1,0:T(8,128)(2,1)S(1)}, u32[]{:S(2)}, u32[]{:S(2)}) collective-permute-start(bf16[2,176,128]{2,1,0:T(8,128)(2,1)S(1)} %pad_maximum_fusion.6), channel_id=1, source_target_pairs={{0,16},{8,24},{16,0},{24,8},{32,48},{40,56},{48,32},{56,40},{1,17}... | collective-permute-start | bytes 270344 | tf_op jit(solution)/shard_map/ppermute | solution.py:29
  47.9 4.4 %collective-permute-done.1.third = bf16[2,176,128]{2,1,0:T(8,128)(2,1)S(1)} collective-permute-done((bf16[2,176,128]{2,1,0:T(8,128)(2,1)S(1)}, bf16[2,176,128]{2,1,0:T(8,128)(2,1)S(1)}, u32[]{:S(2)}, u32[]{:S(2)}) %collective-permute-start.1) | collective-permute-done | bytes 90144 | tf_op jit(solution)/shard_map/ppermute | solution.py:29
  53.2 2.3 collective-permute-start.2
  56.3 4.3 %collective-permute-done.2.fourth = bf16[4,176,128]{2,1,0:T(8,128)(2,1)S(1)} collective-permute-done((bf16[4,176,128]{2,1,0:T(8,128)(2,1)S(1)}, bf16[4,176,128]{2,1,0:T(8,128)(2,1)S(1)}, u32[]{:S(2)}, u32[]{:S(2)}) %collective-permute-start.2) | collective-permute-done | bytes 180256 | tf_op jit(solution)/shard_map/ppermute | solution.py:29
  62.2 3.1 %proj_mm.1 = bf16[4,352,128]{2,1,0:T(8,128)(2,1)} custom-call(s32[4]{0:T(128)} %pad_add_fusion.at, bf16[1,176,128]{2,1,0:T(8,128)(2,1)} %bitcast.45, bf16[1,176,128]{2,1,0:T(8,128)(2,1)} %copy-done.14, bf16[2,176,128]{2,1,0:T(8,128)(2,1)} %copy-done.15, bf16[4,176,128]{2,1,0:T(8,128)(2,1)} %copy-done.17, bf16[512,1024]{1,0:T(8,128)(2,1)} %bitcast.41, ...), custom_call_target="tpu_custom_call" | custom-call | flops 369098752 | bytes 3145728 | tf_op jit(solution)/shard_map/proj_mm/pallas_call | solution.py:102
  65.3 4.5 %all-to-all-start.1 = ((bf16[4,352,128]{2,1,0:T(8,128)(2,1)}), bf16[4,352,128]{2,1,0:T(8,128)(2,1)S(1)}, u32[]{:S(2)}, u32[]{:S(2)}) async-start(bf16[4,352,128]{2,1,0:T(8,128)(2,1)} %proj_mm.1), calls=%async_computation.1 | async-start | bytes 720896 | tf_op jit(solution)/shard_map/all_to_all | solution.py:37
  69.8 6.7 %collective-permute-done.9.refs_1_ = bf16[256,1792]{1,0:T(8,128)(2,1)} collective-permute-done((bf16[256,1792]{1,0:T(8,128)(2,1)S(1)}, bf16[256,1792]{1,0:T(8,128)(2,1)}, u32[]{:S(2)}, u32[]{:S(2)}) %collective-permute-start.9) | collective-permute-done | bytes 917536 | tf_op jit(solution)/shard_map/ppermute | solution.py:24
  76.5 5.7 %collective-permute-done.11.refs_3_ = bf16[256,1792]{1,0:T(8,128)(2,1)} collective-permute-done((bf16[256,1792]{1,0:T(8,128)(2,1)S(1)}, bf16[256,1792]{1,0:T(8,128)(2,1)}, u32[]{:S(2)}, u32[]{:S(2)}) %collective-permute-start.11) | collective-permute-done | bytes 917536 | tf_op jit(solution)/shard_map/ppermute | solution.py:24
  82.2 4.0 %stack.54.own = bf16[1024,1792]{1,0:T(8,128)(2,1)} custom-call(bf16[256,1792]{1,0:T(8,128)(2,1)} %copy-done.1, bf16[256,1792]{1,0:T(8,128)(2,1)} %collective-permute-done.9.refs_1_, bf16[256,1792]{1,0:T(8,128)(2,1)} %collective-permute-done.10.refs_2_, bf16[256,1792]{1,0:T(8,128)(2,1)} %collective-permute-done.11.refs_3_), custom_call_target="tpu_custom_call" | custom-call | tf_op jit(solution)/shard_map/stack/pallas_call | solution.py:61
  86.2 1.9 collective-permute-start.12
  88.4 10.9 %collective-permute-start.4 = (bf16[360,128]{1,0:T(8,128)(2,1)S(1)}, bf16[360,128]{1,0:T(8,128)(2,1)S(1)}, u32[]{:S(2)}, u32[]{:S(2)}) collective-permute-start(bf16[360,128]{1,0:T(8,128)(2,1)S(1)} %pad_maximum_fusion.5), channel_id=1, source_target_pairs={{0,4},{4,0},{1,5},{5,1},{2,6},{6,2},{3,7},{7,3},{8,12},{12,8},{9,1... | collective-permute-start | bytes 276488 | tf_op jit(solution)/shard_map/ppermute | solution.py:29
  99.4 4.7 %collective-permute-done.4 = bf16[360,128]{1,0:T(8,128)(2,1)S(1)} collective-permute-done((bf16[360,128]{1,0:T(8,128)(2,1)S(1)}, bf16[360,128]{1,0:T(8,128)(2,1)S(1)}, u32[]{:S(2)}, u32[]{:S(2)}) %collective-permute-start.4) | collective-permute-done | bytes 92192 | tf_op jit(solution)/shard_map/ppermute | solution.py:29
  105.7 11.7 %all-to-all-start.2 = ((bf16[8,360,128]{2,1,0:T(8,128)(2,1)}), bf16[8,360,128]{2,1,0:T(8,128)(2,1)S(1)}, u32[]{:S(2)}, u32[]{:S(2)}) async-start(bf16[8,360,128]{2,1,0:T(8,128)(2,1)} %broadcast_in_dim.37), calls=%async_computation.2 | async-start | bytes 1474560 | tf_op jit(solution)/shard_map/all_to_all | solution.py:37
  117.4 2.5 collective-permute-start.17
  119.9 2.2 collective-permute-start.18
  122.1 3.0 %collective-permute-start.19 = (bf16[224,1024]{1,0:T(8,128)(2,1)S(1)}, bf16[224,1024]{1,0:T(8,128)(2,1)S(1)}, u32[]{:S(2)}, u32[]{:S(2)}) collective-permute-start(bf16[224,1024]{1,0:T(8,128)(2,1)S(1)} %copy-done.6), channel_id=1, source_target_pairs={{0,384},{128,0},{256,128},{384,256},{1,385},{129,1},{257,129},{385... | collective-permute-start | bytes 1376264 | tf_op jit(solution)/shard_map/ppermute | solution.py:24
  125.2 7.5 %collective-permute-done.17.refs_1_ = bf16[224,1024]{1,0:T(8,128)(2,1)S(1)} collective-permute-done((bf16[224,1024]{1,0:T(8,128)(2,1)S(1)}, bf16[224,1024]{1,0:T(8,128)(2,1)S(1)}, u32[]{:S(2)}, u32[]{:S(2)}) %collective-permute-start.17) | collective-permute-done | bytes 458784 | tf_op jit(solution)/shard_map/ppermute | solution.py:24
  132.7 4.1 %collective-permute-done.18.refs_2_ = bf16[224,1024]{1,0:T(8,128)(2,1)S(1)} collective-permute-done((bf16[224,1024]{1,0:T(8,128)(2,1)S(1)}, bf16[224,1024]{1,0:T(8,128)(2,1)S(1)}, u32[]{:S(2)}, u32[]{:S(2)}) %collective-permute-start.18) | collective-permute-done | bytes 458784 | tf_op jit(solution)/shard_map/ppermute | solution.py:24
  136.8 7.9 %collective-permute-done.19.refs_3_ = bf16[224,1024]{1,0:T(8,128)(2,1)S(1)} collective-permute-done((bf16[224,1024]{1,0:T(8,128)(2,1)S(1)}, bf16[224,1024]{1,0:T(8,128)(2,1)S(1)}, u32[]{:S(2)}, u32[]{:S(2)}) %collective-permute-start.19) | collective-permute-done | bytes 458784 | tf_op jit(solution)/shard_map/ppermute | solution.py:24
  145.4 2.9 %stack.55.own = bf16[896,1024]{1,0:T(8,128)(2,1)} custom-call(bf16[224,1024]{1,0:T(8,128)(2,1)} %refs_0_.1, bf16[224,1024]{1,0:T(8,128)(2,1)} %copy-done.7, bf16[224,1024]{1,0:T(8,128)(2,1)} %copy-done.8, bf16[224,1024]{1,0:T(8,128)(2,1)} %copy-done.9), custom_call_target="tpu_custom_call" | custom-call | tf_op jit(solution)/shard_map/stack/pallas_call | solution.py:61
  148.3 1.9 collective-permute-start.20
  151.1 5.1 %both_mm.1 = (bf16[88,1792]{1,0:T(8,128)(2,1)}, f32[88,1792]{1,0:T(8,128)}) custom-call(s32[4]{0:T(128)} %pad_add_fusion.at, bf16[8,360,128]{2,1,0:T(8,128)(2,1)} %copy-done.2, bf16[1024,1792]{1,0:T(8,128)(2,1)} %stack.54.own, bf16[1024,1792]{1,0:T(8,128)(2,1)} %collective-permute-done.12.other), custom_call_target="tpu_custom_call" | custom-call | flops 1291845632 | bytes 9437184 | tf_op jit(solution)/shard_map/both_mm/pallas_call | solution.py:141
  158.9 1.9 collective-permute-start.7
  160.8 8.4 %collective-permute-start.6 = (f32[2,128]{1,0:T(2,128)S(1)}, f32[2,128]{1,0:T(2,128)S(1)}, u32[]{:S(2)}, u32[]{:S(2)}) collective-permute-start(f32[2,128]{1,0:T(2,128)S(1)} %slice_add_fusion.1), channel_id=1, source_target_pairs={{0,32},{16,48},{32,0},{48,16},{1,33},{17,49},{33,1},{49,17},{2,34}... | collective-permute-start | bytes 3080 | tf_op jit(solution)/shard_map/ppermute | solution.py:29
  169.2 3.7 %collective-permute-start.5 = (f32[2,128]{1,0:T(2,128)S(1)}, f32[2,128]{1,0:T(2,128)S(1)}, u32[]{:S(2)}, u32[]{:S(2)}) collective-permute-start(f32[2,128]{1,0:T(2,128)S(1)} %slice_add_fusion.1), channel_id=1, source_target_pairs={{0,16},{16,0},{32,48},{48,32},{1,17},{17,1},{33,49},{49,33},{2,18}... | collective-permute-start | bytes 3080 | tf_op jit(solution)/shard_map/ppermute | solution.py:29
  172.9 3.0 %collective-permute-done.13 = bf16[88,1792]{1,0:T(8,128)(2,1)S(1)} collective-permute-done((bf16[88,1792]{1,0:T(8,128)(2,1)}, bf16[88,1792]{1,0:T(8,128)(2,1)S(1)}, u32[]{:S(2)}, u32[]{:S(2)}) %collective-permute-start.13) | collective-permute-done | bytes 315424 | tf_op jit(solution)/shard_map/ppermute | solution.py:29
  177.1 1.9 collective-permute-start.14
  179.2 19.0 %collective-permute-done.14 = bf16[48,1792]{1,0:T(8,128)(2,1)S(1)} collective-permute-done((bf16[48,1792]{1,0:T(8,128)(2,1)S(1)}, bf16[48,1792]{1,0:T(8,128)(2,1)S(1)}, u32[]{:S(2)}, u32[]{:S(2)}) %collective-permute-start.14) | collective-permute-done | bytes 172064 | tf_op jit(solution)/shard_map/ppermute | solution.py:29
  198.4 1.9 collective-permute-start.15
  200.3 8.4 %collective-permute-done.15 = bf16[48,896]{1,0:T(8,128)(2,1)S(1)} collective-permute-done((bf16[48,896]{1,0:T(8,128)(2,1)S(1)}, bf16[48,896]{1,0:T(8,128)(2,1)S(1)}, u32[]{:S(2)}, u32[]{:S(2)}) %collective-permute-start.15) | collective-permute-done | bytes 86048 | tf_op jit(solution)/shard_map/ppermute | solution.py:29
  208.8 1.9 collective-permute-start.16
  210.8 6.9 %collective-permute-done.16 = bf16[88,896]{1,0:T(8,128)(2,1)S(1)} collective-permute-done((bf16[88,896]{1,0:T(8,128)(2,1)S(1)}, bf16[88,896]{1,0:T(8,128)(2,1)S(1)}, u32[]{:S(2)}, u32[]{:S(2)}) %collective-permute-start.16) | collective-permute-done | bytes 157728 | tf_op jit(solution)/shard_map/ppermute | solution.py:29
  217.8 1.9 collective-permute-start.21
  219.8 4.5 %near_mm.1 = (f32[176,1024]{1,0:T(8,128)}, bf16[896,1024]{1,0:T(8,128)(2,1)}) custom-call(s32[4]{0:T(128)} %pad_add_fusion.at, bf16[176,896]{1,0:T(8,128)(2,1)} %copy-done.4, bf16[896,1024]{1,0:T(8,128)(2,1)} %stack.55.own, bf16[896,1024]{1,0:T(8,128)(2,1)} %copy-done.3), custom_call_target="tpu_custom_call" | custom-call | flops 322961408 | bytes 5242880 | tf_op jit(solution)/shard_map/near_mm/pallas_call | solution.py:180
  224.2 4.1 %collective-permute-done.21.x = bf16[176,896]{1,0:T(8,128)(2,1)S(1)} collective-permute-done((bf16[176,896]{1,0:T(8,128)(2,1)S(1)}, bf16[176,896]{1,0:T(8,128)(2,1)S(1)}, u32[]{:S(2)}, u32[]{:S(2)}) %collective-permute-start.21) | collective-permute-done | bytes 315424 | tf_op jit(solution)/shard_map/ppermute | solution.py:29
  229.0 3.1 %far_mm.1 = bf16[4,352,128]{2,1,0:T(8,128)(2,1)} custom-call(bf16[176,896]{1,0:T(8,128)(2,1)} %copy-done.16, f32[176,1024]{1,0:T(8,128)} %get-tuple-element.19.part, bf16[896,1024]{1,0:T(8,128)(2,1)} %get-tuple-element.20.rest), custom_call_target="tpu_custom_call" | custom-call | flops 322961408 | bytes 3145728 | tf_op jit(solution)/shard_map/far_mm/pallas_call | solution.py:199
  232.2 4.9 %all-to-all-start.3 = ((bf16[4,352,128]{2,1,0:T(8,128)(2,1)}), bf16[4,352,128]{2,1,0:T(8,128)(2,1)S(1)}, u32[]{:S(2)}, u32[]{:S(2)}) async-start(bf16[4,352,128]{2,1,0:T(8,128)(2,1)} %far_mm.1), calls=%async_computation.3 | async-start | bytes 720896 | tf_op jit(solution)/shard_map/all_to_all | solution.py:37
  237.0 7.2 %all-to-all-done.3 = bf16[4,352,128]{2,1,0:T(8,128)(2,1)S(1)} async-done(((bf16[4,352,128]{2,1,0:T(8,128)(2,1)}), bf16[4,352,128]{2,1,0:T(8,128)(2,1)S(1)}, u32[]{:S(2)}, u32[]{:S(2)}) %all-to-all-start.3) | async-done | bytes 360480 | tf_op jit(solution)/shard_map/all_to_all | solution.py:37
  244.3 8.0 %collective-permute-start.22 = (bf16[176,128]{1,0:T(8,128)(2,1)S(1)}, bf16[176,128]{1,0:T(8,128)(2,1)S(1)}, u32[]{:S(2)}, u32[]{:S(2)}) collective-permute-start(bf16[176,128]{1,0:T(8,128)(2,1)S(1)} %fusion.5), channel_id=1, source_target_pairs={{0,4},{4,0},{1,5},{5,1},{2,6},{6,2},{3,7},{7,3},{8,12},{12,8},{9,1... | collective-permute-start | bytes 135176 | tf_op jit(solution)/shard_map/ppermute | solution.py:29
  252.4 7.1 %collective-permute-done.22 = bf16[176,128]{1,0:T(8,128)(2,1)S(1)} collective-permute-done((bf16[176,128]{1,0:T(8,128)(2,1)S(1)}, bf16[176,128]{1,0:T(8,128)(2,1)S(1)}, u32[]{:S(2)}, u32[]{:S(2)}) %collective-permute-start.22) | collective-permute-done | bytes 45088 | tf_op jit(solution)/shard_map/ppermute | solution.py:29
  (97 shorter events, 17.0 us)
Async XLA Ops:
  0.0 11.5 %copy-start.11 = (bf16[128,1792]{1,0:T(8,128)(2,1)S(1)}, bf16[128,1792]{1,0:T(8,128)(2,1)}, u32[]{:S(2)}) copy-start(bf16[128,1792]{1,0:T(8,128)(2,1)} %param.12) | copy-start | bytes 1376260
  0.0 11.5 %copy-start.12 = (bf16[128,1792]{1,0:T(8,128)(2,1)S(1)}, bf16[128,1792]{1,0:T(8,128)(2,1)}, u32[]{:S(2)}) copy-start(bf16[128,1792]{1,0:T(8,128)(2,1)} %param.11) | copy-start | bytes 1376260
  2.2 18.1 %all-to-all-start = ((bf16[4,128,1024]{2,1,0:T(8,128)(2,1)}), bf16[4,128,1024]{2,1,0:T(8,128)(2,1)S(1)}, u32[]{:S(2)}, u32[]{:S(2)}) async-start(bf16[4,128,1024]{2,1,0:T(8,128)(2,1)} %broadcast_in_dim.34), calls=%async_computation | async-start | bytes 2097152 | tf_op jit(solution)/shard_map/all_to_all | solution.py:37
  11.5 10.7 %copy-start.13 = (bf16[176,128]{1,0:T(8,128)(2,1)S(1)}, bf16[176,128]{1,0:T(8,128)(2,1)}, u32[]{:S(2)}) copy-start(bf16[176,128]{1,0:T(8,128)(2,1)} %param.7) | copy-start | bytes 135172
  11.6 19.4 %collective-permute-start.8 = (bf16[128,1792]{1,0:T(8,128)(2,1)S(1)}, bf16[128,1792]{1,0:T(8,128)(2,1)S(1)}, u32[]{:S(2)}, u32[]{:S(2)}) collective-permute-start(bf16[128,1792]{1,0:T(8,128)(2,1)S(1)} %pad_maximum_fusion.1), channel_id=1, source_target_pairs={{0,8},{8,0},{1,9},{9,1},{2,10},{10,2},{3,11},{11,3},{4,12},{12,4},... | collective-permute-start | bytes 1376264 | tf_op jit(solution)/shard_map/ppermute | solution.py:29
  20.3 40.3 %copy-start = (bf16[4,128,1024]{2,1,0:T(8,128)(2,1)}, bf16[4,128,1024]{2,1,0:T(8,128)(2,1)S(1)}, u32[]{:S(2)}) copy-start(bf16[4,128,1024]{2,1,0:T(8,128)(2,1)S(1)} %all-to-all-done) | copy-start | bytes 3145732
  20.3 40.3 %collective-permute-start.3 = (bf16[512,1024]{1,0:T(8,128)(2,1)S(1)}, bf16[512,1024]{1,0:T(8,128)(2,1)S(1)}, u32[]{:S(2)}, u32[]{:S(2)}) collective-permute-start(bf16[512,1024]{1,0:T(8,128)(2,1)S(1)} %bitcast.40), channel_id=1, source_target_pairs={{0,64},{64,0},{1,65},{65,1},{2,66},{66,2},{3,67},{67,3},{4,68},{68... | collective-permute-start | bytes 3145736 | tf_op jit(solution)/shard_map/ppermute | solution.py:29
  22.2 19.9 %collective-permute-start = (bf16[1,176,128]{2,1,0:T(8,128)(2,1)S(1)}, bf16[1,176,128]{2,1,0:T(8,128)(2,1)S(1)}, u32[]{:S(2)}, u32[]{:S(2)}) collective-permute-start(bf16[1,176,128]{2,1,0:T(8,128)(2,1)S(1)} %bitcast.46), channel_id=1, source_target_pairs={{0,32},{8,40},{16,48},{24,56},{32,0},{40,8},{48,16},{56,24},{1,33}... | collective-permute-start | bytes 135176 | tf_op jit(solution)/shard_map/ppermute | solution.py:29
  31.0 0.8 copy-start.10
  32.8 32.4 %copy-start.1 = (bf16[256,1792]{1,0:T(8,128)(2,1)}, bf16[256,1792]{1,0:T(8,128)(2,1)S(1)}, u32[]{:S(2)}) copy-start(bf16[256,1792]{1,0:T(8,128)(2,1)S(1)} %pad_maximum_fusion.refs_0_) | copy-start | bytes 2752516
  32.9 43.6 %collective-permute-start.9 = (bf16[256,1792]{1,0:T(8,128)(2,1)S(1)}, bf16[256,1792]{1,0:T(8,128)(2,1)}, u32[]{:S(2)}, u32[]{:S(2)}) collective-permute-start(bf16[256,1792]{1,0:T(8,128)(2,1)S(1)} %pad_maximum_fusion.refs_0_), channel_id=1, source_target_pairs={{0,128},{128,256},{256,384},{384,0},{1,129},{129,257},{257,385},{3... | collective-permute-start | bytes 2752520 | tf_op jit(solution)/shard_map/ppermute | solution.py:24
  36.8 39.7 %collective-permute-start.10 = (bf16[256,1792]{1,0:T(8,128)(2,1)S(1)}, bf16[256,1792]{1,0:T(8,128)(2,1)}, u32[]{:S(2)}, u32[]{:S(2)}) collective-permute-start(bf16[256,1792]{1,0:T(8,128)(2,1)S(1)} %pad_maximum_fusion.refs_0_), channel_id=1, source_target_pairs={{0,256},{128,384},{256,0},{384,128},{1,257},{129,385},{257,1},{385... | collective-permute-start | bytes 2752520 | tf_op jit(solution)/shard_map/ppermute | solution.py:24
  38.8 43.4 %collective-permute-start.11 = (bf16[256,1792]{1,0:T(8,128)(2,1)S(1)}, bf16[256,1792]{1,0:T(8,128)(2,1)}, u32[]{:S(2)}, u32[]{:S(2)}) collective-permute-start(bf16[256,1792]{1,0:T(8,128)(2,1)S(1)} %pad_maximum_fusion.refs_0_), channel_id=1, source_target_pairs={{0,384},{128,0},{256,128},{384,256},{1,385},{129,1},{257,129},{385... | collective-permute-start | bytes 2752520 | tf_op jit(solution)/shard_map/ppermute | solution.py:24
  42.1 0.6 copy-start.14
  42.7 9.6 %collective-permute-start.1 = (bf16[2,176,128]{2,1,0:T(8,128)(2,1)S(1)}, bf16[2,176,128]{2,1,0:T(8,128)(2,1)S(1)}, u32[]{:S(2)}, u32[]{:S(2)}) collective-permute-start(bf16[2,176,128]{2,1,0:T(8,128)(2,1)S(1)} %pad_maximum_fusion.6), channel_id=1, source_target_pairs={{0,16},{8,24},{16,0},{24,8},{32,48},{40,56},{48,32},{56,40},{1,17}... | collective-permute-start | bytes 270344 | tf_op jit(solution)/shard_map/ppermute | solution.py:29
  52.4 8.3 %copy-start.15 = (bf16[2,176,128]{2,1,0:T(8,128)(2,1)}, bf16[2,176,128]{2,1,0:T(8,128)(2,1)S(1)}, u32[]{:S(2)}) copy-start(bf16[2,176,128]{2,1,0:T(8,128)(2,1)S(1)} %collective-permute-done.1.third) | copy-start | bytes 270340
  53.2 16.6 %copy-start.19 = (f32[128]{0:T(128)S(1)}, f32[128]{0:T(128)}, u32[]{:S(2)}) copy-start(f32[128]{0:T(128)} %param.10) | copy-start | bytes 1540
  53.2 7.4 %collective-permute-start.2 = (bf16[4,176,128]{2,1,0:T(8,128)(2,1)S(1)}, bf16[4,176,128]{2,1,0:T(8,128)(2,1)S(1)}, u32[]{:S(2)}, u32[]{:S(2)}) collective-permute-start(bf16[4,176,128]{2,1,0:T(8,128)(2,1)S(1)} %pad_maximum_fusion.3), channel_id=1, source_target_pairs={{0,8},{8,0},{16,24},{24,16},{32,40},{40,32},{48,56},{56,48},{1,9},... | collective-permute-start | bytes 540680 | tf_op jit(solution)/shard_map/ppermute | solution.py:29
  60.6 0.7 copy-start.17
  61.3 1.0 copy-start.5
  65.3 22.9 %all-to-all-start.1 = ((bf16[4,352,128]{2,1,0:T(8,128)(2,1)}), bf16[4,352,128]{2,1,0:T(8,128)(2,1)S(1)}, u32[]{:S(2)}, u32[]{:S(2)}) async-start(bf16[4,352,128]{2,1,0:T(8,128)(2,1)} %proj_mm.1), calls=%async_computation.1 | async-start | bytes 720896 | tf_op jit(solution)/shard_map/all_to_all | solution.py:37
  69.8 18.4 %copy-start.18 = (bf16[176,128]{1,0:T(8,128)(2,1)S(1)}, bf16[176,128]{1,0:T(8,128)(2,1)}, u32[]{:S(2)}) copy-start(bf16[176,128]{1,0:T(8,128)(2,1)} %param.8) | copy-start | bytes 135172
  86.2 64.0 %collective-permute-start.12 = (bf16[1024,1792]{1,0:T(8,128)(2,1)}, bf16[1024,1792]{1,0:T(8,128)(2,1)}, u32[]{:S(2)}, u32[]{:S(2)}) collective-permute-start(bf16[1024,1792]{1,0:T(8,128)(2,1)} %stack.54.own), channel_id=1, source_target_pairs={{0,64},{64,0},{1,65},{65,1},{2,66},{66,2},{3,67},{67,3},{4,68},{68... | collective-permute-start | bytes 11010056 | tf_op jit(solution)/shard_map/ppermute | solution.py:29
  88.4 15.8 %collective-permute-start.4 = (bf16[360,128]{1,0:T(8,128)(2,1)S(1)}, bf16[360,128]{1,0:T(8,128)(2,1)S(1)}, u32[]{:S(2)}, u32[]{:S(2)}) collective-permute-start(bf16[360,128]{1,0:T(8,128)(2,1)S(1)} %pad_maximum_fusion.5), channel_id=1, source_target_pairs={{0,4},{4,0},{1,5},{5,1},{2,6},{6,2},{3,7},{7,3},{8,12},{12,8},{9,1... | collective-permute-start | bytes 276488 | tf_op jit(solution)/shard_map/ppermute | solution.py:29
  99.4 18.0 %copy-start.6 = (bf16[224,1024]{1,0:T(8,128)(2,1)S(1)}, bf16[224,1024]{1,0:T(8,128)(2,1)}, u32[]{:S(2)}) copy-start(bf16[224,1024]{1,0:T(8,128)(2,1)} %refs_0_.1) | copy-start | bytes 1376260
  105.7 44.5 %all-to-all-start.2 = ((bf16[8,360,128]{2,1,0:T(8,128)(2,1)}), bf16[8,360,128]{2,1,0:T(8,128)(2,1)S(1)}, u32[]{:S(2)}, u32[]{:S(2)}) async-start(bf16[8,360,128]{2,1,0:T(8,128)(2,1)} %broadcast_in_dim.37), calls=%async_computation.2 | async-start | bytes 1474560 | tf_op jit(solution)/shard_map/all_to_all | solution.py:37
  117.4 15.3 %collective-permute-start.17 = (bf16[224,1024]{1,0:T(8,128)(2,1)S(1)}, bf16[224,1024]{1,0:T(8,128)(2,1)S(1)}, u32[]{:S(2)}, u32[]{:S(2)}) collective-permute-start(bf16[224,1024]{1,0:T(8,128)(2,1)S(1)} %copy-done.6), channel_id=1, source_target_pairs={{0,128},{128,256},{256,384},{384,0},{1,129},{129,257},{257,385},{3... | collective-permute-start | bytes 1376264 | tf_op jit(solution)/shard_map/ppermute | solution.py:24
  119.9 16.8 %collective-permute-start.18 = (bf16[224,1024]{1,0:T(8,128)(2,1)S(1)}, bf16[224,1024]{1,0:T(8,128)(2,1)S(1)}, u32[]{:S(2)}, u32[]{:S(2)}) collective-permute-start(bf16[224,1024]{1,0:T(8,128)(2,1)S(1)} %copy-done.6), channel_id=1, source_target_pairs={{0,256},{128,384},{256,0},{384,128},{1,257},{129,385},{257,1},{385... | collective-permute-start | bytes 1376264 | tf_op jit(solution)/shard_map/ppermute | solution.py:24
  122.1 22.5 %collective-permute-start.19 = (bf16[224,1024]{1,0:T(8,128)(2,1)S(1)}, bf16[224,1024]{1,0:T(8,128)(2,1)S(1)}, u32[]{:S(2)}, u32[]{:S(2)}) collective-permute-start(bf16[224,1024]{1,0:T(8,128)(2,1)S(1)} %copy-done.6), channel_id=1, source_target_pairs={{0,384},{128,0},{256,128},{384,256},{1,385},{129,1},{257,129},{385... | collective-permute-start | bytes 1376264 | tf_op jit(solution)/shard_map/ppermute | solution.py:24
  132.7 11.9 %copy-start.7 = (bf16[224,1024]{1,0:T(8,128)(2,1)}, bf16[224,1024]{1,0:T(8,128)(2,1)S(1)}, u32[]{:S(2)}) copy-start(bf16[224,1024]{1,0:T(8,128)(2,1)S(1)} %collective-permute-done.17.refs_1_) | copy-start | bytes 1376260
  136.8 7.9 %copy-start.8 = (bf16[224,1024]{1,0:T(8,128)(2,1)}, bf16[224,1024]{1,0:T(8,128)(2,1)S(1)}, u32[]{:S(2)}) copy-start(bf16[224,1024]{1,0:T(8,128)(2,1)S(1)} %collective-permute-done.18.refs_2_) | copy-start | bytes 1376260
  144.6 0.8 copy-start.9
  148.3 69.5 %collective-permute-start.20 = (bf16[896,1024]{1,0:T(8,128)(2,1)}, bf16[896,1024]{1,0:T(8,128)(2,1)S(1)}, u32[]{:S(2)}, u32[]{:S(2)}) collective-permute-start(bf16[896,1024]{1,0:T(8,128)(2,1)} %stack.55.own), channel_id=1, source_target_pairs={{0,64},{64,0},{1,65},{65,1},{2,66},{66,2},{3,67},{67,3},{4,68},{68... | collective-permute-start | bytes 5505032 | tf_op jit(solution)/shard_map/ppermute | solution.py:29
  150.2 0.9 copy-start.2
  156.2 19.7 %collective-permute-start.13 = (bf16[88,1792]{1,0:T(8,128)(2,1)}, bf16[88,1792]{1,0:T(8,128)(2,1)S(1)}, u32[]{:S(2)}, u32[]{:S(2)}) collective-permute-start(bf16[88,1792]{1,0:T(8,128)(2,1)} %get-tuple-element.16), channel_id=1, source_target_pairs={{0,16},{16,0},{32,48},{48,32},{1,17},{17,1},{33,49},{49,33},{2,18}... | collective-permute-start | bytes 946184 | tf_op jit(solution)/shard_map/ppermute | solution.py:29
  158.9 20.1 %collective-permute-start.7 = (f32[2,128]{1,0:T(2,128)S(1)}, f32[2,128]{1,0:T(2,128)S(1)}, u32[]{:S(2)}, u32[]{:S(2)}) collective-permute-start(f32[2,128]{1,0:T(2,128)S(1)} %slice_add_fusion.1), channel_id=1, source_target_pairs={{0,48},{16,32},{32,16},{48,0},{1,49},{17,33},{33,17},{49,1},{2,50}... | collective-permute-start | bytes 3080 | tf_op jit(solution)/shard_map/ppermute | solution.py:29
  160.8 18.2 %collective-permute-start.6 = (f32[2,128]{1,0:T(2,128)S(1)}, f32[2,128]{1,0:T(2,128)S(1)}, u32[]{:S(2)}, u32[]{:S(2)}) collective-permute-start(f32[2,128]{1,0:T(2,128)S(1)} %slice_add_fusion.1), channel_id=1, source_target_pairs={{0,32},{16,48},{32,0},{48,16},{1,33},{17,49},{33,1},{49,17},{2,34}... | collective-permute-start | bytes 3080 | tf_op jit(solution)/shard_map/ppermute | solution.py:29
  169.2 9.8 %collective-permute-start.5 = (f32[2,128]{1,0:T(2,128)S(1)}, f32[2,128]{1,0:T(2,128)S(1)}, u32[]{:S(2)}, u32[]{:S(2)}) collective-permute-start(f32[2,128]{1,0:T(2,128)S(1)} %slice_add_fusion.1), channel_id=1, source_target_pairs={{0,16},{16,0},{32,48},{48,32},{1,17},{17,1},{33,49},{49,33},{2,18}... | collective-permute-start | bytes 3080 | tf_op jit(solution)/shard_map/ppermute | solution.py:29
  177.1 21.1 %collective-permute-start.14 = (bf16[48,1792]{1,0:T(8,128)(2,1)S(1)}, bf16[48,1792]{1,0:T(8,128)(2,1)S(1)}, u32[]{:S(2)}, u32[]{:S(2)}) collective-permute-start(bf16[48,1792]{1,0:T(8,128)(2,1)S(1)} %dynamic-slice_convert_fusion), channel_id=1, source_target_pairs={{0,32},{16,48},{32,0},{48,16},{1,33},{17,49},{33,1},{49,17},{2,34}... | collective-permute-start | bytes 516104 | tf_op jit(solution)/shard_map/ppermute | solution.py:29
  198.4 10.3 %collective-permute-start.15 = (bf16[48,896]{1,0:T(8,128)(2,1)S(1)}, bf16[48,896]{1,0:T(8,128)(2,1)S(1)}, u32[]{:S(2)}, u32[]{:S(2)}) collective-permute-start(bf16[48,896]{1,0:T(8,128)(2,1)S(1)} %fusion.2), channel_id=1, source_target_pairs={{0,32},{16,48},{32,0},{48,16},{1,33},{17,49},{33,1},{49,17},{2,34}... | collective-permute-start | bytes 258056 | tf_op jit(solution)/shard_map/ppermute | solution.py:29
  208.8 8.9 %collective-permute-start.16 = (bf16[88,896]{1,0:T(8,128)(2,1)S(1)}, bf16[88,896]{1,0:T(8,128)(2,1)S(1)}, u32[]{:S(2)}, u32[]{:S(2)}) collective-permute-start(bf16[88,896]{1,0:T(8,128)(2,1)S(1)} %pad_maximum_fusion.4), channel_id=1, source_target_pairs={{0,16},{16,0},{32,48},{48,32},{1,17},{17,1},{33,49},{49,33},{2,18}... | collective-permute-start | bytes 473096 | tf_op jit(solution)/shard_map/ppermute | solution.py:29
  217.8 2.0 copy-start.4
  217.8 2.0 copy-start.3
  217.8 10.5 %collective-permute-start.21 = (bf16[176,896]{1,0:T(8,128)(2,1)S(1)}, bf16[176,896]{1,0:T(8,128)(2,1)S(1)}, u32[]{:S(2)}, u32[]{:S(2)}) collective-permute-start(bf16[176,896]{1,0:T(8,128)(2,1)S(1)} %pad_maximum_fusion.2.x), channel_id=1, source_target_pairs={{0,8},{8,0},{1,9},{9,1},{2,10},{10,2},{3,11},{11,3},{4,12},{12,4},... | collective-permute-start | bytes 946184 | tf_op jit(solution)/shard_map/ppermute | solution.py:29
  228.3 0.7 copy-start.16
  232.2 12.1 %all-to-all-start.3 = ((bf16[4,352,128]{2,1,0:T(8,128)(2,1)}), bf16[4,352,128]{2,1,0:T(8,128)(2,1)S(1)}, u32[]{:S(2)}, u32[]{:S(2)}) async-start(bf16[4,352,128]{2,1,0:T(8,128)(2,1)} %far_mm.1), calls=%async_computation.3 | async-start | bytes 720896 | tf_op jit(solution)/shard_map/all_to_all | solution.py:37
  244.3 15.1 %collective-permute-start.22 = (bf16[176,128]{1,0:T(8,128)(2,1)S(1)}, bf16[176,128]{1,0:T(8,128)(2,1)S(1)}, u32[]{:S(2)}, u32[]{:S(2)}) collective-permute-start(bf16[176,128]{1,0:T(8,128)(2,1)S(1)} %fusion.5), channel_id=1, source_target_pairs={{0,4},{4,0},{1,5},{5,1},{2,6},{6,2},{3,7},{7,3},{8,12},{12,8},{9,1... | collective-permute-start | bytes 135176 | tf_op jit(solution)/shard_map/ppermute | solution.py:29
